TPU v7x, 16 devices: a whole 2x2x2 slice. The times are simulated.
16 devices in a mesh: tp: 4 (over z, y), dp: 4 (over x, core).
Axes of the slice: x: 2, y: 2, z: 2, core: 2. Of those that a mesh axis runs over, the one named last changes fastest.
Arguments:
- tok_ids: int32 [32, 1024], P('dp')
- emb_table: bfloat16 [50272, 1024], P('tp')
- pos_table: bfloat16 [2050, 1024], replicated
- ln1_gain: bfloat16 [1024], replicated
- ln1_bias: bfloat16 [1024], replicated
- w_qkv: bfloat16 [1024, 3, 16, 64], P(None, None, 'tp')
- b_qkv: bfloat16 [3, 16, 64], P(None, 'tp')
- w_out: bfloat16 [16, 64, 1024], P('tp')
- b_out: bfloat16 [1024], replicated
- ln2_gain: bfloat16 [1024], replicated
- ln2_bias: bfloat16 [1024], replicated
- w_up: bfloat16 [1024, 4096], P(None, 'tp')
- b_up: bfloat16 [4096], P('tp')
- w_down: bfloat16 [4096, 1024], P('tp')
- b_down: bfloat16 [1024], replicated
- out_grad: bfloat16 [32, 1024, 1024], P('dp', 'tp')
Outputs:
- output 1: bfloat16 [32, 1024, 1024], P('dp', 'tp')
- output 2: float32 [50272, 1024], P('tp')
- output 3: float32 [2050, 1024], replicated
- output 4: float32 [1024], replicated
- output 5: float32 [1024], replicated
- output 6: float32 [1024, 3, 16, 64], P(None, None, 'tp')
- output 7: float32 [3, 16, 64], P(None, 'tp')
- output 8: float32 [16, 64, 1024], P('tp')
- output 9: float32 [1024], replicated
- output 10: float32 [1024], replicated
- output 11: float32 [1024], replicated
- output 12: float32 [1024, 4096], P(None, 'tp')
- output 13: float32 [4096], P('tp')
- output 14: float32 [4096, 1024], P('tp')
- output 15: float32 [1024], replicated
All inputs are finite; a program needn't handle non-finite values.
Results may differ from a plain program's by a relative error of at most 0.0153794.
Values are sent between devices in bfloat16 or wider.
A program may use at most 1 GiB of HBM per device.

v0:
```python
import jax
import jax.numpy as jnp
from jax import lax
from jax.sharding import PartitionSpec as P

POS_OFFSET = 2
LN_EPS = 1e-5


def norm_forward(x_in, ln_gain, ln_shift):
    row_mean = jnp.mean(x_in, axis=-1, keepdims=True)
    centered = x_in - row_mean
    inv_std = lax.rsqrt(jnp.mean(centered * centered, axis=-1, keepdims=True) + LN_EPS)
    normed = centered * inv_std
    return normed * ln_gain + ln_shift, normed, inv_std


def norm_backward(d_y, normed, inv_std, ln_gain):
    d_norm = d_y * ln_gain
    d_x = inv_std * (d_norm - jnp.mean(d_norm, axis=-1, keepdims=True)
                     - normed * jnp.mean(d_norm * normed, axis=-1, keepdims=True))
    return d_x, jnp.sum(d_y * normed, axis=(0, 1)), jnp.sum(d_y, axis=(0, 1))


def solution(mesh):
    tp_size = mesh.shape["tp"]

    def local_step(tok_ids, emb_table, pos_table, ln1_gain, ln1_bias, w_qkv, b_qkv, w_out, b_out,
                   ln2_gain, ln2_bias, w_up, b_up, w_down, b_down, out_grad):
        tp_index = lax.axis_index("tp")
        seq_len = tok_ids.shape[1]
        vocab_local, d_model = emb_table.shape
        seq_local = seq_len // tp_size
        pos_rows = pos_table.shape[0]
        attn_scale = w_qkv.shape[3] ** -0.5
        gain_one = ln1_gain.astype(jnp.float32)
        gain_two = ln2_gain.astype(jnp.float32)

        local_ids = tok_ids - tp_index * vocab_local
        is_owned = (local_ids >= 0) & (local_ids < vocab_local)
        emb_rows = jnp.take(emb_table, jnp.where(is_owned, local_ids, 0), axis=0)
        emb_rows = jnp.where(is_owned[:, :, None], emb_rows, jnp.zeros((), jnp.bfloat16))
        embedded = lax.psum_scatter(emb_rows, "tp", scatter_dimension=1, tiled=True)
        pos_here = lax.dynamic_slice_in_dim(pos_table, POS_OFFSET + tp_index * seq_local, seq_local, axis=0)
        resid_x = embedded.astype(jnp.float32) + pos_here.astype(jnp.float32)[None]

        ln1_y, normed1, inv_std1 = norm_forward(resid_x, gain_one, ln1_bias.astype(jnp.float32))
        hid1_full = lax.all_gather(ln1_y.astype(jnp.bfloat16), "tp", axis=1, tiled=True)
        qkv_heads = (jnp.einsum("bsd,djhe->jbhse", hid1_full, w_qkv, preferred_element_type=jnp.float32)
                     + b_qkv.astype(jnp.float32)[:, None, :, None, :]).astype(jnp.bfloat16)
        q_heads, k_heads, v_heads = qkv_heads[0], qkv_heads[1], qkv_heads[2]
        scores = jnp.einsum("bhqe,bhke->bhqk", q_heads, k_heads, preferred_element_type=jnp.float32) * attn_scale
        causal = lax.broadcasted_iota(jnp.int32, (seq_len, seq_len), 0) >= lax.broadcasted_iota(jnp.int32, (seq_len, seq_len), 1)
        attn_probs = jax.nn.softmax(jnp.where(causal, scores, -1e30), axis=-1)
        probs_bf = attn_probs.astype(jnp.bfloat16)
        context = jnp.einsum("bhqk,bhke->bqhe", probs_bf, v_heads, preferred_element_type=jnp.float32).astype(jnp.bfloat16)
        attn_part = jnp.einsum("crif,ife->cre", context, w_out, preferred_element_type=jnp.float32).astype(jnp.bfloat16)
        attn_out = lax.psum_scatter(attn_part, "tp", scatter_dimension=1, tiled=True)
        resid_x1 = resid_x + attn_out.astype(jnp.float32) + b_out.astype(jnp.float32)

        ln2_y, normed2, inv_std2 = norm_forward(resid_x1, gain_two, ln2_bias.astype(jnp.float32))
        hid2_full = lax.all_gather(ln2_y.astype(jnp.bfloat16), "tp", axis=1, tiled=True)
        up_pre = jnp.einsum("bsd,df->bsf", hid2_full, w_up, preferred_element_type=jnp.float32) + b_up.astype(jnp.float32)
        act_f32, gelu_pull = jax.vjp(jax.nn.gelu, up_pre)
        act_bf = act_f32.astype(jnp.bfloat16)
        down_part = jnp.einsum("bsf,fd->bsd", act_bf, w_down, preferred_element_type=jnp.float32).astype(jnp.bfloat16)
        down_out = lax.psum_scatter(down_part, "tp", scatter_dimension=1, tiled=True)
        layer_out = (resid_x1 + down_out.astype(jnp.float32) + b_down.astype(jnp.float32)).astype(jnp.bfloat16)

        d_out32 = out_grad.astype(jnp.float32)
        grad_full = lax.all_gather(out_grad, "tp", axis=1, tiled=True)
        d_w_down = jnp.einsum("bsf,bsd->fd", act_bf, grad_full, preferred_element_type=jnp.float32)
        d_act = jnp.einsum("bsd,fd->bsf", grad_full, w_down, preferred_element_type=jnp.float32)
        d_up = gelu_pull(d_act)[0]
        d_up_bf = d_up.astype(jnp.bfloat16)
        d_w_up = jnp.einsum("bsd,bsf->df", hid2_full, d_up_bf, preferred_element_type=jnp.float32)
        d_hid2_part = jnp.einsum("bsf,df->bsd", d_up_bf, w_up, preferred_element_type=jnp.float32).astype(jnp.bfloat16)
        d_hid2 = lax.psum_scatter(d_hid2_part, "tp", scatter_dimension=1, tiled=True)
        d_ln2_in, d_ln2_gain, d_ln2_bias = norm_backward(d_hid2.astype(jnp.float32), normed2, inv_std2, gain_two)
        d_resid1 = d_out32 + d_ln2_in

        d_attn_full = lax.all_gather(d_resid1.astype(jnp.bfloat16), "tp", axis=1, tiled=True)
        d_w_out = jnp.einsum("crif,cre->ife", context, d_attn_full, preferred_element_type=jnp.float32)
        d_context = jnp.einsum("cre,ife->cirf", d_attn_full, w_out, preferred_element_type=jnp.float32).astype(jnp.bfloat16)
        d_probs = jnp.einsum("bhqe,bhke->bhqk", d_context, v_heads, preferred_element_type=jnp.float32)
        d_v = jnp.einsum("bhqk,bhqe->bhke", probs_bf, d_context, preferred_element_type=jnp.float32)
        d_scores = attn_probs * (d_probs - jnp.sum(d_probs * attn_probs, axis=-1, keepdims=True)) * attn_scale
        d_scores_bf = d_scores.astype(jnp.bfloat16)
        d_q = jnp.einsum("bhqk,bhke->bhqe", d_scores_bf, k_heads, preferred_element_type=jnp.float32)
        d_k = jnp.einsum("bhqk,bhqe->bhke", d_scores_bf, q_heads, preferred_element_type=jnp.float32)
        d_qkv = jnp.stack([d_q, d_k, d_v])
        d_qkv_bf = d_qkv.astype(jnp.bfloat16)
        d_w_qkv = jnp.einsum("bsd,jbhse->djhe", hid1_full, d_qkv_bf, preferred_element_type=jnp.float32)
        d_hid1_part = jnp.einsum("jbhse,djhe->bsd", d_qkv_bf, w_qkv, preferred_element_type=jnp.float32).astype(jnp.bfloat16)
        d_hid1 = lax.psum_scatter(d_hid1_part, "tp", scatter_dimension=1, tiled=True)
        d_ln1_in, d_ln1_gain, d_ln1_bias = norm_backward(d_hid1.astype(jnp.float32), normed1, inv_std1, gain_one)
        d_resid = d_resid1 + d_ln1_in

        d_pos_local = lax.psum(jnp.sum(d_resid, axis=0), "dp")
        d_pos_seq = lax.all_gather(d_pos_local, "tp", axis=0, tiled=True)
        d_pos = jnp.pad(d_pos_seq, ((POS_OFFSET, pos_rows - seq_len - POS_OFFSET), (0, 0)))

        d_tok_full = lax.all_gather(d_resid, "tp", axis=1, tiled=True)
        seg_ids = jnp.where(is_owned, local_ids, vocab_local).reshape(-1)
        d_emb = jax.ops.segment_sum(d_tok_full.reshape(-1, d_model), seg_ids, num_segments=vocab_local)

        small_sums = lax.psum(jnp.stack([d_ln1_gain, d_ln1_bias, jnp.sum(d_resid1, axis=(0, 1)),
                                         d_ln2_gain, d_ln2_bias, jnp.sum(d_out32, axis=(0, 1))]), ("tp", "dp"))
        d_emb, d_w_qkv, d_b_qkv, d_w_out, d_w_up, d_b_up, d_w_down = lax.psum(
            (d_emb, d_w_qkv, jnp.sum(d_qkv, axis=(1, 3)), d_w_out, d_w_up, jnp.sum(d_up, axis=(0, 1)), d_w_down), "dp")
        return (layer_out, d_emb, d_pos, small_sums[0], small_sums[1], d_w_qkv, d_b_qkv, d_w_out,
                small_sums[2], small_sums[3], small_sums[4], d_w_up, d_b_up, d_w_down, small_sums[5])

    replicated = P()
    in_specs = (P("dp", None), P("tp", None), replicated, replicated, replicated,
                P(None, None, "tp", None), P(None, "tp", None), P("tp", None, None), replicated,
                replicated, replicated, P(None, "tp"), P("tp"), P("tp", None), replicated,
                P("dp", "tp", None))
    out_specs = (P("dp", "tp", None), P("tp", None), replicated, replicated, replicated,
                 P(None, None, "tp", None), P(None, "tp", None), P("tp", None, None), replicated,
                 replicated, replicated, P(None, "tp"), P("tp"), P("tp", None), replicated)
    return jax.shard_map(local_step, mesh=mesh, in_specs=in_specs, out_specs=out_specs, check_vma=False)
```

profile of v0, /device:TPU:0, one launch (start us, length us, event | category | flops | bytes accessed | tf_op | source)
XLA Modules:
  0.0 3588.5 jit_solution(12673564249268118801)
XLA Ops:
  9.6 52.1 %gather_fusion = bf16[8192,1024]{1,0:T(8,128)(2,1)} fusion(bf16[12568,1024]{1,0:T(8,128)(2,1)} %param.17, s32[8192]{0:T(1024)S(1)} %bitcast_clamp_fusion), kind=kCustom, calls=%fused_computation | custom fusion | bytes 33587200 | tf_op jit(solution)/shard_map/jit(_take)/gather | solution.py:41
  78.2 150.9 %reduce-scatter.6.cloned.1.call-done = bf16[8,256,1024]{2,1,0:T(8,128)(2,1)} async-done(((bf16[8,1024,1024]{2,1,0:T(8,128)(2,1)}), bf16[8,256,1024]{2,1,0:T(8,128)(2,1)}) %reduce-scatter.6.cloned.1.call-update) | async-done | bytes 4194320 | tf_op jit(solution)/shard_map/reduce_scatter | solution.py:43
  240.2 153.0 %all-gather.7.cloned.1.call-done = bf16[8,1024,1024]{2,1,0:T(8,128)(2,1)} async-done(((bf16[8,256,1024]{2,1,0:T(8,128)(2,1)}), bf16[8,1024,1024]{2,1,0:T(8,128)(2,1)}) %all-gather.7.cloned.1.call-update) | async-done | bytes 16777232 | tf_op jit(solution)/shard_map/all_gather | solution.py:48
  413.3 55.9 %fusion.121 = (f32[8,4,1024]{2,1,0:T(4,128)S(1)}, f32[8,4,1024,1024]{2,3,1,0:T(8,128)}) fusion(pred[1024,1024]{0,1:T(8,128)(4,1)S(1)} %iota_compare_fusion, bf16[3,8,4,1024,64]{3,4,2,0,1:T(8,128)(2,1)} %fusion.39), kind=kOutput, calls=%fused_computation.142 | convolution fusion | flops 4429186048 | bytes 143785984 | tf_op jit(solution)/shard_map/sub | solution.py:54
  469.2 44.7 %fusion.83 = bf16[8,4,64,1024]{3,2,1,0:T(8,128)(2,1)} fusion(bf16[3,8,4,1024,64]{3,4,2,0,1:T(8,128)(2,1)} %fusion.39, f32[8,4,1024,1024]{2,3,1,0:T(8,128)} %get-tuple-element.49, f32[8,4,1024]{2,1,0:T(4,128)S(1)} %get-tuple-element.48), kind=kOutput, calls=%fused_computation.101 | convolution fusion | flops 4364173312 | bytes 142737408 | tf_op jit(solution)/shard_map/bhqk,bhke->bqhe/dot_general | solution.py:56
  525.4 149.2 %reduce-scatter.8.cloned.1.call-done = bf16[8,256,1024]{2,1,0:T(8,128)(2,1)} async-done(((bf16[8,1024,1024]{2,1,0:T(8,128)(2,1)}), bf16[8,256,1024]{2,1,0:T(8,128)(2,1)}) %reduce-scatter.8.cloned.1.call-update) | async-done | bytes 4194320 | tf_op jit(solution)/shard_map/reduce_scatter | solution.py:58
  687.8 153.1 %all-gather.9.cloned.1.call-done = bf16[8,1024,1024]{2,1,0:T(8,128)(2,1)} async-done(((bf16[8,256,1024]{2,1,0:T(8,128)(2,1)}), bf16[8,1024,1024]{2,1,0:T(8,128)(2,1)}) %all-gather.9.cloned.1.call-update) | async-done | bytes 16777232 | tf_op jit(solution)/shard_map/all_gather | solution.py:62
  867.3 128.9 %all-gather.11.cloned.1.call-done = bf16[8,1024,1024]{2,1,0:T(8,128)(2,1)} async-done(((bf16[8,256,1024]{2,1,0:T(8,128)(2,1)}), bf16[8,1024,1024]{2,1,0:T(8,128)(2,1)}) %all-gather.11.cloned.1.call-update) | async-done | bytes 16777232 | tf_op jit(solution)/shard_map/all_gather | solution.py:71
  996.2 47.4 %fusion.122 = (f32[1024]{0:T(1024)}, bf16[8,1024,1024]{2,1,0:T(8,128)(2,1)}) fusion(f32[8,1024,1024]{2,1,0:T(8,128)} %fusion.92, f32[1024]{0:T(1024)S(1)} %convert_element_type.121, bf16[8,1024,1024]{2,1,0:T(8,128)(2,1)} %all-gather.11.cloned.1.call-done, bf16[1024,1024]{1,0:T(8,128)(2,1)S(1)} %copy-done), kind=kOutput, calls=%fused_computation.143 | convolution fusion | flops 17364418560 | bytes 69214208 | tf_op jit(solution)/shard_map/bsd,fd->bsf/dot_general | solution.py:73
  1043.7 26.6 convolution_convert_fusion
  1070.4 149.9 %reduce-scatter.12.cloned.1.call-done = bf16[8,256,1024]{2,1,0:T(8,128)(2,1)} async-done(((bf16[8,1024,1024]{2,1,0:T(8,128)(2,1)}), bf16[8,256,1024]{2,1,0:T(8,128)(2,1)}) %reduce-scatter.12.cloned.1.call-update) | async-done | bytes 4194320 | tf_op jit(solution)/shard_map/reduce_scatter | solution.py:78
  1236.0 30.4 convolution_convert_fusion.1
  1266.5 123.2 %all-gather.13.cloned.1.call-done = bf16[8,1024,1024]{2,1,0:T(8,128)(2,1)} async-done(((bf16[8,256,1024]{2,1,0:T(8,128)(2,1)}), bf16[8,1024,1024]{2,1,0:T(8,128)(2,1)}) %all-gather.13.cloned.1.call-update) | async-done | bytes 16777232 | tf_op jit(solution)/shard_map/all_gather | solution.py:82
  1408.3 46.9 %fusion.64 = f32[8,4,1024,1024]{2,3,1,0:T(8,128)} fusion(bf16[8,1024,4,64]{1,3,2,0:T(8,128)(2,1)} %fusion.80, bf16[3,8,4,1024,64]{3,4,2,0,1:T(8,128)(2,1)} %fusion.39), kind=kOutput, calls=%fused_computation.91 | convolution fusion | flops 4294967296 | bytes 142606336 | tf_op jit(solution)/shard_map/bhqe,bhke->bhqk/dot_general | solution.py:85
  1455.2 163.3 %fusion.73 = f32[1,8,4,1024,64]{3,4,2,1,0:T(8,128)} fusion(f32[8,4,1024,1024]{2,3,1,0:T(8,128)} %fusion.64, bf16[3,8,4,1024,64]{3,4,2,0,1:T(8,128)(2,1)} %fusion.39, f32[8,4,1024,1024]{2,3,1,0:T(8,128)} %get-tuple-element.49, f32[8,4,1024]{2,1,0:T(4,128)S(1)} %copy-done.55), kind=kOutput, calls=%fused_computation.97 | convolution fusion | flops 4529882112 | bytes 549715968 | tf_op jit(solution)/shard_map/bhqk,bhke->bhqe/dot_general | solution.py:89
  1618.5 163.3 %fusion.76 = f32[1,8,4,1024,64]{3,4,2,1,0:T(8,128)} fusion(f32[8,4,1024,1024]{2,3,1,0:T(8,128)} %fusion.64, bf16[3,8,4,1024,64]{3,4,2,0,1:T(8,128)(2,1)} %fusion.39, f32[8,4,1024,1024]{2,3,1,0:T(8,128)} %get-tuple-element.49, f32[8,4,1024]{2,1,0:T(4,128)S(1)} %copy-done.55), kind=kOutput, calls=%fused_computation.98 | convolution fusion | flops 4529882112 | bytes 549715968 | tf_op jit(solution)/shard_map/bhqk,bhqe->bhke/dot_general | solution.py:90
  1781.8 47.8 %fusion.68 = f32[1,8,4,1024,64]{3,4,2,1,0:T(8,128)} fusion(bf16[8,1024,4,64]{1,3,2,0:T(8,128)(2,1)} %fusion.80, f32[8,4,1024,1024]{2,3,1,0:T(8,128)} %get-tuple-element.49, f32[8,4,1024]{2,1,0:T(4,128)S(1)} %copy-done.55), kind=kOutput, calls=%fused_computation.96 | convolution fusion | flops 4362076160 | bytes 146931712 | tf_op jit(solution)/shard_map/bhqk,bhqe->bhke/dot_general | solution.py:86
  1850.3 149.4 %reduce-scatter.14.cloned.1.call-done = bf16[8,256,1024]{2,1,0:T(8,128)(2,1)} async-done(((bf16[8,1024,1024]{2,1,0:T(8,128)(2,1)}), bf16[8,256,1024]{2,1,0:T(8,128)(2,1)}) %reduce-scatter.14.cloned.1.call-update) | async-done | bytes 4194320 | tf_op jit(solution)/shard_map/reduce_scatter | solution.py:95
  2052.2 29.1 convolution_bitcast_fusion
  2114.5 206.5 %all-gather.15.cloned.1.call-done = f32[8,1024,1024]{2,1,0:T(8,128)} async-done(((f32[8,256,1024]{2,1,0:T(8,128)}), f32[8,1024,1024]{2,1,0:T(8,128)}) %all-gather.15.cloned.1.call-update) | async-done | bytes 33554448 | tf_op jit(solution)/shard_map/all_gather | solution.py:103
  2321.0 92.0 %scatter_custom_fusion = f32[12568,1024]{1,0:T(8,128)} fusion(s32[8192]{0:T(1024)S(1)} %bitcast.162, f32[8192,1024]{1,0:T(8,128)} %bitcast.175, f32[]{:T(128)} %constant.57.clone.1), kind=kCustom, calls=%fused_computation.31 | custom fusion | flops 8388608 | bytes 51479040 | tf_op jit(solution)/shard_map/scatter-add | solution.py:105
  2413.1 1061.9 %all-reduce.5.cloned.1.call-done = (f32[12568,1024]{1,0:T(8,128)}, f32[256,1024]{1,0:T(8,128)}, f32[1024,3,4,64]{0,3,2,1:T(8,128)}, f32[4,64,1024]{2,1,0:T(8,128...) async-done(((f32[12568,1024]{1,0:T(8,128)}, f32[256,1024]{1,0:T(8,128)}, f32[1024,3,4,64]{0,3,2,1:T(8,128)}, f32[4,64,1024]{2,1,0:T(8,128)}, f32[1024,1024]{1,0:T(8,128)}, ...) | async-done | bytes 65110032 | tf_op jit(solution)/shard_map/psum | solution.py:109
  3495.3 33.3 psum.65
  3536.2 35.9 copy.79
  (187 shorter events, 278.4 us)
Async XLA Ops:
  7.2 989.0 %copy-start = (bf16[1024,1024]{1,0:T(8,128)(2,1)S(1)}, bf16[1024,1024]{1,0:T(8,128)(2,1)}, u32[]{:S(2)}) copy-start(bf16[1024,1024]{1,0:T(8,128)(2,1)} %param.29) | copy-start | bytes 6291460
  7.2 221.8 %reduce-scatter.6.cloned.1.call-start = ((), (), s32[]{:S(2)}) async-start(), calls=%async_computation.5 | async-start | bytes 20971520 | tf_op jit(solution)/shard_map/reduce_scatter | solution.py:43
  76.3 316.9 %all-gather.7.cloned.1.call-start = ((), (), s32[]{:S(2)}) async-start(), calls=%async_computation.6 | async-start | bytes 20971520 | tf_op jit(solution)/shard_map/all_gather | solution.py:48
  76.9 162.4 %copy-start.36 = (f32[1024]{0:T(1024)}, f32[1024]{0:T(1024)S(1)}, u32[]{:S(2)}) copy-start(f32[1024]{0:T(1024)S(1)} %convert_element_type.106) | copy-start | bytes 12292
  78.1 161.2 %copy-start.9 = (f32[256,1024]{1,0:T(8,128)}, f32[256,1024]{1,0:T(8,128)S(1)}, u32[]{:S(2)}) copy-start(f32[256,1024]{1,0:T(8,128)S(1)} %dynamic-slice_convert_fusion) | copy-start | bytes 3145732
  239.4 435.3 %reduce-scatter.8.cloned.1.call-start = ((), (), s32[]{:S(2)}) async-start(), calls=%async_computation.7 | async-start | bytes 20971520 | tf_op jit(solution)/shard_map/reduce_scatter | solution.py:58
  524.8 316.1 %all-gather.9.cloned.1.call-start = ((), (), s32[]{:S(2)}) async-start(), calls=%async_computation.8 | async-start | bytes 20971520 | tf_op jit(solution)/shard_map/all_gather | solution.py:62
  525.4 701.7 %copy-start.23 = (f32[1024]{0:T(1024)}, f32[1024]{0:T(1024)S(1)}, u32[]{:S(2)}) copy-start(f32[1024]{0:T(1024)S(1)} %convert_element_type.117) | copy-start | bytes 12292
  525.4 701.6 %copy-start.27 = (f32[1024]{0:T(1024)}, f32[1024]{0:T(1024)S(1)}, u32[]{:S(2)}) copy-start(f32[1024]{0:T(1024)S(1)} %convert_element_type.118) | copy-start | bytes 12292
  680.6 546.5 %copy-start.19 = (f32[8,256]{1,0:T(8,128)}, f32[8,256]{1,0:T(8,128)S(1)}, u32[]{:S(2)}) copy-start(f32[8,256]{1,0:T(8,128)S(1)} %broadcast_multiply_fusion.4) | copy-start | bytes 24580
  683.0 544.1 %copy-start.21 = (f32[8,256]{1,0:T(8,128)}, f32[8,256]{1,0:T(8,128)S(1)}, u32[]{:S(2)}) copy-start(f32[8,256]{1,0:T(8,128)S(1)} %add_rsqrt_fusion) | copy-start | bytes 24580
  687.1 309.1 %all-gather.11.cloned.1.call-start = ((), (), s32[]{:S(2)}) async-start(), calls=%async_computation.10 | async-start | bytes 20971520 | tf_op jit(solution)/shard_map/all_gather | solution.py:71
  687.7 532.6 %reduce-scatter.12.cloned.1.call-start = ((), (), s32[]{:S(2)}) async-start(), calls=%async_computation.11 | async-start | bytes 20971520 | tf_op jit(solution)/shard_map/reduce_scatter | solution.py:78
  687.7 548.3 %copy-start.38 = (f32[1024]{0:T(1024)}, f32[1024]{0:T(1024)S(1)}, u32[]{:S(2)}) copy-start(f32[1024]{0:T(1024)S(1)} %convert_element_type.121) | copy-start | bytes 12292
  1070.3 319.4 %all-gather.13.cloned.1.call-start = ((), (), s32[]{:S(2)}) async-start(), calls=%async_computation.12 | async-start | bytes 20971520 | tf_op jit(solution)/shard_map/all_gather | solution.py:82
  1236.0 614.3 %reduce-scatter.10.cloned.1.call-start = ((), (), s32[]{:S(2)}) async-start(), calls=%async_computation.9 | async-start | bytes 20971520 | tf_op jit(solution)/shard_map/reduce_scatter | solution.py:67
  1266.5 733.2 %reduce-scatter.14.cloned.1.call-start = ((), (), s32[]{:S(2)}) async-start(), calls=%async_computation.13 | async-start | bytes 20971520 | tf_op jit(solution)/shard_map/reduce_scatter | solution.py:95
  1849.6 150.1 %copy-start.11 = (f32[256,1024]{1,0:T(8,128)S(1)}, f32[256,1024]{1,0:T(8,128)}, u32[]{:S(2)}) copy-start(f32[256,1024]{1,0:T(8,128)} %copy-done.9) | copy-start | bytes 3145732
  1849.6 150.1 %copy-start.20 = (f32[8,256]{1,0:T(8,128)S(1)}, f32[8,256]{1,0:T(8,128)}, u32[]{:S(2)}) copy-start(f32[8,256]{1,0:T(8,128)} %copy-done.19) | copy-start | bytes 24580
  1849.6 150.1 %copy-start.22 = (f32[8,256]{1,0:T(8,128)S(1)}, f32[8,256]{1,0:T(8,128)}, u32[]{:S(2)}) copy-start(f32[8,256]{1,0:T(8,128)} %copy-done.21) | copy-start | bytes 24580
  1849.6 150.0 %copy-start.24 = (f32[1024]{0:T(1024)S(1)}, f32[1024]{0:T(1024)}, u32[]{:S(2)}) copy-start(f32[1024]{0:T(1024)} %copy-done.23) | copy-start | bytes 12292
  1849.7 471.3 %all-gather.15.cloned.1.call-start = ((), (), s32[]{:S(2)}) async-start(), calls=%async_computation.14 | async-start | bytes 41943040 | tf_op jit(solution)/shard_map/all_gather | solution.py:103
  2027.4 1447.6 %all-reduce.5.cloned.1.call-start = ((), (), s32[]{:S(2)}) async-start(), calls=%async_computation.16 | async-start | bytes 130220032 | tf_op jit(solution)/shard_map/psum | solution.py:109
  2413.1 1116.1 %all-gather.17.cloned.1.call-start = ((), (), s32[]{:S(2)}) async-start(), calls=%async_computation.15 | async-start | bytes 5242880 | tf_op jit(solution)/shard_map/all_gather | solution.py:100
  (44 other events, 1676.3 us)
Sparse Core Ops, SparseCore 0:
  76.4 152.5 reduce-scatter.5
  239.5 153.6 all-gather.6
  524.9 149.7 reduce-scatter.7
  687.2 153.6 all-gather.8
  842.5 153.6 all-gather.10
  1070.4 149.7 reduce-scatter.11
  1236.1 153.6 all-gather.12
  1392.8 149.7 reduce-scatter.9
  1849.8 149.7 reduce-scatter.13
  2027.5 293.3 all-gather.14
  2413.2 1061.8 all-reduce.4
  3476.7 49.5 all-gather.16
where the time goes:
time: 3600 us; the launch traced here: 3590 us
  waiting for transfers between devices  2430 us (68%)
  matrix products  809 us (22%)
  other arithmetic  182 us (5%)
  local copies, waits for them, and re-layouts  110 us (3%)
  blocking collectives  44.8 us (1%)
    psum x1, waiting for transfers between devices, local_step(): lax.psum((d_emb, d_w_qkv, jnp.sum(d_qkv, axis=(1, 3)), d_w_out, d_w_up, j...  1060 us
    all_gather x1, waiting for transfers between devices, local_step(): d_tok_full = lax.all_gather(d_resid, 'tp', axis=1, tiled=True)  206 us
    dot_general x1, matrix products, local_step(): jnp.einsum('bhqk,bhke->bhqe', d_scores_bf, k_heads, preferred_element_typ...  163 us
    dot_general x1, matrix products, local_step(): jnp.einsum('bhqk,bhqe->bhke', d_scores_bf, q_heads, preferred_element_typ...  163 us
    all_gather x1, waiting for transfers between devices, local_step(): lax.all_gather(ln2_y.astype(jnp.bfloat16), 'tp', axis=1, tiled=True)  153 us
    all_gather x1, waiting for transfers between devices, local_step(): lax.all_gather(ln1_y.astype(jnp.bfloat16), 'tp', axis=1, tiled=True)  153 us
    reduce_scatter x1, waiting for transfers between devices, local_step(): embedded = lax.psum_scatter(emb_rows, 'tp', scatter_dimension=1, tiled=True)  151 us
    reduce_scatter x1, waiting for transfers between devices, local_step(): lax.psum_scatter(d_hid2_part, 'tp', scatter_dimension=1, tiled=True)  150 us
  transfers between devices with their start and end apart: 12, of which 10 were waited for; matrix products, arithmetic and copies ran while one was open for 17% of the time, Pallas kernels for 0%

commit v1 on v0

v1 whole, which is shorter than its diff:
```python
import functools

import jax
import jax.numpy as jnp
from jax import lax
from jax.experimental import pallas as pl
from jax.experimental.pallas import tpu as pltpu
from jax.sharding import Mesh, PartitionSpec as P

F32 = jnp.float32
BF16 = jnp.bfloat16

BLK = 256


def dot_nt(a, b):
    return lax.dot_general(a, b, (((1,), (1,)), ((), ())), preferred_element_type=F32)


def dot_nn(a, b):
    return lax.dot_general(a, b, (((1,), (0,)), ((), ())), preferred_element_type=F32)


def head_only(x, head):
    half = x.shape[1] // 2
    lane = lax.broadcasted_iota(jnp.int32, x.shape, 1)
    keep = (lane < half) if head == 0 else (lane >= half)
    return jnp.where(keep, x, jnp.zeros((), x.dtype))


def attn_fwd_kernel(qkv_ref, ctx_ref, lse_ref, ctx_t):
    seq, width = ctx_ref.shape
    half = width // 2
    scale = half ** -0.5
    q2 = qkv_ref[:, 0:width] * jnp.asarray(scale, BF16)
    v_t = qkv_ref[:, 2 * width:3 * width].T
    for head in range(2):
        q_h = head_only(q2, head)
        v_h = v_t[head * half:(head + 1) * half, :]
        for i in range(seq // BLK):
            lo, hi = i * BLK, (i + 1) * BLK
            s = dot_nt(qkv_ref[0:hi, width:2 * width], q_h[lo:hi, :])
            diag = s[lo:hi]
            key = lax.broadcasted_iota(jnp.int32, (BLK, BLK), 0)
            qry = lax.broadcasted_iota(jnp.int32, (BLK, BLK), 1)
            diag = jnp.where(key <= qry, diag, -1e30)
            top = jnp.max(diag, axis=0, keepdims=True)
            if i:
                top = jnp.maximum(top, jnp.max(s[0:lo], axis=0, keepdims=True))
            p_diag = jnp.exp(diag - top)
            total = jnp.sum(p_diag, axis=0, keepdims=True)
            if i:
                p_left = jnp.exp(s[0:lo] - top)
                total = total + jnp.sum(p_left, axis=0, keepdims=True)
            inv = 1.0 / total
            acc = dot_nn(v_h[:, lo:hi], (p_diag * inv).astype(BF16))
            if i:
                acc = acc + dot_nn(v_h[:, 0:lo], (p_left * inv).astype(BF16))
            ctx_t[head * half:(head + 1) * half, lo:hi] = acc
            lse_ref[head:head + 1, lo:hi] = top + jnp.log(total)
    ctx_ref[...] = ctx_t[...].T.astype(BF16)


def attn_fwd(qkv, n_seq, seq, n_pair):
    width = 128
    return pl.pallas_call(
        attn_fwd_kernel,
        grid=(n_seq, n_pair),
        in_specs=[pl.BlockSpec((seq, 3 * width), lambda b, p: (b, p))],
        out_specs=[pl.BlockSpec((seq, width), lambda b, p: (b, p)),
                   pl.BlockSpec((None, None, 2, seq), lambda b, p: (b, p, 0, 0))],
        out_shape=[jax.ShapeDtypeStruct((n_seq * seq, n_pair * width), BF16),
                   jax.ShapeDtypeStruct((n_seq, n_pair, 2, seq), F32)],
        scratch_shapes=[pltpu.VMEM((width, seq), F32)],
        name="attn_fwd",
        cost_estimate=pl.CostEstimate(flops=n_seq * n_pair * 8 * seq * seq * 256 * 10 // 16, bytes_accessed=n_seq * seq * n_pair * width * 8,
                                      transcendentals=n_seq * n_pair * seq * seq),
        compiler_params=pltpu.CompilerParams(vmem_limit_bytes=48 * 1024 * 1024),
    )(qkv)


def attn_bwd_kernel(qkv_ref, ctx_ref, dctx_ref, lse_ref, dqkv_ref, dk_t, dv_t):
    seq, width = ctx_ref.shape
    half = width // 2
    scale = half ** -0.5
    q2 = qkv_ref[:, 0:width] * jnp.asarray(scale, BF16)
    q_t = q2.T
    do_t = dctx_ref[...].T
    lse_c = jnp.concatenate([lse_ref[...], jnp.zeros((6, seq), F32)], axis=0).T
    prod = dctx_ref[...].astype(F32) * ctx_ref[...].astype(F32)
    for i in range(seq // BLK):
        lo, hi = i * BLK, (i + 1) * BLK
        dq = []
        for head in range(2):
            rows = slice(head * half, (head + 1) * half)
            mean = jnp.sum(head_only(prod[lo:hi], head), axis=1, keepdims=True)
            lse = lse_c[lo:hi, head:head + 1]
            q_h = head_only(q2[lo:hi], head)
            do_h = head_only(dctx_ref[lo:hi, :], head)
            s = dot_nt(q_h, qkv_ref[0:hi, width:2 * width])
            dp = dot_nt(do_h, qkv_ref[0:hi, 2 * width:3 * width])
            qry = lax.broadcasted_iota(jnp.int32, (BLK, BLK), 0)
            key = lax.broadcasted_iota(jnp.int32, (BLK, BLK), 1)
            p_diag = jnp.where(key <= qry, jnp.exp(s[:, lo:hi] - lse), 0.0)
            ds_diag = (p_diag * (dp[:, lo:hi] - mean)).astype(BF16)
            pb_diag = p_diag.astype(BF16)
            dv_t[rows, lo:hi] = dot_nn(do_t[rows, lo:hi], pb_diag)
            dk_t[rows, lo:hi] = dot_nn(q_t[rows, lo:hi], ds_diag)
            dq_h = dot_nn(ds_diag, qkv_ref[lo:hi, width:2 * width])
            if i:
                p_left = jnp.exp(s[:, 0:lo] - lse)
                ds_left = (p_left * (dp[:, 0:lo] - mean)).astype(BF16)
                pb_left = p_left.astype(BF16)
                dv_t[rows, 0:lo] += dot_nn(do_t[rows, lo:hi], pb_left)
                dk_t[rows, 0:lo] += dot_nn(q_t[rows, lo:hi], ds_left)
                dq_h = dq_h + dot_nn(ds_left, qkv_ref[0:lo, width:2 * width])
            dq.append(dq_h)
        lane = lax.broadcasted_iota(jnp.int32, (BLK, width), 1)
        dqkv_ref[lo:hi, 0:width] = (jnp.where(lane < half, dq[0], dq[1]) * scale).astype(BF16)
    dqkv_ref[:, width:2 * width] = dk_t[...].T.astype(BF16)
    dqkv_ref[:, 2 * width:3 * width] = dv_t[...].T.astype(BF16)


def attn_bwd(qkv, ctx, dctx, lse, n_seq, seq, n_pair):
    width = 128
    return pl.pallas_call(
        attn_bwd_kernel,
        grid=(n_seq, n_pair),
        in_specs=[pl.BlockSpec((seq, 3 * width), lambda b, p: (b, p)),
                  pl.BlockSpec((seq, width), lambda b, p: (b, p)),
                  pl.BlockSpec((seq, width), lambda b, p: (b, p)),
                  pl.BlockSpec((None, None, 2, seq), lambda b, p: (b, p, 0, 0))],
        out_specs=pl.BlockSpec((seq, 3 * width), lambda b, p: (b, p)),
        out_shape=jax.ShapeDtypeStruct((n_seq * seq, n_pair * 3 * width), BF16),
        scratch_shapes=[pltpu.VMEM((width, seq), F32), pltpu.VMEM((width, seq), F32)],
        name="attn_bwd",
        cost_estimate=pl.CostEstimate(flops=n_seq * n_pair * 20 * seq * seq * 256 * 10 // 16, bytes_accessed=n_seq * seq * n_pair * width * 16,
                                      transcendentals=n_seq * n_pair * seq * seq),
        compiler_params=pltpu.CompilerParams(vmem_limit_bytes=48 * 1024 * 1024),
    )(qkv, ctx, dctx, lse)


LANES = 128


def accum_kernel(n_block, cap, sub_rows, width, pos_ref, first_ref, *refs):
    tok_refs = refs[:n_block]
    out_ref = refs[n_block]
    n_sub = len(sub_rows)
    acc = refs[n_block + 1:n_block + 1 + n_sub]
    buf, stage, in_sem, out_sem = refs[n_block + 1 + n_sub:]
    tiles = width // LANES
    group = 8 * tiles

    def fetch(block):
        return pltpu.make_async_copy(tok_refs[block], buf.at[block % 2], in_sem.at[block % 2])

    fetch(0).start()
    for s in range(n_sub):
        def clear(i, _, s=s):
            acc[s][pl.ds(pl.multiple_of(i * group, group), group), :] = jnp.zeros((group, LANES), F32)
            return 0
        lax.fori_loop(0, sub_rows[s] // 8, clear, 0)
    for block in range(n_block):
        if block + 1 < n_block:
            fetch(block + 1).start()
        fetch(block).wait()

        def widen(g, _, block=block):
            rows = buf[block % 2, pl.ds(pl.multiple_of(g * 16, 16), 16), :].astype(F32)
            base = pl.multiple_of(g * 2 * group, 2 * group)
            for h in range(2):
                for c in range(tiles):
                    stage[pl.ds(base + h * group + c * 8, 8), :] = rows[h * 8:(h + 1) * 8, c * LANES:(c + 1) * LANES]
            return 0
        lax.fori_loop(0, cap // 16, widen, 0)

        starts = [first_ref[block * (n_sub + 1) + s] for s in range(n_sub + 1)]
        counts = [starts[s + 1] - starts[s] for s in range(n_sub)]
        longest = functools.reduce(jnp.maximum, counts)

        def add_rows(i, _, block=block, starts=starts, counts=counts):
            for s in range(n_sub):
                valid = i < counts[s]
                slot = jnp.where(valid, starts[s] + i, 0)
                at = jnp.where(valid, pos_ref[block * cap + slot], 0)
                src = (slot >> 3) * group + (slot & 7)
                row = stage[pl.ds(src, tiles, stride=8), :]
                row = jnp.where(valid, row, 0.0)
                acc[s][pl.ds(at, tiles, stride=8), :] += row
            return 0
        lax.fori_loop(0, longest, add_rows, 0)
    done = 0
    copies = []
    for s in range(n_sub):
        n = sub_rows[s] * tiles
        copies.append(pltpu.make_async_copy(acc[s], out_ref.at[pl.ds(done, n), :], out_sem.at[s]))
        copies[-1].start()
        done += n
    for c in copies:
        c.wait()


def accum(tok_blocks, pos, first, sub_rows, width):
    n_block = len(tok_blocks)
    cap = tok_blocks[0].shape[0]
    n_sub = len(sub_rows)
    tiles = width // LANES
    return pl.pallas_call(
        functools.partial(accum_kernel, n_block, cap, sub_rows, width),
        in_specs=[pl.BlockSpec(memory_space=pltpu.SMEM), pl.BlockSpec(memory_space=pltpu.SMEM)]
        + [pl.BlockSpec(memory_space=pl.ANY)] * n_block,
        out_specs=pl.BlockSpec(memory_space=pl.ANY),
        out_shape=jax.ShapeDtypeStruct((sum(sub_rows) * tiles, LANES), F32),
        scratch_shapes=[pltpu.VMEM((r * tiles, LANES), F32) for r in sub_rows]
        + [pltpu.VMEM((2, cap, width), BF16), pltpu.VMEM((cap * tiles, LANES), F32),
           pltpu.SemaphoreType.DMA((2,)), pltpu.SemaphoreType.DMA((n_sub,))],
        name="table_accum",
        compiler_params=pltpu.CompilerParams(vmem_limit_bytes=63 * 1024 * 1024),
    )(pos, first, *tok_blocks)


POS_OFFSET = 2
LN_EPS = 1e-5
SLOTS = 768
LOW = 32
GELU_S = 0.7978845608028654
GELU_A = 0.044715


def dot_tn(a, b):
    return lax.dot_general(a, b, (((0,), (0,)), ((), ())), preferred_element_type=F32)


def norm_forward(x_in, gain, shift):
    mean = jnp.mean(x_in, axis=-1, keepdims=True)
    centered = x_in - mean
    inv_std = lax.rsqrt(jnp.mean(centered * centered, axis=-1, keepdims=True) + LN_EPS)
    normed = centered * inv_std
    return normed * gain + shift, normed, inv_std


def norm_backward(d_y, normed, inv_std, gain):
    d_norm = d_y * gain
    d_x = inv_std * (d_norm - jnp.mean(d_norm, axis=-1, keepdims=True)
                     - normed * jnp.mean(d_norm * normed, axis=-1, keepdims=True))
    return d_x, jnp.sum(d_y * normed, axis=0), jnp.sum(d_y, axis=0)


def before(n):
    return (lax.broadcasted_iota(jnp.int32, (n, n), 1) < lax.broadcasted_iota(jnp.int32, (n, n), 0)).astype(BF16)


def rank_in_class(hot):
    n_blk, n_tok, n_cls = hot.shape
    ones = hot.astype(BF16).reshape(n_blk, n_tok // 128, 128, n_cls)
    within = jnp.einsum("ij,bnjk->bnik", before(128), ones, preferred_element_type=F32)
    sums = jnp.sum(ones.astype(F32), axis=2)
    ahead = jnp.einsum("mn,bnk->bmk", before(n_tok // 128), sums.astype(BF16), preferred_element_type=F32)
    rank = jnp.sum((within + ahead[:, :, None, :]) * ones.astype(F32), axis=3)
    return rank.reshape(n_blk, n_tok).astype(jnp.int32), jnp.sum(sums, axis=1).astype(jnp.int32)


def compact(rank, valid, value):
    n_high = SLOTS // LOW
    high = ((rank // LOW)[:, :, None] == jnp.arange(n_high)) & valid[:, :, None]
    low = ((rank % LOW)[:, :, None] == jnp.arange(LOW)).astype(F32)
    parts = jnp.concatenate([low * (value // 128).astype(F32)[:, :, None], low * (value % 128).astype(F32)[:, :, None]], axis=2)
    out = jnp.einsum("bjh,bjl->bhl", high.astype(BF16), parts.astype(BF16), preferred_element_type=F32).astype(jnp.int32)
    return (out[:, :, :LOW] * 128 + out[:, :, LOW:]).reshape(rank.shape[0], SLOTS)


def solution(mesh):
    n_tp, n_dp = mesh.shape["tp"], mesh.shape["dp"]
    n_core = 2
    n_x = n_dp // n_core
    mesh3 = Mesh(mesh.devices.reshape(n_tp, n_x, n_core), ("tp", "xx", "cc"))
    dp = ("xx", "cc")
    tp_swap = [[(i, i ^ k) for i in range(n_tp)] for k in range(n_tp)]
    pair = [(0, 1), (1, 0)]

    def local_step(tok_ids, emb_table, pos_table, ln1_gain, ln1_bias, w_qkv, b_qkv, w_out, b_out,
                   ln2_gain, ln2_bias, w_up, b_up, w_down, b_down, out_grad):
        tp_index, x_index, c_index = lax.axis_index("tp"), lax.axis_index("xx"), lax.axis_index("cc")
        dp_index = x_index * n_core + c_index
        n_seq_dp, seq = tok_ids.shape
        n_seq = n_seq_dp // n_tp
        n_tok = n_seq * seq
        rows, width = emb_table.shape
        n_sub = 4
        sub = -(-rows // n_sub // 8) * 8
        sub_rows = (sub,) * (n_sub - 1) + (rows - (n_sub - 1) * sub,)
        seq_local = seq // n_tp
        ff = w_up.shape[1]
        gain1, bias1 = ln1_gain.astype(F32), ln1_bias.astype(F32)
        gain2, bias2 = ln2_gain.astype(F32), ln2_bias.astype(F32)

        def half(w, axis):
            n = w.shape[axis] // n_core
            return lax.dynamic_slice_in_dim(w, c_index * n, n, axis)

        def gather_rows(w):
            return lax.all_gather(w, ("tp", "cc"), axis=0, tiled=True)

        def swap(v, axis, k=1):
            return lax.ppermute(v, axis, tp_swap[k] if axis == "tp" else pair)

        wqkv_t = gather_rows(jnp.transpose(half(w_qkv, 2), (1, 2, 3, 0)).reshape(-1, width))
        wout_w = gather_rows(half(w_out, 0).reshape(-1, width))
        wup_t = gather_rows(half(w_up, 1).T)
        wdown_w = gather_rows(half(w_down, 0))
        n_pair = wout_w.shape[0] // 128
        biases = lax.all_gather(jnp.concatenate([
            b_qkv.reshape(3, n_core, -1, b_qkv.shape[2]).transpose(1, 0, 2, 3).reshape(-1), b_up]), "tp", axis=0)
        bqkv_w = biases[:, :-ff].reshape(-1).astype(F32)
        bup_w = biases[:, -ff:].reshape(-1).astype(F32)

        ids_all = lax.all_gather(tok_ids, dp, axis=0, tiled=True).reshape(n_dp * n_tp, n_tok)
        local = ids_all - tp_index * rows
        sub_of = sum(((local >= s * sub).astype(jnp.int32) for s in range(1, n_sub)), jnp.zeros_like(local))
        owned = (local >= 0) & (local < rows)
        hot = owned[:, :, None] & (sub_of[:, :, None] == jnp.arange(n_sub))
        rank, counts = rank_in_class(hot)
        first = jnp.concatenate([jnp.zeros_like(counts[:, :1]), jnp.cumsum(counts, axis=1)], axis=1)
        rank = rank + jnp.sum(jnp.where(hot, first[:, None, :-1], 0), axis=2)
        most = jnp.stack([jnp.max(jnp.sum(((ids_all >= o * rows) & (ids_all < (o + 1) * rows)).astype(jnp.int32), axis=1))
                          for o in range(n_tp)])
        rounds = (jnp.max(most) + SLOTS - 1) // SLOTS

        def lists(r):
            at = rank - r * SLOTS
            return compact(at, owned & (at >= 0) & (at < SLOTS), jnp.where(owned, local, 0))

        own_ids = lax.dynamic_index_in_dim(ids_all, dp_index * n_tp + tp_index, 0, keepdims=True)
        own_owner = sum(((own_ids >= o * rows).astype(jnp.int32) for o in range(1, n_tp)), jnp.zeros_like(own_ids))
        own_local = own_ids - own_owner * rows
        own_sub = sum(((own_local >= s * sub).astype(jnp.int32) for s in range(1, n_sub)), jnp.zeros_like(own_ids))
        own_hot = (own_owner * n_sub + own_sub)[:, :, None] == jnp.arange(n_tp * n_sub)
        own_rank, own_counts = rank_in_class(own_hot)
        own_first = jnp.cumsum(own_counts.reshape(n_tp, n_sub), axis=1) - own_counts.reshape(n_tp, n_sub)
        own_rank = (own_rank + jnp.sum(jnp.where(own_hot, own_first.reshape(1, 1, -1), 0), axis=2))[0]
        own_owner = own_owner[0]

        def own_lists(r):
            at = jnp.broadcast_to(own_rank - r * SLOTS, (n_tp, n_tok))
            mine = own_owner == jnp.arange(n_tp)[:, None]
            return compact(at, mine & (at >= 0) & (at < SLOTS), jnp.broadcast_to(jnp.arange(n_tok), (n_tp, n_tok)))

        def fetch_rows(r, my_lists):
            sent = [jnp.take(emb_table, lax.dynamic_index_in_dim(my_lists, tp_index ^ k, 0, keepdims=False), axis=0)
                    for k in range(n_tp)]
            got = jnp.concatenate([sent[0]] + [swap(sent[k], "tp", k) for k in range(1, n_tp)], axis=0)
            at = own_rank - r * SLOTS
            valid = (at >= 0) & (at < SLOTS)
            place = jnp.where(valid, (own_owner ^ tp_index) * SLOTS + at, 0)
            return jnp.take(got, place, axis=0), valid

        lists0 = lists(0)
        my_lists0 = lax.dynamic_slice_in_dim(lists0, dp_index * n_tp, n_tp, 0)
        emb_rows, _ = fetch_rows(0, my_lists0)

        def more_rows(carry):
            r, emb = carry
            got, valid = fetch_rows(r, lax.dynamic_slice_in_dim(lists(r), dp_index * n_tp, n_tp, 0))
            return r + 1, jnp.where(valid[:, None], got, emb)

        _, emb_rows = lax.while_loop(lambda c: c[0] < rounds, more_rows, (jnp.int32(1), emb_rows))

        og_parts = out_grad.reshape(n_tp, n_seq, seq_local, width)
        og = jnp.zeros((n_seq, seq, width), BF16)
        for k in range(n_tp):
            part = lax.dynamic_index_in_dim(og_parts, tp_index ^ k, 0, keepdims=False)
            part = swap(part, "tp", k) if k else part
            og = lax.dynamic_update_slice_in_dim(og, part, (tp_index ^ k) * seq_local, 1)
        og = og.reshape(n_tok, width)

        pos_rows = lax.slice_in_dim(pos_table, POS_OFFSET, POS_OFFSET + seq, axis=0)
        resid_x = (emb_rows.reshape(n_seq, seq, width).astype(F32) + pos_rows.astype(F32)[None]).reshape(n_tok, width)
        y1, normed1, inv_std1 = norm_forward(resid_x, gain1, bias1)
        hid1 = y1.astype(BF16)
        qkv = (dot_nt(hid1, wqkv_t) + bqkv_w).astype(BF16)
        ctx, lse = attn_fwd(qkv, n_seq, seq, n_pair)
        resid_x1 = resid_x + dot_nn(ctx, wout_w).astype(BF16).astype(F32) + b_out.astype(F32)
        y2, normed2, inv_std2 = norm_forward(resid_x1, gain2, bias2)
        hid2 = y2.astype(BF16)
        d_act = dot_nt(og, wdown_w).astype(BF16)
        z = dot_nt(hid2, wup_t) + bup_w
        th = jnp.tanh(GELU_S * (z + GELU_A * z * z * z))
        act = (0.5 * z * (1.0 + th)).astype(BF16)
        d_up = d_act.astype(F32) * (0.5 * (1.0 + th) + 0.5 * z * (1.0 - th * th) * (GELU_S * (1.0 + 3.0 * GELU_A * z * z)))
        d_b_up = jnp.sum(d_up, axis=0)
        d_up = d_up.astype(BF16)
        out = (resid_x1 + dot_nn(act, wdown_w).astype(BF16).astype(F32) + b_down.astype(F32)).astype(BF16)

        out4 = out.reshape(n_seq, seq, width)
        layer_out = jnp.zeros((n_tp, n_seq, seq_local, width), BF16)
        for k in range(n_tp):
            part = lax.dynamic_slice_in_dim(out4, (tp_index ^ k) * seq_local, seq_local, 1)
            part = swap(part, "tp", k) if k else part
            layer_out = lax.dynamic_update_slice_in_dim(layer_out, part[None], tp_index ^ k, 0)
        layer_out = layer_out.reshape(n_seq_dp, seq_local, width)

        def reduce_rows(g):
            g = lax.psum_scatter(g, ("tp", "cc"), scatter_dimension=0, tiled=True)
            g = g + swap(g, "xx")
            return g

        def share_core(g):
            return lax.all_gather(g, "cc", axis=0, tiled=True)

        d_wdown = reduce_rows(dot_tn(act, og))
        d_wup = reduce_rows(dot_tn(d_up, hid2))
        d_y2 = dot_nn(d_up, wup_t).astype(BF16).astype(F32)
        d_ln2, d_gain2, d_bias2 = norm_backward(d_y2, normed2, inv_std2, gain2)
        d_resid1 = og.astype(F32) + d_ln2
        d_attn = d_resid1.astype(BF16)
        d_wout = reduce_rows(dot_tn(ctx, d_attn))
        d_ctx = dot_nt(d_attn, wout_w).astype(BF16)
        d_qkv = attn_bwd(qkv, ctx, d_ctx, lse, n_seq, seq, n_pair)
        d_wqkv = reduce_rows(dot_tn(d_qkv, hid1))
        d_y1 = dot_nn(d_qkv, wqkv_t).astype(BF16).astype(F32)
        d_ln1, d_gain1, d_bias1 = norm_backward(d_y1, normed1, inv_std1, gain1)
        d_resid = d_resid1 + d_ln1

        def token_blocks(r):
            own = own_lists(r)
            d_tok = d_resid.astype(BF16)
            blocks = []
            for k in range(n_tp):
                part = jnp.take(d_tok, lax.dynamic_index_in_dim(own, tp_index ^ k, 0, keepdims=False), axis=0)
                blocks.append(swap(part, "tp", k) if k else part)
            other = [swap(b, "xx") for b in blocks]
            here = blocks + other
            return here + [swap(b, "cc") for b in here]

        def in_block_order(table):
            out = []
            for dc in range(n_core):
                for dx in range(n_x):
                    for k in range(n_tp):
                        d = (x_index ^ dx) * n_core + (c_index ^ dc)
                        out.append(lax.dynamic_index_in_dim(table, d * n_tp + (tp_index ^ k), 0, keepdims=False))
            return jnp.stack(out)

        block_rows = in_block_order(lists0)
        in_sub = sum(((block_rows >= s * sub).astype(jnp.int32) for s in range(1, n_sub)), jnp.zeros_like(block_rows))
        in_sub = block_rows - in_sub * sub
        pos_at = (in_sub // 8) * (width // 16) + in_sub % 8
        block_first = jnp.minimum(in_block_order(first), SLOTS)
        image = accum(token_blocks(0), pos_at.reshape(-1), block_first.reshape(-1), sub_rows, width)
        tiles = width // 128
        d_emb = image.reshape(rows // 8, tiles, 8, 128).transpose(0, 2, 1, 3).reshape(rows, width)

        def more_grads(carry):
            r, table = carry
            at = rank - r * SLOTS
            there = owned & (at >= 0) & (at < SLOTS)
            dest = compact(at, there, jnp.where(owned, local, 0) + 1)
            dest = jnp.where(dest == 0, rows, dest - 1)
            grads = jnp.concatenate(token_blocks(r), axis=0).astype(F32)
            return r + 1, table.at[in_block_order(dest).reshape(-1)].add(grads, mode="drop")

        _, d_emb = lax.while_loop(lambda c: c[0] < rounds, more_grads, (jnp.int32(1), d_emb))

        d_pos_sum = jnp.sum(d_resid.reshape(n_seq, seq, width), axis=0)
        d_pos_seq = gather_rows(reduce_rows(d_pos_sum))
        d_pos = jnp.pad(d_pos_seq, ((POS_OFFSET, pos_table.shape[0] - seq - POS_OFFSET), (0, 0)))

        small = lax.psum(jnp.concatenate([
            jnp.sum(d_qkv.astype(F32), axis=0), d_b_up, d_gain1, d_bias1, jnp.sum(d_resid1, axis=0),
            d_gain2, d_bias2, jnp.sum(og.astype(F32), axis=0)]), ("tp", "xx", "cc"))
        n_b = b_qkv.size
        d_b_qkv = lax.dynamic_slice_in_dim(small, tp_index * n_b, n_b).reshape(n_core, 3, -1, b_qkv.shape[2])
        d_b_qkv = d_b_qkv.transpose(1, 0, 2, 3).reshape(b_qkv.shape)
        d_b_up = lax.dynamic_slice_in_dim(small, n_tp * n_b + tp_index * ff, ff)
        vec = small[n_tp * (n_b + ff):].reshape(6, width)

        d_w_qkv = share_core(d_wqkv).reshape(n_core, 3, -1, w_qkv.shape[3], width).transpose(4, 1, 0, 2, 3).reshape(w_qkv.shape)
        d_w_out = share_core(d_wout).reshape(w_out.shape)
        d_w_up = share_core(d_wup).T
        d_w_down = share_core(d_wdown)
        return (layer_out, d_emb, d_pos, vec[0], vec[1], d_w_qkv, d_b_qkv, d_w_out,
                vec[2], vec[3], vec[4], d_w_up, d_b_up, d_w_down, vec[5])

    rep = P()
    in_specs = (P(dp, None), P("tp", None), rep, rep, rep,
                P(None, None, "tp", None), P(None, "tp", None), P("tp", None, None), rep,
                rep, rep, P(None, "tp"), P("tp"), P("tp", None), rep,
                P(dp, "tp", None))
    out_specs = (P(dp, "tp", None), P("tp", None), rep, rep, rep,
                 P(None, None, "tp", None), P(None, "tp", None), P("tp", None, None), rep,
                 rep, rep, P(None, "tp"), P("tp"), P("tp", None), rep)
    return jax.shard_map(local_step, mesh=mesh3, in_specs=in_specs, out_specs=out_specs, check_vma=False)
```

time: 3600 us -> 1380 us (0.38)
  waiting for transfers between devices: 2430 us -> 442 us
  matrix products: 809 us -> 274 us
  Pallas kernels: 0 us -> 243 us
  other arithmetic: 182 us -> 93.2 us
  local copies, waits for them, and re-layouts: 110 us -> 179 us
  blocking collectives: 44.8 us -> 105 us
    psum x1 -> x0, waiting for transfers between devices: 1060 us -> none  [local_step(): lax.psum((d_emb, d_w_qkv, jnp.sum(d_qkv, axis=(1, 3)), d_w_out, d_w_up, j...]
    all_gather x6 -> x9, waiting for transfers between devices: 765 us -> 0.05 us  [the longest x4 0.03 us: share_core(): return lax.all_gather(g, 'cc', axis=0, tiled=True)]
    dot_general x17 -> x18, matrix products: 753 us -> 274 us  [the longest x4 112 us: dot_nt(): lax.dot_general(a, b, (((1,), (1,)), ((), ())), preferred_element_type=F32)]
    reduce_scatter x5, waiting for transfers between devices: 599 us -> 219 us  [reduce_rows(): g = lax.psum_scatter(g, ('tp', 'cc'), scatter_dimension=0, tiled=True)]
    pallas_call x0 -> x3, Pallas kernels: none -> 243 us  [the longest x1 109 us: accum(): pl.pallas_call(functools.partial(accum_kernel, n_block, cap, sub_rows, wi...]
    ppermute x0 -> x29, waiting for transfers between devices: none -> 222 us  [swap(): return lax.ppermute(v, axis, tp_swap[k] if axis == 'tp' else pair)]
    scatter-add x1 -> x0, other arithmetic: 92 us -> none  [local_step(): jax.ops.segment_sum(d_tok_full.reshape(-1, d_model), seg_ids, num_segment...]
    all_gather x0 -> x2, blocking collectives: none -> 72.7 us  [the longest x1 67.3 us: local_step(): lax.all_gather(jnp.concatenate([b_qkv.reshape(3, n_core, -1, b_qkv.shape[...]
  transfers between devices with their start and end apart: 12 -> 43, of which waited for: 10 -> 13; matrix products, arithmetic and copies ran while one was open for 17% -> 32% of each run, Pallas kernels for 0% -> 18%
where the time goes in v1:
time: 1380 us; the launch traced here: 1390 us
  waiting for transfers between devices  442 us (32%)
  matrix products  274 us (20%)
  Pallas kernels  243 us (18%)
  local copies, waits for them, and re-layouts  179 us (13%)
  blocking collectives  105 us (8%)
  other arithmetic  93.2 us (7%)
  starting transfers between devices  30.8 us (2%)
  between operations  18.2 us (1%)
    ppermute x29, waiting for transfers between devices, swap(): return lax.ppermute(v, axis, tp_swap[k] if axis == 'tp' else pair)  222 us
    reduce_scatter x5, waiting for transfers between devices, reduce_rows(): g = lax.psum_scatter(g, ('tp', 'cc'), scatter_dimension=0, tiled=True)  219 us
    dot_general x4, matrix products, dot_nt(): lax.dot_general(a, b, (((1,), (1,)), ((), ())), preferred_element_type=F32)  112 us
    pallas_call x1, Pallas kernels, accum(): pl.pallas_call(functools.partial(accum_kernel, n_block, cap, sub_rows, wi...  109 us
    dot_general x4, matrix products, dot_nn(): lax.dot_general(a, b, (((1,), (0,)), ((), ())), preferred_element_type=F32)  82.5 us
    dot_general x4, matrix products, dot_tn(): lax.dot_general(a, b, (((0,), (0,)), ((), ())), preferred_element_type=F32)  76.2 us
    pallas_call x1, Pallas kernels, attn_bwd(): pl.pallas_call(attn_bwd_kernel, grid=(n_seq, n_pair), in_specs=[pl.BlockS...  67.8 us
    all_gather x1, blocking collectives, local_step(): lax.all_gather(jnp.concatenate([b_qkv.reshape(3, n_core, -1, b_qkv.shape[...  67.3 us
  transfers between devices with their start and end apart: 43, of which 13 were waited for; matrix products, arithmetic and copies ran while one was open for 32% of the time, Pallas kernels for 18%

profile of v1, /device:TPU:0, one launch (start us, length us, event | category | flops | bytes accessed | tf_op | source)
XLA Modules:
  0.0 1389.1 jit_solution(8377087981922925235)
XLA Ops:
  87.5 67.3 %all-gather.1 = bf16[4,1,1792]{2,1,0:T(2,128)(2,1)S(1)} all-gather(bf16[1,1,1792]{2,1,0:T(2,128)(2,1)S(1)} %reshape.1432), channel_id=2, replica_groups=mesh['tp'=4,'xx'=2,'cc'=2] {'tp'}, dimensions={0}, use_global_device_ids=true | all-gather | bytes 17920 | tf_op jit(solution)/shard_map/all_gather | solution.py:313
  196.4 32.8 %collective-permute-done.25 = bf16[2,256,1024]{2,1,0:T(8,128)(2,1)} collective-permute-done((bf16[2,256,1024]{2,1,0:T(8,128)(2,1)}, bf16[2,256,1024]{2,1,0:T(8,128)(2,1)}, u32[]{:S(2)}, u32[]{:S(2)}) %collective-permute-start.25) | collective-permute-done | bytes 1048608 | tf_op jit(solution)/shard_map/ppermute | solution.py:306
  270.2 19.4 %add_convert_fusion.qkv_ref = bf16[2048,3072]{1,0:T(8,128)(2,1)} fusion(bf16[2048,1024]{1,0:T(8,128)(2,1)} %add_convert_fusion.3, bf16[3072,1024]{1,0:T(8,128)(2,1)} %all-gather.12.cloned.1.call-done, f32[3072]{0:T(1024)S(1)} %copy-done.43), kind=kOutput, calls=%fused_computation.232 | convolution fusion | flops 12897484800 | bytes 23080960 | tf_op jit(solution)/shard_map/dot_general | solution.py:17
  289.6 66.2 %attn_fwd.1 = (bf16[2048,1024]{1,0:T(8,128)(2,1)S(1)}, f32[2,8,2,1024]{3,2,1,0:T(2,128)S(1)}) custom-call(bf16[2048,3072]{1,0:T(8,128)(2,1)} %add_convert_fusion.qkv_ref), custom_call_target="tpu_custom_call" | custom-call | flops 21474836480 | bytes 16777216 | tf_op jit(solution)/shard_map/attn_fwd/pallas_call | solution.py:66
  371.8 36.1 %multiply_convert_fusion = (bf16[2048,4096]{1,0:T(8,128)(2,1)}, f32[2048,4096]{1,0:T(8,128)}) fusion(f32[4096]{0:T(1024)S(1)} %bitcast.208, bf16[4096,1024]{0,1:T(8,128)(2,1)} %all-gather.16.cloned.1.call-done, f32[2048,1024]{1,0:T(8,128)} %copy-done.10, f32[1024]{0:T(1024)S(1)} %copy-done.48, f32[1024]{0:T(1024)S(1)} %copy-done.38, ...), kind=kOutput, calls=%fused_computation.230 | convolution fusion | flops 17274241024 | bytes 67149824 | tf_op jit(solution)/shard_map/dot_general | solution.py:17
  407.8 46.6 %fusion.185 = (f32[4096]{0:T(1024)}, bf16[2048,4096]{1,0:T(8,128)(2,1)}) fusion(f32[2048,4096]{1,0:T(8,128)} %get-tuple-element.1193, f32[4096]{0:T(1024)S(1)} %bitcast.209, bf16[2048,1024]{1,0:T(8,128)(2,1)} %bitcast.41, bf16[4096,1024]{1,0:T(8,128)(2,1)} %all-gather.18.cloned.1.call-done), kind=kOutput, calls=%fused_computation.563 | convolution fusion | flops 17372803072 | bytes 62947328 | tf_op jit(solution)/shard_map/dot_general | solution.py:17
  454.5 26.7 %fusion.82 = (f32[1024]{0:T(1024)}, f32[2048]{0:T(1024)S(1)}, f32[2048]{0:T(1024)S(1)}, f32[1024]{0:T(1024)}, bf16[2048,1024]{1,0:T(8,128)(2,1)}) fusion(f32[2048,1024]{1,0:T(8,128)S(1)} %copy-done.11, f32[2048]{0:T(1024)S(1)} %add_rsqrt_fusion, f32[2048]{0:T(1024)S(1)} %broadcast_multiply_fusion.4, f32[1024]{0:T(1024)S(1)} %copy-done.38, ...), kind=kOutput, calls=%fused_computation.253 | convolution fusion | flops 17202933760 | bytes 37793792 | tf_op jit(solution)/shard_map/dot_general | solution.py:21
  508.9 67.8 %attn_bwd.1 = bf16[2048,3072]{1,0:T(8,128)(2,1)} custom-call(bf16[2048,3072]{1,0:T(8,128)(2,1)} %add_convert_fusion.qkv_ref, bf16[2048,1024]{1,0:T(8,128)(2,1)S(1)} %copy-done.4, bf16[2048,1024]{1,0:T(8,128)(2,1)} %convolution_convert_fusion.2.dctx_ref, f32[2,8,2,1024]{3,2,1,0:T(2,128)S(1)} %get-tuple-element.865.lse_ref), custom_call_target="tpu_custom_call" | custom-call | flops 53687091200 | bytes 33554432 | tf_op jit(solution)/shard_map/attn_bwd/pallas_call | solution.py:126
  576.7 21.6 %fusion.83 = (f32[1024]{0:T(1024)}, f32[2048]{0:T(1024)S(1)}, f32[2048]{0:T(1024)S(1)}, f32[1024]{0:T(1024)}, bf16[2048,1024]{1,0:T(8,128)(2,1)}) fusion(bf16[2048,1024]{1,0:T(8,128)(2,1)S(1)} %copy-done.6, f32[2048]{0:T(1024)S(1)} %copy-done.33, f32[2048]{0:T(1024)S(1)} %copy-done.31, f32[1024,1024]{1,0:T(8,128)S(1)} %copy-done.8, ...), kind=kOutput, calls=%fused_computation.254 | convolution fusion | flops 12912158720 | bytes 31502336 | tf_op jit(solution)/shard_map/dot_general | solution.py:21
  614.4 19.7 %fusion.186 = f32[3072,1024]{1,0:T(8,128)} fusion(bf16[2048,3072]{1,0:T(8,128)(2,1)} %attn_bwd.1, bf16[2048,1024]{1,0:T(8,128)(2,1)} %add_convert_fusion.3), kind=kOutput, calls=%fused_computation.564 | convolution fusion | flops 12884901888 | bytes 29360128 | tf_op jit(solution)/shard_map/dot_general | solution.py:232
  634.7 26.5 %fusion.84 = f32[4096,1024]{1,0:T(8,128)} fusion(bf16[2048,4096]{1,0:T(8,128)(2,1)} %get-tuple-element.1190, f32[2048,1024]{1,0:T(8,128)} %copy-done.10, f32[1024]{0:T(1024)S(1)} %copy-done.49, f32[1024]{0:T(1024)S(1)} %copy-done.38, f32[2048]{0:T(1024)S(1)} %add_rsqrt_fusion, f32[2048]{0:T(1024)S(1)} %broadcast_multiply_fusion.4), kind=kOutput, calls=%fused_computation.257 | convolution fusion | flops 17190354944 | bytes 41967616 | tf_op jit(solution)/shard_map/dot_general | solution.py:232
  661.3 23.9 %fusion.187 = f32[4096,1024]{1,0:T(8,128)} fusion(bf16[2048,4096]{1,0:T(8,128)(2,1)} %get-tuple-element.1192, bf16[2048,1024]{1,0:T(8,128)(2,1)} %bitcast.41), kind=kOutput, calls=%fused_computation.565 | convolution fusion | flops 17179869184 | bytes 37748736 | tf_op jit(solution)/shard_map/dot_general | solution.py:232
  715.0 33.3 %reduce-scatter.8.cloned.1.call-done = f32[384,1024]{1,0:T(8,128)} async-done(((f32[3072,1024]{1,0:T(8,128)}), f32[384,1024]{1,0:T(8,128)}) %reduce-scatter.8.cloned.1.call-update) | async-done | bytes 1572880 | tf_op jit(solution)/shard_map/reduce_scatter | solution.py:404
  750.0 34.3 %collective-permute-done.43 = f32[384,1024]{1,0:T(8,128)S(1)} collective-permute-done((f32[384,1024]{1,0:T(8,128)}, f32[384,1024]{1,0:T(8,128)S(1)}, u32[]{:S(2)}, u32[]{:S(2)}) %collective-permute-start.43) | collective-permute-done | bytes 1572896 | tf_op jit(solution)/shard_map/ppermute | solution.py:306
  788.0 74.2 %reduce-scatter.12.cloned.1.call-done = f32[512,1024]{1,0:T(8,128)} async-done(((f32[4096,1024]{1,0:T(8,128)}), f32[512,1024]{1,0:T(8,128)}) %reduce-scatter.12.cloned.1.call-update) | async-done | bytes 2097168 | tf_op jit(solution)/shard_map/reduce_scatter | solution.py:404
  863.8 111.6 %reduce-scatter.14.cloned.1.call-done = f32[512,1024]{1,0:T(8,128)} async-done(((f32[4096,1024]{1,0:T(8,128)}), f32[512,1024]{1,0:T(8,128)}) %reduce-scatter.14.cloned.1.call-update) | async-done | bytes 2097168 | tf_op jit(solution)/shard_map/reduce_scatter | solution.py:404
  980.2 23.5 %add_convert_fusion.1 = bf16[2048,1024]{1,0:T(8,128)(2,1)S(1)} fusion(f32[2048,1024]{1,0:T(8,128)} %copy-done.10, f32[1024]{0:T(1024)S(1)} %convert_element_type.521, bf16[2048,4096]{1,0:T(8,128)(2,1)} %get-tuple-element.1192, bf16[4096,1024]{1,0:T(8,128)(2,1)} %all-gather.18.cloned.1.call-done), kind=kOutput, calls=%fused_computation.261 | convolution fusion | flops 17190354944 | bytes 37752832 | tf_op jit(solution)/shard_map/dot_general | solution.py:21
  1045.7 17.1 %collective-permute-done.22 = bf16[2,256,1024]{2,1,0:T(8,128)(2,1)} collective-permute-done((bf16[2,256,1024]{2,1,0:T(8,128)(2,1)}, bf16[2,256,1024]{2,1,0:T(8,128)(2,1)}, u32[]{:S(2)}, u32[]{:S(2)}) %collective-permute-start.22) | collective-permute-done | bytes 1048608 | tf_op jit(solution)/shard_map/ppermute | solution.py:306
  1072.6 24.5 %collective-permute-done.27.refs_1_ = bf16[768,1024]{1,0:T(8,128)(2,1)S(1)} collective-permute-done((bf16[768,1024]{1,0:T(8,128)(2,1)}, bf16[768,1024]{1,0:T(8,128)(2,1)S(1)}, u32[]{:S(2)}, u32[]{:S(2)}) %collective-permute-start.27) | collective-permute-done | bytes 1572896 | tf_op jit(solution)/shard_map/ppermute | solution.py:306
  1098.9 34.8 %collective-permute-done.28.refs_2_ = bf16[768,1024]{1,0:T(8,128)(2,1)} collective-permute-done((bf16[768,1024]{1,0:T(8,128)(2,1)}, bf16[768,1024]{1,0:T(8,128)(2,1)}, u32[]{:S(2)}, u32[]{:S(2)}) %collective-permute-start.28) | collective-permute-done | bytes 1572896 | tf_op jit(solution)/shard_map/ppermute | solution.py:306
  1146.5 24.4 %collective-permute-done.32.refs_6_ = bf16[768,1024]{1,0:T(8,128)(2,1)} collective-permute-done((bf16[768,1024]{1,0:T(8,128)(2,1)}, bf16[768,1024]{1,0:T(8,128)(2,1)}, u32[]{:S(2)}, u32[]{:S(2)}) %collective-permute-start.32) | collective-permute-done | bytes 1572896 | tf_op jit(solution)/shard_map/ppermute | solution.py:306
  1171.0 31.5 %collective-permute-done.33.refs_7_ = bf16[768,1024]{1,0:T(8,128)(2,1)} collective-permute-done((bf16[768,1024]{1,0:T(8,128)(2,1)}, bf16[768,1024]{1,0:T(8,128)(2,1)}, u32[]{:S(2)}, u32[]{:S(2)}) %collective-permute-start.33) | collective-permute-done | bytes 1572896 | tf_op jit(solution)/shard_map/ppermute | solution.py:306
  1202.5 32.6 %psum.7 = f32[13312]{0:T(1024)S(1)} all-reduce(f32[13312]{0:T(1024)S(1)} %constant_dynamic-update-slice_fusion.19), channel_id=1, replica_groups=mesh['tp'=4,'xx'=2,'cc'=2] {'tp','xx','cc'}, use_global_device_ids=true, to_apply=%region_45.50 | all-reduce | flops 13312 | bytes 106496 | tf_op jit(solution)/shard_map/psum | solution.py:469
  1248.1 109.2 %table_accum.1 = f32[100544,128]{1,0:T(8,128)} custom-call(s32[12288]{0:T(1024)} %fusion.145.pos_ref, s32[80]{0:T(128)} %min.12.first_ref, bf16[768,1024]{1,0:T(8,128)(2,1)} %broadcast_select_fusion.14.refs_0_, bf16[768,1024]{1,0:T(8,128)(2,1)} %copy-done.25, bf16[768,1024]{1,0:T(8,128)(2,1)} %collective-permute-done.28.refs_2_, ...), custom_call_target="tpu_custom_call" | custom-call | tf_op jit(solution)/shard_map/table_accum/pallas_call | solution.py:209
  (410 shorter events, 365.3 us)
Async XLA Ops:
  7.2 263.0 %all-gather.12.cloned.1.call-start = ((), (), s32[]{:S(2)}) async-start(), calls=%async_computation.5 | async-start | bytes 7077888 | tf_op jit(solution)/shard_map/all_gather | solution.py:303
  9.5 348.3 %all-gather.14.cloned.1.call-start = ((), (), s32[]{:S(2)}) async-start(), calls=%async_computation.6 | async-start | bytes 2359296 | tf_op jit(solution)/shard_map/all_gather | solution.py:303
  10.3 361.4 %all-gather.16.cloned.1.call-start = ((), (), s32[]{:S(2)}) async-start(), calls=%async_computation.7 | async-start | bytes 9437184 | tf_op jit(solution)/shard_map/all_gather | solution.py:303
  12.6 395.2 %all-gather.18.cloned.1.call-start = ((), (), s32[]{:S(2)}) async-start(), calls=%async_computation.8 | async-start | bytes 9437184 | tf_op jit(solution)/shard_map/all_gather | solution.py:303
  16.3 168.6 %collective-permute-start.24 = (bf16[2,256,1024]{2,1,0:T(8,128)(2,1)}, bf16[2,256,1024]{2,1,0:T(8,128)(2,1)S(1)}, u32[]{:S(2)}, u32[]{:S(2)}) collective-permute-start(bf16[2,256,1024]{2,1,0:T(8,128)(2,1)} %get-tuple-element.1126), channel_id=1, source_target_pairs={{0,4},{4,0},{8,12},{12,8},{1,5},{5,1},{9,13},{13,9},{2,6},{6,2},{1... | collective-permute-start | bytes 3145736 | tf_op jit(solution)/shard_map/ppermute | solution.py:306
  47.5 185.1 %collective-permute-start.20 = (bf16[768,1024]{1,0:T(8,128)(2,1)}, bf16[768,1024]{1,0:T(8,128)(2,1)}, u32[]{:S(2)}, u32[]{:S(2)}) collective-permute-start(bf16[768,1024]{1,0:T(8,128)(2,1)} %broadcast_select_fusion.15), channel_id=1, source_target_pairs={{0,12},{4,8},{8,4},{12,0},{1,13},{5,9},{9,5},{13,1},{2,14},{6,10},... | collective-permute-start | bytes 4718600 | tf_op jit(solution)/shard_map/ppermute | solution.py:306
  66.1 166.5 %collective-permute-start.19 = (bf16[768,1024]{1,0:T(8,128)(2,1)}, bf16[768,1024]{1,0:T(8,128)(2,1)}, u32[]{:S(2)}, u32[]{:S(2)}) collective-permute-start(bf16[768,1024]{1,0:T(8,128)(2,1)} %broadcast_select_fusion.16), channel_id=1, source_target_pairs={{0,8},{4,12},{8,0},{12,4},{1,9},{5,13},{9,1},{13,5},{2,10},{6,14},... | collective-permute-start | bytes 4718600 | tf_op jit(solution)/shard_map/ppermute | solution.py:306
  83.2 149.5 %collective-permute-start.18 = (bf16[768,1024]{1,0:T(8,128)(2,1)}, bf16[768,1024]{1,0:T(8,128)(2,1)}, u32[]{:S(2)}, u32[]{:S(2)}) collective-permute-start(bf16[768,1024]{1,0:T(8,128)(2,1)} %broadcast_select_fusion.17), channel_id=1, source_target_pairs={{0,4},{4,0},{8,12},{12,8},{1,5},{5,1},{9,13},{13,9},{2,6},{6,2},{1... | collective-permute-start | bytes 4718600 | tf_op jit(solution)/shard_map/ppermute | solution.py:306
  87.3 598.0 %reduce-scatter.10.cloned.1.call-start = ((), (), s32[]{:S(2)}) async-start(), calls=%async_computation.13 | async-start | bytes 4718592 | tf_op jit(solution)/shard_map/reduce_scatter | solution.py:404
  497.4 203.1 %reduce-scatter.6.cloned.1.call-start = ((), (), s32[]{:S(2)}) async-start(), calls=%async_computation.9 | async-start | bytes 4718592 | tf_op jit(solution)/shard_map/reduce_scatter | solution.py:404
  614.3 134.0 %reduce-scatter.8.cloned.1.call-start = ((), (), s32[]{:S(2)}) async-start(), calls=%async_computation.11 | async-start | bytes 14155776 | tf_op jit(solution)/shard_map/reduce_scatter | solution.py:404
  634.1 228.1 %reduce-scatter.12.cloned.1.call-start = ((), (), s32[]{:S(2)}) async-start(), calls=%async_computation.15 | async-start | bytes 18874368 | tf_op jit(solution)/shard_map/reduce_scatter | solution.py:404
  661.2 314.1 %reduce-scatter.14.cloned.1.call-start = ((), (), s32[]{:S(2)}) async-start(), calls=%async_computation.17 | async-start | bytes 18874368 | tf_op jit(solution)/shard_map/reduce_scatter | solution.py:404
  685.3 672.1 %all-gather.24.cloned.1.call-start = ((), (), s32[]{:S(2)}) async-start(), calls=%async_computation.14 | async-start | bytes 1572864 | tf_op jit(solution)/shard_map/all_gather | solution.py:409
  700.5 656.9 %all-gather.20.cloned.1.call-start = ((), (), s32[]{:S(2)}) async-start(), calls=%async_computation.10 | async-start | bytes 4718592 | tf_op jit(solution)/shard_map/all_gather | solution.py:303
  714.9 649.5 %all-gather.22.cloned.1.call-start = ((), (), s32[]{:S(2)}) async-start(), calls=%async_computation.12 | async-start | bytes 4718592 | tf_op jit(solution)/shard_map/all_gather | solution.py:409
  787.0 581.3 %all-gather.26.cloned.1.call-start = ((), (), s32[]{:S(2)}) async-start(), calls=%async_computation.16 | async-start | bytes 6291456 | tf_op jit(solution)/shard_map/all_gather | solution.py:409
  862.1 114.7 %collective-permute-start.45 = (f32[512,1024]{1,0:T(8,128)}, f32[512,1024]{1,0:T(8,128)S(1)}, u32[]{:S(2)}, u32[]{:S(2)}) collective-permute-start(f32[512,1024]{1,0:T(8,128)} %reduce-scatter.12.cloned.1.call-done), channel_id=1, source_target_pairs={{0,2},{2,0},{1,3},{3,1},{4,6},{6,4},{5,7},{7,5},{8,10},{10,8},{9,1... | collective-permute-start | bytes 6291464 | tf_op jit(solution)/shard_map/ppermute | solution.py:306
  975.3 89.5 %collective-permute-start.46 = (f32[512,1024]{1,0:T(8,128)}, f32[512,1024]{1,0:T(8,128)}, u32[]{:S(2)}, u32[]{:S(2)}) collective-permute-start(f32[512,1024]{1,0:T(8,128)} %reduce-scatter.14.cloned.1.call-done), channel_id=1, source_target_pairs={{0,2},{2,0},{1,3},{3,1},{4,6},{6,4},{5,7},{7,5},{8,10},{10,8},{9,1... | collective-permute-start | bytes 6291464 | tf_op jit(solution)/shard_map/ppermute | solution.py:306
  980.1 393.7 %all-gather.28.cloned.1.call-start = ((), (), s32[]{:S(2)}) async-start(), calls=%async_computation.18 | async-start | bytes 6291456 | tf_op jit(solution)/shard_map/all_gather | solution.py:409
  1145.9 102.2 %collective-permute-start.36 = (bf16[768,1024]{1,0:T(8,128)(2,1)}, bf16[768,1024]{1,0:T(8,128)(2,1)}, u32[]{:S(2)}, u32[]{:S(2)}) collective-permute-start(bf16[768,1024]{1,0:T(8,128)(2,1)} %collective-permute-done.28.refs_2_), channel_id=1, source_target_pairs={{0,1},{1,0},{2,3},{3,2},{4,5},{5,4},{6,7},{7,6},{8,9},{9,8},{10,11... | collective-permute-start | bytes 4718600 | tf_op jit(solution)/shard_map/ppermute | solution.py:306
  1146.0 102.1 %collective-permute-start.37 = (bf16[768,1024]{1,0:T(8,128)(2,1)}, bf16[768,1024]{1,0:T(8,128)(2,1)}, u32[]{:S(2)}, u32[]{:S(2)}) collective-permute-start(bf16[768,1024]{1,0:T(8,128)(2,1)} %collective-permute-done.29.refs_3_), channel_id=1, source_target_pairs={{0,1},{1,0},{2,3},{3,2},{4,5},{5,4},{6,7},{7,6},{8,9},{9,8},{10,11... | collective-permute-start | bytes 4718600 | tf_op jit(solution)/shard_map/ppermute | solution.py:306
  1146.5 101.6 %collective-permute-start.39 = (bf16[768,1024]{1,0:T(8,128)(2,1)}, bf16[768,1024]{1,0:T(8,128)(2,1)}, u32[]{:S(2)}, u32[]{:S(2)}) collective-permute-start(bf16[768,1024]{1,0:T(8,128)(2,1)} %collective-permute-done.31.refs_5_), channel_id=1, source_target_pairs={{0,1},{1,0},{2,3},{3,2},{4,5},{5,4},{6,7},{7,6},{8,9},{9,8},{10,11... | collective-permute-start | bytes 4718600 | tf_op jit(solution)/shard_map/ppermute | solution.py:306
  1171.0 77.1 %collective-permute-start.40 = (bf16[768,1024]{1,0:T(8,128)(2,1)}, bf16[768,1024]{1,0:T(8,128)(2,1)}, u32[]{:S(2)}, u32[]{:S(2)}) collective-permute-start(bf16[768,1024]{1,0:T(8,128)(2,1)} %collective-permute-done.32.refs_6_), channel_id=1, source_target_pairs={{0,1},{1,0},{2,3},{3,2},{4,5},{5,4},{6,7},{7,6},{8,9},{9,8},{10,11... | collective-permute-start | bytes 4718600 | tf_op jit(solution)/shard_map/ppermute | solution.py:306
  (81 other events, 2705.9 us)
Sparse Core Ops, SparseCore 0:
  9.8 69.3 all-gather.11
  81.1 45.9 all-gather.13
  129.5 96.4 all-gather.15
  227.7 50.3 all-gather.17
  497.5 45.1 reduce-scatter.9
  614.4 45.1 reduce-scatter.5
  663.1 85.2 reduce-scatter.7
  752.4 109.6 reduce-scatter.11
  865.7 109.6 reduce-scatter.13
  976.7 6.9 all-gather.23
  985.6 65.5 all-gather.19
  1052.6 11.3 all-gather.21
  1066.0 13.2 all-gather.25
  1080.8 13.2 all-gather.27

commit v2 on v1

v2 whole, which is shorter than its diff:
```python
import functools

import jax
import jax.numpy as jnp
from jax import lax
from jax.experimental import pallas as pl
from jax.experimental.pallas import tpu as pltpu
from jax.sharding import Mesh, PartitionSpec as P


F32 = jnp.float32
BF16 = jnp.bfloat16
MIB = 1024 * 1024
WIDEN = 32

BLK = 256


def dot_nt(a, b):
    return lax.dot_general(a, b, (((1,), (1,)), ((), ())), preferred_element_type=F32)


def dot_nn(a, b):
    return lax.dot_general(a, b, (((1,), (0,)), ((), ())), preferred_element_type=F32)


def head_only(x, head):
    half = x.shape[1] // 2
    lane = lax.broadcasted_iota(jnp.int32, x.shape, 1)
    keep = (lane < half) if head == 0 else (lane >= half)
    return jnp.where(keep, x, jnp.zeros((), x.dtype))


def attn_fwd_kernel(qkv_ref, ctx_ref, lse_ref, ctx_t):
    seq, width = ctx_ref.shape
    half = width // 2
    scale = half ** -0.5
    q2 = qkv_ref[:, 0:width] * jnp.asarray(scale, BF16)
    v_t = qkv_ref[:, 2 * width:3 * width].T
    tasks = [(head, i) for i in range(seq // BLK) for head in range(2)]

    def scores(head, i):
        return dot_nt(qkv_ref[0:(i + 1) * BLK, width:2 * width], head_only(q2[i * BLK:(i + 1) * BLK], head))

    ready = scores(*tasks[0])
    for n, (head, i) in enumerate(tasks):
        s = ready
        if n + 1 < len(tasks):
            ready = scores(*tasks[n + 1])
        lo, hi = i * BLK, (i + 1) * BLK
        v_h = v_t[head * half:(head + 1) * half, :]
        key = lax.broadcasted_iota(jnp.int32, (BLK, BLK), 0)
        qry = lax.broadcasted_iota(jnp.int32, (BLK, BLK), 1)
        diag = jnp.where(key <= qry, s[lo:hi], -1e30)
        top = jnp.max(diag, axis=0, keepdims=True)
        if i:
            top = jnp.maximum(top, jnp.max(s[0:lo], axis=0, keepdims=True))
        p_diag = jnp.exp(diag - top)
        total = jnp.sum(p_diag, axis=0, keepdims=True)
        if i:
            p_left = jnp.exp(s[0:lo] - top)
            total = total + jnp.sum(p_left, axis=0, keepdims=True)
        inv = 1.0 / total
        acc = dot_nn(v_h[:, lo:hi], (p_diag * inv).astype(BF16))
        if i:
            acc = acc + dot_nn(v_h[:, 0:lo], (p_left * inv).astype(BF16))
        ctx_t[head * half:(head + 1) * half, lo:hi] = acc
        lse_ref[head:head + 1, lo:hi] = top + jnp.log(total)
    ctx_ref[...] = ctx_t[...].T.astype(BF16)


def attn_fwd(qkv, n_seq, seq, n_pair):
    width = 128
    return pl.pallas_call(
        attn_fwd_kernel,
        grid=(n_seq, n_pair),
        in_specs=[pl.BlockSpec((seq, 3 * width), lambda b, p: (b, p))],
        out_specs=[pl.BlockSpec((seq, width), lambda b, p: (b, p)),
                   pl.BlockSpec((None, None, 2, seq), lambda b, p: (b, p, 0, 0))],
        out_shape=[jax.ShapeDtypeStruct((n_seq * seq, n_pair * width), BF16),
                   jax.ShapeDtypeStruct((n_seq, n_pair, 2, seq), F32)],
        scratch_shapes=[pltpu.VMEM((width, seq), F32)],
        name="attn_fwd",
        cost_estimate=pl.CostEstimate(flops=n_seq * n_pair * 8 * seq * seq * 256 * 10 // 16, bytes_accessed=n_seq * seq * n_pair * width * 8,
                                      transcendentals=n_seq * n_pair * seq * seq),
        compiler_params=pltpu.CompilerParams(vmem_limit_bytes=48 * 1024 * 1024),
    )(qkv)


def attn_bwd_kernel(qkv_ref, ctx_ref, dctx_ref, lse_ref, dqkv_ref, dk_t, dv_t):
    seq, width = ctx_ref.shape
    half = width // 2
    scale = half ** -0.5
    q2 = qkv_ref[:, 0:width] * jnp.asarray(scale, BF16)
    q_t = q2.T
    do_t = dctx_ref[...].T
    lse_c = jnp.concatenate([lse_ref[...], jnp.zeros((6, seq), F32)], axis=0).T
    prod = dctx_ref[...].astype(F32) * ctx_ref[...].astype(F32)
    tasks = [(head, i) for i in range(seq // BLK) for head in range(2)]

    def scores(head, i):
        lo, hi = i * BLK, (i + 1) * BLK
        return (dot_nt(head_only(q2[lo:hi], head), qkv_ref[0:hi, width:2 * width]),
                dot_nt(head_only(dctx_ref[lo:hi, :], head), qkv_ref[0:hi, 2 * width:3 * width]))

    dq = []
    ready = scores(*tasks[0])
    for n, (head, i) in enumerate(tasks):
        s, dp = ready
        if n + 1 < len(tasks):
            ready = scores(*tasks[n + 1])
        lo, hi = i * BLK, (i + 1) * BLK
        rows = slice(head * half, (head + 1) * half)
        mean = jnp.sum(head_only(prod[lo:hi], head), axis=1, keepdims=True)
        lse = lse_c[lo:hi, head:head + 1]
        qry = lax.broadcasted_iota(jnp.int32, (BLK, BLK), 0)
        key = lax.broadcasted_iota(jnp.int32, (BLK, BLK), 1)
        p_diag = jnp.where(key <= qry, jnp.exp(s[:, lo:hi] - lse), 0.0)
        ds_diag = (p_diag * (dp[:, lo:hi] - mean)).astype(BF16)
        dv_t[rows, lo:hi] = dot_nn(do_t[rows, lo:hi], p_diag.astype(BF16))
        dk_t[rows, lo:hi] = dot_nn(q_t[rows, lo:hi], ds_diag)
        dq_h = dot_nn(ds_diag, qkv_ref[lo:hi, width:2 * width])
        if i:
            p_left = jnp.exp(s[:, 0:lo] - lse)
            ds_left = (p_left * (dp[:, 0:lo] - mean)).astype(BF16)
            dv_t[rows, 0:lo] += dot_nn(do_t[rows, lo:hi], p_left.astype(BF16))
            dk_t[rows, 0:lo] += dot_nn(q_t[rows, lo:hi], ds_left)
            dq_h = dq_h + dot_nn(ds_left, qkv_ref[0:lo, width:2 * width])
        dq.append(dq_h)
        if head == 1:
            lane = lax.broadcasted_iota(jnp.int32, (BLK, width), 1)
            dqkv_ref[lo:hi, 0:width] = (jnp.where(lane < half, dq[0], dq[1]) * scale).astype(BF16)
            dq = []
    dqkv_ref[:, width:2 * width] = dk_t[...].T.astype(BF16)
    dqkv_ref[:, 2 * width:3 * width] = dv_t[...].T.astype(BF16)


def attn_bwd(qkv, ctx, dctx, lse, n_seq, seq, n_pair):
    width = 128
    return pl.pallas_call(
        attn_bwd_kernel,
        grid=(n_seq, n_pair),
        in_specs=[pl.BlockSpec((seq, 3 * width), lambda b, p: (b, p)),
                  pl.BlockSpec((seq, width), lambda b, p: (b, p)),
                  pl.BlockSpec((seq, width), lambda b, p: (b, p)),
                  pl.BlockSpec((None, None, 2, seq), lambda b, p: (b, p, 0, 0))],
        out_specs=pl.BlockSpec((seq, 3 * width), lambda b, p: (b, p)),
        out_shape=jax.ShapeDtypeStruct((n_seq * seq, n_pair * 3 * width), BF16),
        scratch_shapes=[pltpu.VMEM((width, seq), F32), pltpu.VMEM((width, seq), F32)],
        name="attn_bwd",
        cost_estimate=pl.CostEstimate(flops=n_seq * n_pair * 20 * seq * seq * 256 * 10 // 16, bytes_accessed=n_seq * seq * n_pair * width * 16,
                                      transcendentals=n_seq * n_pair * seq * seq),
        compiler_params=pltpu.CompilerParams(vmem_limit_bytes=48 * 1024 * 1024),
    )(qkv, ctx, dctx, lse)


LN_EPS = 1e-5
GELU_S = 0.7978845608028654
GELU_A = 0.044715


def row_mean(v):
    return jnp.sum(v, axis=1, keepdims=True) * (1.0 / v.shape[1])


def row_stats(v):
    centered = v - row_mean(v)
    inv_std = lax.rsqrt(row_mean(centered * centered) + LN_EPS)
    return centered * inv_std, inv_std


def norm_back(d_y, x_in, gain):
    normed, inv_std = row_stats(x_in)
    d_norm = d_y * gain
    d_x = inv_std * (d_norm - row_mean(d_norm) - normed * row_mean(d_norm * normed))
    return d_x, d_y * normed


def col_sum(v):
    return jnp.sum(v, axis=0, keepdims=True)


def to_image(rows, image, base):
    tiles = rows.shape[1] // 128
    for h in range(rows.shape[0] // 8):
        for c in range(tiles):
            image[pl.ds(base + (h * tiles + c) * 8, 8), :] = rows[h * 8:(h + 1) * 8, c * 128:(c + 1) * 128]


def from_image(image, base, n_rows, width):
    tiles = width // 128
    return jnp.concatenate([jnp.concatenate([image[pl.ds(base + (h * tiles + c) * 8, 8), :] for c in range(tiles)], axis=1)
                            for h in range(n_rows // 8)], axis=0)


def pick_rows(code_ref, first, stage, image, n_rows, tiles):
    def pick(g, _):
        base = pl.multiple_of(g * 16 * tiles, 16 * tiles)
        for j in range(16):
            row = stage[pl.ds(code_ref[first + g * 16 + j], tiles, stride=8), :]
            image[pl.ds(base + (j // 8) * 8 * tiles + j % 8, tiles, stride=8), :] = row
        return 0

    lax.fori_loop(0, n_rows // 16, pick, 0)


def embed_kernel(n_blk, cap, code_ref, *refs):
    tok_refs = refs[:n_blk]
    pos_ref, gain_ref, bias_ref, x_ref, hid_ref, stage, image = refs[n_blk:]
    rows, width = x_ref.shape
    tiles = width // 128

    @pl.when(pl.program_id(0) == 0)
    def _():
        for b in range(n_blk):
            def widen(g, _, b=b):
                part = tok_refs[b][pl.ds(pl.multiple_of(g * WIDEN, WIDEN), WIDEN), :].astype(F32)
                to_image(part, stage, pl.multiple_of((b * cap + g * WIDEN) * tiles, WIDEN * tiles))
                return 0

            lax.fori_loop(0, cap // WIDEN, widen, 0)

    pick_rows(code_ref, pl.program_id(0) * rows, stage, image, rows, tiles)
    part = 64
    for i in range(rows // part):
        at = slice(i * part, (i + 1) * part)
        x = from_image(image, i * part * tiles, part, width) + pos_ref[at, :].astype(F32)
        x_ref[at, :] = x
        normed, _ = row_stats(x)
        hid_ref[at, :] = (normed * gain_ref[...] + bias_ref[...]).astype(BF16)


def embed(code, blocks, pos_rows, gain, bias, n_tok):
    cap, width = blocks[0].shape
    seq = pos_rows.shape[0]
    rows = 256
    per_seq = seq // rows
    n_blk = len(blocks)
    vec = pl.BlockSpec((1, width), lambda i: (0, 0))
    return pl.pallas_call(
        functools.partial(embed_kernel, n_blk, cap),
        grid=(n_tok // rows,),
        in_specs=[pl.BlockSpec(memory_space=pltpu.SMEM)]
        + [pl.BlockSpec((cap, width), lambda i: (0, 0), pipeline_mode=pl.Buffered(1))] * n_blk
        + [pl.BlockSpec((rows, width), lambda i: (i % per_seq, 0)), vec, vec],
        out_specs=[pl.BlockSpec((rows, width), lambda i: (i, 0))] * 2,
        out_shape=[jax.ShapeDtypeStruct((n_tok, width), F32), jax.ShapeDtypeStruct((n_tok, width), BF16)],
        scratch_shapes=[pltpu.VMEM((n_blk * cap * width // 128, 128), F32), pltpu.VMEM((rows * width // 128, 128), F32)],
        name="embed_norm",
        cost_estimate=pl.CostEstimate(flops=15_000_000_000, bytes_accessed=n_tok * width * 10, transcendentals=0),
        compiler_params=pltpu.CompilerParams(vmem_limit_bytes=48 * MIB),
    )(code, *blocks, pos_rows, gain, bias)


def pack_kernel(n_blk, code_ref, tok_ref, *refs):
    out_refs = refs[:n_blk]
    stage, image = refs[n_blk:]
    n_tok, width = tok_ref.shape
    cap = out_refs[0].shape[0]
    tiles = width // 128

    def widen(g, _):
        part = tok_ref[pl.ds(pl.multiple_of(g * WIDEN, WIDEN), WIDEN), :].astype(F32)
        to_image(part, stage, pl.multiple_of(g * WIDEN * tiles, WIDEN * tiles))
        return 0

    lax.fori_loop(0, n_tok // WIDEN, widen, 0)
    for b in range(n_blk):
        pick_rows(code_ref, b * cap, stage, image, cap, tiles)

        def narrow(g, _, b=b):
            part = from_image(image, pl.multiple_of(g * WIDEN * tiles, WIDEN * tiles), WIDEN, width)
            out_refs[b][pl.ds(pl.multiple_of(g * WIDEN, WIDEN), WIDEN), :] = part.astype(BF16)
            return 0

        lax.fori_loop(0, cap // WIDEN, narrow, 0)


def pack(code, tok, cap):
    n_tok, width = tok.shape
    n_blk = code.shape[0] // cap
    return pl.pallas_call(
        functools.partial(pack_kernel, n_blk),
        in_specs=[pl.BlockSpec(memory_space=pltpu.SMEM), pl.BlockSpec(memory_space=pltpu.VMEM)],
        out_specs=[pl.BlockSpec(memory_space=pltpu.VMEM)] * n_blk,
        out_shape=[jax.ShapeDtypeStruct((cap, width), BF16)] * n_blk,
        scratch_shapes=[pltpu.VMEM((n_tok * width // 128, 128), F32), pltpu.VMEM((cap * width // 128, 128), F32)],
        name="token_pack",
        cost_estimate=pl.CostEstimate(flops=15_000_000_000, bytes_accessed=n_tok * width * 5, transcendentals=0),
        compiler_params=pltpu.CompilerParams(vmem_limit_bytes=40 * MIB),
    )(code, tok)


def proj_kernel(c_ref, w_ref, x_ref, b_ref, gain_ref, bias_ref, x1_ref, hid_ref):
    part = x_ref.shape[0] // 2
    for i in range(2):
        at = slice(i * part, (i + 1) * part)
        x1 = x_ref[at, :] + dot_nn(c_ref[at, :], w_ref[...].reshape(c_ref.shape[1], -1)).astype(BF16).astype(F32) + b_ref[...]
        x1_ref[at, :] = x1
        normed, _ = row_stats(x1)
        hid_ref[at, :] = (normed * gain_ref[...] + bias_ref[...]).astype(BF16)


def proj_norm(ctx, w, start, x, b, gain, bias):
    n_tok, width = x.shape
    n_row = ctx.shape[1] // w.shape[0]
    rows = 512
    vec = pl.BlockSpec((1, width), lambda i: (0, 0))
    mat = pl.BlockSpec((rows, width), lambda i: (i, 0))
    return pl.pallas_call(
        proj_kernel,
        grid=(n_tok // rows,),
        in_specs=[pl.BlockSpec((rows, ctx.shape[1]), lambda i: (i, 0)), pl.BlockSpec((w.shape[0], n_row, width), lambda i: (0, start // n_row, 0)), mat, vec, vec, vec],
        out_specs=[mat, mat],
        out_shape=[jax.ShapeDtypeStruct((n_tok, width), F32), jax.ShapeDtypeStruct((n_tok, width), BF16)],
        name="proj_norm",
        cost_estimate=pl.CostEstimate(flops=2 * n_tok * ctx.shape[1] * width, bytes_accessed=n_tok * width * 12, transcendentals=0),
        compiler_params=pltpu.CompilerParams(vmem_limit_bytes=40 * MIB),
    )(ctx, w, x, b, gain, bias)


def ffn_kernel(part, h_ref, og_ref, wu_ref, wd_ref, b_ref, act_ref, dup_ref, db_ref):
    total = jnp.zeros(db_ref.shape, F32)
    for i in range(h_ref.shape[0] // part):
        at = slice(i * part, (i + 1) * part)
        z = dot_nt(h_ref[at, :], wu_ref[0]) + b_ref[...]
        d_act = dot_nt(og_ref[at, :], wd_ref[0])
        z2 = z * z
        gate = 0.5 * jnp.tanh(z * (GELU_S + (GELU_S * GELU_A) * z2)) + 0.5
        act = z * gate
        d_up = d_act * (gate + act * (1.0 - gate) * (2.0 * GELU_S + (6.0 * GELU_S * GELU_A) * z2))
        act_ref[at, :] = act.astype(BF16)
        dup_ref[at, :] = d_up.astype(BF16)
        total = total + col_sum(d_up)
    db_ref[...] = total


def ffn(hid, og, w, b_up, part=1024):
    n_tok, width = hid.shape
    ff = b_up.shape[1]
    n_piece = w.shape[0]
    bn = ff // n_piece
    whole = pl.BlockSpec((n_tok, width), lambda i: (0, 0), pipeline_mode=pl.Buffered(1))
    ospec = pl.BlockSpec((n_tok, bn), lambda i: (0, i))
    vec = pl.BlockSpec((1, bn), lambda i: (0, i))
    return pl.pallas_call(
        functools.partial(ffn_kernel, part),
        grid=(n_piece,),
        in_specs=[whole, whole, pl.BlockSpec((1, bn, width), lambda i: (i, 0, 0)), pl.BlockSpec((1, bn, width), lambda i: (i, 1, 0)), vec],
        out_specs=[ospec, ospec, vec],
        out_shape=[jax.ShapeDtypeStruct((n_tok, ff), BF16), jax.ShapeDtypeStruct((n_tok, ff), BF16), jax.ShapeDtypeStruct((1, ff), F32)],
        name="ffn",
        cost_estimate=pl.CostEstimate(flops=4 * n_tok * ff * width, bytes_accessed=4 * n_tok * ff + 4 * ff * width, transcendentals=n_tok * ff),
        compiler_params=pltpu.CompilerParams(vmem_limit_bytes=48 * MIB),
    )(hid, og, w, w, b_up)


def back2_kernel(dup_ref, w_ref, x1_ref, og_ref, gain_ref, dr_ref, da_ref, sums_ref):
    @pl.when(pl.program_id(0) == 0)
    def _():
        sums_ref[...] = jnp.zeros(sums_ref.shape, F32)

    n_part = 2
    part = dr_ref.shape[0] // n_part
    w = w_ref[...].reshape(dup_ref.shape[1], -1)
    d_ys = [dot_nn(dup_ref[i * part:(i + 1) * part, :], w) for i in range(n_part)]
    for i in range(n_part):
        at = slice(i * part, (i + 1) * part)
        d_y = d_ys[i].astype(BF16).astype(F32)
        d_x, d_gain = norm_back(d_y, x1_ref[at, :], gain_ref[...])
        og = og_ref[at, :].astype(F32)
        d_resid = og + d_x
        dr_ref[at, :] = d_resid
        da_ref[at, :] = d_resid.astype(BF16)
        sums_ref[0:1, :] += col_sum(d_gain)
        sums_ref[1:2, :] += col_sum(d_y)
        sums_ref[2:3, :] += col_sum(d_resid)
        sums_ref[3:4, :] += col_sum(og)


def back2(d_up, w, x1, og, gain):
    n_tok, width = x1.shape
    ff = d_up.shape[1]
    rows = 256
    mat = pl.BlockSpec((rows, width), lambda i: (i, 0))
    return pl.pallas_call(
        back2_kernel,
        grid=(n_tok // rows,),
        in_specs=[pl.BlockSpec((rows, ff), lambda i: (i, 0)), pl.BlockSpec((w.shape[0], ff // w.shape[0], width), lambda i: (0, 0, 0), pipeline_mode=pl.Buffered(1)),
                  mat, mat, pl.BlockSpec((1, width), lambda i: (0, 0))],
        out_specs=[mat, mat, pl.BlockSpec((8, width), lambda i: (0, 0))],
        out_shape=[jax.ShapeDtypeStruct((n_tok, width), F32), jax.ShapeDtypeStruct((n_tok, width), BF16), jax.ShapeDtypeStruct((8, width), F32)],
        name="ffn_back",
        cost_estimate=pl.CostEstimate(flops=2 * n_tok * ff * width, bytes_accessed=2 * n_tok * ff + n_tok * width * 12, transcendentals=0),
        compiler_params=pltpu.CompilerParams(vmem_limit_bytes=48 * MIB),
    )(d_up, w, x1, og, gain)


def back1_kernel(dq_ref, w_ref, x_ref, dr_ref, gain_ref, tok_ref, pos_ref, sums_ref, bsum_ref):
    @pl.when((pl.program_id(0) == 0) & (pl.program_id(1) == 0))
    def _():
        sums_ref[...] = jnp.zeros(sums_ref.shape, F32)
        bsum_ref[...] = jnp.zeros(bsum_ref.shape, F32)

    @pl.when(pl.program_id(1) == 0)
    def _():
        pos_ref[...] = jnp.zeros(pos_ref.shape, F32)

    n_part = 2
    part = tok_ref.shape[0] // n_part
    d_ys = [dot_nn(dq_ref[i * part:(i + 1) * part, :], w_ref[...]) for i in range(n_part)]
    for i in range(n_part):
        at = slice(i * part, (i + 1) * part)
        d_y = d_ys[i].astype(BF16).astype(F32)
        d_x, d_gain = norm_back(d_y, x_ref[at, :], gain_ref[...])
        d_resid = dr_ref[at, :] + d_x
        tok_ref[at, :] = d_resid.astype(BF16)
        pos_ref[at, :] += d_resid
        sums_ref[0:1, :] += col_sum(d_gain)
        sums_ref[1:2, :] += col_sum(d_y)
        bsum_ref[0:1, :] += col_sum(dq_ref[at, :].astype(F32))


def back1(d_qkv, w_qkv, x, d_resid1, gain, n_seq, pos_rows):
    n_tok, width = x.shape
    n_cols = d_qkv.shape[1]
    rows = 256
    per_seq = n_tok // n_seq // rows
    mat = pl.BlockSpec((rows, width), lambda i, b: (b * per_seq + i, 0))
    return pl.pallas_call(
        back1_kernel,
        grid=(per_seq, n_seq),
        in_specs=[pl.BlockSpec((rows, n_cols), lambda i, b: (b * per_seq + i, 0)),
                  pl.BlockSpec((n_cols, width), lambda i, b: (0, 0), pipeline_mode=pl.Buffered(1)),
                  mat, mat, pl.BlockSpec((1, width), lambda i, b: (0, 0))],
        out_specs=[mat, pl.BlockSpec((rows, width), lambda i, b: (i, 0)), pl.BlockSpec((8, width), lambda i, b: (0, 0)),
                   pl.BlockSpec((8, n_cols), lambda i, b: (0, 0))],
        out_shape=[jax.ShapeDtypeStruct((n_tok, width), BF16), jax.ShapeDtypeStruct((pos_rows, width), F32),
                   jax.ShapeDtypeStruct((8, width), F32), jax.ShapeDtypeStruct((8, n_cols), F32)],
        name="qkv_back",
        cost_estimate=pl.CostEstimate(flops=2 * n_tok * n_cols * width, bytes_accessed=2 * n_tok * n_cols + n_tok * width * 12, transcendentals=0),
        compiler_params=pltpu.CompilerParams(vmem_limit_bytes=48 * MIB),
    )(d_qkv, w_qkv, x, d_resid1, gain)


def assemble_kernel(n, me_ref, *refs):
    out_ref = refs[n]
    k = me_ref[0] ^ pl.program_id(0)
    for j in range(n):
        @pl.when(k == j)
        def _(j=j):
            out_ref[...] = refs[j][...].reshape(out_ref.shape)


def assemble(me, parts, out_shape, block):
    at = 1 if len(out_shape) == 4 else 0
    return pl.pallas_call(
        functools.partial(assemble_kernel, len(parts)),
        grid_spec=pltpu.PrefetchScalarGridSpec(
            num_scalar_prefetch=1, grid=(len(parts),),
            in_specs=[pl.BlockSpec(p.shape, lambda i, m: (0, 0, 0), pipeline_mode=pl.Buffered(1)) for p in parts],
            out_specs=pl.BlockSpec(block, lambda i, m: tuple(i if d == at else 0 for d in range(len(block))))),
        out_shape=jax.ShapeDtypeStruct(out_shape, parts[0].dtype),
        name="assemble",
        cost_estimate=pl.CostEstimate(flops=4_000_000_000, bytes_accessed=16 * MIB, transcendentals=0),
        compiler_params=pltpu.CompilerParams(vmem_limit_bytes=24 * MIB),
    )(me, *parts)


LANES = 128


def accum_kernel(n_block, cap, sub_rows, width, where_ref, first_ref, *refs):
    tok_refs = refs[:n_block]
    out_ref = refs[n_block]
    n_sub = len(sub_rows)
    acc = refs[n_block + 1:n_block + 1 + n_sub]
    buf, stage, in_sem, out_sem = refs[n_block + 1 + n_sub:]
    tiles = width // LANES
    group = 8 * tiles

    def fetch(block):
        return pltpu.make_async_copy(tok_refs[block], buf.at[block % 2], in_sem.at[block % 2])

    fetch(0).start()
    for s in range(n_sub):
        def clear(i, _, s=s):
            acc[s][pl.ds(pl.multiple_of(i * group, group), group), :] = jnp.zeros((group, LANES), F32)
            return 0

        lax.fori_loop(0, sub_rows[s] // 8, clear, 0)

    def add_rows(s, slot, n):
        codes = [where_ref[slot + j] for j in range(n)]
        at = [code >> 16 for code in codes]
        rows = [stage[pl.ds(code & 0xffff, tiles, stride=8), :] for code in codes]
        sums = [acc[s][pl.ds(a, tiles, stride=8), :] for a in at]
        for j in range(n):
            for i in range(j):
                sums[j] = jnp.where(at[i] == at[j], sums[i], sums[j])
            sums[j] = sums[j] + rows[j]
        for j in range(n):
            acc[s][pl.ds(at[j], tiles, stride=8), :] = sums[j]

    for block in range(n_block):
        if block + 1 < n_block:
            fetch(block + 1).start()
        fetch(block).wait()

        def widen(g, _, block=block):
            rows = buf[block % 2, pl.ds(pl.multiple_of(g * WIDEN, WIDEN), WIDEN), :].astype(F32)
            base = pl.multiple_of(g * (WIDEN // 8) * group, (WIDEN // 8) * group)
            for h in range(WIDEN // 8):
                for c in range(tiles):
                    stage[pl.ds(base + h * group + c * 8, 8), :] = rows[h * 8:(h + 1) * 8, c * LANES:(c + 1) * LANES]
            return 0

        lax.fori_loop(0, cap // WIDEN, widen, 0)

        starts = [first_ref[block * (n_sub + 1) + s] for s in range(n_sub + 1)]
        counts = [starts[s + 1] - starts[s] for s in range(n_sub)]
        both = functools.reduce(jnp.minimum, counts) // 2
        begin = [block * cap + starts[s] for s in range(n_sub)]

        def together(i, _, begin=begin):
            for s in range(n_sub):
                add_rows(s, begin[s] + 2 * i, 2)
            return 0

        lax.fori_loop(0, both, together, 0)
        for s in range(n_sub):
            fours = (counts[s] - 2 * both) // 4

            def alone(i, _, s=s, begin=begin, both=both):
                add_rows(s, begin[s] + 2 * both + 4 * i, 4)
                return 0

            lax.fori_loop(0, fours, alone, 0)

            def single(i, _, s=s, begin=begin):
                add_rows(s, begin[s] + i, 1)
                return 0

            lax.fori_loop(2 * both + 4 * fours, counts[s], single, 0)
    done = 0
    copies = []
    for s in range(n_sub):
        n = sub_rows[s] * tiles
        copies.append(pltpu.make_async_copy(acc[s], out_ref.at[pl.ds(done, n), :], out_sem.at[s]))
        copies[-1].start()
        done += n
    for c in copies:
        c.wait()


def accum(tok_blocks, code, first, sub_rows, width):
    n_block = len(tok_blocks)
    cap = tok_blocks[0].shape[0]
    n_sub = len(sub_rows)
    tiles = width // LANES
    return pl.pallas_call(
        functools.partial(accum_kernel, n_block, cap, sub_rows, width),
        in_specs=[pl.BlockSpec(memory_space=pltpu.SMEM), pl.BlockSpec(memory_space=pltpu.SMEM)]
        + [pl.BlockSpec(memory_space=pl.ANY)] * n_block,
        out_specs=pl.BlockSpec(memory_space=pl.ANY),
        out_shape=jax.ShapeDtypeStruct((sum(sub_rows) * tiles, LANES), F32),
        scratch_shapes=[pltpu.VMEM((r * tiles, LANES), F32) for r in sub_rows]
        + [pltpu.VMEM((2, cap, width), BF16), pltpu.VMEM((cap * tiles, LANES), F32),
           pltpu.SemaphoreType.DMA((2,)), pltpu.SemaphoreType.DMA((n_sub,))],
        name="table_accum",
        cost_estimate=pl.CostEstimate(flops=50_000_000_000, bytes_accessed=100_000_000, transcendentals=0),
        compiler_params=pltpu.CompilerParams(vmem_limit_bytes=63 * 1024 * 1024),
    )(code, first, *tok_blocks)


def dot_tn(a, b):
    return lax.dot_general(a, b, (((0,), (0,)), ((), ())), preferred_element_type=F32)


def grad_kernel(has_plus, core_ref, a_ref, b_ref, *refs):
    out_ref = refs[-1]
    n = a_ref.shape[1]
    g = dot_tn(a_ref[...], b_ref[...])
    out_ref[0:n, :] = g + refs[0][0:n, :] if has_plus else g
    if out_ref.shape[0] > n:
        out_ref[n:, :] = jnp.zeros((out_ref.shape[0] - n, out_ref.shape[1]), F32)


def grad_pieces(core, a, b, n_tp, piece, which, n_which, plus=None, into=None):
    n_tok, n_cols = a.shape
    width = b.shape[1]
    bn = n_cols // (4 * n_tp)
    out_spec = pl.BlockSpec((piece, width), lambda p, c: (n_which * p + which, 0))
    in_specs = [pl.BlockSpec((n_tok, bn), lambda p, c: (0, 4 * (p // 2) + 2 * c[0] + p % 2)),
                pl.BlockSpec((n_tok, width), lambda p, c: (0, 0), pipeline_mode=pl.Buffered(1))]
    args = [a, b]
    if plus is not None:
        in_specs.append(pl.BlockSpec((piece, width), lambda p, c: (p, 0)))
        args.append(plus)
    if into is not None:
        in_specs.append(pl.BlockSpec(memory_space=pl.ANY))
        args.append(into)
    return pl.pallas_call(
        functools.partial(grad_kernel, plus is not None),
        grid_spec=pltpu.PrefetchScalarGridSpec(num_scalar_prefetch=1, grid=(2 * n_tp,), in_specs=in_specs, out_specs=out_spec),
        out_shape=jax.ShapeDtypeStruct((2 * n_tp * n_which * piece, width), F32),
        input_output_aliases={} if into is None else {len(args): 0},
        name="weight_grad",
        cost_estimate=pl.CostEstimate(flops=n_tok * n_cols * width, bytes_accessed=n_tok * (n_cols + 2 * width) + 2 * n_cols * width,
                                      transcendentals=0),
        compiler_params=pltpu.CompilerParams(vmem_limit_bytes=32 * MIB),
    )(core, *args)


def grad_rest_kernel(spans, last, core_ref, a1_ref, b1_ref, a2_ref, b2_ref, *refs):
    out_ref = refs[-1]
    plus = refs[0] if len(refs) > 1 else None
    piece, piece_in = out_ref.shape[0] // 2, (refs[0].shape[0] // 2 if plus is not None else 0)
    for (a_ref, b_ref), (start, stop) in zip(((a1_ref, b1_ref), (a2_ref, b2_ref)), spans):
        half = a_ref.shape[1] // 2
        for i in range(0, 2 * half, 128):
            g = dot_tn(a_ref[:, i:i + 128], b_ref[...])
            for x in range(2):
                lo, hi = max(i, x * half), min(i + 128, (x + 1) * half)
                if lo < hi:
                    to = lo - x * half + start
                    part = g[lo - i:hi - i]
                    if plus is not None:
                        part = part + plus[x * piece_in + to:x * piece_in + to + hi - lo, :]
                    out_ref[x * piece + to:x * piece + to + hi - lo, :] = part
        for x in range(2):
            if stop > start + half:
                out_ref[x * piece + start + half:x * piece + stop, :] = jnp.zeros((stop - start - half, out_ref.shape[1]), F32)
    if last:
        for x in range(2):
            out_ref[x * piece + spans[-1][1]:(x + 1) * piece, :] = refs[1][x, 0] + refs[2][x * last:(x + 1) * last, :]


def grad_rest(core, a1, b1, a2, b2, n_tp, spans, plus=None, tail=None):
    n_tok, width = b1.shape
    last = tail[0].shape[2] if tail else 0
    piece = spans[-1][1] + last
    whole = pl.BlockSpec((n_tok, width), lambda t, c: (0, 0), pipeline_mode=pl.Buffered(1))
    in_specs, args = [], []
    for a, b in ((a1, b1), (a2, b2)):
        in_specs += [pl.BlockSpec((n_tok, a.shape[1] // (2 * n_tp)), lambda t, c: (0, 2 * t + c[0])), whole]
        args += [a, b]
    if plus is not None:
        in_specs.append(pl.BlockSpec((plus.shape[0] // n_tp, width), lambda t, c: (t, 0)))
        args.append(plus)
    if tail:
        in_specs.append(pl.BlockSpec((2, 1, last, width), lambda t, c: (t, c[0], 0, 0)))
        in_specs.append(pl.BlockSpec((2 * last, width), lambda t, c: (t, 0)))
        args += tail
    n_cols = a1.shape[1] + a2.shape[1]
    return pl.pallas_call(
        functools.partial(grad_rest_kernel, spans, last),
        grid_spec=pltpu.PrefetchScalarGridSpec(num_scalar_prefetch=1, grid=(n_tp,), in_specs=in_specs,
                                               out_specs=pl.BlockSpec((2 * piece, width), lambda t, c: (t, 0))),
        out_shape=jax.ShapeDtypeStruct((2 * n_tp * piece, width), F32),
        name="weight_grads",
        cost_estimate=pl.CostEstimate(flops=n_tok * n_cols * width, bytes_accessed=n_tok * (n_cols + 4 * width) + 2 * n_cols * width,
                                      transcendentals=0),
        compiler_params=pltpu.CompilerParams(vmem_limit_bytes=40 * MIB),
    )(core, *args)


POS_OFFSET = 2
SLOTS = 704
LOW = 32


def before(n):
    return (lax.broadcasted_iota(jnp.int32, (n, n), 1) < lax.broadcasted_iota(jnp.int32, (n, n), 0)).astype(BF16)


def rank_in_class(hot):
    n_blk, n_tok, n_cls = hot.shape
    ones = hot.astype(BF16).reshape(n_blk, n_tok // 128, 128, n_cls)
    within = jnp.einsum("ij,bnjk->bnik", before(128), ones, preferred_element_type=F32)
    sums = jnp.sum(ones.astype(F32), axis=2)
    ahead = jnp.einsum("mn,bnk->bmk", before(n_tok // 128), sums.astype(BF16), preferred_element_type=F32)
    rank = jnp.sum((within + ahead[:, :, None, :]) * ones.astype(F32), axis=3)
    return rank.reshape(n_blk, n_tok).astype(jnp.int32), jnp.sum(sums, axis=1).astype(jnp.int32)


def compact(rank, valid, value):
    n_high = SLOTS // LOW
    high = ((rank // LOW)[:, :, None] == jnp.arange(n_high)) & valid[:, :, None]
    low = ((rank % LOW)[:, :, None] == jnp.arange(LOW)).astype(F32)
    parts = jnp.concatenate([low * (value // 128).astype(F32)[:, :, None], low * (value % 128).astype(F32)[:, :, None]], axis=2)
    out = jnp.einsum("bjh,bjl->bhl", high.astype(BF16), parts.astype(BF16), preferred_element_type=F32).astype(jnp.int32)
    return (out[:, :, :LOW] * 128 + out[:, :, LOW:]).reshape(rank.shape[0], SLOTS)


def solution(mesh):
    n_tp, n_dp = mesh.shape["tp"], mesh.shape["dp"]
    n_core = 2
    n_x = n_dp // n_core
    mesh3 = Mesh(mesh.devices.reshape(n_tp, n_x, n_core), ("tp", "xx", "cc"))
    dp = ("xx", "cc")
    tp_swap = [[(i, i ^ k) for i in range(n_tp)] for k in range(n_tp)]
    pair = [(0, 1), (1, 0)]

    def local_step(tok_ids, emb_table, pos_table, ln1_gain, ln1_bias, w_qkv, b_qkv, w_out, b_out,
                   ln2_gain, ln2_bias, w_up, b_up, w_down, b_down, out_grad):
        tp_index, x_index, c_index = lax.axis_index("tp"), lax.axis_index("xx"), lax.axis_index("cc")
        dp_index = x_index * n_core + c_index
        n_seq_dp, seq = tok_ids.shape
        n_seq = n_seq_dp // n_tp
        n_tok = n_seq * seq
        rows, width = emb_table.shape
        n_sub = 4
        sub = -(-rows // n_sub // 8) * 8
        sub_rows = (sub,) * (n_sub - 1) + (rows - (n_sub - 1) * sub,)
        seq_local = seq // n_tp
        ff = w_up.shape[1]
        gain1, bias1 = ln1_gain.astype(F32)[None], ln1_bias.astype(F32)[None]
        gain2, bias2 = ln2_gain.astype(F32)[None], ln2_bias.astype(F32)[None]

        def half(w, axis):
            n = w.shape[axis] // n_core
            return lax.dynamic_slice_in_dim(w, c_index * n, n, axis)

        def gather_rows(w):
            return lax.all_gather(w, ("tp", "cc"), axis=0, tiled=True)

        def swap(v, axis, k=1):
            return lax.ppermute(v, axis, tp_swap[k] if axis == "tp" else pair)

        def by_owner(parts):
            out = []
            for p in range(n_tp):
                k = tp_index ^ p
                out.append(jnp.where(k < 2, jnp.where(k == 0, parts[0], parts[1]), jnp.where(k == 2, parts[2], parts[3])))
            return out

        wqkv_t = gather_rows(jnp.transpose(half(w_qkv, 2), (1, 2, 3, 0)).reshape(-1, width))
        n_ff, n_out = ff // n_dp, w_out.shape[0] * w_out.shape[1] // n_dp

        def quarter(w, axis):
            n = w.shape[axis] // n_dp
            return lax.dynamic_slice_in_dim(w, dp_index * n, n, axis)

        w_all = lax.all_gather(jnp.concatenate([quarter(w_up, 1).T, quarter(w_down, 0), quarter(w_out.reshape(-1, width), 0)]),
                               ("tp", "xx", "cc"), axis=0, tiled=True).reshape(n_tp * n_dp, 2 * n_ff + n_out, width)
        wdown_w = w_all[:, n_ff:2 * n_ff].reshape(-1, width)
        wout_w = w_all[:, 2 * n_ff:].reshape(-1, width)
        n_pair = wqkv_t.shape[0] // (3 * 128)
        own_bias = jnp.concatenate([b_qkv.reshape(3, n_core, -1, b_qkv.shape[2]).transpose(1, 0, 2, 3).reshape(-1), b_up])
        biases = jnp.stack(by_owner([swap(own_bias, "tp", k) if k else own_bias for k in range(n_tp)]))
        bqkv_w = biases[:, :-ff].reshape(-1).astype(F32)
        bup_w = biases[:, -ff:].reshape(1, -1).astype(F32)
        pos_rows = lax.slice_in_dim(pos_table, POS_OFFSET, POS_OFFSET + seq, axis=0)

        ids_all = lax.all_gather(tok_ids, dp, axis=0, tiled=True).reshape(n_dp * n_tp, n_tok)
        local = ids_all - tp_index * rows
        sub_of = sum(((local >= s * sub).astype(jnp.int32) for s in range(1, n_sub)), jnp.zeros_like(local))
        owned = (local >= 0) & (local < rows)
        hot = owned[:, :, None] & (sub_of[:, :, None] == jnp.arange(n_sub))
        rank, counts = rank_in_class(hot)
        first = jnp.concatenate([jnp.zeros_like(counts[:, :1]), jnp.cumsum(counts, axis=1)], axis=1)
        rank = rank + jnp.sum(jnp.where(hot, first[:, None, :-1], 0), axis=2)
        most = jnp.stack([jnp.max(jnp.sum(((ids_all >= o * rows) & (ids_all < (o + 1) * rows)).astype(jnp.int32), axis=1))
                          for o in range(n_tp)])
        rounds = (jnp.max(most) + SLOTS - 1) // SLOTS

        def lists(r):
            at = rank - r * SLOTS
            return compact(at, owned & (at >= 0) & (at < SLOTS), jnp.where(owned, local, 0))

        own_ids = lax.dynamic_index_in_dim(ids_all, dp_index * n_tp + tp_index, 0, keepdims=True)
        own_owner = sum(((own_ids >= o * rows).astype(jnp.int32) for o in range(1, n_tp)), jnp.zeros_like(own_ids))
        own_local = own_ids - own_owner * rows
        own_sub = sum(((own_local >= s * sub).astype(jnp.int32) for s in range(1, n_sub)), jnp.zeros_like(own_ids))
        own_hot = (own_owner * n_sub + own_sub)[:, :, None] == jnp.arange(n_tp * n_sub)
        own_rank, own_counts = rank_in_class(own_hot)
        own_first = jnp.cumsum(own_counts.reshape(n_tp, n_sub), axis=1) - own_counts.reshape(n_tp, n_sub)
        own_rank = (own_rank + jnp.sum(jnp.where(own_hot, own_first.reshape(1, 1, -1), 0), axis=2))[0]
        own_owner = own_owner[0]

        def own_lists(r):
            at = jnp.broadcast_to(own_rank - r * SLOTS, (n_tp, n_tok))
            mine = own_owner == jnp.arange(n_tp)[:, None]
            return compact(at, mine & (at >= 0) & (at < SLOTS), jnp.broadcast_to(jnp.arange(n_tok), (n_tp, n_tok)))

        tiles = width // 128

        def rows_here(r, my_lists):
            index = [lax.dynamic_index_in_dim(my_lists, tp_index ^ k, 0, keepdims=False) for k in range(n_tp)]
            first_two = jnp.take(emb_table, jnp.concatenate([index[3], index[1]]), axis=0, mode="clip")
            rest, first_two = lax.optimization_barrier((jnp.concatenate([index[2], index[0]]), first_two))
            last_two = jnp.take(emb_table, rest, axis=0, mode="clip")
            sent = [last_two[SLOTS:], first_two[SLOTS:], last_two[:SLOTS], first_two[:SLOTS]]
            got = list(sent)
            for k in range(1, n_tp):
                got[k] = swap(sent[k], "tp", k)
            at = own_rank - r * SLOTS
            valid = (at >= 0) & (at < SLOTS)
            return got, jnp.where(valid, (own_owner ^ tp_index) * SLOTS + at, 0), valid

        def norm_rows(x):
            normed, _ = row_stats(x)
            return (normed * gain1 + bias1).astype(BF16)

        lists0 = lists(0)
        my_lists0 = lax.dynamic_slice_in_dim(lists0, dp_index * n_tp, n_tp, 0)
        got0, place0, _ = rows_here(0, my_lists0)
        code0 = (place0 // 8) * (8 * tiles) + place0 % 8
        got0, out_grad = lax.optimization_barrier((got0, out_grad))
        resid_x, hid1 = embed(code0, got0, pos_rows, gain1, bias1, n_tok)

        def more_rows(carry):
            r, x, _ = carry
            got, place, valid = rows_here(r, lax.dynamic_slice_in_dim(lists(r), dp_index * n_tp, n_tp, 0))
            new = jnp.take(jnp.concatenate(got), place, axis=0, mode="clip").astype(F32) + jnp.tile(pos_rows.astype(F32), (n_seq, 1))
            x = jnp.where(valid[:, None], new, x)
            return r + 1, x, norm_rows(x)

        _, resid_x, hid1 = lax.while_loop(lambda c: c[0] < rounds, more_rows, (jnp.int32(1), resid_x, hid1))

        og_parts = out_grad.reshape(n_tp, n_seq, seq_local, width)
        parts = [lax.dynamic_index_in_dim(og_parts, tp_index ^ k, 0, keepdims=False) for k in range(n_tp)]
        parts = [swap(part, "tp", k) if k else part for k, part in enumerate(parts)]
        me = jnp.reshape(tp_index, (1,))
        og = assemble(me, parts, (n_seq, n_tp, seq_local, width), (n_seq, 1, seq_local, width)).reshape(n_tok, width)

        qkv = (dot_nt(hid1, wqkv_t) + bqkv_w).astype(BF16)
        ctx, lse = attn_fwd(qkv, n_seq, seq, n_pair)
        resid_x1, hid2 = proj_norm(ctx, w_all, 2 * n_ff, resid_x, b_out.astype(F32)[None], gain2, bias2)
        act, d_up, d_b_up = ffn(hid2, og, w_all, bup_w)
        out = (resid_x1 + dot_nn(act, wdown_w).astype(BF16).astype(F32) + b_down.astype(F32)).astype(BF16)

        out4 = out.reshape(n_seq, seq, width)
        parts = [lax.dynamic_slice_in_dim(out4, (tp_index ^ k) * seq_local, seq_local, 1) for k in range(n_tp)]
        parts = [swap(part, "tp", k) if k else part for k, part in enumerate(parts)]
        layer_out = assemble(me, parts, (n_seq_dp, seq_local, width), (n_seq, seq_local, width))

        core = jnp.reshape(c_index, (1,))

        def piece_of(n_rows):
            return -(-n_rows // (4 * n_tp) // 24) * 24

        def pick_pieces(g, start, n_rows):
            n = n_rows // (n_x * n_core)
            g = g.reshape(n_x, n_core, -1, width)[:, :, start:start + n]
            return g.transpose(1, 0, 2, 3).reshape(n_rows, width)

        p_ff = piece_of(n_tp * ff)
        down_theirs = swap(grad_pieces(1 - core, act, og, n_tp, p_ff, 0, 1), "cc")
        up_theirs = swap(grad_pieces(1 - core, d_up, hid2, n_tp, p_ff, 0, 1), "cc")
        ff_grads = grad_pieces(core, act, og, n_tp, p_ff, 0, 2, plus=down_theirs)
        ff_grads = grad_pieces(core, d_up, hid2, n_tp, p_ff, 1, 2, plus=up_theirs, into=ff_grads)
        ff_grads = lax.psum_scatter(ff_grads, ("tp", "xx"), scatter_dimension=0, tiled=True)
        ff_grads = lax.all_gather(ff_grads, dp, axis=0, tiled=True)

        d_resid1, d_attn, sums2 = back2(d_up, w_all, resid_x1, og, gain2)
        d_ctx = dot_nt(d_attn, wout_w).astype(BF16)
        d_qkv = attn_bwd(qkv, ctx, d_ctx, lse, n_seq, seq, n_pair)
        p_out = piece_of(wout_w.shape[0])
        spans = ((0, p_out), (p_out, p_out + piece_of(wqkv_t.shape[0])))
        n_small = n_tp * (b_qkv.size + ff) // width + 6
        p_pos = -(-(seq + n_small) // (24 * n_tp * n_dp)) * 24
        rest_theirs = swap(grad_rest(1 - core, ctx, d_attn, d_qkv, hid1, n_tp, spans), "cc")
        d_tok, pos_all, sums1, sums_qkv = back1(d_qkv, wqkv_t, resid_x, d_resid1, gain1, n_seq, p_pos * n_tp * n_dp)

        def token_blocks(r):
            own = own_lists(r)
            place = jnp.concatenate([lax.dynamic_index_in_dim(own, tp_index ^ k, 0, keepdims=False) for k in range(n_tp)])
            parts = pack((place // 8) * (8 * tiles) + place % 8, d_tok, SLOTS)
            blocks = [swap(part, "tp", k) if k else part for k, part in enumerate(parts)]
            other = []
            for b in blocks:
                other.append(swap(b, "xx"))
            return blocks + other + [swap(b, "cc") for b in blocks + other]

        def in_block_order(table):
            out = []
            for dc in range(n_core):
                for dx in range(n_x):
                    for k in range(n_tp):
                        d = (x_index ^ dx) * n_core + (c_index ^ dc)
                        out.append(lax.dynamic_index_in_dim(table, d * n_tp + (tp_index ^ k), 0, keepdims=False))
            return jnp.stack(out)

        block_rows = in_block_order(lists0)
        in_sub = sum(((block_rows >= s * sub).astype(jnp.int32) for s in range(1, n_sub)), jnp.zeros_like(block_rows))
        in_sub = block_rows - in_sub * sub
        slot = jnp.arange(SLOTS)
        code = (((in_sub // 8) * (8 * tiles) + in_sub % 8) << 16) | ((slot // 8) * (8 * tiles) + slot % 8)
        block_first = jnp.minimum(in_block_order(first), SLOTS)
        d_w_down = pick_pieces(ff_grads, 0, ff)
        d_w_up = pick_pieces(ff_grads, p_ff, ff).T
        blocks0, d_w_down, d_w_up = lax.optimization_barrier((token_blocks(0), d_w_down, d_w_up))
        image = accum(blocks0, code.reshape(-1), block_first.reshape(-1), sub_rows, width)
        d_emb = image.reshape(rows // 8, tiles, 8, 128).transpose(0, 2, 1, 3).reshape(rows, width)

        def more_grads(carry):
            r, table = carry
            at = rank - r * SLOTS
            there = owned & (at >= 0) & (at < SLOTS)
            dest = compact(at, there, jnp.where(owned, local, 0) + 1)
            dest = jnp.where(dest == 0, rows, dest - 1)
            grads = jnp.concatenate(token_blocks(r), axis=0).astype(F32)
            return r + 1, table.at[in_block_order(dest).reshape(-1)].add(grads, mode="drop")

        _, d_emb = lax.while_loop(lambda c: c[0] < rounds, more_grads, (jnp.int32(1), d_emb))

        small = jnp.concatenate([sums_qkv[0], d_b_up[0], sums1[:2].reshape(-1), sums2[:4].reshape(-1)]).reshape(-1, width)
        small = jnp.concatenate([small, jnp.zeros((pos_all.shape[0] - seq - n_small, width), F32)])
        pos_all = lax.dynamic_update_slice_in_dim(pos_all, small, seq, 0).reshape(n_tp * n_x, n_core, p_pos, width)
        pos_theirs = swap(lax.dynamic_index_in_dim(pos_all, 1 - c_index, 1, keepdims=False).reshape(-1, width), "cc")
        rest = grad_rest(core, ctx, d_attn, d_qkv, hid1, n_tp, spans, plus=rest_theirs, tail=(pos_all, pos_theirs))
        rest = lax.psum_scatter(rest, ("tp", "xx"), scatter_dimension=0, tiled=True)
        rest_w = lax.all_gather(rest[:spans[1][1]], dp, axis=0, tiled=True)
        whole = lax.all_gather(rest[spans[1][1]:], ("tp", "xx", "cc"), axis=0, tiled=True)
        d_pos = jnp.pad(whole[:seq], ((POS_OFFSET, pos_table.shape[0] - seq - POS_OFFSET), (0, 0)))
        small = whole[seq:seq + n_small].reshape(-1)
        n_b = b_qkv.size
        d_b_qkv = lax.dynamic_slice_in_dim(small, tp_index * n_b, n_b).reshape(n_core, 3, -1, b_qkv.shape[2])
        d_b_qkv = d_b_qkv.transpose(1, 0, 2, 3).reshape(b_qkv.shape)
        d_b_up = lax.dynamic_slice_in_dim(small, n_tp * n_b + tp_index * ff, ff)
        d_gain1, d_bias1, d_gain2, d_bias2, d_b_out, d_b_down = small[n_tp * (n_b + ff):].reshape(6, width)

        d_w_out = pick_pieces(rest_w, 0, w_out.shape[0] * w_out.shape[1]).reshape(w_out.shape)
        d_w_qkv = pick_pieces(rest_w, p_out, n_b).reshape(n_core, 3, -1, w_qkv.shape[3], width).transpose(4, 1, 0, 2, 3).reshape(w_qkv.shape)
        return (layer_out, d_emb, d_pos, d_gain1, d_bias1, d_w_qkv, d_b_qkv, d_w_out,
                d_b_out, d_gain2, d_bias2, d_w_up, d_b_up, d_w_down, d_b_down)

    rep = P()
    in_specs = (P(dp, None), P("tp", None), rep, rep, rep,
                P(None, None, "tp", None), P(None, "tp", None), P("tp", None, None), rep,
                rep, rep, P(None, "tp"), P("tp"), P("tp", None), rep,
                P(dp, "tp", None))
    out_specs = (P(dp, "tp", None), P("tp", None), rep, rep, rep,
                 P(None, None, "tp", None), P(None, "tp", None), P("tp", None, None), rep,
                 rep, rep, P(None, "tp"), P("tp"), P("tp", None), rep)

    return jax.shard_map(local_step, mesh=mesh3, in_specs=in_specs, out_specs=out_specs, check_vma=False)
```

time: 1380 us -> 1170 us (0.85); the launches traced: 1390 us -> 1150 us
  matrix products: 274 us -> 51.6 us
  Pallas kernels: 243 us -> 392 us
  blocking collectives: 105 us -> 5.42 us
  other arithmetic: 93.2 us -> 12.1 us
  waiting for transfers between devices: 442 us -> 499 us
  local copies, waits for them, and re-layouts: 179 us -> 144 us
    pallas_call x0 -> x14, Pallas kernels: none -> 230 us  [the longest x1 56.2 us: ffn(): pl.pallas_call(functools.partial(ffn_kernel, part), grid=(n_piece,), in_s...]
    ppermute x29 -> x31, waiting for transfers between devices: 222 us -> 337 us  [swap(): return lax.ppermute(v, axis, tp_swap[k] if axis == 'tp' else pair)]
    dot_general x4 -> x2, matrix products: 112 us -> 25.6 us  [dot_nt(): lax.dot_general(a, b, (((1,), (1,)), ((), ())), preferred_element_type=F32)]
    dot_general x4 -> x0, matrix products: 76.2 us -> none  [dot_tn(): lax.dot_general(a, b, (((0,), (0,)), ((), ())), preferred_element_type=F32)]
    all_gather x1 -> x0, blocking collectives: 67.3 us -> none  [local_step(): lax.all_gather(jnp.concatenate([b_qkv.reshape(3, n_core, -1, b_qkv.shape[...]
    gather x9 -> x2, local copies, waits for them, and re-layouts: 105 us -> 40.2 us  [the longest x1 20.4 us: rows_here(): jnp.take(emb_table, jnp.concatenate([index[3], index[1]]), axis=0, mode='...]
    dot_general x4 -> x1, matrix products: 82.5 us -> 23.3 us  [dot_nn(): lax.dot_general(a, b, (((1,), (0,)), ((), ())), preferred_element_type=F32)]
    reduce_scatter x5 -> x2, waiting for transfers between devices: 219 us -> 162 us  [the longest x1 132 us: local_step(): lax.psum_scatter(ff_grads, ('tp', 'xx'), scatter_dimension=0, tiled=True)]
  transfers between devices with their start and end apart: 43 -> 38, of which waited for: 13 -> 16; matrix products, arithmetic and copies ran while one was open for 32% -> 15% of each run, Pallas kernels for 18% -> 13%
where the time goes in v2:
time: 1170 us; the launch traced here: 1150 us
  waiting for transfers between devices  499 us (43%)
  Pallas kernels  392 us (34%)
  local copies, waits for them, and re-layouts  144 us (12%)
  matrix products  51.6 us (4%)
  starting transfers between devices  29 us (2%)
  between operations  18.2 us (2%)
  other arithmetic  12.1 us (1%)
    ppermute x31, waiting for transfers between devices, swap(): return lax.ppermute(v, axis, tp_swap[k] if axis == 'tp' else pair)  337 us
    reduce_scatter x1, waiting for transfers between devices, local_step(): lax.psum_scatter(ff_grads, ('tp', 'xx'), scatter_dimension=0, tiled=True)  132 us
    pallas_call x1, Pallas kernels, accum(): pl.pallas_call(functools.partial(accum_kernel, n_block, cap, sub_rows, wi...  60.9 us
    pallas_call x1, Pallas kernels, attn_bwd(): pl.pallas_call(attn_bwd_kernel, grid=(n_seq, n_pair), in_specs=[pl.BlockS...  59.9 us
    pallas_call x1, Pallas kernels, ffn(): pl.pallas_call(functools.partial(ffn_kernel, part), grid=(n_piece,), in_s...  56.2 us
    pallas_call x4, Pallas kernels, grad_pieces(): pl.pallas_call(functools.partial(grad_kernel, plus is not None), grid_spe...  55.8 us
    pallas_call x1, Pallas kernels, attn_fwd(): pl.pallas_call(attn_fwd_kernel, grid=(n_seq, n_pair), in_specs=[pl.BlockS...  41.2 us
    reduce_scatter x1, waiting for transfers between devices, local_step(): rest = lax.psum_scatter(rest, ('tp', 'xx'), scatter_dimension=0, tiled=True)  30.2 us
  transfers between devices with their start and end apart: 38, of which 16 were waited for; matrix products, arithmetic and copies ran while one was open for 15% of the time, Pallas kernels for 13%

profile of v2, /device:TPU:0, one launch (start us, length us, event | category | flops | bytes accessed | tf_op | source)
XLA Modules:
  0.0 1151.6 jit_solution(14214348294049602082)
XLA Ops:
  30.1 20.4 %gather_fusion.3 = bf16[1408,1024]{1,0:T(8,128)(2,1)} fusion(bf16[12568,1024]{1,0:T(8,128)(2,1)} %param.21, s32[2048]{0:T(1024)S(1)} %pad_clamp_fusion.3), kind=kCustom, calls=%fused_computation.3 | custom fusion | bytes 5772800 | tf_op jit(solution)/shard_map/jit(_take)/gather | solution.py:791
  50.4 19.8 %gather_fusion.4 = bf16[1408,1024]{1,0:T(8,128)(2,1)} fusion(bf16[12568,1024]{1,0:T(8,128)(2,1)} %param.21, s32[2048]{0:T(1024)S(1)} %pad_clamp_fusion.2), kind=kCustom, calls=%fused_computation.4 | custom fusion | bytes 5772800 | tf_op jit(solution)/shard_map/jit(_take)/gather | solution.py:793
  93.7 67.7 %collective-permute-done.22 = bf16[1792]{0:T(1024)(128)(2,1)S(1)} collective-permute-done((bf16[1792]{0:T(1024)(128)(2,1)S(1)}, bf16[1792]{0:T(1024)(128)(2,1)S(1)}, u32[]{:S(2)}, u32[]{:S(2)}) %collective-permute-start.22) | collective-permute-done | bytes 3616 | tf_op jit(solution)/shard_map/ppermute | solution.py:729
  185.8 30.0 %collective-permute-done.26.refs_3_ = bf16[2,256,1024]{2,1,0:T(8,128)(2,1)S(1)} collective-permute-done((bf16[2,256,1024]{2,1,0:T(8,128)(2,1)S(1)}, bf16[2,256,1024]{2,1,0:T(8,128)(2,1)S(1)}, u32[]{:S(2)}, u32[]{:S(2)}) %collective-permute-start.26) | collective-permute-done | bytes 1048608 | tf_op jit(solution)/shard_map/ppermute | solution.py:729
  215.8 18.5 %collective-permute-done.25.refs_2_ = bf16[2,256,1024]{2,1,0:T(8,128)(2,1)S(1)} collective-permute-done((bf16[2,256,1024]{2,1,0:T(8,128)(2,1)S(1)}, bf16[2,256,1024]{2,1,0:T(8,128)(2,1)S(1)}, u32[]{:S(2)}, u32[]{:S(2)}) %collective-permute-start.25) | collective-permute-done | bytes 1048608 | tf_op jit(solution)/shard_map/ppermute | solution.py:729
  240.8 19.4 %add_convert_fusion.1.qkv_ref = bf16[2048,3072]{1,0:T(8,128)(2,1)} fusion(bf16[2048,1024]{1,0:T(8,128)(2,1)} %get-tuple-element.969.b2_ref, bf16[3072,1024]{1,0:T(8,128)(2,1)} %all-gather.6.cloned.1.call-done.w_ref, f32[3072]{0:T(1024)} %reshape.1196), kind=kOutput, calls=%fused_computation.193 | convolution fusion | flops 12897484800 | bytes 23080960 | tf_op jit(solution)/shard_map/dot_general | solution.py:20
  260.2 41.2 %attn_fwd.1 = (bf16[2048,1024]{1,0:T(8,128)(2,1)S(1)}, f32[2,8,2,1024]{3,2,1,0:T(2,128)S(1)}) custom-call(bf16[2048,3072]{1,0:T(8,128)(2,1)} %add_convert_fusion.1.qkv_ref), custom_call_target="tpu_custom_call" | custom-call | flops 21474836480 | bytes 16777216 | tf_op jit(solution)/shard_map/attn_fwd/pallas_call | solution.py:74
  317.2 56.2 %ffn.1 = (bf16[2048,4096]{1,0:T(8,128)(2,1)}, bf16[2048,4096]{1,0:T(8,128)(2,1)}, f32[1,4096]{1,0:T(1,128)S(1)}) custom-call(bf16[2048,1024]{1,0:T(8,128)(2,1)S(1)} %get-tuple-element.973.h_ref.b_ref, bf16[2048,1024]{1,0:T(8,128)(2,1)} %bitcast.158, bf16[16,576,1024]{2,1,0:T(8,128)(2,1)} %bitcast.170, bf16[16,576,1024]{2,1,0:T(8,128)(2,1)} %bitcast.171, ...), custom_call_target="tpu_custom_call" | custom-call | flops 34359738368 | bytes 50331648 | tf_op jit(solution)/shard_map/ffn/pallas_call | solution.py:346
  373.4 29.7 %ffn_back.1 = (f32[2048,1024]{1,0:T(8,128)}, bf16[2048,1024]{1,0:T(8,128)(2,1)S(1)}, f32[8,1024]{1,0:T(8,128)S(1)}) custom-call(bf16[2048,4096]{1,0:T(8,128)(2,1)} %get-tuple-element.976.dup_ref.a_ref, bf16[16,576,1024]{2,1,0:T(8,128)(2,1)} %bitcast.172, f32[2048,1024]{1,0:T(8,128)} %get-tuple-element.972.x1_ref, bf16[2048,1024]{1,0:T(8,128)(2,1)} %bitcast.159, ...), custom_call_target="tpu_custom_call" | custom-call | flops 17179869184 | bytes 41943040 | tf_op jit(solution)/shard_map/ffn_back/pallas_call | solution.py:386
  409.3 59.9 %attn_bwd.1.dq_ref.a2_ref = bf16[2048,3072]{1,0:T(8,128)(2,1)} custom-call(bf16[2048,3072]{1,0:T(8,128)(2,1)} %add_convert_fusion.1.qkv_ref, bf16[2048,1024]{1,0:T(8,128)(2,1)S(1)} %copy-done.3, bf16[2048,1024]{1,0:T(8,128)(2,1)} %convolution_convert_fusion.1.dctx_ref, f32[2,8,2,1024]{3,2,1,0:T(2,128)S(1)} %get-tuple-element.978.lse_ref), custom_call_target="tpu_custom_call" | custom-call | flops 53687091200 | bytes 33554432 | tf_op jit(solution)/shard_map/attn_bwd/pallas_call | solution.py:140
  482.3 27.5 %qkv_back.1 = (bf16[2048,1024]{1,0:T(8,128)(2,1)}, f32[1152,1024]{1,0:T(8,128)S(1)}, f32[8,1024]{1,0:T(8,128)S(1)}, f32[8,3072]{1,0:T(8,128)S(1)}) custom-call(bf16[2048,3072]{1,0:T(8,128)(2,1)} %attn_bwd.1.dq_ref.a2_ref, bf16[3072,1024]{1,0:T(8,128)(2,1)} %all-gather.6.cloned.1.call-done.w_ref, f32[2048,1024]{1,0:T(8,128)} %get-tuple-element.971.x_ref, ...), custom_call_target="tpu_custom_call" | custom-call | flops 12884901888 | bytes 37748736 | tf_op jit(solution)/shard_map/qkv_back/pallas_call | solution.py:430
  522.2 15.9 %weight_grads.3 = f32[2688,1024]{1,0:T(8,128)} custom-call(s32[1]{0:T(128)} %bitcast.42.core_ref, bf16[2048,1024]{1,0:T(8,128)(2,1)S(1)} %copy-done.4, bf16[2048,1024]{1,0:T(8,128)(2,1)S(1)} %copy-done.6, bf16[2048,3072]{1,0:T(8,128)(2,1)} %attn_bwd.1.dq_ref.a2_ref, bf16[2048,1024]{1,0:T(8,128)(2,1)} %get-tuple-element.969.b2_ref, ...), custom_call_target="tpu_custom_call" | custom-call | flops 8589934592 | bytes 25165824 | tf_op jit(solution)/shard_map/weight_grads/pallas_call | solution.py:656
  540.4 14.0 %weight_grad.5 = f32[2112,1024]{1,0:T(8,128)} custom-call(s32[1]{0:T(128)S(6)} %sub.268.core_ref, bf16[2048,4096]{1,0:T(8,128)(2,1)} %get-tuple-element.975.a_ref, bf16[2048,1024]{1,0:T(8,128)(2,1)S(1)} %bitcast.160), custom_call_target="tpu_custom_call" | custom-call | flops 8589934592 | bytes 20971520 | tf_op jit(solution)/shard_map/weight_grad/pallas_call | solution.py:603
  599.4 30.2 %reduce-scatter.5.cloned.1.call-done = f32[336,1024]{1,0:T(8,128)} async-done(((f32[2688,1024]{1,0:T(8,128)}), f32[336,1024]{1,0:T(8,128)}) %reduce-scatter.5.cloned.1.call-update) | async-done | bytes 1376272 | tf_op jit(solution)/shard_map/reduce_scatter | solution.py:914
  634.0 131.5 %reduce-scatter.3.cloned.1.call-done = f32[528,1024]{1,0:T(8,128)} async-done(((f32[4224,1024]{1,0:T(8,128)}), f32[528,1024]{1,0:T(8,128)}) %reduce-scatter.3.cloned.1.call-update) | async-done | bytes 2162704 | tf_op jit(solution)/shard_map/reduce_scatter | solution.py:854
  775.4 23.3 %add_convert_fusion.2 = bf16[2048,1024]{1,0:T(8,128)(2,1)S(1)} fusion(f32[2048,1024]{1,0:T(8,128)} %get-tuple-element.972.x1_ref, f32[1024]{0:T(1024)S(1)} %convert_element_type.444, bf16[2048,4096]{1,0:T(8,128)(2,1)} %get-tuple-element.975.a_ref, bf16[4096,1024]{1,0:T(8,128)(2,1)} %bitcast.177), kind=kOutput, calls=%fused_computation.194 | convolution fusion | flops 17190354944 | bytes 37752832 | tf_op jit(solution)/shard_map/dot_general | solution.py:24
  813.3 15.0 %collective-permute-done.29.refs_3_ = bf16[2,256,1024]{2,1,0:T(8,128)(2,1)S(1)} collective-permute-done((bf16[2,256,1024]{2,1,0:T(8,128)(2,1)S(1)}, bf16[2,256,1024]{2,1,0:T(8,128)(2,1)S(1)}, u32[]{:S(2)}, u32[]{:S(2)}) %collective-permute-start.29) | collective-permute-done | bytes 1048608 | tf_op jit(solution)/shard_map/ppermute | solution.py:729
  830.8 27.7 %collective-permute-done.28.refs_2_ = bf16[2,256,1024]{2,1,0:T(8,128)(2,1)S(1)} collective-permute-done((bf16[2,256,1024]{2,1,0:T(8,128)(2,1)S(1)}, bf16[2,256,1024]{2,1,0:T(8,128)(2,1)S(1)}, u32[]{:S(2)}, u32[]{:S(2)}) %collective-permute-start.28) | collective-permute-done | bytes 1048608 | tf_op jit(solution)/shard_map/ppermute | solution.py:729
  863.1 31.5 %collective-permute-done.30.refs_1_ = bf16[704,1024]{1,0:T(8,128)(2,1)} collective-permute-done((bf16[704,1024]{1,0:T(8,128)(2,1)S(1)}, bf16[704,1024]{1,0:T(8,128)(2,1)}, u32[]{:S(2)}, u32[]{:S(2)}) %collective-permute-start.30) | collective-permute-done | bytes 1441824 | tf_op jit(solution)/shard_map/ppermute | solution.py:729
  896.1 28.2 %collective-permute-done.32.refs_3_ = bf16[704,1024]{1,0:T(8,128)(2,1)} collective-permute-done((bf16[704,1024]{1,0:T(8,128)(2,1)S(1)}, bf16[704,1024]{1,0:T(8,128)(2,1)}, u32[]{:S(2)}, u32[]{:S(2)}) %collective-permute-start.32) | collective-permute-done | bytes 1441824 | tf_op jit(solution)/shard_map/ppermute | solution.py:729
  929.9 43.6 %collective-permute-done.34.refs_5_ = bf16[704,1024]{1,0:T(8,128)(2,1)} collective-permute-done((bf16[704,1024]{1,0:T(8,128)(2,1)}, bf16[704,1024]{1,0:T(8,128)(2,1)}, u32[]{:S(2)}, u32[]{:S(2)}) %collective-permute-start.34) | collective-permute-done | bytes 1441824 | tf_op jit(solution)/shard_map/ppermute | solution.py:729
  974.0 30.4 %collective-permute-done.35.refs_6_ = bf16[704,1024]{1,0:T(8,128)(2,1)} collective-permute-done((bf16[704,1024]{1,0:T(8,128)(2,1)}, bf16[704,1024]{1,0:T(8,128)(2,1)}, u32[]{:S(2)}, u32[]{:S(2)}) %collective-permute-start.35) | collective-permute-done | bytes 1441824 | tf_op jit(solution)/shard_map/ppermute | solution.py:729
  1004.4 29.3 %collective-permute-done.36.refs_7_ = bf16[704,1024]{1,0:T(8,128)(2,1)} collective-permute-done((bf16[704,1024]{1,0:T(8,128)(2,1)}, bf16[704,1024]{1,0:T(8,128)(2,1)}, u32[]{:S(2)}, u32[]{:S(2)}) %collective-permute-start.36) | collective-permute-done | bytes 1441824 | tf_op jit(solution)/shard_map/ppermute | solution.py:729
  1082.6 60.9 %table_accum.1 = f32[100544,128]{1,0:T(8,128)} custom-call(s32[11264]{0:T(1024)} %fusion.118.where_ref, s32[80]{0:T(128)} %min.12.first_ref, bf16[704,1024]{1,0:T(8,128)(2,1)} %copy-done.14, bf16[704,1024]{1,0:T(8,128)(2,1)} %collective-permute-done.30.refs_1_, bf16[704,1024]{1,0:T(8,128)(2,1)} %collective-permute-done.31.refs_2_, ...), custom_call_target="tpu_custom_call" | custom-call | flops 49999998976 | bytes 100000000 | tf_op jit(solution)/shard_map/table_accum/pallas_call | solution.py:561
  (338 shorter events, 261.5 us)
Async XLA Ops:
  7.2 233.0 %all-gather.6.cloned.1.call-start = ((), (), s32[]{:S(2)}) async-start(), calls=%async_computation.2 | async-start | bytes 7077888 | tf_op jit(solution)/shard_map/all_gather | solution.py:726
  9.4 294.0 %all-gather.8.cloned.1.call-start = ((), (), s32[]{:S(2)}) async-start(), calls=%async_computation.3 | async-start | bytes 20054016 | tf_op jit(solution)/shard_map/all_gather | solution.py:745
  11.3 70.8 %collective-permute-start.23 = (bf16[1792]{0:T(1024)(128)(2,1)S(1)}, bf16[1792]{0:T(1024)(128)(2,1)S(1)}, u32[]{:S(2)}, u32[]{:S(2)}) collective-permute-start(bf16[1792]{0:T(1024)(128)(2,1)S(1)} %dynamic-update-slice.17), channel_id=1, source_target_pairs={{0,12},{4,8},{8,4},{12,0},{1,13},{5,9},{9,5},{13,1},{2,14},{6,10},... | collective-permute-start | bytes 10760 | tf_op jit(solution)/shard_map/ppermute | solution.py:729
  19.2 610.4 %reduce-scatter.5.cloned.1.call-start = ((), (), s32[]{:S(2)}) async-start(), calls=%async_computation.6 | async-start | bytes 12386304 | tf_op jit(solution)/shard_map/reduce_scatter | solution.py:914
  73.6 94.9 %collective-permute-start.19 = (bf16[704,1024]{1,0:T(8,128)(2,1)}, bf16[704,1024]{1,0:T(8,128)(2,1)S(1)}, u32[]{:S(2)}, u32[]{:S(2)}) collective-permute-start(bf16[704,1024]{1,0:T(8,128)(2,1)} %get-tuple-element.1206), channel_id=1, source_target_pairs={{0,8},{4,12},{8,0},{12,4},{1,9},{5,13},{9,1},{13,5},{2,10},{6,14},... | collective-permute-start | bytes 4325384 | tf_op jit(solution)/shard_map/ppermute | solution.py:729
  76.0 92.6 %collective-permute-start.20 = (bf16[704,1024]{1,0:T(8,128)(2,1)}, bf16[704,1024]{1,0:T(8,128)(2,1)}, u32[]{:S(2)}, u32[]{:S(2)}) collective-permute-start(bf16[704,1024]{1,0:T(8,128)(2,1)} %get-tuple-element.1204), channel_id=1, source_target_pairs={{0,12},{4,8},{8,4},{12,0},{1,13},{5,9},{9,5},{13,1},{2,14},{6,10},... | collective-permute-start | bytes 4325384 | tf_op jit(solution)/shard_map/ppermute | solution.py:729
  77.6 91.0 %collective-permute-start.18 = (bf16[704,1024]{1,0:T(8,128)(2,1)}, bf16[704,1024]{1,0:T(8,128)(2,1)}, u32[]{:S(2)}, u32[]{:S(2)}) collective-permute-start(bf16[704,1024]{1,0:T(8,128)(2,1)} %get-tuple-element.1205), channel_id=1, source_target_pairs={{0,4},{4,0},{8,12},{12,8},{1,5},{5,1},{9,13},{13,9},{2,6},{6,2},{1... | collective-permute-start | bytes 4325384 | tf_op jit(solution)/shard_map/ppermute | solution.py:729
  81.7 79.7 %collective-permute-start.22 = (bf16[1792]{0:T(1024)(128)(2,1)S(1)}, bf16[1792]{0:T(1024)(128)(2,1)S(1)}, u32[]{:S(2)}, u32[]{:S(2)}) collective-permute-start(bf16[1792]{0:T(1024)(128)(2,1)S(1)} %dynamic-update-slice.17), channel_id=1, source_target_pairs={{0,8},{4,12},{8,0},{12,4},{1,9},{5,13},{9,1},{13,5},{2,10},{6,14},... | collective-permute-start | bytes 10760 | tf_op jit(solution)/shard_map/ppermute | solution.py:729
  82.1 85.7 %collective-permute-start.21 = (bf16[1792]{0:T(1024)(128)(2,1)S(1)}, bf16[1792]{0:T(1024)(128)(2,1)S(1)}, u32[]{:S(2)}, u32[]{:S(2)}) collective-permute-start(bf16[1792]{0:T(1024)(128)(2,1)S(1)} %dynamic-update-slice.17), channel_id=1, source_target_pairs={{0,4},{4,0},{8,12},{12,8},{1,5},{5,1},{9,13},{13,9},{2,6},{6,2},{1... | collective-permute-start | bytes 10760 | tf_op jit(solution)/shard_map/ppermute | solution.py:729
  538.1 227.4 %reduce-scatter.3.cloned.1.call-start = ((), (), s32[]{:S(2)}) async-start(), calls=%async_computation.4 | async-start | bytes 19464192 | tf_op jit(solution)/shard_map/reduce_scatter | solution.py:854
  599.3 439.9 %all-gather.14.cloned.1.call-start = ((), (), s32[]{:S(2)}) async-start(), calls=%async_computation.8 | async-start | bytes 5406720 | tf_op jit(solution)/shard_map/all_gather | solution.py:915
  631.9 414.1 %all-gather.12.cloned.1.call-start = ((), (), s32[]{:S(2)}) async-start(), calls=%async_computation.7 | async-start | bytes 5013504 | tf_op jit(solution)/shard_map/all_gather | solution.py:916
  633.7 421.8 %all-gather.10.cloned.1.call-start = ((), (), s32[]{:S(2)}) async-start(), calls=%async_computation.5 | async-start | bytes 10813440 | tf_op jit(solution)/shard_map/all_gather | solution.py:855
  810.2 84.4 %collective-permute-start.30 = (bf16[704,1024]{1,0:T(8,128)(2,1)S(1)}, bf16[704,1024]{1,0:T(8,128)(2,1)}, u32[]{:S(2)}, u32[]{:S(2)}) collective-permute-start(bf16[704,1024]{1,0:T(8,128)(2,1)S(1)} %get-tuple-element.982), channel_id=1, source_target_pairs={{0,4},{4,0},{8,12},{12,8},{1,5},{5,1},{9,13},{13,9},{2,6},{6,2},{1... | collective-permute-start | bytes 4325384 | tf_op jit(solution)/shard_map/ppermute | solution.py:729
  811.9 82.8 %collective-permute-start.31 = (bf16[704,1024]{1,0:T(8,128)(2,1)S(1)}, bf16[704,1024]{1,0:T(8,128)(2,1)}, u32[]{:S(2)}, u32[]{:S(2)}) collective-permute-start(bf16[704,1024]{1,0:T(8,128)(2,1)S(1)} %get-tuple-element.983), channel_id=1, source_target_pairs={{0,8},{4,12},{8,0},{12,4},{1,9},{5,13},{9,1},{13,5},{2,10},{6,14},... | collective-permute-start | bytes 4325384 | tf_op jit(solution)/shard_map/ppermute | solution.py:729
  828.4 95.9 %collective-permute-start.32 = (bf16[704,1024]{1,0:T(8,128)(2,1)S(1)}, bf16[704,1024]{1,0:T(8,128)(2,1)}, u32[]{:S(2)}, u32[]{:S(2)}) collective-permute-start(bf16[704,1024]{1,0:T(8,128)(2,1)S(1)} %get-tuple-element.984), channel_id=1, source_target_pairs={{0,12},{4,8},{8,4},{12,0},{1,13},{5,9},{9,5},{13,1},{2,14},{6,10},... | collective-permute-start | bytes 4325384 | tf_op jit(solution)/shard_map/ppermute | solution.py:729
  859.5 64.8 %collective-permute-start.37 = (bf16[704,1024]{1,0:T(8,128)(2,1)S(1)}, bf16[704,1024]{1,0:T(8,128)(2,1)S(1)}, u32[]{:S(2)}, u32[]{:S(2)}) collective-permute-start(bf16[704,1024]{1,0:T(8,128)(2,1)S(1)} %get-tuple-element.985.refs_0_), channel_id=1, source_target_pairs={{0,1},{1,0},{2,3},{3,2},{4,5},{5,4},{6,7},{7,6},{8,9},{9,8},{10,11... | collective-permute-start | bytes 4325384 | tf_op jit(solution)/shard_map/ppermute | solution.py:729
  894.6 78.8 %collective-permute-start.34 = (bf16[704,1024]{1,0:T(8,128)(2,1)}, bf16[704,1024]{1,0:T(8,128)(2,1)}, u32[]{:S(2)}, u32[]{:S(2)}) collective-permute-start(bf16[704,1024]{1,0:T(8,128)(2,1)} %collective-permute-done.30.refs_1_), channel_id=1, source_target_pairs={{0,2},{2,0},{1,3},{3,1},{4,6},{6,4},{5,7},{7,5},{8,10},{10,8},{9,1... | collective-permute-start | bytes 4325384 | tf_op jit(solution)/shard_map/ppermute | solution.py:729
  924.3 80.1 %collective-permute-start.35 = (bf16[704,1024]{1,0:T(8,128)(2,1)}, bf16[704,1024]{1,0:T(8,128)(2,1)}, u32[]{:S(2)}, u32[]{:S(2)}) collective-permute-start(bf16[704,1024]{1,0:T(8,128)(2,1)} %collective-permute-done.31.refs_2_), channel_id=1, source_target_pairs={{0,2},{2,0},{1,3},{3,1},{4,6},{6,4},{5,7},{7,5},{8,10},{10,8},{9,1... | collective-permute-start | bytes 4325384 | tf_op jit(solution)/shard_map/ppermute | solution.py:729
  927.0 106.6 %collective-permute-start.36 = (bf16[704,1024]{1,0:T(8,128)(2,1)}, bf16[704,1024]{1,0:T(8,128)(2,1)}, u32[]{:S(2)}, u32[]{:S(2)}) collective-permute-start(bf16[704,1024]{1,0:T(8,128)(2,1)} %collective-permute-done.32.refs_3_), channel_id=1, source_target_pairs={{0,2},{2,0},{1,3},{3,1},{4,6},{6,4},{5,7},{7,5},{8,10},{10,8},{9,1... | collective-permute-start | bytes 4325384 | tf_op jit(solution)/shard_map/ppermute | solution.py:729
  929.6 152.9 %collective-permute-start.40 = (bf16[704,1024]{1,0:T(8,128)(2,1)}, bf16[704,1024]{1,0:T(8,128)(2,1)}, u32[]{:S(2)}, u32[]{:S(2)}) collective-permute-start(bf16[704,1024]{1,0:T(8,128)(2,1)} %collective-permute-done.32.refs_3_), channel_id=1, source_target_pairs={{0,1},{1,0},{2,3},{3,2},{4,5},{5,4},{6,7},{7,6},{8,9},{9,8},{10,11... | collective-permute-start | bytes 4325384 | tf_op jit(solution)/shard_map/ppermute | solution.py:729
  973.5 109.0 %collective-permute-start.41 = (bf16[704,1024]{1,0:T(8,128)(2,1)}, bf16[704,1024]{1,0:T(8,128)(2,1)}, u32[]{:S(2)}, u32[]{:S(2)}) collective-permute-start(bf16[704,1024]{1,0:T(8,128)(2,1)} %copy-done.53), channel_id=1, source_target_pairs={{0,1},{1,0},{2,3},{3,2},{4,5},{5,4},{6,7},{7,6},{8,9},{9,8},{10,11... | collective-permute-start | bytes 4325384 | tf_op jit(solution)/shard_map/ppermute | solution.py:729
  973.5 109.0 %collective-permute-start.42 = (bf16[704,1024]{1,0:T(8,128)(2,1)}, bf16[704,1024]{1,0:T(8,128)(2,1)}, u32[]{:S(2)}, u32[]{:S(2)}) collective-permute-start(bf16[704,1024]{1,0:T(8,128)(2,1)} %collective-permute-done.34.refs_5_), channel_id=1, source_target_pairs={{0,1},{1,0},{2,3},{3,2},{4,5},{5,4},{6,7},{7,6},{8,9},{9,8},{10,11... | collective-permute-start | bytes 4325384 | tf_op jit(solution)/shard_map/ppermute | solution.py:729
  1004.4 78.1 %collective-permute-start.43 = (bf16[704,1024]{1,0:T(8,128)(2,1)}, bf16[704,1024]{1,0:T(8,128)(2,1)}, u32[]{:S(2)}, u32[]{:S(2)}) collective-permute-start(bf16[704,1024]{1,0:T(8,128)(2,1)} %collective-permute-done.35.refs_6_), channel_id=1, source_target_pairs={{0,1},{1,0},{2,3},{3,2},{4,5},{5,4},{6,7},{7,6},{8,9},{9,8},{10,11... | collective-permute-start | bytes 4325384 | tf_op jit(solution)/shard_map/ppermute | solution.py:729
  (69 other events, 2892.7 us)
Sparse Core Ops, SparseCore 0:
  10.4 44.4 all-gather.5
  57.1 174.1 all-gather.7
  538.3 91.2 reduce-scatter.4
  634.4 130.9 reduce-scatter.2
  767.4 33.3 all-gather.13
  803.5 64.8 all-gather.11
  869.9 104.2 all-gather.9

commit v3 on v2

--- a/solution.py
+++ b/solution.py
@@ -135,21 +135,21 @@
     dqkv_ref[:, 2 * width:3 * width] = dv_t[...].T.astype(BF16)
 
 
-def attn_bwd(qkv, ctx, dctx, lse, n_seq, seq, n_pair):
+def attn_bwd(qkv, ctx, dctx, lse, at, seq, n_pair):
     width = 128
     return pl.pallas_call(
         attn_bwd_kernel,
-        grid=(n_seq, n_pair),
-        in_specs=[pl.BlockSpec((seq, 3 * width), lambda b, p: (b, p)),
-                  pl.BlockSpec((seq, width), lambda b, p: (b, p)),
-                  pl.BlockSpec((seq, width), lambda b, p: (b, p)),
-                  pl.BlockSpec((None, None, 2, seq), lambda b, p: (b, p, 0, 0))],
-        out_specs=pl.BlockSpec((seq, 3 * width), lambda b, p: (b, p)),
-        out_shape=jax.ShapeDtypeStruct((n_seq * seq, n_pair * 3 * width), BF16),
+        grid=(n_pair,),
+        in_specs=[pl.BlockSpec((seq, 3 * width), lambda p: (at, p)),
+                  pl.BlockSpec((seq, width), lambda p: (at, p)),
+                  pl.BlockSpec((seq, width), lambda p: (at, p)),
+                  pl.BlockSpec((None, None, 2, seq), lambda p: (at, p, 0, 0))],
+        out_specs=pl.BlockSpec((seq, 3 * width), lambda p: (0, p)),
+        out_shape=jax.ShapeDtypeStruct((seq, n_pair * 3 * width), BF16),
         scratch_shapes=[pltpu.VMEM((width, seq), F32), pltpu.VMEM((width, seq), F32)],
         name="attn_bwd",
-        cost_estimate=pl.CostEstimate(flops=n_seq * n_pair * 20 * seq * seq * 256 * 10 // 16, bytes_accessed=n_seq * seq * n_pair * width * 16,
-                                      transcendentals=n_seq * n_pair * seq * seq),
+        cost_estimate=pl.CostEstimate(flops=n_pair * 20 * seq * seq * 256 * 10 // 16, bytes_accessed=seq * n_pair * width * 16,
+                                      transcendentals=n_pair * seq * seq),
         compiler_params=pltpu.CompilerParams(vmem_limit_bytes=48 * 1024 * 1024),
     )(qkv, ctx, dctx, lse)
 
@@ -396,15 +396,14 @@
     )(d_up, w, x1, og, gain)
 
 
-def back1_kernel(dq_ref, w_ref, x_ref, dr_ref, gain_ref, tok_ref, pos_ref, sums_ref, bsum_ref):
-    @pl.when((pl.program_id(0) == 0) & (pl.program_id(1) == 0))
+def back1_kernel(dq_ref, w_ref, x_ref, dr_ref, gain_ref, *refs):
+    tok_ref, pos_ref, sums_ref, bsum_ref = refs[-4:]
+    before_refs = refs[:-4]
+
+    @pl.when(pl.program_id(0) == 0)
     def _():
-        sums_ref[...] = jnp.zeros(sums_ref.shape, F32)
-        bsum_ref[...] = jnp.zeros(bsum_ref.shape, F32)
-
-    @pl.when(pl.program_id(1) == 0)
-    def _():
-        pos_ref[...] = jnp.zeros(pos_ref.shape, F32)
+        sums_ref[...] = before_refs[1][...] if before_refs else jnp.zeros(sums_ref.shape, F32)
+        bsum_ref[...] = before_refs[2][...] if before_refs else jnp.zeros(bsum_ref.shape, F32)
 
     n_part = 2
     part = tok_ref.shape[0] // n_part
@@ -415,32 +414,53 @@
         d_x, d_gain = norm_back(d_y, x_ref[at, :], gain_ref[...])
         d_resid = dr_ref[at, :] + d_x
         tok_ref[at, :] = d_resid.astype(BF16)
-        pos_ref[at, :] += d_resid
+        pos_ref[at, :] = before_refs[0][at, :] + d_resid if before_refs else d_resid
         sums_ref[0:1, :] += col_sum(d_gain)
         sums_ref[1:2, :] += col_sum(d_y)
         bsum_ref[0:1, :] += col_sum(dq_ref[at, :].astype(F32))
 
 
-def back1(d_qkv, w_qkv, x, d_resid1, gain, n_seq, pos_rows):
-    n_tok, width = x.shape
-    n_cols = d_qkv.shape[1]
+def back1(d_qkv, w_qkv, x, d_resid1, gain, at, pos_rows, earlier=None):
+    seq, n_cols = d_qkv.shape
+    width = x.shape[1]
     rows = 256
-    per_seq = n_tok // n_seq // rows
-    mat = pl.BlockSpec((rows, width), lambda i, b: (b * per_seq + i, 0))
+    steps = seq // rows
+    mat = pl.BlockSpec((rows, width), lambda i: (at * steps + i, 0))
+    out = pl.BlockSpec((rows, width), lambda i: (i, 0))
+    few = [pl.BlockSpec((8, width), lambda i: (0, 0)), pl.BlockSpec((8, n_cols), lambda i: (0, 0))]
     return pl.pallas_call(
         back1_kernel,
-        grid=(per_seq, n_seq),
-        in_specs=[pl.BlockSpec((rows, n_cols), lambda i, b: (b * per_seq + i, 0)),
-                  pl.BlockSpec((n_cols, width), lambda i, b: (0, 0), pipeline_mode=pl.Buffered(1)),
-                  mat, mat, pl.BlockSpec((1, width), lambda i, b: (0, 0))],
-        out_specs=[mat, pl.BlockSpec((rows, width), lambda i, b: (i, 0)), pl.BlockSpec((8, width), lambda i, b: (0, 0)),
-                   pl.BlockSpec((8, n_cols), lambda i, b: (0, 0))],
-        out_shape=[jax.ShapeDtypeStruct((n_tok, width), BF16), jax.ShapeDtypeStruct((pos_rows, width), F32),
+        grid=(steps,),
+        in_specs=[pl.BlockSpec((rows, n_cols), lambda i: (i, 0)),
+                  pl.BlockSpec((n_cols, width), lambda i: (0, 0), pipeline_mode=pl.Buffered(1)),
+                  mat, mat, pl.BlockSpec((1, width), lambda i: (0, 0))] + ([out] + few if earlier else []),
+        out_specs=[out, out] + few,
+        out_shape=[jax.ShapeDtypeStruct((seq, width), BF16), jax.ShapeDtypeStruct((pos_rows, width), F32),
                    jax.ShapeDtypeStruct((8, width), F32), jax.ShapeDtypeStruct((8, n_cols), F32)],
         name="qkv_back",
-        cost_estimate=pl.CostEstimate(flops=2 * n_tok * n_cols * width, bytes_accessed=2 * n_tok * n_cols + n_tok * width * 12, transcendentals=0),
+        cost_estimate=pl.CostEstimate(flops=2 * seq * n_cols * width, bytes_accessed=2 * seq * n_cols + seq * width * 12, transcendentals=0),
         compiler_params=pltpu.CompilerParams(vmem_limit_bytes=48 * MIB),
-    )(d_qkv, w_qkv, x, d_resid1, gain)
+    )(d_qkv, w_qkv, x, d_resid1, gain, *(earlier or ()))
+
+
+def ff_out_kernel(n, start, g_ref, down_ref, up_ref):
+    down_ref[...] = g_ref[0, 0:n, :]
+    up_ref[...] = g_ref[0, start:start + n, :].T
+
+
+def ff_out(g, n, start, n_x, n_core):
+    n_piece, rows, width = g.shape
+    place = lambda p: (p % n_core) * n_x + p // n_core
+    return pl.pallas_call(
+        functools.partial(ff_out_kernel, n, start),
+        grid=(n_piece,),
+        in_specs=[pl.BlockSpec((1, rows, width), lambda p: (p, 0, 0))],
+        out_specs=[pl.BlockSpec((n, width), lambda p: (place(p), 0)), pl.BlockSpec((width, n), lambda p: (0, place(p)))],
+        out_shape=[jax.ShapeDtypeStruct((n_piece * n, width), F32), jax.ShapeDtypeStruct((width, n_piece * n), F32)],
+        name="ff_grads_out",
+        cost_estimate=pl.CostEstimate(flops=8_000_000_000, bytes_accessed=n_piece * rows * width * 8, transcendentals=0),
+        compiler_params=pltpu.CompilerParams(vmem_limit_bytes=24 * MIB),
+    )(g)
 
 
 def assemble_kernel(n, me_ref, *refs):
@@ -479,10 +499,16 @@
     tiles = width // LANES
     group = 8 * tiles
 
-    def fetch(block):
-        return pltpu.make_async_copy(tok_refs[block], buf.at[block % 2], in_sem.at[block % 2])
-
-    fetch(0).start()
+    def fetch(block, n):
+        return pltpu.make_async_copy(tok_refs[n], buf.at[block % 2], in_sem.at[block % 2])
+
+    def fetch_next(block):
+        for n in range(n_block):
+            @pl.when(block == n)
+            def _(n=n):
+                fetch(block, n).start()
+
+    fetch_next(0)
     for s in range(n_sub):
         def clear(i, _, s=s):
             acc[s][pl.ds(pl.multiple_of(i * group, group), group), :] = jnp.zeros((group, LANES), F32)
@@ -502,12 +528,11 @@
         for j in range(n):
             acc[s][pl.ds(at[j], tiles, stride=8), :] = sums[j]
 
-    for block in range(n_block):
-        if block + 1 < n_block:
-            fetch(block + 1).start()
-        fetch(block).wait()
-
-        def widen(g, _, block=block):
+    def add_block(block, _):
+        fetch_next(block + 1)
+        fetch(block, 0).wait()
+
+        def widen(g, _):
             rows = buf[block % 2, pl.ds(pl.multiple_of(g * WIDEN, WIDEN), WIDEN), :].astype(F32)
             base = pl.multiple_of(g * (WIDEN // 8) * group, (WIDEN // 8) * group)
             for h in range(WIDEN // 8):
@@ -522,7 +547,7 @@
         both = functools.reduce(jnp.minimum, counts) // 2
         begin = [block * cap + starts[s] for s in range(n_sub)]
 
-        def together(i, _, begin=begin):
+        def together(i, _):
             for s in range(n_sub):
                 add_rows(s, begin[s] + 2 * i, 2)
             return 0
@@ -531,17 +556,20 @@
         for s in range(n_sub):
             fours = (counts[s] - 2 * both) // 4
 
-            def alone(i, _, s=s, begin=begin, both=both):
+            def alone(i, _, s=s):
                 add_rows(s, begin[s] + 2 * both + 4 * i, 4)
                 return 0
 
             lax.fori_loop(0, fours, alone, 0)
 
-            def single(i, _, s=s, begin=begin):
+            def single(i, _, s=s):
                 add_rows(s, begin[s] + i, 1)
                 return 0
 
             lax.fori_loop(2 * both + 4 * fours, counts[s], single, 0)
+        return 0
+
+    lax.fori_loop(0, n_block, add_block, 0)
     done = 0
     copies = []
     for s in range(n_sub):
@@ -612,14 +640,19 @@
     )(core, *args)
 
 
-def grad_rest_kernel(spans, last, core_ref, a1_ref, b1_ref, a2_ref, b2_ref, *refs):
-    out_ref = refs[-1]
-    plus = refs[0] if len(refs) > 1 else None
-    piece, piece_in = out_ref.shape[0] // 2, (refs[0].shape[0] // 2 if plus is not None else 0)
-    for (a_ref, b_ref), (start, stop) in zip(((a1_ref, b1_ref), (a2_ref, b2_ref)), spans):
-        half = a_ref.shape[1] // 2
+def grad_rest_kernel(spans, last, n_a2, core_ref, a1_ref, b1_ref, b2_ref, *refs):
+    a2_refs, refs, out_ref = refs[:n_a2], refs[n_a2:-1], refs[-1]
+    plus = refs[0] if refs else None
+    piece, piece_in = out_ref.shape[0] // 2, (plus.shape[0] // 2 if refs else 0)
+    rows = b2_ref.shape[0] // n_a2
+    for which, (start, stop) in enumerate(spans):
+        half = (a2_refs[0] if which else a1_ref).shape[1] // 2
         for i in range(0, 2 * half, 128):
-            g = dot_tn(a_ref[:, i:i + 128], b_ref[...])
+            cols = slice(i, i + 128)
+            if which:
+                g = sum(dot_tn(a_ref[:, cols], b2_ref[n * rows:(n + 1) * rows, :]) for n, a_ref in enumerate(a2_refs))
+            else:
+                g = dot_tn(a1_ref[:, cols], b1_ref[...])
             for x in range(2):
                 lo, hi = max(i, x * half), min(i + 128, (x + 1) * half)
                 if lo < hi:
@@ -641,10 +674,8 @@
     last = tail[0].shape[2] if tail else 0
     piece = spans[-1][1] + last
     whole = pl.BlockSpec((n_tok, width), lambda t, c: (0, 0), pipeline_mode=pl.Buffered(1))
-    in_specs, args = [], []
-    for a, b in ((a1, b1), (a2, b2)):
-        in_specs += [pl.BlockSpec((n_tok, a.shape[1] // (2 * n_tp)), lambda t, c: (0, 2 * t + c[0])), whole]
-        args += [a, b]
+    cols = [pl.BlockSpec((a.shape[0], a.shape[1] // (2 * n_tp)), lambda t, c: (0, 2 * t + c[0])) for a in (a1, *a2)]
+    in_specs, args = [cols[0], whole, whole] + cols[1:], [a1, b1, b2, *a2]
     if plus is not None:
         in_specs.append(pl.BlockSpec((plus.shape[0] // n_tp, width), lambda t, c: (t, 0)))
         args.append(plus)
@@ -652,9 +683,9 @@
         in_specs.append(pl.BlockSpec((2, 1, last, width), lambda t, c: (t, c[0], 0, 0)))
         in_specs.append(pl.BlockSpec((2 * last, width), lambda t, c: (t, 0)))
         args += tail
-    n_cols = a1.shape[1] + a2.shape[1]
-    return pl.pallas_call(
-        functools.partial(grad_rest_kernel, spans, last),
+    n_cols = a1.shape[1] + a2[0].shape[1]
+    return pl.pallas_call(
+        functools.partial(grad_rest_kernel, spans, last, len(a2)),
         grid_spec=pltpu.PrefetchScalarGridSpec(num_scalar_prefetch=1, grid=(n_tp,), in_specs=in_specs,
                                                out_specs=pl.BlockSpec((2 * piece, width), lambda t, c: (t, 0))),
         out_shape=jax.ShapeDtypeStruct((2 * n_tp * piece, width), F32),
@@ -667,6 +698,7 @@
 
 POS_OFFSET = 2
 SLOTS = 704
+GRAD_SLOTS = 384
 LOW = 32
 
 
@@ -684,13 +716,13 @@
     return rank.reshape(n_blk, n_tok).astype(jnp.int32), jnp.sum(sums, axis=1).astype(jnp.int32)
 
 
-def compact(rank, valid, value):
-    n_high = SLOTS // LOW
+def compact(rank, valid, value, slots):
+    n_high = slots // LOW
     high = ((rank // LOW)[:, :, None] == jnp.arange(n_high)) & valid[:, :, None]
     low = ((rank % LOW)[:, :, None] == jnp.arange(LOW)).astype(F32)
     parts = jnp.concatenate([low * (value // 128).astype(F32)[:, :, None], low * (value % 128).astype(F32)[:, :, None]], axis=2)
     out = jnp.einsum("bjh,bjl->bhl", high.astype(BF16), parts.astype(BF16), preferred_element_type=F32).astype(jnp.int32)
-    return (out[:, :, :LOW] * 128 + out[:, :, LOW:]).reshape(rank.shape[0], SLOTS)
+    return (out[:, :, :LOW] * 128 + out[:, :, LOW:]).reshape(rank.shape[0], slots)
 
 
 def solution(mesh):
@@ -735,6 +767,9 @@
                 out.append(jnp.where(k < 2, jnp.where(k == 0, parts[0], parts[1]), jnp.where(k == 2, parts[2], parts[3])))
             return out
 
+        ids_all = lax.all_gather(tok_ids, dp, axis=0, tiled=True)
+        ids_all, w_up, w_down, w_out, b_qkv, b_up = lax.optimization_barrier((ids_all, w_up, w_down, w_out, b_qkv, b_up))
+
         wqkv_t = gather_rows(jnp.transpose(half(w_qkv, 2), (1, 2, 3, 0)).reshape(-1, width))
         n_ff, n_out = ff // n_dp, w_out.shape[0] * w_out.shape[1] // n_dp
 
@@ -753,7 +788,6 @@
         bup_w = biases[:, -ff:].reshape(1, -1).astype(F32)
         pos_rows = lax.slice_in_dim(pos_table, POS_OFFSET, POS_OFFSET + seq, axis=0)
 
-        ids_all = lax.all_gather(tok_ids, dp, axis=0, tiled=True).reshape(n_dp * n_tp, n_tok)
         local = ids_all - tp_index * rows
         sub_of = sum(((local >= s * sub).astype(jnp.int32) for s in range(1, n_sub)), jnp.zeros_like(local))
         owned = (local >= 0) & (local < rows)
@@ -761,28 +795,46 @@
         rank, counts = rank_in_class(hot)
         first = jnp.concatenate([jnp.zeros_like(counts[:, :1]), jnp.cumsum(counts, axis=1)], axis=1)
         rank = rank + jnp.sum(jnp.where(hot, first[:, None, :-1], 0), axis=2)
-        most = jnp.stack([jnp.max(jnp.sum(((ids_all >= o * rows) & (ids_all < (o + 1) * rows)).astype(jnp.int32), axis=1))
-                          for o in range(n_tp)])
-        rounds = (jnp.max(most) + SLOTS - 1) // SLOTS
+        owner_counts = jnp.stack([jnp.sum(((ids_all >= o * rows) & (ids_all < (o + 1) * rows)).astype(jnp.int32), axis=1)
+                                  for o in range(n_tp)])
+        grad_rounds = (jnp.max(owner_counts) + GRAD_SLOTS - 1) // GRAD_SLOTS
+        rounds = (jnp.max(jnp.sum(owner_counts.reshape(n_tp, -1, n_seq), axis=2)) + SLOTS - 1) // SLOTS
+
+        def after_first(ranks, totals):
+            return (ranks + (jnp.cumsum(totals, axis=1) - totals)[:, :, None]).reshape(ranks.shape[0], -1)
+
+        def grad_lists(r):
+            at = rank - r * GRAD_SLOTS
+            return compact(at, owned & (at >= 0) & (at < GRAD_SLOTS), jnp.where(owned, local, 0), GRAD_SLOTS)
+
+        my_rank = lax.dynamic_slice_in_dim(rank, dp_index * n_seq_dp, n_seq_dp, 0)
+        my_total = lax.dynamic_slice_in_dim(first[:, -1], dp_index * n_seq_dp, n_seq_dp, 0)
+        my_rank = after_first(my_rank.reshape(n_tp, n_seq, seq), my_total.reshape(n_tp, n_seq))
+        my_owned = lax.dynamic_slice_in_dim(owned, dp_index * n_seq_dp, n_seq_dp, 0).reshape(n_tp, n_tok)
+        my_local = lax.dynamic_slice_in_dim(local, dp_index * n_seq_dp, n_seq_dp, 0).reshape(n_tp, n_tok)
 
         def lists(r):
-            at = rank - r * SLOTS
-            return compact(at, owned & (at >= 0) & (at < SLOTS), jnp.where(owned, local, 0))
-
-        own_ids = lax.dynamic_index_in_dim(ids_all, dp_index * n_tp + tp_index, 0, keepdims=True)
+            at = my_rank - r * SLOTS
+            return compact(at, my_owned & (at >= 0) & (at < SLOTS), jnp.where(my_owned, my_local, 0), SLOTS)
+
+        own_ids = lax.dynamic_slice_in_dim(ids_all, dp_index * n_seq_dp + tp_index * n_seq, n_seq, 0)
         own_owner = sum(((own_ids >= o * rows).astype(jnp.int32) for o in range(1, n_tp)), jnp.zeros_like(own_ids))
         own_local = own_ids - own_owner * rows
         own_sub = sum(((own_local >= s * sub).astype(jnp.int32) for s in range(1, n_sub)), jnp.zeros_like(own_ids))
         own_hot = (own_owner * n_sub + own_sub)[:, :, None] == jnp.arange(n_tp * n_sub)
         own_rank, own_counts = rank_in_class(own_hot)
-        own_first = jnp.cumsum(own_counts.reshape(n_tp, n_sub), axis=1) - own_counts.reshape(n_tp, n_sub)
-        own_rank = (own_rank + jnp.sum(jnp.where(own_hot, own_first.reshape(1, 1, -1), 0), axis=2))[0]
-        own_owner = own_owner[0]
-
-        def own_lists(r):
-            at = jnp.broadcast_to(own_rank - r * SLOTS, (n_tp, n_tok))
-            mine = own_owner == jnp.arange(n_tp)[:, None]
-            return compact(at, mine & (at >= 0) & (at < SLOTS), jnp.broadcast_to(jnp.arange(n_tok), (n_tp, n_tok)))
+        own_counts = own_counts.reshape(n_seq, n_tp, n_sub)
+        own_first = jnp.cumsum(own_counts, axis=2) - own_counts
+        own_rank = own_rank + jnp.sum(jnp.where(own_hot, own_first.reshape(n_seq, 1, -1), 0), axis=2)
+        own_total = jnp.sum(own_counts, axis=2)
+        own_shift = jnp.cumsum(own_total, axis=0) - own_total
+        own_place = sum(jnp.where(own_owner == o, own_shift[:, o:o + 1], 0) for o in range(n_tp))
+        own_place = (own_place + own_rank).reshape(-1)
+
+        def own_lists(r, b):
+            at = jnp.broadcast_to(own_rank[b] - r * GRAD_SLOTS, (n_tp, seq))
+            mine = own_owner[b] == jnp.arange(n_tp)[:, None]
+            return compact(at, mine & (at >= 0) & (at < GRAD_SLOTS), jnp.broadcast_to(jnp.arange(seq), (n_tp, seq)), GRAD_SLOTS)
 
         tiles = width // 128
 
@@ -795,24 +847,22 @@
             got = list(sent)
             for k in range(1, n_tp):
                 got[k] = swap(sent[k], "tp", k)
-            at = own_rank - r * SLOTS
+            at = own_place - r * SLOTS
             valid = (at >= 0) & (at < SLOTS)
-            return got, jnp.where(valid, (own_owner ^ tp_index) * SLOTS + at, 0), valid
+            return got, jnp.where(valid, (own_owner.reshape(-1) ^ tp_index) * SLOTS + at, 0), valid
 
         def norm_rows(x):
             normed, _ = row_stats(x)
             return (normed * gain1 + bias1).astype(BF16)
 
-        lists0 = lists(0)
-        my_lists0 = lax.dynamic_slice_in_dim(lists0, dp_index * n_tp, n_tp, 0)
-        got0, place0, _ = rows_here(0, my_lists0)
+        got0, place0, _ = rows_here(0, lists(0))
         code0 = (place0 // 8) * (8 * tiles) + place0 % 8
         got0, out_grad = lax.optimization_barrier((got0, out_grad))
         resid_x, hid1 = embed(code0, got0, pos_rows, gain1, bias1, n_tok)
 
         def more_rows(carry):
             r, x, _ = carry
-            got, place, valid = rows_here(r, lax.dynamic_slice_in_dim(lists(r), dp_index * n_tp, n_tp, 0))
+            got, place, valid = rows_here(r, lists(r))
             new = jnp.take(jnp.concatenate(got), place, axis=0, mode="clip").astype(F32) + jnp.tile(pos_rows.astype(F32), (n_seq, 1))
             x = jnp.where(valid[:, None], new, x)
             return r + 1, x, norm_rows(x)
@@ -856,61 +906,70 @@
 
         d_resid1, d_attn, sums2 = back2(d_up, w_all, resid_x1, og, gain2)
         d_ctx = dot_nt(d_attn, wout_w).astype(BF16)
-        d_qkv = attn_bwd(qkv, ctx, d_ctx, lse, n_seq, seq, n_pair)
+        n_small = n_tp * (b_qkv.size + ff) // width + 6
+        p_pos = -(-(seq + n_small) // (24 * n_tp * n_dp)) * 24
         p_out = piece_of(wout_w.shape[0])
         spans = ((0, p_out), (p_out, p_out + piece_of(wqkv_t.shape[0])))
-        n_small = n_tp * (b_qkv.size + ff) // width + 6
-        p_pos = -(-(seq + n_small) // (24 * n_tp * n_dp)) * 24
-        rest_theirs = swap(grad_rest(1 - core, ctx, d_attn, d_qkv, hid1, n_tp, spans), "cc")
-        d_tok, pos_all, sums1, sums_qkv = back1(d_qkv, wqkv_t, resid_x, d_resid1, gain1, n_seq, p_pos * n_tp * n_dp)
-
-        def token_blocks(r):
-            own = own_lists(r)
+
+        def token_blocks(r, b, d_tok):
+            own = own_lists(r, b)
             place = jnp.concatenate([lax.dynamic_index_in_dim(own, tp_index ^ k, 0, keepdims=False) for k in range(n_tp)])
-            parts = pack((place // 8) * (8 * tiles) + place % 8, d_tok, SLOTS)
+            parts = pack((place // 8) * (8 * tiles) + place % 8, d_tok, GRAD_SLOTS)
             blocks = [swap(part, "tp", k) if k else part for k, part in enumerate(parts)]
             other = []
-            for b in blocks:
-                other.append(swap(b, "xx"))
-            return blocks + other + [swap(b, "cc") for b in blocks + other]
-
-        def in_block_order(table):
+            for block in blocks:
+                other.append(swap(block, "xx"))
+            return blocks + other + [swap(block, "cc") for block in blocks + other]
+
+        d_qkv0 = attn_bwd(qkv, ctx, d_ctx, lse, 0, seq, n_pair)
+        d_tok0, *sums0 = back1(d_qkv0, wqkv_t, resid_x, d_resid1, gain1, 0, p_pos * n_tp * n_dp)
+        blocks0 = token_blocks(0, 0, d_tok0)
+        d_qkv1 = attn_bwd(qkv, ctx, d_ctx, lse, 1, seq, n_pair)
+        d_tok1, pos_all, sums1, sums_qkv = back1(d_qkv1, wqkv_t, resid_x, d_resid1, gain1, 1, p_pos * n_tp * n_dp, earlier=sums0)
+        blocks1 = token_blocks(0, 1, d_tok1)
+        d_qkvs = [d_qkv0, d_qkv1]
+        rest_theirs = swap(grad_rest(1 - core, ctx, d_attn, d_qkvs, hid1, n_tp, spans), "cc")
+
+        def in_block_order(table, b):
             out = []
             for dc in range(n_core):
                 for dx in range(n_x):
                     for k in range(n_tp):
                         d = (x_index ^ dx) * n_core + (c_index ^ dc)
-                        out.append(lax.dynamic_index_in_dim(table, d * n_tp + (tp_index ^ k), 0, keepdims=False))
-            return jnp.stack(out)
-
-        block_rows = in_block_order(lists0)
+                        out.append(lax.dynamic_index_in_dim(table, (d * n_tp + (tp_index ^ k)) * n_seq + b, 0, keepdims=False))
+            return out
+
+        def both_orders(table):
+            return jnp.stack(in_block_order(table, 0) + in_block_order(table, 1))
+
+        d_w_down, d_w_up = ff_out(ff_grads.reshape(n_dp, -1, width), n_ff, p_ff, n_x, n_core)
+        blocks0[0], d_w_down, d_w_up = lax.optimization_barrier((blocks0[0], d_w_down, d_w_up))
+        block_rows = both_orders(grad_lists(0))
         in_sub = sum(((block_rows >= s * sub).astype(jnp.int32) for s in range(1, n_sub)), jnp.zeros_like(block_rows))
         in_sub = block_rows - in_sub * sub
-        slot = jnp.arange(SLOTS)
+        slot = jnp.arange(GRAD_SLOTS)
         code = (((in_sub // 8) * (8 * tiles) + in_sub % 8) << 16) | ((slot // 8) * (8 * tiles) + slot % 8)
-        block_first = jnp.minimum(in_block_order(first), SLOTS)
-        d_w_down = pick_pieces(ff_grads, 0, ff)
-        d_w_up = pick_pieces(ff_grads, p_ff, ff).T
-        blocks0, d_w_down, d_w_up = lax.optimization_barrier((token_blocks(0), d_w_down, d_w_up))
-        image = accum(blocks0, code.reshape(-1), block_first.reshape(-1), sub_rows, width)
+        code = code.reshape(-1)
+        block_first = jnp.minimum(both_orders(first), GRAD_SLOTS).reshape(-1)
+        image = accum(blocks0 + blocks1, code, block_first, sub_rows, width)
         d_emb = image.reshape(rows // 8, tiles, 8, 128).transpose(0, 2, 1, 3).reshape(rows, width)
 
         def more_grads(carry):
             r, table = carry
-            at = rank - r * SLOTS
-            there = owned & (at >= 0) & (at < SLOTS)
-            dest = compact(at, there, jnp.where(owned, local, 0) + 1)
+            at = rank - r * GRAD_SLOTS
+            there = owned & (at >= 0) & (at < GRAD_SLOTS)
+            dest = compact(at, there, jnp.where(owned, local, 0) + 1, GRAD_SLOTS)
             dest = jnp.where(dest == 0, rows, dest - 1)
-            grads = jnp.concatenate(token_blocks(r), axis=0).astype(F32)
-            return r + 1, table.at[in_block_order(dest).reshape(-1)].add(grads, mode="drop")
-
-        _, d_emb = lax.while_loop(lambda c: c[0] < rounds, more_grads, (jnp.int32(1), d_emb))
+            grads = jnp.concatenate(token_blocks(r, 0, d_tok0) + token_blocks(r, 1, d_tok1), axis=0).astype(F32)
+            return r + 1, table.at[both_orders(dest).reshape(-1)].add(grads, mode="drop")
+
+        _, d_emb = lax.while_loop(lambda c: c[0] < grad_rounds, more_grads, (jnp.int32(1), d_emb))
 
         small = jnp.concatenate([sums_qkv[0], d_b_up[0], sums1[:2].reshape(-1), sums2[:4].reshape(-1)]).reshape(-1, width)
         small = jnp.concatenate([small, jnp.zeros((pos_all.shape[0] - seq - n_small, width), F32)])
         pos_all = lax.dynamic_update_slice_in_dim(pos_all, small, seq, 0).reshape(n_tp * n_x, n_core, p_pos, width)
         pos_theirs = swap(lax.dynamic_index_in_dim(pos_all, 1 - c_index, 1, keepdims=False).reshape(-1, width), "cc")
-        rest = grad_rest(core, ctx, d_attn, d_qkv, hid1, n_tp, spans, plus=rest_theirs, tail=(pos_all, pos_theirs))
+        rest = grad_rest(core, ctx, d_attn, d_qkvs, hid1, n_tp, spans, plus=rest_theirs, tail=(pos_all, pos_theirs))
         rest = lax.psum_scatter(rest, ("tp", "xx"), scatter_dimension=0, tiled=True)
         rest_w = lax.all_gather(rest[:spans[1][1]], dp, axis=0, tiled=True)
         whole = lax.all_gather(rest[spans[1][1]:], ("tp", "xx", "cc"), axis=0, tiled=True)

time: 1170 us -> 1170 us (level)
  waiting for transfers between devices: 499 us -> 469 us
  Pallas kernels: 392 us -> 412 us
    ppermute x31 -> x46, waiting for transfers between devices: 337 us -> 307 us  [swap(): return lax.ppermute(v, axis, tp_swap[k] if axis == 'tp' else pair)]
    transpose x5 -> x2, local copies, waits for them, and re-layouts: 22.9 us -> 2.41 us  [pick_pieces(): return g.transpose(1, 0, 2, 3).reshape(n_rows, width)]
    pallas_call x4 -> x7, Pallas kernels: 116 us -> 126 us  [the longest x2 62.1 us: attn_bwd(): pl.pallas_call(attn_bwd_kernel, grid=(n_pair,), in_specs=[pl.BlockSpec((s...]
    ppermute x31 -> x46, starting transfers between devices: 28.5 us -> 35.5 us  [swap(): return lax.ppermute(v, axis, tp_swap[k] if axis == 'tp' else pair)]
    unnamed x116 -> x145, local copies, waits for them, and re-layouts: 21.8 us -> 26.9 us
  transfers between devices with their start and end apart: 38 -> 53, of which waited for: 16 -> 19; matrix products, arithmetic and copies ran while one was open for 15% -> 14% of each run, Pallas kernels for 13% -> 14%
where the time goes in v3:
time: 1170 us; the launch traced here: 1150 us
  waiting for transfers between devices  469 us (40%)
  Pallas kernels  412 us (35%)
  local copies, waits for them, and re-layouts  133 us (11%)
  matrix products  51 us (4%)
  starting transfers between devices  35.7 us (3%)
  between operations  19.3 us (2%)
  other arithmetic  14.6 us (1%)
    ppermute x46, waiting for transfers between devices, swap(): return lax.ppermute(v, axis, tp_swap[k] if axis == 'tp' else pair)  307 us
    reduce_scatter x1, waiting for transfers between devices, local_step(): lax.psum_scatter(ff_grads, ('tp', 'xx'), scatter_dimension=0, tiled=True)  131 us
    pallas_call x1, Pallas kernels, accum(): pl.pallas_call(functools.partial(accum_kernel, n_block, cap, sub_rows, wi...  64.6 us
    pallas_call x2, Pallas kernels, attn_bwd(): pl.pallas_call(attn_bwd_kernel, grid=(n_pair,), in_specs=[pl.BlockSpec((s...  62.1 us
    pallas_call x4, Pallas kernels, grad_pieces(): pl.pallas_call(functools.partial(grad_kernel, plus is not None), grid_spe...  56.3 us
    pallas_call x1, Pallas kernels, ffn(): pl.pallas_call(functools.partial(ffn_kernel, part), grid=(n_piece,), in_s...  56.3 us
    pallas_call x1, Pallas kernels, attn_fwd(): pl.pallas_call(attn_fwd_kernel, grid=(n_seq, n_pair), in_specs=[pl.BlockS...  41.2 us
    ppermute x46, starting transfers between devices, swap(): return lax.ppermute(v, axis, tp_swap[k] if axis == 'tp' else pair)  35.5 us
  transfers between devices with their start and end apart: 53, of which 19 were waited for; matrix products, arithmetic and copies ran while one was open for 14% of the time, Pallas kernels for 14%

profile of v3, /device:TPU:0, one launch (start us, length us, event | category | flops | bytes accessed | tf_op | source)
XLA Modules:
  0.0 1149.2 jit_solution(8650977255449947047)
XLA Ops:
  32.8 20.6 %gather_fusion.3 = bf16[1408,1024]{1,0:T(8,128)(2,1)} fusion(bf16[12568,1024]{1,0:T(8,128)(2,1)} %param.21, s32[2048]{0:T(1024)S(1)} %pad_clamp_fusion.3), kind=kCustom, calls=%fused_computation.3 | custom fusion | bytes 5772800 | tf_op jit(solution)/shard_map/jit(_take)/gather | solution.py:843
  53.4 19.4 %gather_fusion.4 = bf16[1408,1024]{1,0:T(8,128)(2,1)} fusion(bf16[12568,1024]{1,0:T(8,128)(2,1)} %param.21, s32[2048]{0:T(1024)S(1)} %pad_clamp_fusion.2), kind=kCustom, calls=%fused_computation.4 | custom fusion | bytes 5772800 | tf_op jit(solution)/shard_map/jit(_take)/gather | solution.py:845
  93.1 71.4 %collective-permute-done.37 = bf16[1792]{0:T(1024)(128)(2,1)S(1)} collective-permute-done((bf16[1792]{0:T(1024)(128)(2,1)S(1)}, bf16[1792]{0:T(1024)(128)(2,1)S(1)}, u32[]{:S(2)}, u32[]{:S(2)}) %collective-permute-start.37) | collective-permute-done | bytes 3616 | tf_op jit(solution)/shard_map/ppermute | solution.py:761
  186.5 31.2 %collective-permute-done.41.refs_3_ = bf16[2,256,1024]{2,1,0:T(8,128)(2,1)S(1)} collective-permute-done((bf16[2,256,1024]{2,1,0:T(8,128)(2,1)S(1)}, bf16[2,256,1024]{2,1,0:T(8,128)(2,1)S(1)}, u32[]{:S(2)}, u32[]{:S(2)}) %collective-permute-start.41) | collective-permute-done | bytes 1048608 | tf_op jit(solution)/shard_map/ppermute | solution.py:761
  217.7 18.7 %collective-permute-done.40.refs_2_ = bf16[2,256,1024]{2,1,0:T(8,128)(2,1)S(1)} collective-permute-done((bf16[2,256,1024]{2,1,0:T(8,128)(2,1)S(1)}, bf16[2,256,1024]{2,1,0:T(8,128)(2,1)S(1)}, u32[]{:S(2)}, u32[]{:S(2)}) %collective-permute-start.40) | collective-permute-done | bytes 1048608 | tf_op jit(solution)/shard_map/ppermute | solution.py:761
  249.2 19.4 %add_convert_fusion.1.qkv_ref = bf16[2048,3072]{1,0:T(8,128)(2,1)} fusion(bf16[2048,1024]{1,0:T(8,128)(2,1)} %get-tuple-element.1259.b2_ref, bf16[3072,1024]{1,0:T(8,128)(2,1)} %all-gather.6.cloned.1.call-done.w_ref, f32[3072]{0:T(1024)S(1)} %copy-done.41), kind=kOutput, calls=%fused_computation.280 | convolution fusion | flops 12897484800 | bytes 23080960 | tf_op jit(solution)/shard_map/dot_general | solution.py:20
  268.5 41.2 %attn_fwd.1 = (bf16[2048,1024]{1,0:T(8,128)(2,1)S(1)}, f32[2,8,2,1024]{3,2,1,0:T(2,128)S(1)}) custom-call(bf16[2048,3072]{1,0:T(8,128)(2,1)} %add_convert_fusion.1.qkv_ref), custom_call_target="tpu_custom_call" | custom-call | flops 21474836480 | bytes 16777216 | tf_op jit(solution)/shard_map/attn_fwd/pallas_call | solution.py:74
  326.7 56.3 %ffn.1 = (bf16[2048,4096]{1,0:T(8,128)(2,1)}, bf16[2048,4096]{1,0:T(8,128)(2,1)}, f32[1,4096]{1,0:T(1,128)S(1)}) custom-call(bf16[2048,1024]{1,0:T(8,128)(2,1)S(1)} %get-tuple-element.1268.h_ref.b_ref, bf16[2048,1024]{1,0:T(8,128)(2,1)} %bitcast.198, bf16[16,576,1024]{2,1,0:T(8,128)(2,1)} %bitcast.211, bf16[16,576,1024]{2,1,0:T(8,128)(2,1)} %bitcast.212, ...), custom_call_target="tpu_custom_call" | custom-call | flops 34359738368 | bytes 50331648 | tf_op jit(solution)/shard_map/ffn/pallas_call | solution.py:346
  383.0 29.7 %ffn_back.1 = (f32[2048,1024]{1,0:T(8,128)}, bf16[2048,1024]{1,0:T(8,128)(2,1)S(1)}, f32[8,1024]{1,0:T(8,128)S(1)}) custom-call(bf16[2048,4096]{1,0:T(8,128)(2,1)} %get-tuple-element.1271.dup_ref.a_ref, bf16[16,576,1024]{2,1,0:T(8,128)(2,1)} %bitcast.213, f32[2048,1024]{1,0:T(8,128)} %get-tuple-element.1267.x1_ref, bf16[2048,1024]{1,0:T(8,128)(2,1)} %bitcast.199, ...), custom_call_target="tpu_custom_call" | custom-call | flops 17179869184 | bytes 41943040 | tf_op jit(solution)/shard_map/ffn_back/pallas_call | solution.py:386
  418.9 30.7 %attn_bwd.3.dq_ref.refs_1_ = bf16[1024,3072]{1,0:T(8,128)(2,1)} custom-call(bf16[2048,3072]{1,0:T(8,128)(2,1)} %add_convert_fusion.1.qkv_ref, bf16[2048,1024]{1,0:T(8,128)(2,1)S(1)} %copy-done.4, bf16[2048,1024]{1,0:T(8,128)(2,1)} %convolution_convert_fusion.3.dctx_ref, f32[2,8,2,1024]{3,2,1,0:T(2,128)S(1)} %get-tuple-element.1273.lse_ref), custom_call_target="tpu_custom_call" | custom-call | flops 26843545600 | bytes 16777216 | tf_op jit(solution)/shard_map/attn_bwd/pallas_call | solution.py:140
  449.7 31.4 %attn_bwd.2.dq_ref.refs_0_ = bf16[1024,3072]{1,0:T(8,128)(2,1)} custom-call(bf16[2048,3072]{1,0:T(8,128)(2,1)} %add_convert_fusion.1.qkv_ref, bf16[2048,1024]{1,0:T(8,128)(2,1)S(1)} %copy-done.4, bf16[2048,1024]{1,0:T(8,128)(2,1)} %convolution_convert_fusion.3.dctx_ref, f32[2,8,2,1024]{3,2,1,0:T(2,128)S(1)} %get-tuple-element.1273.lse_ref), custom_call_target="tpu_custom_call" | custom-call | flops 26843545600 | bytes 16777216 | tf_op jit(solution)/shard_map/attn_bwd/pallas_call | solution.py:140
  493.8 16.0 %qkv_back.2 = (bf16[1024,1024]{1,0:T(8,128)(2,1)}, f32[1152,1024]{1,0:T(8,128)S(1)}, f32[8,1024]{1,0:T(8,128)S(1)}, f32[8,3072]{1,0:T(8,128)S(1)}) custom-call(bf16[1024,3072]{1,0:T(8,128)(2,1)} %attn_bwd.2.dq_ref.refs_0_, bf16[3072,1024]{1,0:T(8,128)(2,1)} %all-gather.6.cloned.1.call-done.w_ref, f32[2048,1024]{1,0:T(8,128)} %get-tuple-element.1266.x_ref, ...), custom_call_target="tpu_custom_call" | custom-call | flops 6442450944 | bytes 18874368 | tf_op jit(solution)/shard_map/qkv_back/pallas_call | solution.py:431
  511.9 15.5 %qkv_back.3 = (bf16[1024,1024]{1,0:T(8,128)(2,1)S(1)}, f32[1152,1024]{1,0:T(8,128)S(1)}, f32[8,1024]{1,0:T(8,128)S(1)}, f32[8,3072]{1,0:T(8,128)S(1)}) custom-call(bf16[1024,3072]{1,0:T(8,128)(2,1)} %attn_bwd.3.dq_ref.refs_1_, bf16[3072,1024]{1,0:T(8,128)(2,1)} %all-gather.6.cloned.1.call-done.w_ref, f32[2048,1024]{1,0:T(8,128)} %get-tuple-element.1266.x_ref, ...), custom_call_target="tpu_custom_call" | custom-call | flops 6442450944 | bytes 18874368 | tf_op jit(solution)/shard_map/qkv_back/pallas_call | solution.py:431
  541.5 16.1 %weight_grads.3 = f32[2688,1024]{1,0:T(8,128)} custom-call(s32[1]{0:T(128)} %bitcast.42.core_ref, bf16[2048,1024]{1,0:T(8,128)(2,1)S(1)} %copy-done.5, bf16[2048,1024]{1,0:T(8,128)(2,1)S(1)} %copy-done.7, bf16[2048,1024]{1,0:T(8,128)(2,1)} %get-tuple-element.1259.b2_ref, bf16[1024,3072]{1,0:T(8,128)(2,1)} %attn_bwd.2.dq_ref.refs_0_, ...), custom_call_target="tpu_custom_call" | custom-call | flops 8589934592 | bytes 25165824 | tf_op jit(solution)/shard_map/weight_grads/pallas_call | solution.py:687
  619.3 30.7 %reduce-scatter.5.cloned.1.call-done = f32[336,1024]{1,0:T(8,128)} async-done(((f32[2688,1024]{1,0:T(8,128)}), f32[336,1024]{1,0:T(8,128)}) %reduce-scatter.5.cloned.1.call-update) | async-done | bytes 1376272 | tf_op jit(solution)/shard_map/reduce_scatter | solution.py:973
  654.5 131.4 %reduce-scatter.3.cloned.1.call-done = f32[528,1024]{1,0:T(8,128)} async-done(((f32[4224,1024]{1,0:T(8,128)}), f32[528,1024]{1,0:T(8,128)}) %reduce-scatter.3.cloned.1.call-update) | async-done | bytes 2162704 | tf_op jit(solution)/shard_map/reduce_scatter | solution.py:904
  822.3 15.8 %collective-permute-done.63.refs_18_ = bf16[384,1024]{1,0:T(8,128)(2,1)} collective-permute-done((bf16[384,1024]{1,0:T(8,128)(2,1)S(1)}, bf16[384,1024]{1,0:T(8,128)(2,1)}, u32[]{:S(2)}, u32[]{:S(2)}) %collective-permute-start.63) | collective-permute-done | bytes 786464 | tf_op jit(solution)/shard_map/ppermute | solution.py:761
  840.8 22.5 %add_convert_fusion.2 = bf16[2048,1024]{1,0:T(8,128)(2,1)} fusion(f32[2048,1024]{1,0:T(8,128)} %get-tuple-element.1267.x1_ref, f32[1024]{0:T(1024)S(1)} %convert_element_type.404, bf16[2048,4096]{1,0:T(8,128)(2,1)S(1)} %bitcast.216, bf16[4096,1024]{1,0:T(8,128)(2,1)} %bitcast.218), kind=kOutput, calls=%fused_computation.281 | convolution fusion | flops 17190354944 | bytes 37752832 | tf_op jit(solution)/shard_map/dot_general | solution.py:24
  909.6 21.3 %collective-permute-done.43.refs_2_ = bf16[2,256,1024]{2,1,0:T(8,128)(2,1)} collective-permute-done((bf16[2,256,1024]{2,1,0:T(8,128)(2,1)}, bf16[2,256,1024]{2,1,0:T(8,128)(2,1)}, u32[]{:S(2)}, u32[]{:S(2)}) %collective-permute-start.43) | collective-permute-done | bytes 1048608 | tf_op jit(solution)/shard_map/ppermute | solution.py:761
  937.7 30.7 %collective-permute-done.67.refs_22_ = bf16[384,1024]{1,0:T(8,128)(2,1)S(1)} collective-permute-done((bf16[384,1024]{1,0:T(8,128)(2,1)}, bf16[384,1024]{1,0:T(8,128)(2,1)S(1)}, u32[]{:S(2)}, u32[]{:S(2)}) %collective-permute-start.67) | collective-permute-done | bytes 786464 | tf_op jit(solution)/shard_map/ppermute | solution.py:761
  973.3 28.9 %collective-permute-done.68.refs_23_ = bf16[384,1024]{1,0:T(8,128)(2,1)} collective-permute-done((bf16[384,1024]{1,0:T(8,128)(2,1)}, bf16[384,1024]{1,0:T(8,128)(2,1)}, u32[]{:S(2)}, u32[]{:S(2)}) %collective-permute-start.68) | collective-permute-done | bytes 786464 | tf_op jit(solution)/shard_map/ppermute | solution.py:761
  1004.3 20.1 %collective-permute-done.51.refs_5_ = bf16[384,1024]{1,0:T(8,128)(2,1)} collective-permute-done((bf16[384,1024]{1,0:T(8,128)(2,1)}, bf16[384,1024]{1,0:T(8,128)(2,1)}, u32[]{:S(2)}, u32[]{:S(2)}) %collective-permute-start.51) | collective-permute-done | bytes 786464 | tf_op jit(solution)/shard_map/ppermute | solution.py:761
  1041.7 15.8 %collective-permute-done.53.refs_7_ = bf16[384,1024]{1,0:T(8,128)(2,1)} collective-permute-done((bf16[384,1024]{1,0:T(8,128)(2,1)}, bf16[384,1024]{1,0:T(8,128)(2,1)}, u32[]{:S(2)}, u32[]{:S(2)}) %collective-permute-start.53) | collective-permute-done | bytes 786464 | tf_op jit(solution)/shard_map/ppermute | solution.py:761
  1076.2 64.6 %table_accum.1 = f32[100544,128]{1,0:T(8,128)} custom-call(s32[12288]{0:T(1024)} %fusion.143.where_ref, s32[160]{0:T(256)} %min.12.first_ref, bf16[384,1024]{1,0:T(8,128)(2,1)} %copy-done.18, bf16[384,1024]{1,0:T(8,128)(2,1)} %collective-permute-done.47.refs_1_, bf16[384,1024]{1,0:T(8,128)(2,1)} %collective-permute-done.48.refs_2_, ...), custom_call_target="tpu_custom_call" | custom-call | flops 49999998976 | bytes 100000000 | tf_op jit(solution)/shard_map/table_accum/pallas_call | solution.py:589
  (469 shorter events, 330.4 us)
Async XLA Ops:
  7.2 241.4 %all-gather.6.cloned.1.call-start = ((), (), s32[]{:S(2)}) async-start(), calls=%async_computation.2 | async-start | bytes 7077888 | tf_op jit(solution)/shard_map/all_gather | solution.py:758
  9.4 302.3 %all-gather.8.cloned.1.call-start = ((), (), s32[]{:S(2)}) async-start(), calls=%async_computation.3 | async-start | bytes 20054016 | tf_op jit(solution)/shard_map/all_gather | solution.py:780
  18.2 67.9 %collective-permute-start.38 = (bf16[1792]{0:T(1024)(128)(2,1)S(1)}, bf16[1792]{0:T(1024)(128)(2,1)S(1)}, u32[]{:S(2)}, u32[]{:S(2)}) collective-permute-start(bf16[1792]{0:T(1024)(128)(2,1)S(1)} %dynamic-update-slice.33), channel_id=1, source_target_pairs={{0,12},{4,8},{8,4},{12,0},{1,13},{5,9},{9,5},{13,1},{2,14},{6,10},... | collective-permute-start | bytes 10760 | tf_op jit(solution)/shard_map/ppermute | solution.py:761
  26.3 623.7 %reduce-scatter.5.cloned.1.call-start = ((), (), s32[]{:S(2)}) async-start(), calls=%async_computation.6 | async-start | bytes 12386304 | tf_op jit(solution)/shard_map/reduce_scatter | solution.py:973
  76.1 93.2 %collective-permute-start.34 = (bf16[704,1024]{1,0:T(8,128)(2,1)}, bf16[704,1024]{1,0:T(8,128)(2,1)S(1)}, u32[]{:S(2)}, u32[]{:S(2)}) collective-permute-start(bf16[704,1024]{1,0:T(8,128)(2,1)} %get-tuple-element.1576), channel_id=1, source_target_pairs={{0,8},{4,12},{8,0},{12,4},{1,9},{5,13},{9,1},{13,5},{2,10},{6,14},... | collective-permute-start | bytes 4325384 | tf_op jit(solution)/shard_map/ppermute | solution.py:761
  80.4 89.0 %collective-permute-start.35 = (bf16[704,1024]{1,0:T(8,128)(2,1)}, bf16[704,1024]{1,0:T(8,128)(2,1)}, u32[]{:S(2)}, u32[]{:S(2)}) collective-permute-start(bf16[704,1024]{1,0:T(8,128)(2,1)} %get-tuple-element.1574), channel_id=1, source_target_pairs={{0,12},{4,8},{8,4},{12,0},{1,13},{5,9},{9,5},{13,1},{2,14},{6,10},... | collective-permute-start | bytes 4325384 | tf_op jit(solution)/shard_map/ppermute | solution.py:761
  81.8 87.5 %collective-permute-start.33 = (bf16[704,1024]{1,0:T(8,128)(2,1)}, bf16[704,1024]{1,0:T(8,128)(2,1)}, u32[]{:S(2)}, u32[]{:S(2)}) collective-permute-start(bf16[704,1024]{1,0:T(8,128)(2,1)} %get-tuple-element.1575), channel_id=1, source_target_pairs={{0,4},{4,0},{8,12},{12,8},{1,5},{5,1},{9,13},{13,9},{2,6},{6,2},{1... | collective-permute-start | bytes 4325384 | tf_op jit(solution)/shard_map/ppermute | solution.py:761
  85.7 78.9 %collective-permute-start.37 = (bf16[1792]{0:T(1024)(128)(2,1)S(1)}, bf16[1792]{0:T(1024)(128)(2,1)S(1)}, u32[]{:S(2)}, u32[]{:S(2)}) collective-permute-start(bf16[1792]{0:T(1024)(128)(2,1)S(1)} %dynamic-update-slice.33), channel_id=1, source_target_pairs={{0,8},{4,12},{8,0},{12,4},{1,9},{5,13},{9,1},{13,5},{2,10},{6,14},... | collective-permute-start | bytes 10760 | tf_op jit(solution)/shard_map/ppermute | solution.py:761
  86.1 82.5 %collective-permute-start.36 = (bf16[1792]{0:T(1024)(128)(2,1)S(1)}, bf16[1792]{0:T(1024)(128)(2,1)S(1)}, u32[]{:S(2)}, u32[]{:S(2)}) collective-permute-start(bf16[1792]{0:T(1024)(128)(2,1)S(1)} %dynamic-update-slice.33), channel_id=1, source_target_pairs={{0,4},{4,0},{8,12},{12,8},{1,5},{5,1},{9,13},{13,9},{2,6},{6,2},{1... | collective-permute-start | bytes 10760 | tf_op jit(solution)/shard_map/ppermute | solution.py:761
  173.6 62.7 %collective-permute-start.40 = (bf16[2,256,1024]{2,1,0:T(8,128)(2,1)S(1)}, bf16[2,256,1024]{2,1,0:T(8,128)(2,1)S(1)}, u32[]{:S(2)}, u32[]{:S(2)}) collective-permute-start(bf16[2,256,1024]{2,1,0:T(8,128)(2,1)S(1)} %get-tuple-element.1571), channel_id=1, source_target_pairs={{0,8},{4,12},{8,0},{12,4},{1,9},{5,13},{9,1},{13,5},{2,10},{6,14},... | collective-permute-start | bytes 3145736 | tf_op jit(solution)/shard_map/ppermute | solution.py:761
  174.0 64.7 %collective-permute-start.39 = (bf16[2,256,1024]{2,1,0:T(8,128)(2,1)S(1)}, bf16[2,256,1024]{2,1,0:T(8,128)(2,1)S(1)}, u32[]{:S(2)}, u32[]{:S(2)}) collective-permute-start(bf16[2,256,1024]{2,1,0:T(8,128)(2,1)S(1)} %get-tuple-element.1572), channel_id=1, source_target_pairs={{0,4},{4,0},{8,12},{12,8},{1,5},{5,1},{9,13},{13,9},{2,6},{6,2},{1... | collective-permute-start | bytes 3145736 | tf_op jit(solution)/shard_map/ppermute | solution.py:761
  557.6 228.3 %reduce-scatter.3.cloned.1.call-start = ((), (), s32[]{:S(2)}) async-start(), calls=%async_computation.4 | async-start | bytes 19464192 | tf_op jit(solution)/shard_map/reduce_scatter | solution.py:904
  619.2 410.7 %all-gather.14.cloned.1.call-start = ((), (), s32[]{:S(2)}) async-start(), calls=%async_computation.8 | async-start | bytes 5406720 | tf_op jit(solution)/shard_map/all_gather | solution.py:974
  652.4 405.7 %all-gather.12.cloned.1.call-start = ((), (), s32[]{:S(2)}) async-start(), calls=%async_computation.7 | async-start | bytes 5013504 | tf_op jit(solution)/shard_map/all_gather | solution.py:975
  654.1 413.8 %all-gather.10.cloned.1.call-start = ((), (), s32[]{:S(2)}) async-start(), calls=%async_computation.5 | async-start | bytes 10813440 | tf_op jit(solution)/shard_map/all_gather | solution.py:905
  803.9 63.6 %collective-permute-start.69 = (bf16[384,1024]{1,0:T(8,128)(2,1)S(1)}, bf16[384,1024]{1,0:T(8,128)(2,1)}, u32[]{:S(2)}, u32[]{:S(2)}) collective-permute-start(bf16[384,1024]{1,0:T(8,128)(2,1)S(1)} %get-tuple-element.1287.refs_16_), channel_id=1, source_target_pairs={{0,1},{1,0},{2,3},{3,2},{4,5},{5,4},{6,7},{7,6},{8,9},{9,8},{10,11... | collective-permute-start | bytes 2359304 | tf_op jit(solution)/shard_map/ppermute | solution.py:761
  810.4 60.0 %collective-permute-start.65 = (bf16[384,1024]{1,0:T(8,128)(2,1)S(1)}, bf16[384,1024]{1,0:T(8,128)(2,1)}, u32[]{:S(2)}, u32[]{:S(2)}) collective-permute-start(bf16[384,1024]{1,0:T(8,128)(2,1)S(1)} %get-tuple-element.1287.refs_16_), channel_id=1, source_target_pairs={{0,2},{2,0},{1,3},{3,1},{4,6},{6,4},{5,7},{7,5},{8,10},{10,8},{9,1... | collective-permute-start | bytes 2359304 | tf_op jit(solution)/shard_map/ppermute | solution.py:761
  870.4 60.5 %collective-permute-start.43 = (bf16[2,256,1024]{2,1,0:T(8,128)(2,1)}, bf16[2,256,1024]{2,1,0:T(8,128)(2,1)}, u32[]{:S(2)}, u32[]{:S(2)}) collective-permute-start(bf16[2,256,1024]{2,1,0:T(8,128)(2,1)} %get-tuple-element.1567), channel_id=1, source_target_pairs={{0,8},{4,12},{8,0},{12,4},{1,9},{5,13},{9,1},{13,5},{2,10},{6,14},... | collective-permute-start | bytes 3145736 | tf_op jit(solution)/shard_map/ppermute | solution.py:761
  870.5 62.0 %collective-permute-start.42 = (bf16[2,256,1024]{2,1,0:T(8,128)(2,1)}, bf16[2,256,1024]{2,1,0:T(8,128)(2,1)}, u32[]{:S(2)}, u32[]{:S(2)}) collective-permute-start(bf16[2,256,1024]{2,1,0:T(8,128)(2,1)} %get-tuple-element.1568), channel_id=1, source_target_pairs={{0,4},{4,0},{8,12},{12,8},{1,5},{5,1},{9,13},{13,9},{2,6},{6,2},{1... | collective-permute-start | bytes 3145736 | tf_op jit(solution)/shard_map/ppermute | solution.py:761
  935.4 66.8 %collective-permute-start.68 = (bf16[384,1024]{1,0:T(8,128)(2,1)}, bf16[384,1024]{1,0:T(8,128)(2,1)}, u32[]{:S(2)}, u32[]{:S(2)}) collective-permute-start(bf16[384,1024]{1,0:T(8,128)(2,1)} %collective-permute-done.64.refs_19_), channel_id=1, source_target_pairs={{0,2},{2,0},{1,3},{3,1},{4,6},{6,4},{5,7},{7,5},{8,10},{10,8},{9,1... | collective-permute-start | bytes 2359304 | tf_op jit(solution)/shard_map/ppermute | solution.py:761
  936.0 67.7 %collective-permute-start.55 = (bf16[384,1024]{1,0:T(8,128)(2,1)}, bf16[384,1024]{1,0:T(8,128)(2,1)}, u32[]{:S(2)}, u32[]{:S(2)}) collective-permute-start(bf16[384,1024]{1,0:T(8,128)(2,1)} %collective-permute-done.47.refs_1_), channel_id=1, source_target_pairs={{0,1},{1,0},{2,3},{3,2},{4,5},{5,4},{6,7},{7,6},{8,9},{9,8},{10,11... | collective-permute-start | bytes 2359304 | tf_op jit(solution)/shard_map/ppermute | solution.py:761
  936.2 88.2 %collective-permute-start.51 = (bf16[384,1024]{1,0:T(8,128)(2,1)}, bf16[384,1024]{1,0:T(8,128)(2,1)}, u32[]{:S(2)}, u32[]{:S(2)}) collective-permute-start(bf16[384,1024]{1,0:T(8,128)(2,1)} %collective-permute-done.47.refs_1_), channel_id=1, source_target_pairs={{0,2},{2,0},{1,3},{3,1},{4,6},{6,4},{5,7},{7,5},{8,10},{10,8},{9,1... | collective-permute-start | bytes 2359304 | tf_op jit(solution)/shard_map/ppermute | solution.py:761
  968.4 56.0 %collective-permute-start.56 = (bf16[384,1024]{1,0:T(8,128)(2,1)}, bf16[384,1024]{1,0:T(8,128)(2,1)}, u32[]{:S(2)}, u32[]{:S(2)}) collective-permute-start(bf16[384,1024]{1,0:T(8,128)(2,1)} %collective-permute-done.48.refs_2_), channel_id=1, source_target_pairs={{0,1},{1,0},{2,3},{3,2},{4,5},{5,4},{6,7},{7,6},{8,9},{9,8},{10,11... | collective-permute-start | bytes 2359304 | tf_op jit(solution)/shard_map/ppermute | solution.py:761
  1003.7 53.8 %collective-permute-start.53 = (bf16[384,1024]{1,0:T(8,128)(2,1)}, bf16[384,1024]{1,0:T(8,128)(2,1)}, u32[]{:S(2)}, u32[]{:S(2)}) collective-permute-start(bf16[384,1024]{1,0:T(8,128)(2,1)} %collective-permute-done.49.refs_3_), channel_id=1, source_target_pairs={{0,2},{2,0},{1,3},{3,1},{4,6},{6,4},{5,7},{7,5},{8,10},{10,8},{9,1... | collective-permute-start | bytes 2359304 | tf_op jit(solution)/shard_map/ppermute | solution.py:761
  (96 other events, 2810.5 us)
Sparse Core Ops, SparseCore 0:
  10.4 44.5 all-gather.5
  57.2 175.3 all-gather.7
  557.7 92.2 reduce-scatter.4
  654.8 131.0 reduce-scatter.2
  787.9 39.5 all-gather.13
  829.5 86.1 all-gather.11
  917.2 97.5 all-gather.9

commit v4 on v3

--- a/solution.py
+++ b/solution.py
@@ -443,24 +443,42 @@
     )(d_qkv, w_qkv, x, d_resid1, gain, *(earlier or ()))
 
 
-def ff_out_kernel(n, start, g_ref, down_ref, up_ref):
-    down_ref[...] = g_ref[0, 0:n, :]
-    up_ref[...] = g_ref[0, start:start + n, :].T
-
-
-def ff_out(g, n, start, n_x, n_core):
-    n_piece, rows, width = g.shape
-    place = lambda p: (p % n_core) * n_x + p // n_core
-    return pl.pallas_call(
-        functools.partial(ff_out_kernel, n, start),
-        grid=(n_piece,),
-        in_specs=[pl.BlockSpec((1, rows, width), lambda p: (p, 0, 0))],
-        out_specs=[pl.BlockSpec((n, width), lambda p: (place(p), 0)), pl.BlockSpec((width, n), lambda p: (0, place(p)))],
-        out_shape=[jax.ShapeDtypeStruct((n_piece * n, width), F32), jax.ShapeDtypeStruct((width, n_piece * n), F32)],
-        name="ff_grads_out",
-        cost_estimate=pl.CostEstimate(flops=8_000_000_000, bytes_accessed=n_piece * rows * width * 8, transcendentals=0),
-        compiler_params=pltpu.CompilerParams(vmem_limit_bytes=24 * MIB),
-    )(g)
+def pieces_out_kernel(n_in, spans, me_ref, *refs):
+    out_refs = refs[n_in:]
+    for p in range(n_in):
+        @pl.when(pl.program_id(0) == p)
+        def _(p=p):
+            for (start, n, turned), out_ref in zip(spans, out_refs):
+                part = refs[p][start:start + n, :]
+                out_ref[...] = part.T if turned else part
+
+
+def pieces_out(me, pieces, spans):
+    rows, width = pieces[0].shape
+    n_in = len(pieces)
+
+    def place(p, m):
+        return (m[1] ^ (p // 2)) * 2 + (m[0] ^ (p % 2))
+
+    out_specs, out_shape = [], []
+    for start, n, turned in spans:
+        if turned:
+            out_specs.append(pl.BlockSpec((width, n), lambda p, m: (0, place(p, m))))
+            out_shape.append(jax.ShapeDtypeStruct((width, n_in * n), F32))
+        else:
+            out_specs.append(pl.BlockSpec((n, width), lambda p, m: (place(p, m), 0)))
+            out_shape.append(jax.ShapeDtypeStruct((n_in * n, width), F32))
+    return pl.pallas_call(
+        functools.partial(pieces_out_kernel, n_in, spans),
+        grid_spec=pltpu.PrefetchScalarGridSpec(
+            num_scalar_prefetch=1, grid=(n_in,),
+            in_specs=[pl.BlockSpec((rows, width), lambda p, m: (0, 0), pipeline_mode=pl.Buffered(1))] * n_in,
+            out_specs=out_specs),
+        out_shape=out_shape,
+        name="grads_out",
+        cost_estimate=pl.CostEstimate(flops=8_000_000_000, bytes_accessed=n_in * rows * width * 8, transcendentals=0),
+        compiler_params=pltpu.CompilerParams(vmem_limit_bytes=32 * MIB),
+    )(me, *pieces)
 
 
 def assemble_kernel(n, me_ref, *refs):
@@ -777,8 +795,9 @@
             n = w.shape[axis] // n_dp
             return lax.dynamic_slice_in_dim(w, dp_index * n, n, axis)
 
-        w_all = lax.all_gather(jnp.concatenate([quarter(w_up, 1).T, quarter(w_down, 0), quarter(w_out.reshape(-1, width), 0)]),
-                               ("tp", "xx", "cc"), axis=0, tiled=True).reshape(n_tp * n_dp, 2 * n_ff + n_out, width)
+        own_w = jnp.concatenate([quarter(w_up, 1).T, quarter(w_down, 0), quarter(w_out.reshape(-1, width), 0)])
+        w_all = lax.all_gather(own_w, ("tp", "xx", "cc"), axis=0, tiled=True)
+        w_all = w_all.reshape(n_tp * n_dp, 2 * n_ff + n_out, width)
         wdown_w = w_all[:, n_ff:2 * n_ff].reshape(-1, width)
         wout_w = w_all[:, 2 * n_ff:].reshape(-1, width)
         n_pair = wqkv_t.shape[0] // (3 * 128)
@@ -891,10 +910,11 @@
         def piece_of(n_rows):
             return -(-n_rows // (4 * n_tp) // 24) * 24
 
-        def pick_pieces(g, start, n_rows):
-            n = n_rows // (n_x * n_core)
-            g = g.reshape(n_x, n_core, -1, width)[:, :, start:start + n]
-            return g.transpose(1, 0, 2, 3).reshape(n_rows, width)
+        def every_piece(g):
+            other = swap(g, "xx")
+            return [g, other, swap(g, "cc"), swap(other, "cc")]
+
+        x_and_core = jnp.stack([x_index, c_index])
 
         p_ff = piece_of(n_tp * ff)
         down_theirs = swap(grad_pieces(1 - core, act, og, n_tp, p_ff, 0, 1), "cc")
@@ -902,7 +922,7 @@
         ff_grads = grad_pieces(core, act, og, n_tp, p_ff, 0, 2, plus=down_theirs)
         ff_grads = grad_pieces(core, d_up, hid2, n_tp, p_ff, 1, 2, plus=up_theirs, into=ff_grads)
         ff_grads = lax.psum_scatter(ff_grads, ("tp", "xx"), scatter_dimension=0, tiled=True)
-        ff_grads = lax.all_gather(ff_grads, dp, axis=0, tiled=True)
+        ff_grads = every_piece(ff_grads)
 
         d_resid1, d_attn, sums2 = back2(d_up, w_all, resid_x1, og, gain2)
         d_ctx = dot_nt(d_attn, wout_w).astype(BF16)
@@ -942,8 +962,7 @@
         def both_orders(table):
             return jnp.stack(in_block_order(table, 0) + in_block_order(table, 1))
 
-        d_w_down, d_w_up = ff_out(ff_grads.reshape(n_dp, -1, width), n_ff, p_ff, n_x, n_core)
-        blocks0[0], d_w_down, d_w_up = lax.optimization_barrier((blocks0[0], d_w_down, d_w_up))
+        d_w_down, d_w_up = pieces_out(x_and_core, ff_grads, ((0, n_ff, False), (p_ff, n_ff, True)))
         block_rows = both_orders(grad_lists(0))
         in_sub = sum(((block_rows >= s * sub).astype(jnp.int32) for s in range(1, n_sub)), jnp.zeros_like(block_rows))
         in_sub = block_rows - in_sub * sub
@@ -971,7 +990,7 @@
         pos_theirs = swap(lax.dynamic_index_in_dim(pos_all, 1 - c_index, 1, keepdims=False).reshape(-1, width), "cc")
         rest = grad_rest(core, ctx, d_attn, d_qkvs, hid1, n_tp, spans, plus=rest_theirs, tail=(pos_all, pos_theirs))
         rest = lax.psum_scatter(rest, ("tp", "xx"), scatter_dimension=0, tiled=True)
-        rest_w = lax.all_gather(rest[:spans[1][1]], dp, axis=0, tiled=True)
+        rest_w = every_piece(rest[:spans[1][1]])
         whole = lax.all_gather(rest[spans[1][1]:], ("tp", "xx", "cc"), axis=0, tiled=True)
         d_pos = jnp.pad(whole[:seq], ((POS_OFFSET, pos_table.shape[0] - seq - POS_OFFSET), (0, 0)))
         small = whole[seq:seq + n_small].reshape(-1)
@@ -981,8 +1000,9 @@
         d_b_up = lax.dynamic_slice_in_dim(small, n_tp * n_b + tp_index * ff, ff)
         d_gain1, d_bias1, d_gain2, d_bias2, d_b_out, d_b_down = small[n_tp * (n_b + ff):].reshape(6, width)
 
-        d_w_out = pick_pieces(rest_w, 0, w_out.shape[0] * w_out.shape[1]).reshape(w_out.shape)
-        d_w_qkv = pick_pieces(rest_w, p_out, n_b).reshape(n_core, 3, -1, w_qkv.shape[3], width).transpose(4, 1, 0, 2, 3).reshape(w_qkv.shape)
+        d_w_out, d_w_qkv = pieces_out(x_and_core, rest_w, ((0, n_out, False), (p_out, n_b // n_dp, False)))
+        d_w_out = d_w_out.reshape(w_out.shape)
+        d_w_qkv = d_w_qkv.reshape(n_core, 3, -1, w_qkv.shape[3], width).transpose(4, 1, 0, 2, 3).reshape(w_qkv.shape)
         return (layer_out, d_emb, d_pos, d_gain1, d_bias1, d_w_qkv, d_b_qkv, d_w_out,
                 d_b_out, d_gain2, d_bias2, d_w_up, d_b_up, d_w_down, d_b_down)
 

time: 1170 us -> 1150 us (0.983)
  waiting for transfers between devices: 469 us -> 438 us
    reduce_scatter x1, waiting for transfers between devices: 131 us -> 35.3 us  [local_step(): lax.psum_scatter(ff_grads, ('tp', 'xx'), scatter_dimension=0, tiled=True)]
    ppermute x46 -> x52, waiting for transfers between devices: 307 us -> 403 us  [swap(): return lax.ppermute(v, axis, tp_swap[k] if axis == 'tp' else pair)]
    reduce_scatter x1, waiting for transfers between devices: 30.7 us -> 0.01 us  [local_step(): rest = lax.psum_scatter(rest, ('tp', 'xx'), scatter_dimension=0, tiled=True)]
    ppermute x46 -> x52, starting transfers between devices: 35.5 us -> 42.8 us  [swap(): return lax.ppermute(v, axis, tp_swap[k] if axis == 'tp' else pair)]
    unnamed x145 -> x160, local copies, waits for them, and re-layouts: 26.9 us -> 27.2 us
  transfers between devices with their start and end apart: 53 -> 57, of which waited for: 19 -> 19; matrix products, arithmetic and copies ran while one was open for 14% -> 14% of each run, Pallas kernels for 14% -> 20%
where the time goes in v4:
time: 1150 us; the launch traced here: 1130 us
  waiting for transfers between devices  438 us (38%)
  Pallas kernels  418 us (36%)
  local copies, waits for them, and re-layouts  127 us (11%)
  matrix products  53.3 us (5%)
  starting transfers between devices  43 us (4%)
  between operations  19.1 us (2%)
  other arithmetic  16.6 us (1%)
    ppermute x52, waiting for transfers between devices, swap(): return lax.ppermute(v, axis, tp_swap[k] if axis == 'tp' else pair)  403 us
    pallas_call x1, Pallas kernels, accum(): pl.pallas_call(functools.partial(accum_kernel, n_block, cap, sub_rows, wi...  64.5 us
    pallas_call x2, Pallas kernels, attn_bwd(): pl.pallas_call(attn_bwd_kernel, grid=(n_pair,), in_specs=[pl.BlockSpec((s...  62.1 us
    pallas_call x4, Pallas kernels, grad_pieces(): pl.pallas_call(functools.partial(grad_kernel, plus is not None), grid_spe...  56.3 us
    pallas_call x1, Pallas kernels, ffn(): pl.pallas_call(functools.partial(ffn_kernel, part), grid=(n_piece,), in_s...  56.2 us
    ppermute x52, starting transfers between devices, swap(): return lax.ppermute(v, axis, tp_swap[k] if axis == 'tp' else pair)  42.8 us
    pallas_call x1, Pallas kernels, attn_fwd(): pl.pallas_call(attn_fwd_kernel, grid=(n_seq, n_pair), in_specs=[pl.BlockS...  41.2 us
    reduce_scatter x1, waiting for transfers between devices, local_step(): lax.psum_scatter(ff_grads, ('tp', 'xx'), scatter_dimension=0, tiled=True)  35.3 us
  transfers between devices with their start and end apart: 57, of which 19 were waited for; matrix products, arithmetic and copies ran while one was open for 14% of the time, Pallas kernels for 20%

profile of v4, /device:TPU:0, one launch (start us, length us, event | category | flops | bytes accessed | tf_op | source)
XLA Modules:
  0.0 1129.4 jit_solution(9862393732677584579)
XLA Ops:
  32.8 20.6 %gather_fusion.3 = bf16[1408,1024]{1,0:T(8,128)(2,1)} fusion(bf16[12568,1024]{1,0:T(8,128)(2,1)} %param.21, s32[2048]{0:T(1024)S(1)} %pad_clamp_fusion.3), kind=kCustom, calls=%fused_computation.3 | custom fusion | bytes 5772800 | tf_op jit(solution)/shard_map/jit(_take)/gather | solution.py:862
  53.4 19.4 %gather_fusion.4 = bf16[1408,1024]{1,0:T(8,128)(2,1)} fusion(bf16[12568,1024]{1,0:T(8,128)(2,1)} %param.21, s32[2048]{0:T(1024)S(1)} %pad_clamp_fusion.2), kind=kCustom, calls=%fused_computation.4 | custom fusion | bytes 5772800 | tf_op jit(solution)/shard_map/jit(_take)/gather | solution.py:864
  93.1 71.5 %collective-permute-done.37 = bf16[1792]{0:T(1024)(128)(2,1)S(1)} collective-permute-done((bf16[1792]{0:T(1024)(128)(2,1)S(1)}, bf16[1792]{0:T(1024)(128)(2,1)S(1)}, u32[]{:S(2)}, u32[]{:S(2)}) %collective-permute-start.37) | collective-permute-done | bytes 3616 | tf_op jit(solution)/shard_map/ppermute | solution.py:779
  186.5 31.2 %collective-permute-done.41.refs_3_ = bf16[2,256,1024]{2,1,0:T(8,128)(2,1)S(1)} collective-permute-done((bf16[2,256,1024]{2,1,0:T(8,128)(2,1)S(1)}, bf16[2,256,1024]{2,1,0:T(8,128)(2,1)S(1)}, u32[]{:S(2)}, u32[]{:S(2)}) %collective-permute-start.41) | collective-permute-done | bytes 1048608 | tf_op jit(solution)/shard_map/ppermute | solution.py:779
  217.7 18.7 %collective-permute-done.40.refs_2_ = bf16[2,256,1024]{2,1,0:T(8,128)(2,1)S(1)} collective-permute-done((bf16[2,256,1024]{2,1,0:T(8,128)(2,1)S(1)}, bf16[2,256,1024]{2,1,0:T(8,128)(2,1)S(1)}, u32[]{:S(2)}, u32[]{:S(2)}) %collective-permute-start.40) | collective-permute-done | bytes 1048608 | tf_op jit(solution)/shard_map/ppermute | solution.py:779
  248.6 19.4 %add_convert_fusion.1.qkv_ref = bf16[2048,3072]{1,0:T(8,128)(2,1)} fusion(bf16[2048,1024]{1,0:T(8,128)(2,1)} %get-tuple-element.1258.b2_ref, bf16[3072,1024]{1,0:T(8,128)(2,1)} %all-gather.4.cloned.1.call-done.w_ref, f32[3072]{0:T(1024)S(1)} %copy-done.45), kind=kOutput, calls=%fused_computation.280 | convolution fusion | flops 12897484800 | bytes 23080960 | tf_op jit(solution)/shard_map/dot_general | solution.py:20
  268.0 41.2 %attn_fwd.1 = (bf16[2048,1024]{1,0:T(8,128)(2,1)S(1)}, f32[2,8,2,1024]{3,2,1,0:T(2,128)S(1)}) custom-call(bf16[2048,3072]{1,0:T(8,128)(2,1)} %add_convert_fusion.1.qkv_ref), custom_call_target="tpu_custom_call" | custom-call | flops 21474836480 | bytes 16777216 | tf_op jit(solution)/shard_map/attn_fwd/pallas_call | solution.py:74
  326.2 56.2 %ffn.1 = (bf16[2048,4096]{1,0:T(8,128)(2,1)}, bf16[2048,4096]{1,0:T(8,128)(2,1)}, f32[1,4096]{1,0:T(1,128)S(1)}) custom-call(bf16[2048,1024]{1,0:T(8,128)(2,1)S(1)} %get-tuple-element.1267.h_ref.b_ref, bf16[2048,1024]{1,0:T(8,128)(2,1)} %bitcast.193, bf16[16,576,1024]{2,1,0:T(8,128)(2,1)} %bitcast.206, bf16[16,576,1024]{2,1,0:T(8,128)(2,1)} %bitcast.207, ...), custom_call_target="tpu_custom_call" | custom-call | flops 34359738368 | bytes 50331648 | tf_op jit(solution)/shard_map/ffn/pallas_call | solution.py:346
  382.4 29.7 %ffn_back.1 = (f32[2048,1024]{1,0:T(8,128)}, bf16[2048,1024]{1,0:T(8,128)(2,1)S(1)}, f32[8,1024]{1,0:T(8,128)S(1)}) custom-call(bf16[2048,4096]{1,0:T(8,128)(2,1)} %get-tuple-element.1270.dup_ref.a_ref, bf16[16,576,1024]{2,1,0:T(8,128)(2,1)} %bitcast.208, f32[2048,1024]{1,0:T(8,128)} %get-tuple-element.1266.x1_ref, bf16[2048,1024]{1,0:T(8,128)(2,1)} %bitcast.194, ...), custom_call_target="tpu_custom_call" | custom-call | flops 17179869184 | bytes 41943040 | tf_op jit(solution)/shard_map/ffn_back/pallas_call | solution.py:386
  418.3 30.7 %attn_bwd.3.dq_ref.refs_1_ = bf16[1024,3072]{1,0:T(8,128)(2,1)} custom-call(bf16[2048,3072]{1,0:T(8,128)(2,1)} %add_convert_fusion.1.qkv_ref, bf16[2048,1024]{1,0:T(8,128)(2,1)S(1)} %copy-done.4, bf16[2048,1024]{1,0:T(8,128)(2,1)} %convolution_convert_fusion.3.dctx_ref, f32[2,8,2,1024]{3,2,1,0:T(2,128)S(1)} %get-tuple-element.1272.lse_ref), custom_call_target="tpu_custom_call" | custom-call | flops 26843545600 | bytes 16777216 | tf_op jit(solution)/shard_map/attn_bwd/pallas_call | solution.py:140
  449.0 31.4 %attn_bwd.2.dq_ref.refs_0_ = bf16[1024,3072]{1,0:T(8,128)(2,1)} custom-call(bf16[2048,3072]{1,0:T(8,128)(2,1)} %add_convert_fusion.1.qkv_ref, bf16[2048,1024]{1,0:T(8,128)(2,1)S(1)} %copy-done.4, bf16[2048,1024]{1,0:T(8,128)(2,1)} %convolution_convert_fusion.3.dctx_ref, f32[2,8,2,1024]{3,2,1,0:T(2,128)S(1)} %get-tuple-element.1272.lse_ref), custom_call_target="tpu_custom_call" | custom-call | flops 26843545600 | bytes 16777216 | tf_op jit(solution)/shard_map/attn_bwd/pallas_call | solution.py:140
  511.3 16.2 %qkv_back.3 = (bf16[1024,1024]{1,0:T(8,128)(2,1)}, f32[1152,1024]{1,0:T(8,128)S(1)}, f32[8,1024]{1,0:T(8,128)S(1)}, f32[8,3072]{1,0:T(8,128)S(1)}) custom-call(bf16[1024,3072]{1,0:T(8,128)(2,1)} %attn_bwd.3.dq_ref.refs_1_, bf16[3072,1024]{1,0:T(8,128)(2,1)} %all-gather.4.cloned.1.call-done.w_ref, f32[2048,1024]{1,0:T(8,128)} %get-tuple-element.1265.x_ref, ...), custom_call_target="tpu_custom_call" | custom-call | flops 6442450944 | bytes 18874368 | tf_op jit(solution)/shard_map/qkv_back/pallas_call | solution.py:431
  644.9 20.0 %collective-permute-done.60.refs_17_ = bf16[384,1024]{1,0:T(8,128)(2,1)} collective-permute-done((bf16[384,1024]{1,0:T(8,128)(2,1)S(1)}, bf16[384,1024]{1,0:T(8,128)(2,1)}, u32[]{:S(2)}, u32[]{:S(2)}) %collective-permute-start.60) | collective-permute-done | bytes 786464 | tf_op jit(solution)/shard_map/ppermute | solution.py:779
  675.0 17.3 %collective-permute-done.62.refs_19_ = bf16[384,1024]{1,0:T(8,128)(2,1)} collective-permute-done((bf16[384,1024]{1,0:T(8,128)(2,1)S(1)}, bf16[384,1024]{1,0:T(8,128)(2,1)}, u32[]{:S(2)}, u32[]{:S(2)}) %collective-permute-start.62) | collective-permute-done | bytes 786464 | tf_op jit(solution)/shard_map/ppermute | solution.py:779
  692.4 22.7 %add_convert_fusion.2 = bf16[2048,1024]{1,0:T(8,128)(2,1)} fusion(f32[2048,1024]{1,0:T(8,128)} %get-tuple-element.1266.x1_ref, f32[1024]{0:T(1024)S(1)} %convert_element_type.404, bf16[2048,4096]{1,0:T(8,128)(2,1)S(1)} %bitcast.211, bf16[4096,1024]{1,0:T(8,128)(2,1)} %bitcast.214), kind=kOutput, calls=%fused_computation.281 | convolution fusion | flops 17190354944 | bytes 37752832 | tf_op jit(solution)/shard_map/dot_general | solution.py:24
  726.5 24.6 %collective-permute-done.47.refs_3_ = bf16[384,1024]{1,0:T(8,128)(2,1)S(1)} collective-permute-done((bf16[384,1024]{1,0:T(8,128)(2,1)S(1)}, bf16[384,1024]{1,0:T(8,128)(2,1)S(1)}, u32[]{:S(2)}, u32[]{:S(2)}) %collective-permute-start.47) | collective-permute-done | bytes 786464 | tf_op jit(solution)/shard_map/ppermute | solution.py:779
  753.0 20.5 %collective-permute-done.44.refs_3_ = bf16[2,256,1024]{2,1,0:T(8,128)(2,1)S(1)} collective-permute-done((bf16[2,256,1024]{2,1,0:T(8,128)(2,1)S(1)}, bf16[2,256,1024]{2,1,0:T(8,128)(2,1)S(1)}, u32[]{:S(2)}, u32[]{:S(2)}) %collective-permute-start.44) | collective-permute-done | bytes 1048608 | tf_op jit(solution)/shard_map/ppermute | solution.py:779
  773.5 33.5 %collective-permute-done.43.refs_2_ = bf16[2,256,1024]{2,1,0:T(8,128)(2,1)S(1)} collective-permute-done((bf16[2,256,1024]{2,1,0:T(8,128)(2,1)S(1)}, bf16[2,256,1024]{2,1,0:T(8,128)(2,1)S(1)}, u32[]{:S(2)}, u32[]{:S(2)}) %collective-permute-start.43) | collective-permute-done | bytes 1048608 | tf_op jit(solution)/shard_map/ppermute | solution.py:779
  818.7 19.7 %collective-permute-done.65.refs_22_ = bf16[384,1024]{1,0:T(8,128)(2,1)} collective-permute-done((bf16[384,1024]{1,0:T(8,128)(2,1)}, bf16[384,1024]{1,0:T(8,128)(2,1)}, u32[]{:S(2)}, u32[]{:S(2)}) %collective-permute-start.65) | collective-permute-done | bytes 786464 | tf_op jit(solution)/shard_map/ppermute | solution.py:779
  843.3 28.7 %collective-permute-done.66.refs_23_ = bf16[384,1024]{1,0:T(8,128)(2,1)S(1)} collective-permute-done((bf16[384,1024]{1,0:T(8,128)(2,1)}, bf16[384,1024]{1,0:T(8,128)(2,1)S(1)}, u32[]{:S(2)}, u32[]{:S(2)}) %collective-permute-start.66) | collective-permute-done | bytes 786464 | tf_op jit(solution)/shard_map/ppermute | solution.py:779
  875.0 26.6 %collective-permute-done.49.refs_5_ = bf16[384,1024]{1,0:T(8,128)(2,1)} collective-permute-done((bf16[384,1024]{1,0:T(8,128)(2,1)}, bf16[384,1024]{1,0:T(8,128)(2,1)}, u32[]{:S(2)}, u32[]{:S(2)}) %collective-permute-start.49) | collective-permute-done | bytes 786464 | tf_op jit(solution)/shard_map/ppermute | solution.py:779
  901.6 35.3 %reduce-scatter.5.cloned.1.call-done.refs_0_ = f32[528,1024]{1,0:T(8,128)} async-done(((f32[4224,1024]{1,0:T(8,128)}), f32[528,1024]{1,0:T(8,128)}) %reduce-scatter.5.cloned.1.call-update) | async-done | bytes 2162704 | tf_op jit(solution)/shard_map/reduce_scatter | solution.py:924
  972.0 61.2 %collective-permute-done.77.refs_1_ = f32[264,1024]{1,0:T(8,128)} collective-permute-done((f32[264,1024]{1,0:T(8,128)}, f32[264,1024]{1,0:T(8,128)}, u32[]{:S(2)}, u32[]{:S(2)}) %collective-permute-start.77) | collective-permute-done | bytes 1081376 | tf_op jit(solution)/shard_map/ppermute | solution.py:779
  1033.7 64.5 %table_accum.1 = f32[100544,128]{1,0:T(8,128)} custom-call(s32[12288]{0:T(1024)} %fusion.143.where_ref, s32[160]{0:T(256)} %min.12.first_ref, bf16[384,1024]{1,0:T(8,128)(2,1)} %copy-done.22, bf16[384,1024]{1,0:T(8,128)(2,1)} %copy-done.63, bf16[384,1024]{1,0:T(8,128)(2,1)} %copy-done.64, bf16[384,1024]{1,0:T(8,128)(2,1)} %copy-done.65, ...), custom_call_target="tpu_custom_call" | custom-call | flops 49999998976 | bytes 100000000 | tf_op jit(solution)/shard_map/table_accum/pallas_call | solution.py:607
  (490 shorter events, 349.5 us)
Async XLA Ops:
  7.2 241.4 %all-gather.4.cloned.1.call-start = ((), (), s32[]{:S(2)}) async-start(), calls=%async_computation.2 | async-start | bytes 7077888 | tf_op jit(solution)/shard_map/all_gather | solution.py:776
  9.4 301.8 %all-gather.6.cloned.1.call-start = ((), (), s32[]{:S(2)}) async-start(), calls=%async_computation.3 | async-start | bytes 20054016 | tf_op jit(solution)/shard_map/all_gather | solution.py:799
  18.2 67.8 %collective-permute-start.38 = (bf16[1792]{0:T(1024)(128)(2,1)S(1)}, bf16[1792]{0:T(1024)(128)(2,1)S(1)}, u32[]{:S(2)}, u32[]{:S(2)}) collective-permute-start(bf16[1792]{0:T(1024)(128)(2,1)S(1)} %dynamic-update-slice.33), channel_id=1, source_target_pairs={{0,12},{4,8},{8,4},{12,0},{1,13},{5,9},{9,5},{13,1},{2,14},{6,10},... | collective-permute-start | bytes 10760 | tf_op jit(solution)/shard_map/ppermute | solution.py:779
  26.3 788.9 %reduce-scatter.3.cloned.1.call-start = ((), (), s32[]{:S(2)}) async-start(), calls=%async_computation.4 | async-start | bytes 12386304 | tf_op jit(solution)/shard_map/reduce_scatter | solution.py:992
  76.1 93.3 %collective-permute-start.34 = (bf16[704,1024]{1,0:T(8,128)(2,1)}, bf16[704,1024]{1,0:T(8,128)(2,1)S(1)}, u32[]{:S(2)}, u32[]{:S(2)}) collective-permute-start(bf16[704,1024]{1,0:T(8,128)(2,1)} %get-tuple-element.1574), channel_id=1, source_target_pairs={{0,8},{4,12},{8,0},{12,4},{1,9},{5,13},{9,1},{13,5},{2,10},{6,14},... | collective-permute-start | bytes 4325384 | tf_op jit(solution)/shard_map/ppermute | solution.py:779
  80.3 89.0 %collective-permute-start.35 = (bf16[704,1024]{1,0:T(8,128)(2,1)}, bf16[704,1024]{1,0:T(8,128)(2,1)}, u32[]{:S(2)}, u32[]{:S(2)}) collective-permute-start(bf16[704,1024]{1,0:T(8,128)(2,1)} %get-tuple-element.1572), channel_id=1, source_target_pairs={{0,12},{4,8},{8,4},{12,0},{1,13},{5,9},{9,5},{13,1},{2,14},{6,10},... | collective-permute-start | bytes 4325384 | tf_op jit(solution)/shard_map/ppermute | solution.py:779
  81.8 87.5 %collective-permute-start.33 = (bf16[704,1024]{1,0:T(8,128)(2,1)}, bf16[704,1024]{1,0:T(8,128)(2,1)}, u32[]{:S(2)}, u32[]{:S(2)}) collective-permute-start(bf16[704,1024]{1,0:T(8,128)(2,1)} %get-tuple-element.1573), channel_id=1, source_target_pairs={{0,4},{4,0},{8,12},{12,8},{1,5},{5,1},{9,13},{13,9},{2,6},{6,2},{1... | collective-permute-start | bytes 4325384 | tf_op jit(solution)/shard_map/ppermute | solution.py:779
  85.7 78.9 %collective-permute-start.37 = (bf16[1792]{0:T(1024)(128)(2,1)S(1)}, bf16[1792]{0:T(1024)(128)(2,1)S(1)}, u32[]{:S(2)}, u32[]{:S(2)}) collective-permute-start(bf16[1792]{0:T(1024)(128)(2,1)S(1)} %dynamic-update-slice.33), channel_id=1, source_target_pairs={{0,8},{4,12},{8,0},{12,4},{1,9},{5,13},{9,1},{13,5},{2,10},{6,14},... | collective-permute-start | bytes 10760 | tf_op jit(solution)/shard_map/ppermute | solution.py:779
  86.1 82.5 %collective-permute-start.36 = (bf16[1792]{0:T(1024)(128)(2,1)S(1)}, bf16[1792]{0:T(1024)(128)(2,1)S(1)}, u32[]{:S(2)}, u32[]{:S(2)}) collective-permute-start(bf16[1792]{0:T(1024)(128)(2,1)S(1)} %dynamic-update-slice.33), channel_id=1, source_target_pairs={{0,4},{4,0},{8,12},{12,8},{1,5},{5,1},{9,13},{13,9},{2,6},{6,2},{1... | collective-permute-start | bytes 10760 | tf_op jit(solution)/shard_map/ppermute | solution.py:779
  557.6 379.3 %reduce-scatter.5.cloned.1.call-start = ((), (), s32[]{:S(2)}) async-start(), calls=%async_computation.6 | async-start | bytes 19464192 | tf_op jit(solution)/shard_map/reduce_scatter | solution.py:924
  619.2 485.7 %all-gather.8.cloned.1.call-start = ((), (), s32[]{:S(2)}) async-start(), calls=%async_computation.5 | async-start | bytes 5013504 | tf_op jit(solution)/shard_map/all_gather | solution.py:994
  638.0 80.3 %collective-permute-start.67 = (bf16[384,1024]{1,0:T(8,128)(2,1)S(1)}, bf16[384,1024]{1,0:T(8,128)(2,1)S(1)}, u32[]{:S(2)}, u32[]{:S(2)}) collective-permute-start(bf16[384,1024]{1,0:T(8,128)(2,1)S(1)} %get-tuple-element.1283.refs_16_), channel_id=1, source_target_pairs={{0,1},{1,0},{2,3},{3,2},{4,5},{5,4},{6,7},{7,6},{8,9},{9,8},{10,11... | collective-permute-start | bytes 2359304 | tf_op jit(solution)/shard_map/ppermute | solution.py:779
  643.5 78.1 %collective-permute-start.63 = (bf16[384,1024]{1,0:T(8,128)(2,1)S(1)}, bf16[384,1024]{1,0:T(8,128)(2,1)S(1)}, u32[]{:S(2)}, u32[]{:S(2)}) collective-permute-start(bf16[384,1024]{1,0:T(8,128)(2,1)S(1)} %get-tuple-element.1283.refs_16_), channel_id=1, source_target_pairs={{0,2},{2,0},{1,3},{3,1},{4,6},{6,4},{5,7},{7,5},{8,10},{10,8},{9,1... | collective-permute-start | bytes 2359304 | tf_op jit(solution)/shard_map/ppermute | solution.py:779
  721.5 85.5 %collective-permute-start.43 = (bf16[2,256,1024]{2,1,0:T(8,128)(2,1)S(1)}, bf16[2,256,1024]{2,1,0:T(8,128)(2,1)S(1)}, u32[]{:S(2)}, u32[]{:S(2)}) collective-permute-start(bf16[2,256,1024]{2,1,0:T(8,128)(2,1)S(1)} %get-tuple-element.1565), channel_id=1, source_target_pairs={{0,8},{4,12},{8,0},{12,4},{1,9},{5,13},{9,1},{13,5},{2,10},{6,14},... | collective-permute-start | bytes 3145736 | tf_op jit(solution)/shard_map/ppermute | solution.py:779
  839.8 100.8 %collective-permute-start.54 = (bf16[384,1024]{1,0:T(8,128)(2,1)}, bf16[384,1024]{1,0:T(8,128)(2,1)}, u32[]{:S(2)}, u32[]{:S(2)}) collective-permute-start(bf16[384,1024]{1,0:T(8,128)(2,1)} %copy-done.64), channel_id=1, source_target_pairs={{0,1},{1,0},{2,3},{3,2},{4,5},{5,4},{6,7},{7,6},{8,9},{9,8},{10,11... | collective-permute-start | bytes 2359304 | tf_op jit(solution)/shard_map/ppermute | solution.py:779
  872.0 69.0 %collective-permute-start.50 = (bf16[384,1024]{1,0:T(8,128)(2,1)}, bf16[384,1024]{1,0:T(8,128)(2,1)}, u32[]{:S(2)}, u32[]{:S(2)}) collective-permute-start(bf16[384,1024]{1,0:T(8,128)(2,1)} %copy-done.64), channel_id=1, source_target_pairs={{0,2},{2,0},{1,3},{3,1},{4,6},{6,4},{5,7},{7,5},{8,10},{10,8},{9,1... | collective-permute-start | bytes 2359304 | tf_op jit(solution)/shard_map/ppermute | solution.py:779
  873.3 68.2 %collective-permute-start.55 = (bf16[384,1024]{1,0:T(8,128)(2,1)}, bf16[384,1024]{1,0:T(8,128)(2,1)}, u32[]{:S(2)}, u32[]{:S(2)}) collective-permute-start(bf16[384,1024]{1,0:T(8,128)(2,1)} %copy-done.65), channel_id=1, source_target_pairs={{0,1},{1,0},{2,3},{3,2},{4,5},{5,4},{6,7},{7,6},{8,9},{9,8},{10,11... | collective-permute-start | bytes 2359304 | tf_op jit(solution)/shard_map/ppermute | solution.py:779
  873.3 79.5 %collective-permute-start.51 = (bf16[384,1024]{1,0:T(8,128)(2,1)}, bf16[384,1024]{1,0:T(8,128)(2,1)}, u32[]{:S(2)}, u32[]{:S(2)}) collective-permute-start(bf16[384,1024]{1,0:T(8,128)(2,1)} %copy-done.65), channel_id=1, source_target_pairs={{0,2},{2,0},{1,3},{3,1},{4,6},{6,4},{5,7},{7,5},{8,10},{10,8},{9,1... | collective-permute-start | bytes 2359304 | tf_op jit(solution)/shard_map/ppermute | solution.py:779
  936.9 96.8 %collective-permute-start.82 = (f32[528,1024]{1,0:T(8,128)}, f32[528,1024]{1,0:T(8,128)}, u32[]{:S(2)}, u32[]{:S(2)}) collective-permute-start(f32[528,1024]{1,0:T(8,128)} %reduce-scatter.5.cloned.1.call-done.refs_0_), channel_id=1, source_target_pairs={{0,2},{2,0},{1,3},{3,1},{4,6},{6,4},{5,7},{7,5},{8,10},{10,8},{9,1... | collective-permute-start | bytes 6488072 | tf_op jit(solution)/shard_map/ppermute | solution.py:779
  958.1 75.1 %collective-permute-start.77 = (f32[264,1024]{1,0:T(8,128)}, f32[264,1024]{1,0:T(8,128)}, u32[]{:S(2)}, u32[]{:S(2)}) collective-permute-start(f32[264,1024]{1,0:T(8,128)} %slice.297.refs_0_), channel_id=1, source_target_pairs={{0,2},{2,0},{1,3},{3,1},{4,6},{6,4},{5,7},{7,5},{8,10},{10,8},{9,1... | collective-permute-start | bytes 3244040 | tf_op jit(solution)/shard_map/ppermute | solution.py:779
  965.6 68.1 %collective-permute-start.59 = (bf16[384,1024]{1,0:T(8,128)(2,1)}, bf16[384,1024]{1,0:T(8,128)(2,1)}, u32[]{:S(2)}, u32[]{:S(2)}) collective-permute-start(bf16[384,1024]{1,0:T(8,128)(2,1)} %collective-permute-done.51.refs_7_), channel_id=1, source_target_pairs={{0,1},{1,0},{2,3},{3,2},{4,5},{5,4},{6,7},{7,6},{8,9},{9,8},{10,11... | collective-permute-start | bytes 2359304 | tf_op jit(solution)/shard_map/ppermute | solution.py:779
  971.9 126.4 %collective-permute-start.78 = (f32[264,1024]{1,0:T(8,128)}, f32[264,1024]{1,0:T(8,128)}, u32[]{:S(2)}, u32[]{:S(2)}) collective-permute-start(f32[264,1024]{1,0:T(8,128)} %slice.297.refs_0_), channel_id=1, source_target_pairs={{0,1},{1,0},{2,3},{3,2},{4,5},{5,4},{6,7},{7,6},{8,9},{9,8},{10,11... | collective-permute-start | bytes 3244040 | tf_op jit(solution)/shard_map/ppermute | solution.py:779
  1033.2 80.6 %collective-permute-start.83 = (f32[528,1024]{1,0:T(8,128)}, f32[528,1024]{1,0:T(8,128)}, u32[]{:S(2)}, u32[]{:S(2)}) collective-permute-start(f32[528,1024]{1,0:T(8,128)} %reduce-scatter.5.cloned.1.call-done.refs_0_), channel_id=1, source_target_pairs={{0,1},{1,0},{2,3},{3,2},{4,5},{5,4},{6,7},{7,6},{8,9},{9,8},{10,11... | collective-permute-start | bytes 6488072 | tf_op jit(solution)/shard_map/ppermute | solution.py:779
  1033.7 80.1 %collective-permute-start.84 = (f32[528,1024]{1,0:T(8,128)}, f32[528,1024]{1,0:T(8,128)}, u32[]{:S(2)}, u32[]{:S(2)}) collective-permute-start(f32[528,1024]{1,0:T(8,128)} %collective-permute-done.82.refs_1_), channel_id=1, source_target_pairs={{0,1},{1,0},{2,3},{3,2},{4,5},{5,4},{6,7},{7,6},{8,9},{9,8},{10,11... | collective-permute-start | bytes 6488072 | tf_op jit(solution)/shard_map/ppermute | solution.py:779
  (108 other events, 4082.7 us)
Sparse Core Ops, SparseCore 0:
  10.4 44.5 all-gather.3
  57.2 175.3 all-gather.5
  557.8 102.1 reduce-scatter.2
  664.8 272.0 reduce-scatter.4
  939.0 51.8 all-gather.7

commit v5 on v4

--- a/solution.py
+++ b/solution.py
@@ -83,7 +83,7 @@
         name="attn_fwd",
         cost_estimate=pl.CostEstimate(flops=n_seq * n_pair * 8 * seq * seq * 256 * 10 // 16, bytes_accessed=n_seq * seq * n_pair * width * 8,
                                       transcendentals=n_seq * n_pair * seq * seq),
-        compiler_params=pltpu.CompilerParams(vmem_limit_bytes=48 * 1024 * 1024),
+        compiler_params=pltpu.CompilerParams(vmem_limit_bytes=18 * 1024 * 1024),
     )(qkv)
 
 
@@ -150,7 +150,7 @@
         name="attn_bwd",
         cost_estimate=pl.CostEstimate(flops=n_pair * 20 * seq * seq * 256 * 10 // 16, bytes_accessed=seq * n_pair * width * 16,
                                       transcendentals=n_pair * seq * seq),
-        compiler_params=pltpu.CompilerParams(vmem_limit_bytes=48 * 1024 * 1024),
+        compiler_params=pltpu.CompilerParams(vmem_limit_bytes=22 * 1024 * 1024),
     )(qkv, ctx, dctx, lse)
 
 
@@ -248,7 +248,7 @@
         scratch_shapes=[pltpu.VMEM((n_blk * cap * width // 128, 128), F32), pltpu.VMEM((rows * width // 128, 128), F32)],
         name="embed_norm",
         cost_estimate=pl.CostEstimate(flops=15_000_000_000, bytes_accessed=n_tok * width * 10, transcendentals=0),
-        compiler_params=pltpu.CompilerParams(vmem_limit_bytes=48 * MIB),
+        compiler_params=pltpu.CompilerParams(vmem_limit_bytes=28 * MIB),
     )(code, *blocks, pos_rows, gain, bias)
 
 
@@ -287,7 +287,7 @@
         scratch_shapes=[pltpu.VMEM((n_tok * width // 128, 128), F32), pltpu.VMEM((cap * width // 128, 128), F32)],
         name="token_pack",
         cost_estimate=pl.CostEstimate(flops=15_000_000_000, bytes_accessed=n_tok * width * 5, transcendentals=0),
-        compiler_params=pltpu.CompilerParams(vmem_limit_bytes=40 * MIB),
+        compiler_params=pltpu.CompilerParams(vmem_limit_bytes=16 * MIB),
     )(code, tok)
 
 
@@ -315,7 +315,7 @@
         out_shape=[jax.ShapeDtypeStruct((n_tok, width), F32), jax.ShapeDtypeStruct((n_tok, width), BF16)],
         name="proj_norm",
         cost_estimate=pl.CostEstimate(flops=2 * n_tok * ctx.shape[1] * width, bytes_accessed=n_tok * width * 12, transcendentals=0),
-        compiler_params=pltpu.CompilerParams(vmem_limit_bytes=40 * MIB),
+        compiler_params=pltpu.CompilerParams(vmem_limit_bytes=24 * MIB),
     )(ctx, w, x, b, gain, bias)
 
 
@@ -351,8 +351,38 @@
         out_shape=[jax.ShapeDtypeStruct((n_tok, ff), BF16), jax.ShapeDtypeStruct((n_tok, ff), BF16), jax.ShapeDtypeStruct((1, ff), F32)],
         name="ffn",
         cost_estimate=pl.CostEstimate(flops=4 * n_tok * ff * width, bytes_accessed=4 * n_tok * ff + 4 * ff * width, transcendentals=n_tok * ff),
-        compiler_params=pltpu.CompilerParams(vmem_limit_bytes=48 * MIB),
+        compiler_params=pltpu.CompilerParams(vmem_limit_bytes=26 * MIB),
     )(hid, og, w, w, b_up)
+
+
+def down_kernel(n_tp, me_ref, act_ref, w_ref, x1_ref, b_ref, *out_refs):
+    out = x1_ref[...] + dot_nn(act_ref[...], w_ref[...].reshape(act_ref.shape[1], -1)).astype(BF16).astype(F32) + b_ref[...]
+    k = me_ref[0] ^ (pl.program_id(0) % n_tp)
+    seq = pl.program_id(0) // n_tp
+    for j in range(n_tp):
+        @pl.when(k == j)
+        def _(j=j):
+            out_refs[j][seq] = out.astype(BF16)
+
+
+def down(me, act, w, x1, b, n_seq, n_tp):
+    n_tok, width = x1.shape
+    ff = act.shape[1]
+    rows = n_tok // n_seq // n_tp
+    part = jax.ShapeDtypeStruct((n_seq, rows, width), BF16)
+    return pl.pallas_call(
+        functools.partial(down_kernel, n_tp),
+        grid_spec=pltpu.PrefetchScalarGridSpec(
+            num_scalar_prefetch=1, grid=(n_seq * n_tp,),
+            in_specs=[pl.BlockSpec((rows, ff), lambda i, m: (i, 0)),
+                      pl.BlockSpec((w.shape[0], ff // w.shape[0], width), lambda i, m: (0, 1, 0), pipeline_mode=pl.Buffered(1)),
+                      pl.BlockSpec((rows, width), lambda i, m: (i, 0)), pl.BlockSpec((1, width), lambda i, m: (0, 0))],
+            out_specs=[pl.BlockSpec(part.shape, lambda i, m: (0, 0, 0))] * n_tp),
+        out_shape=[part] * n_tp,
+        name="down",
+        cost_estimate=pl.CostEstimate(flops=2 * n_tok * ff * width, bytes_accessed=2 * n_tok * ff + n_tok * width * 6, transcendentals=0),
+        compiler_params=pltpu.CompilerParams(vmem_limit_bytes=32 * MIB),
+    )(me, act, w, x1, b)
 
 
 def back2_kernel(dup_ref, w_ref, x1_ref, og_ref, gain_ref, dr_ref, da_ref, sums_ref):
@@ -392,7 +422,7 @@
         out_shape=[jax.ShapeDtypeStruct((n_tok, width), F32), jax.ShapeDtypeStruct((n_tok, width), BF16), jax.ShapeDtypeStruct((8, width), F32)],
         name="ffn_back",
         cost_estimate=pl.CostEstimate(flops=2 * n_tok * ff * width, bytes_accessed=2 * n_tok * ff + n_tok * width * 12, transcendentals=0),
-        compiler_params=pltpu.CompilerParams(vmem_limit_bytes=48 * MIB),
+        compiler_params=pltpu.CompilerParams(vmem_limit_bytes=30 * MIB),
     )(d_up, w, x1, og, gain)
 
 
@@ -439,7 +469,7 @@
                    jax.ShapeDtypeStruct((8, width), F32), jax.ShapeDtypeStruct((8, n_cols), F32)],
         name="qkv_back",
         cost_estimate=pl.CostEstimate(flops=2 * seq * n_cols * width, bytes_accessed=2 * seq * n_cols + seq * width * 12, transcendentals=0),
-        compiler_params=pltpu.CompilerParams(vmem_limit_bytes=48 * MIB),
+        compiler_params=pltpu.CompilerParams(vmem_limit_bytes=26 * MIB),
     )(d_qkv, w_qkv, x, d_resid1, gain, *(earlier or ()))
 
 
@@ -477,7 +507,7 @@
         out_shape=out_shape,
         name="grads_out",
         cost_estimate=pl.CostEstimate(flops=8_000_000_000, bytes_accessed=n_in * rows * width * 8, transcendentals=0),
-        compiler_params=pltpu.CompilerParams(vmem_limit_bytes=32 * MIB),
+        compiler_params=pltpu.CompilerParams(vmem_limit_bytes=20 * MIB),
     )(me, *pieces)
 
 
@@ -501,7 +531,7 @@
         out_shape=jax.ShapeDtypeStruct(out_shape, parts[0].dtype),
         name="assemble",
         cost_estimate=pl.CostEstimate(flops=4_000_000_000, bytes_accessed=16 * MIB, transcendentals=0),
-        compiler_params=pltpu.CompilerParams(vmem_limit_bytes=24 * MIB),
+        compiler_params=pltpu.CompilerParams(vmem_limit_bytes=10 * MIB),
     )(me, *parts)
 
 
@@ -654,7 +684,7 @@
         name="weight_grad",
         cost_estimate=pl.CostEstimate(flops=n_tok * n_cols * width, bytes_accessed=n_tok * (n_cols + 2 * width) + 2 * n_cols * width,
                                       transcendentals=0),
-        compiler_params=pltpu.CompilerParams(vmem_limit_bytes=32 * MIB),
+        compiler_params=pltpu.CompilerParams(vmem_limit_bytes=18 * MIB),
     )(core, *args)
 
 
@@ -710,7 +740,7 @@
         name="weight_grads",
         cost_estimate=pl.CostEstimate(flops=n_tok * n_cols * width, bytes_accessed=n_tok * (n_cols + 4 * width) + 2 * n_cols * width,
                                       transcendentals=0),
-        compiler_params=pltpu.CompilerParams(vmem_limit_bytes=40 * MIB),
+        compiler_params=pltpu.CompilerParams(vmem_limit_bytes=32 * MIB),
     )(core, *args)
 
 
@@ -798,7 +828,6 @@
         own_w = jnp.concatenate([quarter(w_up, 1).T, quarter(w_down, 0), quarter(w_out.reshape(-1, width), 0)])
         w_all = lax.all_gather(own_w, ("tp", "xx", "cc"), axis=0, tiled=True)
         w_all = w_all.reshape(n_tp * n_dp, 2 * n_ff + n_out, width)
-        wdown_w = w_all[:, n_ff:2 * n_ff].reshape(-1, width)
         wout_w = w_all[:, 2 * n_ff:].reshape(-1, width)
         n_pair = wqkv_t.shape[0] // (3 * 128)
         own_bias = jnp.concatenate([b_qkv.reshape(3, n_core, -1, b_qkv.shape[2]).transpose(1, 0, 2, 3).reshape(-1), b_up])
@@ -857,6 +886,33 @@
 
         tiles = width // 128
 
+        def own_places(r, b):
+            own = own_lists(r, b)
+            place = jnp.concatenate([lax.dynamic_index_in_dim(own, tp_index ^ k, 0, keepdims=False) for k in range(n_tp)])
+            return (place // 8) * (8 * tiles) + place % 8
+
+        places0 = [own_places(0, b) for b in range(n_seq)]
+
+        def in_block_order(table, b):
+            out = []
+            for dc in range(n_core):
+                for dx in range(n_x):
+                    for k in range(n_tp):
+                        d = (x_index ^ dx) * n_core + (c_index ^ dc)
+                        out.append(lax.dynamic_index_in_dim(table, (d * n_tp + (tp_index ^ k)) * n_seq + b, 0, keepdims=False))
+            return out
+
+        def both_orders(table):
+            return jnp.stack(in_block_order(table, 0) + in_block_order(table, 1))
+
+        block_rows = both_orders(grad_lists(0))
+        in_sub = sum(((block_rows >= s * sub).astype(jnp.int32) for s in range(1, n_sub)), jnp.zeros_like(block_rows))
+        in_sub = block_rows - in_sub * sub
+        slot = jnp.arange(GRAD_SLOTS)
+        code = (((in_sub // 8) * (8 * tiles) + in_sub % 8) << 16) | ((slot // 8) * (8 * tiles) + slot % 8)
+        code = code.reshape(-1)
+        block_first = jnp.minimum(both_orders(first), GRAD_SLOTS).reshape(-1)
+
         def rows_here(r, my_lists):
             index = [lax.dynamic_index_in_dim(my_lists, tp_index ^ k, 0, keepdims=False) for k in range(n_tp)]
             first_two = jnp.take(emb_table, jnp.concatenate([index[3], index[1]]), axis=0, mode="clip")
@@ -898,10 +954,7 @@
         ctx, lse = attn_fwd(qkv, n_seq, seq, n_pair)
         resid_x1, hid2 = proj_norm(ctx, w_all, 2 * n_ff, resid_x, b_out.astype(F32)[None], gain2, bias2)
         act, d_up, d_b_up = ffn(hid2, og, w_all, bup_w)
-        out = (resid_x1 + dot_nn(act, wdown_w).astype(BF16).astype(F32) + b_down.astype(F32)).astype(BF16)
-
-        out4 = out.reshape(n_seq, seq, width)
-        parts = [lax.dynamic_slice_in_dim(out4, (tp_index ^ k) * seq_local, seq_local, 1) for k in range(n_tp)]
+        parts = down(me, act, w_all, resid_x1, b_down.astype(F32)[None], n_seq, n_tp)
         parts = [swap(part, "tp", k) if k else part for k, part in enumerate(parts)]
         layer_out = assemble(me, parts, (n_seq_dp, seq_local, width), (n_seq, seq_local, width))
 
@@ -931,10 +984,8 @@
         p_out = piece_of(wout_w.shape[0])
         spans = ((0, p_out), (p_out, p_out + piece_of(wqkv_t.shape[0])))
 
-        def token_blocks(r, b, d_tok):
-            own = own_lists(r, b)
-            place = jnp.concatenate([lax.dynamic_index_in_dim(own, tp_index ^ k, 0, keepdims=False) for k in range(n_tp)])
-            parts = pack((place // 8) * (8 * tiles) + place % 8, d_tok, GRAD_SLOTS)
+        def token_blocks(places, d_tok):
+            parts = pack(places, d_tok, GRAD_SLOTS)
             blocks = [swap(part, "tp", k) if k else part for k, part in enumerate(parts)]
             other = []
             for block in blocks:
@@ -943,33 +994,14 @@
 
         d_qkv0 = attn_bwd(qkv, ctx, d_ctx, lse, 0, seq, n_pair)
         d_tok0, *sums0 = back1(d_qkv0, wqkv_t, resid_x, d_resid1, gain1, 0, p_pos * n_tp * n_dp)
-        blocks0 = token_blocks(0, 0, d_tok0)
+        blocks0 = token_blocks(places0[0], d_tok0)
         d_qkv1 = attn_bwd(qkv, ctx, d_ctx, lse, 1, seq, n_pair)
         d_tok1, pos_all, sums1, sums_qkv = back1(d_qkv1, wqkv_t, resid_x, d_resid1, gain1, 1, p_pos * n_tp * n_dp, earlier=sums0)
-        blocks1 = token_blocks(0, 1, d_tok1)
+        blocks1 = token_blocks(places0[1], d_tok1)
         d_qkvs = [d_qkv0, d_qkv1]
         rest_theirs = swap(grad_rest(1 - core, ctx, d_attn, d_qkvs, hid1, n_tp, spans), "cc")
 
-        def in_block_order(table, b):
-            out = []
-            for dc in range(n_core):
-                for dx in range(n_x):
-                    for k in range(n_tp):
-                        d = (x_index ^ dx) * n_core + (c_index ^ dc)
-                        out.append(lax.dynamic_index_in_dim(table, (d * n_tp + (tp_index ^ k)) * n_seq + b, 0, keepdims=False))
-            return out
-
-        def both_orders(table):
-            return jnp.stack(in_block_order(table, 0) + in_block_order(table, 1))
-
         d_w_down, d_w_up = pieces_out(x_and_core, ff_grads, ((0, n_ff, False), (p_ff, n_ff, True)))
-        block_rows = both_orders(grad_lists(0))
-        in_sub = sum(((block_rows >= s * sub).astype(jnp.int32) for s in range(1, n_sub)), jnp.zeros_like(block_rows))
-        in_sub = block_rows - in_sub * sub
-        slot = jnp.arange(GRAD_SLOTS)
-        code = (((in_sub // 8) * (8 * tiles) + in_sub % 8) << 16) | ((slot // 8) * (8 * tiles) + slot % 8)
-        code = code.reshape(-1)
-        block_first = jnp.minimum(both_orders(first), GRAD_SLOTS).reshape(-1)
         image = accum(blocks0 + blocks1, code, block_first, sub_rows, width)
         d_emb = image.reshape(rows // 8, tiles, 8, 128).transpose(0, 2, 1, 3).reshape(rows, width)
 
@@ -979,7 +1011,7 @@
             there = owned & (at >= 0) & (at < GRAD_SLOTS)
             dest = compact(at, there, jnp.where(owned, local, 0) + 1, GRAD_SLOTS)
             dest = jnp.where(dest == 0, rows, dest - 1)
-            grads = jnp.concatenate(token_blocks(r, 0, d_tok0) + token_blocks(r, 1, d_tok1), axis=0).astype(F32)
+            grads = jnp.concatenate(token_blocks(own_places(r, 0), d_tok0) + token_blocks(own_places(r, 1), d_tok1), axis=0).astype(F32)
             return r + 1, table.at[both_orders(dest).reshape(-1)].add(grads, mode="drop")
 
         _, d_emb = lax.while_loop(lambda c: c[0] < grad_rounds, more_grads, (jnp.int32(1), d_emb))

time: 1150 us -> 1190 us (1.035)
  local copies, waits for them, and re-layouts: 127 us -> 184 us
  matrix products: 53.3 us -> 29.4 us
  Pallas kernels: 418 us -> 434 us
    unnamed x160 -> x204, local copies, waits for them, and re-layouts: 27.2 us -> 97.4 us
    pallas_call x0 -> x1, Pallas kernels: none -> 23.8 us  [down(): pl.pallas_call(functools.partial(down_kernel, n_tp), grid_spec=pltpu.Pref...]
    dot_general x1 -> x0, matrix products: 22.7 us -> none  [dot_nn(): lax.dot_general(a, b, (((1,), (0,)), ((), ())), preferred_element_type=F32)]
  transfers between devices with their start and end apart: 57 -> 57, of which waited for: 19 -> 18; matrix products, arithmetic and copies ran while one was open for 14% -> 10% of each run, Pallas kernels for 20% -> 20%
where the time goes in v5:
time: 1190 us; the launch traced here: 1170 us
  Pallas kernels  434 us (36%)
  waiting for transfers between devices  429 us (36%)
  local copies, waits for them, and re-layouts  184 us (15%)
  starting transfers between devices  42 us (4%)
  matrix products  29.4 us (2%)
  between operations  19.2 us (2%)
  other arithmetic  16.1 us (1%)
    ppermute x52, waiting for transfers between devices, swap(): return lax.ppermute(v, axis, tp_swap[k] if axis == 'tp' else pair)  392 us
    unnamed x204, local copies, waits for them, and re-layouts  97.4 us
    pallas_call x1, Pallas kernels, accum(): pl.pallas_call(functools.partial(accum_kernel, n_block, cap, sub_rows, wi...  64.5 us
    pallas_call x2, Pallas kernels, attn_bwd(): pl.pallas_call(attn_bwd_kernel, grid=(n_pair,), in_specs=[pl.BlockSpec((s...  62.7 us
    pallas_call x1, Pallas kernels, ffn(): pl.pallas_call(functools.partial(ffn_kernel, part), grid=(n_piece,), in_s...  56.2 us
    pallas_call x4, Pallas kernels, grad_pieces(): pl.pallas_call(functools.partial(grad_kernel, plus is not None), grid_spe...  52 us
    ppermute x52, starting transfers between devices, swap(): return lax.ppermute(v, axis, tp_swap[k] if axis == 'tp' else pair)  41.7 us
    pallas_call x1, Pallas kernels, attn_fwd(): pl.pallas_call(attn_fwd_kernel, grid=(n_seq, n_pair), in_specs=[pl.BlockS...  41.6 us
  transfers between devices with their start and end apart: 57, of which 18 were waited for; matrix products, arithmetic and copies ran while one was open for 10% of the time, Pallas kernels for 20%

profile of v5, /device:TPU:0, one launch (start us, length us, event | category | flops | bytes accessed | tf_op | source)
XLA Modules:
  0.0 1167.8 jit_solution(4001200671794182926)
XLA Ops:
  32.8 20.6 %gather_fusion.3 = bf16[1408,1024]{1,0:T(8,128)(2,1)} fusion(bf16[12568,1024]{1,0:T(8,128)(2,1)} %param.21, s32[2048]{0:T(1024)S(1)} %pad_clamp_fusion.3), kind=kCustom, calls=%fused_computation.3 | custom fusion | bytes 5772800 | tf_op jit(solution)/shard_map/jit(_take)/gather | solution.py:918
  53.5 19.4 %gather_fusion.4 = bf16[1408,1024]{1,0:T(8,128)(2,1)} fusion(bf16[12568,1024]{1,0:T(8,128)(2,1)} %param.21, s32[2048]{0:T(1024)S(1)} %pad_clamp_fusion.2), kind=kCustom, calls=%fused_computation.4 | custom fusion | bytes 5772800 | tf_op jit(solution)/shard_map/jit(_take)/gather | solution.py:920
  90.9 74.0 %collective-permute-done.37 = bf16[1792]{0:T(1024)(128)(2,1)S(1)} collective-permute-done((bf16[1792]{0:T(1024)(128)(2,1)S(1)}, bf16[1792]{0:T(1024)(128)(2,1)S(1)}, u32[]{:S(2)}, u32[]{:S(2)}) %collective-permute-start.37) | collective-permute-done | bytes 3616 | tf_op jit(solution)/shard_map/ppermute | solution.py:809
  186.5 31.2 %collective-permute-done.41.refs_3_ = bf16[2,256,1024]{2,1,0:T(8,128)(2,1)S(1)} collective-permute-done((bf16[2,256,1024]{2,1,0:T(8,128)(2,1)S(1)}, bf16[2,256,1024]{2,1,0:T(8,128)(2,1)S(1)}, u32[]{:S(2)}, u32[]{:S(2)}) %collective-permute-start.41) | collective-permute-done | bytes 1048608 | tf_op jit(solution)/shard_map/ppermute | solution.py:809
  217.7 18.8 %collective-permute-done.40.refs_2_ = bf16[2,256,1024]{2,1,0:T(8,128)(2,1)S(1)} collective-permute-done((bf16[2,256,1024]{2,1,0:T(8,128)(2,1)S(1)}, bf16[2,256,1024]{2,1,0:T(8,128)(2,1)S(1)}, u32[]{:S(2)}, u32[]{:S(2)}) %collective-permute-start.40) | collective-permute-done | bytes 1048608 | tf_op jit(solution)/shard_map/ppermute | solution.py:809
  248.7 19.4 %add_convert_fusion.1.qkv_ref = bf16[2048,3072]{1,0:T(8,128)(2,1)} fusion(bf16[2048,1024]{1,0:T(8,128)(2,1)} %get-tuple-element.1262.b2_ref, bf16[3072,1024]{1,0:T(8,128)(2,1)} %all-gather.4.cloned.1.call-done.w_ref, f32[3072]{0:T(1024)S(1)} %copy-done.70), kind=kOutput, calls=%fused_computation.280 | convolution fusion | flops 12897484800 | bytes 23080960 | tf_op jit(solution)/shard_map/dot_general | solution.py:20
  272.7 41.6 %attn_fwd.1 = (bf16[2048,1024]{1,0:T(8,128)(2,1)S(1)}, f32[2,8,2,1024]{3,2,1,0:T(2,128)S(1)}) custom-call(bf16[2048,3072]{1,0:T(8,128)(2,1)S(1)} %copy-done.44), custom_call_target="tpu_custom_call" | custom-call | flops 21474836480 | bytes 16777216 | tf_op jit(solution)/shard_map/attn_fwd/pallas_call | solution.py:74
  332.0 56.2 %ffn.1 = (bf16[2048,4096]{1,0:T(8,128)(2,1)S(1)}, bf16[2048,4096]{1,0:T(8,128)(2,1)}, f32[1,4096]{1,0:T(1,128)S(1)}) custom-call(bf16[2048,1024]{1,0:T(8,128)(2,1)S(1)} %get-tuple-element.1270.h_ref.b_ref, bf16[2048,1024]{1,0:T(8,128)(2,1)S(1)} %bitcast.192, bf16[16,576,1024]{2,1,0:T(8,128)(2,1)} %bitcast.208, bf16[16,576,1024]{2,1,0:T(8,128)(2,1)} %bitcast.209, ...), custom_call_target="tpu_custom_call" | custom-call | flops 34359738368 | bytes 50331648 | tf_op jit(solution)/shard_map/ffn/pallas_call | solution.py:346
  394.0 28.6 %ffn_back.1 = (f32[2048,1024]{1,0:T(8,128)S(1)}, bf16[2048,1024]{1,0:T(8,128)(2,1)S(1)}, f32[8,1024]{1,0:T(8,128)S(1)}) custom-call(bf16[2048,4096]{1,0:T(8,128)(2,1)} %get-tuple-element.1278.dup_ref.a_ref, bf16[16,576,1024]{2,1,0:T(8,128)(2,1)} %bitcast.210, f32[2048,1024]{1,0:T(8,128)} %copy-done.32, bf16[2048,1024]{1,0:T(8,128)(2,1)S(1)} %bitcast.193, ...), custom_call_target="tpu_custom_call" | custom-call | flops 17179869184 | bytes 41943040 | tf_op jit(solution)/shard_map/ffn_back/pallas_call | solution.py:416
  432.2 31.1 %attn_bwd.3.dq_ref.refs_1_ = bf16[1024,3072]{1,0:T(8,128)(2,1)S(1)} custom-call(bf16[2048,3072]{1,0:T(8,128)(2,1)S(1)} %copy-done.45, bf16[2048,1024]{1,0:T(8,128)(2,1)S(1)} %copy-done.8, bf16[2048,1024]{1,0:T(8,128)(2,1)S(1)} %convolution_convert_fusion.3.dctx_ref, f32[2,8,2,1024]{3,2,1,0:T(2,128)S(1)} %get-tuple-element.1280.lse_ref), custom_call_target="tpu_custom_call" | custom-call | flops 26843545600 | bytes 16777216 | tf_op jit(solution)/shard_map/attn_bwd/pallas_call | solution.py:140
  472.2 31.5 %attn_bwd.2.dq_ref.refs_0_ = bf16[1024,3072]{1,0:T(8,128)(2,1)S(1)} custom-call(bf16[2048,3072]{1,0:T(8,128)(2,1)S(1)} %copy-done.46, bf16[2048,1024]{1,0:T(8,128)(2,1)S(1)} %copy-done.8, bf16[2048,1024]{1,0:T(8,128)(2,1)S(1)} %copy-done.43, f32[2,8,2,1024]{3,2,1,0:T(2,128)S(1)} %get-tuple-element.1280.lse_ref), custom_call_target="tpu_custom_call" | custom-call | flops 26843545600 | bytes 16777216 | tf_op jit(solution)/shard_map/attn_bwd/pallas_call | solution.py:140
  505.9 16.1 %weight_grads.2 = f32[2112,1024]{1,0:T(8,128)} custom-call(s32[1]{0:T(128)S(6)} %sub.321.core_ref, bf16[2048,1024]{1,0:T(8,128)(2,1)S(1)} %copy-done.8, bf16[2048,1024]{1,0:T(8,128)(2,1)S(1)} %copy-done.19, bf16[2048,1024]{1,0:T(8,128)(2,1)} %get-tuple-element.1262.b2_ref, bf16[1024,3072]{1,0:T(8,128)(2,1)S(1)} %attn_bwd.2.dq_ref.refs_0_, ...), custom_call_target="tpu_custom_call" | custom-call | flops 8589934592 | bytes 25165824 | tf_op jit(solution)/shard_map/weight_grads/pallas_call | solution.py:735
  578.0 15.5 %weight_grads.3 = f32[2688,1024]{1,0:T(8,128)} custom-call(s32[1]{0:T(128)} %bitcast.46.core_ref, bf16[2048,1024]{1,0:T(8,128)(2,1)S(1)} %copy-done.9, bf16[2048,1024]{1,0:T(8,128)(2,1)S(1)} %copy-done.20, bf16[2048,1024]{1,0:T(8,128)(2,1)} %get-tuple-element.1262.b2_ref, bf16[1024,3072]{1,0:T(8,128)(2,1)S(1)} %copy-done.6, bf16[1024,3072]{1,0:T(8,128)(2,1)} %copy-done.2, ...), custom_call_target="tpu_custom_call" | custom-call | flops 8589934592 | bytes 25165824 | tf_op jit(solution)/shard_map/weight_grads/pallas_call | solution.py:735
  697.8 21.7 %collective-permute-done.60.refs_17_ = bf16[384,1024]{1,0:T(8,128)(2,1)} collective-permute-done((bf16[384,1024]{1,0:T(8,128)(2,1)S(1)}, bf16[384,1024]{1,0:T(8,128)(2,1)}, u32[]{:S(2)}, u32[]{:S(2)}) %collective-permute-start.60) | collective-permute-done | bytes 786464 | tf_op jit(solution)/shard_map/ppermute | solution.py:809
  729.5 22.4 %collective-permute-done.62.refs_19_ = bf16[384,1024]{1,0:T(8,128)(2,1)} collective-permute-done((bf16[384,1024]{1,0:T(8,128)(2,1)S(1)}, bf16[384,1024]{1,0:T(8,128)(2,1)}, u32[]{:S(2)}, u32[]{:S(2)}) %collective-permute-start.62) | collective-permute-done | bytes 786464 | tf_op jit(solution)/shard_map/ppermute | solution.py:809
  753.2 23.8 %down.1 = (bf16[2,256,1024]{2,1,0:T(8,128)(2,1)S(1)}, bf16[2,256,1024]{2,1,0:T(8,128)(2,1)S(1)}, bf16[2,256,1024]{2,1,0:T(8,128)(2,1)S(1)}, bf16[2,256,1024]{2,1,0:T(8,128)(2,1)S(1)}) custom-call(s32[1]{0:T(128)} %bitcast.10.me_ref, bf16[2048,4096]{1,0:T(8,128)(2,1)} %copy-done.15, bf16[16,576,1024]{2,1,0:T(8,128)(2,1)} %bitcast.211, ...), custom_call_target="tpu_custom_call" | custom-call | flops 17179869184 | bytes 29360128 | tf_op jit(solution)/shard_map/down/pallas_call | solution.py:373
  782.5 28.1 %collective-permute-done.47.refs_3_ = bf16[384,1024]{1,0:T(8,128)(2,1)S(1)} collective-permute-done((bf16[384,1024]{1,0:T(8,128)(2,1)S(1)}, bf16[384,1024]{1,0:T(8,128)(2,1)S(1)}, u32[]{:S(2)}, u32[]{:S(2)}) %collective-permute-start.47) | collective-permute-done | bytes 786464 | tf_op jit(solution)/shard_map/ppermute | solution.py:809
  813.4 30.0 %collective-permute-done.42.refs_1_ = bf16[2,256,1024]{2,1,0:T(8,128)(2,1)S(1)} collective-permute-done((bf16[2,256,1024]{2,1,0:T(8,128)(2,1)S(1)}, bf16[2,256,1024]{2,1,0:T(8,128)(2,1)S(1)}, u32[]{:S(2)}, u32[]{:S(2)}) %collective-permute-start.42) | collective-permute-done | bytes 1048608 | tf_op jit(solution)/shard_map/ppermute | solution.py:809
  845.2 21.4 %collective-permute-done.44.refs_3_ = bf16[2,256,1024]{2,1,0:T(8,128)(2,1)S(1)} collective-permute-done((bf16[2,256,1024]{2,1,0:T(8,128)(2,1)S(1)}, bf16[2,256,1024]{2,1,0:T(8,128)(2,1)S(1)}, u32[]{:S(2)}, u32[]{:S(2)}) %collective-permute-start.44) | collective-permute-done | bytes 1048608 | tf_op jit(solution)/shard_map/ppermute | solution.py:809
  876.0 30.6 %collective-permute-done.66.refs_23_ = bf16[384,1024]{1,0:T(8,128)(2,1)S(1)} collective-permute-done((bf16[384,1024]{1,0:T(8,128)(2,1)}, bf16[384,1024]{1,0:T(8,128)(2,1)S(1)}, u32[]{:S(2)}, u32[]{:S(2)}) %collective-permute-start.66) | collective-permute-done | bytes 786464 | tf_op jit(solution)/shard_map/ppermute | solution.py:809
  910.0 28.1 %collective-permute-done.49.refs_5_ = bf16[384,1024]{1,0:T(8,128)(2,1)} collective-permute-done((bf16[384,1024]{1,0:T(8,128)(2,1)}, bf16[384,1024]{1,0:T(8,128)(2,1)}, u32[]{:S(2)}, u32[]{:S(2)}) %collective-permute-start.49) | collective-permute-done | bytes 786464 | tf_op jit(solution)/shard_map/ppermute | solution.py:809
  938.1 37.2 %reduce-scatter.5.cloned.1.call-done.refs_0_ = f32[528,1024]{1,0:T(8,128)} async-done(((f32[4224,1024]{1,0:T(8,128)}), f32[528,1024]{1,0:T(8,128)}) %reduce-scatter.5.cloned.1.call-update) | async-done | bytes 2162704 | tf_op jit(solution)/shard_map/reduce_scatter | solution.py:977
  1007.7 63.3 %collective-permute-done.77.refs_1_ = f32[264,1024]{1,0:T(8,128)} collective-permute-done((f32[264,1024]{1,0:T(8,128)}, f32[264,1024]{1,0:T(8,128)}, u32[]{:S(2)}, u32[]{:S(2)}) %collective-permute-start.77) | collective-permute-done | bytes 1081376 | tf_op jit(solution)/shard_map/ppermute | solution.py:809
  1071.6 64.5 %table_accum.1 = f32[100544,128]{1,0:T(8,128)} custom-call(s32[12288]{0:T(1024)} %fusion.143.where_ref, s32[160]{0:T(256)} %min.12.first_ref, bf16[384,1024]{1,0:T(8,128)(2,1)} %copy-done.36, bf16[384,1024]{1,0:T(8,128)(2,1)} %copy-done.88, bf16[384,1024]{1,0:T(8,128)(2,1)} %copy-done.89, bf16[384,1024]{1,0:T(8,128)(2,1)} %copy-done.90, ...), custom_call_target="tpu_custom_call" | custom-call | flops 49999998976 | bytes 100000000 | tf_op jit(solution)/shard_map/table_accum/pallas_call | solution.py:637
  (533 shorter events, 373.4 us)
Async XLA Ops:
  7.2 241.5 %all-gather.4.cloned.1.call-start = ((), (), s32[]{:S(2)}) async-start(), calls=%async_computation.2 | async-start | bytes 7077888 | tf_op jit(solution)/shard_map/all_gather | solution.py:806
  9.4 306.9 %all-gather.6.cloned.1.call-start = ((), (), s32[]{:S(2)}) async-start(), calls=%async_computation.3 | async-start | bytes 20054016 | tf_op jit(solution)/shard_map/all_gather | solution.py:829
  26.3 841.3 %reduce-scatter.3.cloned.1.call-start = ((), (), s32[]{:S(2)}) async-start(), calls=%async_computation.4 | async-start | bytes 12386304 | tf_op jit(solution)/shard_map/reduce_scatter | solution.py:1024
  76.3 93.1 %collective-permute-start.34 = (bf16[704,1024]{1,0:T(8,128)(2,1)}, bf16[704,1024]{1,0:T(8,128)(2,1)S(1)}, u32[]{:S(2)}, u32[]{:S(2)}) collective-permute-start(bf16[704,1024]{1,0:T(8,128)(2,1)} %get-tuple-element.1578), channel_id=1, source_target_pairs={{0,8},{4,12},{8,0},{12,4},{1,9},{5,13},{9,1},{13,5},{2,10},{6,14},... | collective-permute-start | bytes 4325384 | tf_op jit(solution)/shard_map/ppermute | solution.py:809
  78.7 90.7 %collective-permute-start.35 = (bf16[704,1024]{1,0:T(8,128)(2,1)}, bf16[704,1024]{1,0:T(8,128)(2,1)}, u32[]{:S(2)}, u32[]{:S(2)}) collective-permute-start(bf16[704,1024]{1,0:T(8,128)(2,1)} %get-tuple-element.1576), channel_id=1, source_target_pairs={{0,12},{4,8},{8,4},{12,0},{1,13},{5,9},{9,5},{13,1},{2,14},{6,10},... | collective-permute-start | bytes 4325384 | tf_op jit(solution)/shard_map/ppermute | solution.py:809
  80.2 89.2 %collective-permute-start.33 = (bf16[704,1024]{1,0:T(8,128)(2,1)}, bf16[704,1024]{1,0:T(8,128)(2,1)}, u32[]{:S(2)}, u32[]{:S(2)}) collective-permute-start(bf16[704,1024]{1,0:T(8,128)(2,1)} %get-tuple-element.1577), channel_id=1, source_target_pairs={{0,4},{4,0},{8,12},{12,8},{1,5},{5,1},{9,13},{13,9},{2,6},{6,2},{1... | collective-permute-start | bytes 4325384 | tf_op jit(solution)/shard_map/ppermute | solution.py:809
  83.9 81.0 %collective-permute-start.37 = (bf16[1792]{0:T(1024)(128)(2,1)S(1)}, bf16[1792]{0:T(1024)(128)(2,1)S(1)}, u32[]{:S(2)}, u32[]{:S(2)}) collective-permute-start(bf16[1792]{0:T(1024)(128)(2,1)S(1)} %dynamic-update-slice.33), channel_id=1, source_target_pairs={{0,8},{4,12},{8,0},{12,4},{1,9},{5,13},{9,1},{13,5},{2,10},{6,14},... | collective-permute-start | bytes 10760 | tf_op jit(solution)/shard_map/ppermute | solution.py:809
  84.5 84.2 %collective-permute-start.36 = (bf16[1792]{0:T(1024)(128)(2,1)S(1)}, bf16[1792]{0:T(1024)(128)(2,1)S(1)}, u32[]{:S(2)}, u32[]{:S(2)}) collective-permute-start(bf16[1792]{0:T(1024)(128)(2,1)S(1)} %dynamic-update-slice.33), channel_id=1, source_target_pairs={{0,4},{4,0},{8,12},{12,8},{1,5},{5,1},{9,13},{13,9},{2,6},{6,2},{1... | collective-permute-start | bytes 10760 | tf_op jit(solution)/shard_map/ppermute | solution.py:809
  593.5 381.8 %reduce-scatter.5.cloned.1.call-start = ((), (), s32[]{:S(2)}) async-start(), calls=%async_computation.6 | async-start | bytes 19464192 | tf_op jit(solution)/shard_map/reduce_scatter | solution.py:977
  680.3 462.4 %all-gather.8.cloned.1.call-start = ((), (), s32[]{:S(2)}) async-start(), calls=%async_computation.5 | async-start | bytes 5013504 | tf_op jit(solution)/shard_map/all_gather | solution.py:1026
  691.7 86.2 %collective-permute-start.67 = (bf16[384,1024]{1,0:T(8,128)(2,1)S(1)}, bf16[384,1024]{1,0:T(8,128)(2,1)S(1)}, u32[]{:S(2)}, u32[]{:S(2)}) collective-permute-start(bf16[384,1024]{1,0:T(8,128)(2,1)S(1)} %get-tuple-element.1291.refs_16_), channel_id=1, source_target_pairs={{0,1},{1,0},{2,3},{3,2},{4,5},{5,4},{6,7},{7,6},{8,9},{9,8},{10,11... | collective-permute-start | bytes 2359304 | tf_op jit(solution)/shard_map/ppermute | solution.py:809
  696.0 82.3 %collective-permute-start.63 = (bf16[384,1024]{1,0:T(8,128)(2,1)S(1)}, bf16[384,1024]{1,0:T(8,128)(2,1)S(1)}, u32[]{:S(2)}, u32[]{:S(2)}) collective-permute-start(bf16[384,1024]{1,0:T(8,128)(2,1)S(1)} %get-tuple-element.1291.refs_16_), channel_id=1, source_target_pairs={{0,2},{2,0},{1,3},{3,1},{4,6},{6,4},{5,7},{7,5},{8,10},{10,8},{9,1... | collective-permute-start | bytes 2359304 | tf_op jit(solution)/shard_map/ppermute | solution.py:809
  871.7 66.4 %collective-permute-start.49 = (bf16[384,1024]{1,0:T(8,128)(2,1)}, bf16[384,1024]{1,0:T(8,128)(2,1)}, u32[]{:S(2)}, u32[]{:S(2)}) collective-permute-start(bf16[384,1024]{1,0:T(8,128)(2,1)} %copy-done.88), channel_id=1, source_target_pairs={{0,2},{2,0},{1,3},{3,1},{4,6},{6,4},{5,7},{7,5},{8,10},{10,8},{9,1... | collective-permute-start | bytes 2359304 | tf_op jit(solution)/shard_map/ppermute | solution.py:809
  872.5 106.5 %collective-permute-start.54 = (bf16[384,1024]{1,0:T(8,128)(2,1)}, bf16[384,1024]{1,0:T(8,128)(2,1)}, u32[]{:S(2)}, u32[]{:S(2)}) collective-permute-start(bf16[384,1024]{1,0:T(8,128)(2,1)} %copy-done.89), channel_id=1, source_target_pairs={{0,1},{1,0},{2,3},{3,2},{4,5},{5,4},{6,7},{7,6},{8,9},{9,8},{10,11... | collective-permute-start | bytes 2359304 | tf_op jit(solution)/shard_map/ppermute | solution.py:809
  906.6 72.7 %collective-permute-start.50 = (bf16[384,1024]{1,0:T(8,128)(2,1)}, bf16[384,1024]{1,0:T(8,128)(2,1)}, u32[]{:S(2)}, u32[]{:S(2)}) collective-permute-start(bf16[384,1024]{1,0:T(8,128)(2,1)} %copy-done.89), channel_id=1, source_target_pairs={{0,2},{2,0},{1,3},{3,1},{4,6},{6,4},{5,7},{7,5},{8,10},{10,8},{9,1... | collective-permute-start | bytes 2359304 | tf_op jit(solution)/shard_map/ppermute | solution.py:809
  908.3 71.6 %collective-permute-start.55 = (bf16[384,1024]{1,0:T(8,128)(2,1)}, bf16[384,1024]{1,0:T(8,128)(2,1)}, u32[]{:S(2)}, u32[]{:S(2)}) collective-permute-start(bf16[384,1024]{1,0:T(8,128)(2,1)} %copy-done.90), channel_id=1, source_target_pairs={{0,1},{1,0},{2,3},{3,2},{4,5},{5,4},{6,7},{7,6},{8,9},{9,8},{10,11... | collective-permute-start | bytes 2359304 | tf_op jit(solution)/shard_map/ppermute | solution.py:809
  908.3 79.9 %collective-permute-start.51 = (bf16[384,1024]{1,0:T(8,128)(2,1)}, bf16[384,1024]{1,0:T(8,128)(2,1)}, u32[]{:S(2)}, u32[]{:S(2)}) collective-permute-start(bf16[384,1024]{1,0:T(8,128)(2,1)} %copy-done.90), channel_id=1, source_target_pairs={{0,2},{2,0},{1,3},{3,1},{4,6},{6,4},{5,7},{7,5},{8,10},{10,8},{9,1... | collective-permute-start | bytes 2359304 | tf_op jit(solution)/shard_map/ppermute | solution.py:809
  975.3 96.3 %collective-permute-start.82 = (f32[528,1024]{1,0:T(8,128)}, f32[528,1024]{1,0:T(8,128)}, u32[]{:S(2)}, u32[]{:S(2)}) collective-permute-start(f32[528,1024]{1,0:T(8,128)} %reduce-scatter.5.cloned.1.call-done.refs_0_), channel_id=1, source_target_pairs={{0,2},{2,0},{1,3},{3,1},{4,6},{6,4},{5,7},{7,5},{8,10},{10,8},{9,1... | collective-permute-start | bytes 6488072 | tf_op jit(solution)/shard_map/ppermute | solution.py:809
  993.4 77.6 %collective-permute-start.77 = (f32[264,1024]{1,0:T(8,128)}, f32[264,1024]{1,0:T(8,128)}, u32[]{:S(2)}, u32[]{:S(2)}) collective-permute-start(f32[264,1024]{1,0:T(8,128)} %slice.292.refs_0_), channel_id=1, source_target_pairs={{0,2},{2,0},{1,3},{3,1},{4,6},{6,4},{5,7},{7,5},{8,10},{10,8},{9,1... | collective-permute-start | bytes 3244040 | tf_op jit(solution)/shard_map/ppermute | solution.py:809
  1001.4 69.7 %collective-permute-start.58 = (bf16[384,1024]{1,0:T(8,128)(2,1)}, bf16[384,1024]{1,0:T(8,128)(2,1)}, u32[]{:S(2)}, u32[]{:S(2)}) collective-permute-start(bf16[384,1024]{1,0:T(8,128)(2,1)} %collective-permute-done.50.refs_6_), channel_id=1, source_target_pairs={{0,1},{1,0},{2,3},{3,2},{4,5},{5,4},{6,7},{7,6},{8,9},{9,8},{10,11... | collective-permute-start | bytes 2359304 | tf_op jit(solution)/shard_map/ppermute | solution.py:809
  1001.6 69.9 %collective-permute-start.59 = (bf16[384,1024]{1,0:T(8,128)(2,1)}, bf16[384,1024]{1,0:T(8,128)(2,1)}, u32[]{:S(2)}, u32[]{:S(2)}) collective-permute-start(bf16[384,1024]{1,0:T(8,128)(2,1)} %collective-permute-done.51.refs_7_), channel_id=1, source_target_pairs={{0,1},{1,0},{2,3},{3,2},{4,5},{5,4},{6,7},{7,6},{8,9},{9,8},{10,11... | collective-permute-start | bytes 2359304 | tf_op jit(solution)/shard_map/ppermute | solution.py:809
  1007.4 128.7 %collective-permute-start.78 = (f32[264,1024]{1,0:T(8,128)}, f32[264,1024]{1,0:T(8,128)}, u32[]{:S(2)}, u32[]{:S(2)}) collective-permute-start(f32[264,1024]{1,0:T(8,128)} %slice.292.refs_0_), channel_id=1, source_target_pairs={{0,1},{1,0},{2,3},{3,2},{4,5},{5,4},{6,7},{7,6},{8,9},{9,8},{10,11... | collective-permute-start | bytes 3244040 | tf_op jit(solution)/shard_map/ppermute | solution.py:809
  1071.0 80.6 %collective-permute-start.83 = (f32[528,1024]{1,0:T(8,128)}, f32[528,1024]{1,0:T(8,128)}, u32[]{:S(2)}, u32[]{:S(2)}) collective-permute-start(f32[528,1024]{1,0:T(8,128)} %reduce-scatter.5.cloned.1.call-done.refs_0_), channel_id=1, source_target_pairs={{0,1},{1,0},{2,3},{3,2},{4,5},{5,4},{6,7},{7,6},{8,9},{9,8},{10,11... | collective-permute-start | bytes 6488072 | tf_op jit(solution)/shard_map/ppermute | solution.py:809
  1071.5 80.1 %collective-permute-start.84 = (f32[528,1024]{1,0:T(8,128)}, f32[528,1024]{1,0:T(8,128)}, u32[]{:S(2)}, u32[]{:S(2)}) collective-permute-start(f32[528,1024]{1,0:T(8,128)} %collective-permute-done.82.refs_1_), channel_id=1, source_target_pairs={{0,1},{1,0},{2,3},{3,2},{4,5},{5,4},{6,7},{7,6},{8,9},{9,8},{10,11... | collective-permute-start | bytes 6488072 | tf_op jit(solution)/shard_map/ppermute | solution.py:809
  (130 other events, 3953.0 us)
Sparse Core Ops, SparseCore 0:
  10.4 44.5 all-gather.3
  57.2 176.0 all-gather.5
  593.6 92.2 reduce-scatter.2
  690.7 284.4 reduce-scatter.4
  977.3 51.8 all-gather.7

commit v6 on v5

--- a/solution.py
+++ b/solution.py
@@ -83,7 +83,7 @@
         name="attn_fwd",
         cost_estimate=pl.CostEstimate(flops=n_seq * n_pair * 8 * seq * seq * 256 * 10 // 16, bytes_accessed=n_seq * seq * n_pair * width * 8,
                                       transcendentals=n_seq * n_pair * seq * seq),
-        compiler_params=pltpu.CompilerParams(vmem_limit_bytes=18 * 1024 * 1024),
+        compiler_params=pltpu.CompilerParams(vmem_limit_bytes=63 * 1024 * 1024),
     )(qkv)
 
 
@@ -150,7 +150,7 @@
         name="attn_bwd",
         cost_estimate=pl.CostEstimate(flops=n_pair * 20 * seq * seq * 256 * 10 // 16, bytes_accessed=seq * n_pair * width * 16,
                                       transcendentals=n_pair * seq * seq),
-        compiler_params=pltpu.CompilerParams(vmem_limit_bytes=22 * 1024 * 1024),
+        compiler_params=pltpu.CompilerParams(vmem_limit_bytes=63 * 1024 * 1024),
     )(qkv, ctx, dctx, lse)
 
 
@@ -248,7 +248,7 @@
         scratch_shapes=[pltpu.VMEM((n_blk * cap * width // 128, 128), F32), pltpu.VMEM((rows * width // 128, 128), F32)],
         name="embed_norm",
         cost_estimate=pl.CostEstimate(flops=15_000_000_000, bytes_accessed=n_tok * width * 10, transcendentals=0),
-        compiler_params=pltpu.CompilerParams(vmem_limit_bytes=28 * MIB),
+        compiler_params=pltpu.CompilerParams(vmem_limit_bytes=63 * 1024 * 1024),
     )(code, *blocks, pos_rows, gain, bias)
 
 
@@ -287,7 +287,7 @@
         scratch_shapes=[pltpu.VMEM((n_tok * width // 128, 128), F32), pltpu.VMEM((cap * width // 128, 128), F32)],
         name="token_pack",
         cost_estimate=pl.CostEstimate(flops=15_000_000_000, bytes_accessed=n_tok * width * 5, transcendentals=0),
-        compiler_params=pltpu.CompilerParams(vmem_limit_bytes=16 * MIB),
+        compiler_params=pltpu.CompilerParams(vmem_limit_bytes=63 * 1024 * 1024),
     )(code, tok)
 
 
@@ -315,7 +315,7 @@
         out_shape=[jax.ShapeDtypeStruct((n_tok, width), F32), jax.ShapeDtypeStruct((n_tok, width), BF16)],
         name="proj_norm",
         cost_estimate=pl.CostEstimate(flops=2 * n_tok * ctx.shape[1] * width, bytes_accessed=n_tok * width * 12, transcendentals=0),
-        compiler_params=pltpu.CompilerParams(vmem_limit_bytes=24 * MIB),
+        compiler_params=pltpu.CompilerParams(vmem_limit_bytes=63 * 1024 * 1024),
     )(ctx, w, x, b, gain, bias)
 
 
@@ -351,7 +351,7 @@
         out_shape=[jax.ShapeDtypeStruct((n_tok, ff), BF16), jax.ShapeDtypeStruct((n_tok, ff), BF16), jax.ShapeDtypeStruct((1, ff), F32)],
         name="ffn",
         cost_estimate=pl.CostEstimate(flops=4 * n_tok * ff * width, bytes_accessed=4 * n_tok * ff + 4 * ff * width, transcendentals=n_tok * ff),
-        compiler_params=pltpu.CompilerParams(vmem_limit_bytes=26 * MIB),
+        compiler_params=pltpu.CompilerParams(vmem_limit_bytes=63 * 1024 * 1024),
     )(hid, og, w, w, b_up)
 
 
@@ -381,7 +381,7 @@
         out_shape=[part] * n_tp,
         name="down",
         cost_estimate=pl.CostEstimate(flops=2 * n_tok * ff * width, bytes_accessed=2 * n_tok * ff + n_tok * width * 6, transcendentals=0),
-        compiler_params=pltpu.CompilerParams(vmem_limit_bytes=32 * MIB),
+        compiler_params=pltpu.CompilerParams(vmem_limit_bytes=63 * 1024 * 1024),
     )(me, act, w, x1, b)
 
 
@@ -422,7 +422,7 @@
         out_shape=[jax.ShapeDtypeStruct((n_tok, width), F32), jax.ShapeDtypeStruct((n_tok, width), BF16), jax.ShapeDtypeStruct((8, width), F32)],
         name="ffn_back",
         cost_estimate=pl.CostEstimate(flops=2 * n_tok * ff * width, bytes_accessed=2 * n_tok * ff + n_tok * width * 12, transcendentals=0),
-        compiler_params=pltpu.CompilerParams(vmem_limit_bytes=30 * MIB),
+        compiler_params=pltpu.CompilerParams(vmem_limit_bytes=63 * 1024 * 1024),
     )(d_up, w, x1, og, gain)
 
 
@@ -469,7 +469,7 @@
                    jax.ShapeDtypeStruct((8, width), F32), jax.ShapeDtypeStruct((8, n_cols), F32)],
         name="qkv_back",
         cost_estimate=pl.CostEstimate(flops=2 * seq * n_cols * width, bytes_accessed=2 * seq * n_cols + seq * width * 12, transcendentals=0),
-        compiler_params=pltpu.CompilerParams(vmem_limit_bytes=26 * MIB),
+        compiler_params=pltpu.CompilerParams(vmem_limit_bytes=63 * 1024 * 1024),
     )(d_qkv, w_qkv, x, d_resid1, gain, *(earlier or ()))
 
 
@@ -507,7 +507,7 @@
         out_shape=out_shape,
         name="grads_out",
         cost_estimate=pl.CostEstimate(flops=8_000_000_000, bytes_accessed=n_in * rows * width * 8, transcendentals=0),
-        compiler_params=pltpu.CompilerParams(vmem_limit_bytes=20 * MIB),
+        compiler_params=pltpu.CompilerParams(vmem_limit_bytes=63 * 1024 * 1024),
     )(me, *pieces)
 
 
@@ -531,7 +531,7 @@
         out_shape=jax.ShapeDtypeStruct(out_shape, parts[0].dtype),
         name="assemble",
         cost_estimate=pl.CostEstimate(flops=4_000_000_000, bytes_accessed=16 * MIB, transcendentals=0),
-        compiler_params=pltpu.CompilerParams(vmem_limit_bytes=10 * MIB),
+        compiler_params=pltpu.CompilerParams(vmem_limit_bytes=63 * 1024 * 1024),
     )(me, *parts)
 
 
@@ -684,7 +684,7 @@
         name="weight_grad",
         cost_estimate=pl.CostEstimate(flops=n_tok * n_cols * width, bytes_accessed=n_tok * (n_cols + 2 * width) + 2 * n_cols * width,
                                       transcendentals=0),
-        compiler_params=pltpu.CompilerParams(vmem_limit_bytes=18 * MIB),
+        compiler_params=pltpu.CompilerParams(vmem_limit_bytes=63 * 1024 * 1024),
     )(core, *args)
 
 
@@ -740,7 +740,7 @@
         name="weight_grads",
         cost_estimate=pl.CostEstimate(flops=n_tok * n_cols * width, bytes_accessed=n_tok * (n_cols + 4 * width) + 2 * n_cols * width,
                                       transcendentals=0),
-        compiler_params=pltpu.CompilerParams(vmem_limit_bytes=32 * MIB),
+        compiler_params=pltpu.CompilerParams(vmem_limit_bytes=63 * 1024 * 1024),
     )(core, *args)
 
 

time: 1190 us -> 1140 us (0.958)
  local copies, waits for them, and re-layouts: 184 us -> 97.4 us
  Pallas kernels: 434 us -> 473 us
    unnamed x204 -> x108, local copies, waits for them, and re-layouts: 97.4 us -> 5.17 us
    pallas_call x4, Pallas kernels: 52 us -> 64.5 us  [grad_pieces(): pl.pallas_call(functools.partial(grad_kernel, plus is not None), grid_spe...]
  transfers between devices with their start and end apart: 57 -> 57, of which waited for: 18 -> 17; matrix products, arithmetic and copies ran while one was open for 10% -> 12% of each run, Pallas kernels for 20% -> 24%
where the time goes in v6:
time: 1140 us; the launch traced here: 1130 us
  Pallas kernels  473 us (41%)
  waiting for transfers between devices  425 us (37%)
  local copies, waits for them, and re-layouts  97.4 us (9%)
  starting transfers between devices  47.3 us (4%)
  matrix products  33.3 us (3%)
  other arithmetic  19.1 us (2%)
  between operations  18.9 us (2%)
    ppermute x52, waiting for transfers between devices, swap(): return lax.ppermute(v, axis, tp_swap[k] if axis == 'tp' else pair)  386 us
    pallas_call x1, Pallas kernels, accum(): pl.pallas_call(functools.partial(accum_kernel, n_block, cap, sub_rows, wi...  64.5 us
    pallas_call x4, Pallas kernels, grad_pieces(): pl.pallas_call(functools.partial(grad_kernel, plus is not None), grid_spe...  64.5 us
    pallas_call x2, Pallas kernels, attn_bwd(): pl.pallas_call(attn_bwd_kernel, grid=(n_pair,), in_specs=[pl.BlockSpec((s...  61.5 us
    pallas_call x1, Pallas kernels, ffn(): pl.pallas_call(functools.partial(ffn_kernel, part), grid=(n_piece,), in_s...  56.5 us
    ppermute x52, starting transfers between devices, swap(): return lax.ppermute(v, axis, tp_swap[k] if axis == 'tp' else pair)  47.1 us
    pallas_call x1, Pallas kernels, attn_fwd(): pl.pallas_call(attn_fwd_kernel, grid=(n_seq, n_pair), in_specs=[pl.BlockS...  41.2 us
    reduce_scatter x1, waiting for transfers between devices, local_step(): lax.psum_scatter(ff_grads, ('tp', 'xx'), scatter_dimension=0, tiled=True)  38.3 us
  transfers between devices with their start and end apart: 57, of which 17 were waited for; matrix products, arithmetic and copies ran while one was open for 12% of the time, Pallas kernels for 24%

profile of v6, /device:TPU:0, one launch (start us, length us, event | category | flops | bytes accessed | tf_op | source)
XLA Modules:
  0.0 1128.1 jit_solution(12960102166999563901)
XLA Ops:
  32.4 20.3 %gather_fusion.3 = bf16[1408,1024]{1,0:T(8,128)(2,1)S(1)} fusion(bf16[12568,1024]{1,0:T(8,128)(2,1)} %param.21, s32[2048]{0:T(1024)S(1)} %pad_clamp_fusion.3), kind=kCustom, calls=%fused_computation.3 | custom fusion | bytes 5772800 | tf_op jit(solution)/shard_map/jit(_take)/gather | solution.py:918
  52.7 19.4 %gather_fusion.4 = bf16[1408,1024]{1,0:T(8,128)(2,1)} fusion(bf16[12568,1024]{1,0:T(8,128)(2,1)} %param.21, s32[2048]{0:T(1024)S(1)} %pad_clamp_fusion.2), kind=kCustom, calls=%fused_computation.4 | custom fusion | bytes 5772800 | tf_op jit(solution)/shard_map/jit(_take)/gather | solution.py:920
  92.8 71.7 %collective-permute-done.37 = bf16[1792]{0:T(1024)(128)(2,1)S(1)} collective-permute-done((bf16[1792]{0:T(1024)(128)(2,1)S(1)}, bf16[1792]{0:T(1024)(128)(2,1)S(1)}, u32[]{:S(2)}, u32[]{:S(2)}) %collective-permute-start.37) | collective-permute-done | bytes 3616 | tf_op jit(solution)/shard_map/ppermute | solution.py:809
  190.8 26.6 %collective-permute-done.41.refs_3_ = bf16[2,256,1024]{2,1,0:T(8,128)(2,1)} collective-permute-done((bf16[2,256,1024]{2,1,0:T(8,128)(2,1)}, bf16[2,256,1024]{2,1,0:T(8,128)(2,1)}, u32[]{:S(2)}, u32[]{:S(2)}) %collective-permute-start.41) | collective-permute-done | bytes 1048608 | tf_op jit(solution)/shard_map/ppermute | solution.py:809
  217.3 18.8 %collective-permute-done.40.refs_2_ = bf16[2,256,1024]{2,1,0:T(8,128)(2,1)} collective-permute-done((bf16[2,256,1024]{2,1,0:T(8,128)(2,1)}, bf16[2,256,1024]{2,1,0:T(8,128)(2,1)}, u32[]{:S(2)}, u32[]{:S(2)}) %collective-permute-start.40) | collective-permute-done | bytes 1048608 | tf_op jit(solution)/shard_map/ppermute | solution.py:809
  250.1 19.4 %add_convert_fusion.1.qkv_ref = bf16[2048,3072]{1,0:T(8,128)(2,1)} fusion(bf16[2048,1024]{1,0:T(8,128)(2,1)} %get-tuple-element.1262.b2_ref, bf16[3072,1024]{1,0:T(8,128)(2,1)} %all-gather.4.cloned.1.call-done.w_ref, f32[3072]{0:T(1024)S(1)} %copy-done.30), kind=kOutput, calls=%fused_computation.280 | convolution fusion | flops 12897484800 | bytes 23080960 | tf_op jit(solution)/shard_map/dot_general | solution.py:20
  269.5 41.2 %attn_fwd.1 = (bf16[2048,1024]{1,0:T(8,128)(2,1)}, f32[2,8,2,1024]{3,2,1,0:T(2,128)}) custom-call(bf16[2048,3072]{1,0:T(8,128)(2,1)} %add_convert_fusion.1.qkv_ref), custom_call_target="tpu_custom_call" | custom-call | flops 21474836480 | bytes 16777216 | tf_op jit(solution)/shard_map/attn_fwd/pallas_call | solution.py:74
  326.4 56.5 %ffn.1 = (bf16[2048,4096]{1,0:T(8,128)(2,1)}, bf16[2048,4096]{1,0:T(8,128)(2,1)}, f32[1,4096]{1,0:T(1,128)}) custom-call(bf16[2048,1024]{1,0:T(8,128)(2,1)} %get-tuple-element.1270.h_ref.b_ref, bf16[2048,1024]{1,0:T(8,128)(2,1)} %bitcast.201, bf16[16,576,1024]{2,1,0:T(8,128)(2,1)} %bitcast.190, bf16[16,576,1024]{2,1,0:T(8,128)(2,1)} %bitcast.191, ...), custom_call_target="tpu_custom_call" | custom-call | flops 34359738368 | bytes 50331648 | tf_op jit(solution)/shard_map/ffn/pallas_call | solution.py:346
  382.9 29.6 %ffn_back.1 = (f32[2048,1024]{1,0:T(8,128)}, bf16[2048,1024]{1,0:T(8,128)(2,1)}, f32[8,1024]{1,0:T(8,128)}) custom-call(bf16[2048,4096]{1,0:T(8,128)(2,1)} %get-tuple-element.1278.dup_ref.a_ref, bf16[16,576,1024]{2,1,0:T(8,128)(2,1)} %bitcast.192, f32[2048,1024]{1,0:T(8,128)} %get-tuple-element.1273.x1_ref, bf16[2048,1024]{1,0:T(8,128)(2,1)} %bitcast.202, ...), custom_call_target="tpu_custom_call" | custom-call | flops 17179869184 | bytes 41943040 | tf_op jit(solution)/shard_map/ffn_back/pallas_call | solution.py:416
  422.1 30.9 %attn_bwd.3.dq_ref.refs_1_ = bf16[1024,3072]{1,0:T(8,128)(2,1)} custom-call(bf16[2048,3072]{1,0:T(8,128)(2,1)} %add_convert_fusion.1.qkv_ref, bf16[2048,1024]{1,0:T(8,128)(2,1)} %get-tuple-element.1265.c_ref.ctx_ref.a1_ref, bf16[2048,1024]{1,0:T(8,128)(2,1)} %convolution_convert_fusion.3.dctx_ref, f32[2,8,2,1024]{3,2,1,0:T(2,128)} %get-tuple-element.1280.lse_ref), custom_call_target="tpu_custom_call" | custom-call | flops 26843545600 | bytes 16777216 | tf_op jit(solution)/shard_map/attn_bwd/pallas_call | solution.py:140
  453.0 30.5 %attn_bwd.2.dq_ref.refs_0_ = bf16[1024,3072]{1,0:T(8,128)(2,1)} custom-call(bf16[2048,3072]{1,0:T(8,128)(2,1)} %add_convert_fusion.1.qkv_ref, bf16[2048,1024]{1,0:T(8,128)(2,1)} %get-tuple-element.1265.c_ref.ctx_ref.a1_ref, bf16[2048,1024]{1,0:T(8,128)(2,1)} %convolution_convert_fusion.3.dctx_ref, f32[2,8,2,1024]{3,2,1,0:T(2,128)} %get-tuple-element.1280.lse_ref), custom_call_target="tpu_custom_call" | custom-call | flops 26843545600 | bytes 16777216 | tf_op jit(solution)/shard_map/attn_bwd/pallas_call | solution.py:140
  542.3 18.0 %weight_grads.3 = f32[2688,1024]{1,0:T(8,128)} custom-call(s32[1]{0:T(128)} %bitcast.46.core_ref, bf16[2048,1024]{1,0:T(8,128)(2,1)} %get-tuple-element.1265.c_ref.ctx_ref.a1_ref, bf16[2048,1024]{1,0:T(8,128)(2,1)} %get-tuple-element.1279.b1_ref, bf16[2048,1024]{1,0:T(8,128)(2,1)} %get-tuple-element.1262.b2_ref, bf16[1024,3072]{1,0:T(8,128)(2,1)} %attn_bwd.2.dq_ref.refs_0_, ...), custom_call_target="tpu_custom_call" | custom-call | flops 8589934592 | bytes 25165824 | tf_op jit(solution)/shard_map/weight_grads/pallas_call | solution.py:735
  591.6 16.9 %weight_grad.6.refs_1_ = f32[4224,1024]{1,0:T(8,128)} custom-call(s32[1]{0:T(128)} %bitcast.46.core_ref, bf16[2048,4096]{1,0:T(8,128)(2,1)} %get-tuple-element.1272.act_ref.a_ref, bf16[2048,1024]{1,0:T(8,128)(2,1)} %bitcast.204, f32[2112,1024]{1,0:T(8,128)} %collective-permute-done.81.refs_0_), custom_call_target="tpu_custom_call" | custom-call | flops 8589934592 | bytes 20971520 | tf_op jit(solution)/shard_map/weight_grad/pallas_call | solution.py:679
  608.5 16.9 %weight_grad.7 = f32[4224,1024]{1,0:T(8,128)} custom-call(s32[1]{0:T(128)} %bitcast.46.core_ref, bf16[2048,4096]{1,0:T(8,128)(2,1)} %get-tuple-element.1278.dup_ref.a_ref, bf16[2048,1024]{1,0:T(8,128)(2,1)} %get-tuple-element.1270.h_ref.b_ref, f32[2112,1024]{1,0:T(8,128)} %collective-permute-done.80.refs_0_, ...), custom_call_target="tpu_custom_call", output_to_operand_aliasing={{}: (4, {})} | custom-call | flops 8589934592 | bytes 20971520 | tf_op jit(solution)/shard_map/weight_grad/pallas_call | solution.py:679
  648.0 18.4 %collective-permute-done.60.refs_17_ = bf16[384,1024]{1,0:T(8,128)(2,1)} collective-permute-done((bf16[384,1024]{1,0:T(8,128)(2,1)}, bf16[384,1024]{1,0:T(8,128)(2,1)}, u32[]{:S(2)}, u32[]{:S(2)}) %collective-permute-start.60) | collective-permute-done | bytes 786464 | tf_op jit(solution)/shard_map/ppermute | solution.py:809
  695.2 26.2 %down.1 = (bf16[2,256,1024]{2,1,0:T(8,128)(2,1)}, bf16[2,256,1024]{2,1,0:T(8,128)(2,1)}, bf16[2,256,1024]{2,1,0:T(8,128)(2,1)}, bf16[2,256,1024]{2,1,0:T(8,128)(2,1)}) custom-call(s32[1]{0:T(128)} %bitcast.10.me_ref, bf16[2048,4096]{1,0:T(8,128)(2,1)} %get-tuple-element.1272.act_ref.a_ref, bf16[16,576,1024]{2,1,0:T(8,128)(2,1)} %bitcast.193, ...), custom_call_target="tpu_custom_call" | custom-call | flops 17179869184 | bytes 29360128 | tf_op jit(solution)/shard_map/down/pallas_call | solution.py:373
  726.9 25.8 %collective-permute-done.47.refs_3_ = bf16[384,1024]{1,0:T(8,128)(2,1)} collective-permute-done((bf16[384,1024]{1,0:T(8,128)(2,1)}, bf16[384,1024]{1,0:T(8,128)(2,1)}, u32[]{:S(2)}, u32[]{:S(2)}) %collective-permute-start.47) | collective-permute-done | bytes 786464 | tf_op jit(solution)/shard_map/ppermute | solution.py:809
  755.3 37.3 %collective-permute-done.42.refs_1_ = bf16[2,256,1024]{2,1,0:T(8,128)(2,1)} collective-permute-done((bf16[2,256,1024]{2,1,0:T(8,128)(2,1)}, bf16[2,256,1024]{2,1,0:T(8,128)(2,1)}, u32[]{:S(2)}, u32[]{:S(2)}) %collective-permute-start.42) | collective-permute-done | bytes 1048608 | tf_op jit(solution)/shard_map/ppermute | solution.py:809
  794.0 30.6 %collective-permute-done.44.refs_3_ = bf16[2,256,1024]{2,1,0:T(8,128)(2,1)} collective-permute-done((bf16[2,256,1024]{2,1,0:T(8,128)(2,1)}, bf16[2,256,1024]{2,1,0:T(8,128)(2,1)}, u32[]{:S(2)}, u32[]{:S(2)}) %collective-permute-start.44) | collective-permute-done | bytes 1048608 | tf_op jit(solution)/shard_map/ppermute | solution.py:809
  832.3 30.4 %collective-permute-done.66.refs_23_ = bf16[384,1024]{1,0:T(8,128)(2,1)S(1)} collective-permute-done((bf16[384,1024]{1,0:T(8,128)(2,1)}, bf16[384,1024]{1,0:T(8,128)(2,1)S(1)}, u32[]{:S(2)}, u32[]{:S(2)}) %collective-permute-start.66) | collective-permute-done | bytes 786464 | tf_op jit(solution)/shard_map/ppermute | solution.py:809
  866.8 28.2 %collective-permute-done.49.refs_5_ = bf16[384,1024]{1,0:T(8,128)(2,1)} collective-permute-done((bf16[384,1024]{1,0:T(8,128)(2,1)}, bf16[384,1024]{1,0:T(8,128)(2,1)}, u32[]{:S(2)}, u32[]{:S(2)}) %collective-permute-start.49) | collective-permute-done | bytes 786464 | tf_op jit(solution)/shard_map/ppermute | solution.py:809
  895.1 38.3 %reduce-scatter.5.cloned.1.call-done.refs_0_ = f32[528,1024]{1,0:T(8,128)} async-done(((f32[4224,1024]{1,0:T(8,128)}), f32[528,1024]{1,0:T(8,128)}) %reduce-scatter.5.cloned.1.call-update) | async-done | bytes 2162704 | tf_op jit(solution)/shard_map/reduce_scatter | solution.py:977
  965.1 63.0 %collective-permute-done.77.refs_1_ = f32[264,1024]{1,0:T(8,128)} collective-permute-done((f32[264,1024]{1,0:T(8,128)}, f32[264,1024]{1,0:T(8,128)}, u32[]{:S(2)}, u32[]{:S(2)}) %collective-permute-start.77) | collective-permute-done | bytes 1081376 | tf_op jit(solution)/shard_map/ppermute | solution.py:809
  1028.6 64.5 %table_accum.1 = f32[100544,128]{1,0:T(8,128)} custom-call(s32[12288]{0:T(1024)} %fusion.143.where_ref, s32[160]{0:T(256)} %min.12.first_ref, bf16[384,1024]{1,0:T(8,128)(2,1)} %get-tuple-element.1283.refs_0_, bf16[384,1024]{1,0:T(8,128)(2,1)} %collective-permute-done.45.refs_1_, bf16[384,1024]{1,0:T(8,128)(2,1)} %collective-permute-done.46.refs_2_, ...), custom_call_target="tpu_custom_call" | custom-call | flops 49999998976 | bytes 100000000 | tf_op jit(solution)/shard_map/table_accum/pallas_call | solution.py:637
  (435 shorter events, 329.6 us)
Async XLA Ops:
  7.2 242.9 %all-gather.4.cloned.1.call-start = ((), (), s32[]{:S(2)}) async-start(), calls=%async_computation.2 | async-start | bytes 7077888 | tf_op jit(solution)/shard_map/all_gather | solution.py:806
  9.5 301.3 %all-gather.6.cloned.1.call-start = ((), (), s32[]{:S(2)}) async-start(), calls=%async_computation.3 | async-start | bytes 20054016 | tf_op jit(solution)/shard_map/all_gather | solution.py:829
  26.4 798.2 %reduce-scatter.3.cloned.1.call-start = ((), (), s32[]{:S(2)}) async-start(), calls=%async_computation.4 | async-start | bytes 12386304 | tf_op jit(solution)/shard_map/reduce_scatter | solution.py:1024
  75.9 93.6 %collective-permute-start.34 = (bf16[704,1024]{1,0:T(8,128)(2,1)}, bf16[704,1024]{1,0:T(8,128)(2,1)}, u32[]{:S(2)}, u32[]{:S(2)}) collective-permute-start(bf16[704,1024]{1,0:T(8,128)(2,1)} %get-tuple-element.1578), channel_id=1, source_target_pairs={{0,8},{4,12},{8,0},{12,4},{1,9},{5,13},{9,1},{13,5},{2,10},{6,14},... | collective-permute-start | bytes 4325384 | tf_op jit(solution)/shard_map/ppermute | solution.py:809
  78.1 91.3 %collective-permute-start.35 = (bf16[704,1024]{1,0:T(8,128)(2,1)}, bf16[704,1024]{1,0:T(8,128)(2,1)}, u32[]{:S(2)}, u32[]{:S(2)}) collective-permute-start(bf16[704,1024]{1,0:T(8,128)(2,1)} %get-tuple-element.1576), channel_id=1, source_target_pairs={{0,12},{4,8},{8,4},{12,0},{1,13},{5,9},{9,5},{13,1},{2,14},{6,10},... | collective-permute-start | bytes 4325384 | tf_op jit(solution)/shard_map/ppermute | solution.py:809
  79.6 89.9 %collective-permute-start.33 = (bf16[704,1024]{1,0:T(8,128)(2,1)}, bf16[704,1024]{1,0:T(8,128)(2,1)}, u32[]{:S(2)}, u32[]{:S(2)}) collective-permute-start(bf16[704,1024]{1,0:T(8,128)(2,1)} %get-tuple-element.1577), channel_id=1, source_target_pairs={{0,4},{4,0},{8,12},{12,8},{1,5},{5,1},{9,13},{13,9},{2,6},{6,2},{1... | collective-permute-start | bytes 4325384 | tf_op jit(solution)/shard_map/ppermute | solution.py:809
  84.2 80.3 %collective-permute-start.37 = (bf16[1792]{0:T(1024)(128)(2,1)S(1)}, bf16[1792]{0:T(1024)(128)(2,1)S(1)}, u32[]{:S(2)}, u32[]{:S(2)}) collective-permute-start(bf16[1792]{0:T(1024)(128)(2,1)S(1)} %dynamic-update-slice.33), channel_id=1, source_target_pairs={{0,8},{4,12},{8,0},{12,4},{1,9},{5,13},{9,1},{13,5},{2,10},{6,14},... | collective-permute-start | bytes 10760 | tf_op jit(solution)/shard_map/ppermute | solution.py:809
  84.6 83.5 %collective-permute-start.36 = (bf16[1792]{0:T(1024)(128)(2,1)S(1)}, bf16[1792]{0:T(1024)(128)(2,1)S(1)}, u32[]{:S(2)}, u32[]{:S(2)}) collective-permute-start(bf16[1792]{0:T(1024)(128)(2,1)S(1)} %dynamic-update-slice.33), channel_id=1, source_target_pairs={{0,4},{4,0},{8,12},{12,8},{1,5},{5,1},{9,13},{13,9},{2,6},{6,2},{1... | collective-permute-start | bytes 10760 | tf_op jit(solution)/shard_map/ppermute | solution.py:809
  560.3 373.0 %reduce-scatter.5.cloned.1.call-start = ((), (), s32[]{:S(2)}) async-start(), calls=%async_computation.6 | async-start | bytes 19464192 | tf_op jit(solution)/shard_map/reduce_scatter | solution.py:977
  625.4 477.1 %all-gather.8.cloned.1.call-start = ((), (), s32[]{:S(2)}) async-start(), calls=%async_computation.5 | async-start | bytes 5013504 | tf_op jit(solution)/shard_map/all_gather | solution.py:1026
  639.4 82.0 %collective-permute-start.67 = (bf16[384,1024]{1,0:T(8,128)(2,1)}, bf16[384,1024]{1,0:T(8,128)(2,1)}, u32[]{:S(2)}, u32[]{:S(2)}) collective-permute-start(bf16[384,1024]{1,0:T(8,128)(2,1)} %get-tuple-element.1291.refs_16_), channel_id=1, source_target_pairs={{0,1},{1,0},{2,3},{3,2},{4,5},{5,4},{6,7},{7,6},{8,9},{9,8},{10,11... | collective-permute-start | bytes 2359304 | tf_op jit(solution)/shard_map/ppermute | solution.py:809
  646.5 74.9 %collective-permute-start.63 = (bf16[384,1024]{1,0:T(8,128)(2,1)}, bf16[384,1024]{1,0:T(8,128)(2,1)}, u32[]{:S(2)}, u32[]{:S(2)}) collective-permute-start(bf16[384,1024]{1,0:T(8,128)(2,1)} %get-tuple-element.1291.refs_16_), channel_id=1, source_target_pairs={{0,2},{2,0},{1,3},{3,1},{4,6},{6,4},{5,7},{7,5},{8,10},{10,8},{9,1... | collective-permute-start | bytes 2359304 | tf_op jit(solution)/shard_map/ppermute | solution.py:809
  752.8 71.9 %collective-permute-start.44 = (bf16[2,256,1024]{2,1,0:T(8,128)(2,1)}, bf16[2,256,1024]{2,1,0:T(8,128)(2,1)}, u32[]{:S(2)}, u32[]{:S(2)}) collective-permute-start(bf16[2,256,1024]{2,1,0:T(8,128)(2,1)} %get-tuple-element.1277), channel_id=1, source_target_pairs={{0,12},{4,8},{8,4},{12,0},{1,13},{5,9},{9,5},{13,1},{2,14},{6,10},... | collective-permute-start | bytes 3145736 | tf_op jit(solution)/shard_map/ppermute | solution.py:809
  754.1 72.4 %collective-permute-start.68 = (bf16[384,1024]{1,0:T(8,128)(2,1)}, bf16[384,1024]{1,0:T(8,128)(2,1)S(1)}, u32[]{:S(2)}, u32[]{:S(2)}) collective-permute-start(bf16[384,1024]{1,0:T(8,128)(2,1)} %collective-permute-done.60.refs_17_), channel_id=1, source_target_pairs={{0,1},{1,0},{2,3},{3,2},{4,5},{5,4},{6,7},{7,6},{8,9},{9,8},{10,11... | collective-permute-start | bytes 2359304 | tf_op jit(solution)/shard_map/ppermute | solution.py:809
  754.1 73.9 %collective-permute-start.64 = (bf16[384,1024]{1,0:T(8,128)(2,1)}, bf16[384,1024]{1,0:T(8,128)(2,1)S(1)}, u32[]{:S(2)}, u32[]{:S(2)}) collective-permute-start(bf16[384,1024]{1,0:T(8,128)(2,1)} %collective-permute-done.60.refs_17_), channel_id=1, source_target_pairs={{0,2},{2,0},{1,3},{3,1},{4,6},{6,4},{5,7},{7,5},{8,10},{10,8},{9,1... | collective-permute-start | bytes 2359304 | tf_op jit(solution)/shard_map/ppermute | solution.py:809
  829.5 106.9 %collective-permute-start.54 = (bf16[384,1024]{1,0:T(8,128)(2,1)}, bf16[384,1024]{1,0:T(8,128)(2,1)}, u32[]{:S(2)}, u32[]{:S(2)}) collective-permute-start(bf16[384,1024]{1,0:T(8,128)(2,1)} %collective-permute-done.46.refs_2_), channel_id=1, source_target_pairs={{0,1},{1,0},{2,3},{3,2},{4,5},{5,4},{6,7},{7,6},{8,9},{9,8},{10,11... | collective-permute-start | bytes 2359304 | tf_op jit(solution)/shard_map/ppermute | solution.py:809
  862.8 74.0 %collective-permute-start.50 = (bf16[384,1024]{1,0:T(8,128)(2,1)}, bf16[384,1024]{1,0:T(8,128)(2,1)}, u32[]{:S(2)}, u32[]{:S(2)}) collective-permute-start(bf16[384,1024]{1,0:T(8,128)(2,1)} %collective-permute-done.46.refs_2_), channel_id=1, source_target_pairs={{0,2},{2,0},{1,3},{3,1},{4,6},{6,4},{5,7},{7,5},{8,10},{10,8},{9,1... | collective-permute-start | bytes 2359304 | tf_op jit(solution)/shard_map/ppermute | solution.py:809
  865.1 72.1 %collective-permute-start.55 = (bf16[384,1024]{1,0:T(8,128)(2,1)}, bf16[384,1024]{1,0:T(8,128)(2,1)}, u32[]{:S(2)}, u32[]{:S(2)}) collective-permute-start(bf16[384,1024]{1,0:T(8,128)(2,1)} %collective-permute-done.47.refs_3_), channel_id=1, source_target_pairs={{0,1},{1,0},{2,3},{3,2},{4,5},{5,4},{6,7},{7,6},{8,9},{9,8},{10,11... | collective-permute-start | bytes 2359304 | tf_op jit(solution)/shard_map/ppermute | solution.py:809
  865.2 79.0 %collective-permute-start.51 = (bf16[384,1024]{1,0:T(8,128)(2,1)}, bf16[384,1024]{1,0:T(8,128)(2,1)}, u32[]{:S(2)}, u32[]{:S(2)}) collective-permute-start(bf16[384,1024]{1,0:T(8,128)(2,1)} %collective-permute-done.47.refs_3_), channel_id=1, source_target_pairs={{0,2},{2,0},{1,3},{3,1},{4,6},{6,4},{5,7},{7,5},{8,10},{10,8},{9,1... | collective-permute-start | bytes 2359304 | tf_op jit(solution)/shard_map/ppermute | solution.py:809
  933.3 95.2 %collective-permute-start.82 = (f32[528,1024]{1,0:T(8,128)}, f32[528,1024]{1,0:T(8,128)}, u32[]{:S(2)}, u32[]{:S(2)}) collective-permute-start(f32[528,1024]{1,0:T(8,128)} %reduce-scatter.5.cloned.1.call-done.refs_0_), channel_id=1, source_target_pairs={{0,2},{2,0},{1,3},{3,1},{4,6},{6,4},{5,7},{7,5},{8,10},{10,8},{9,1... | collective-permute-start | bytes 6488072 | tf_op jit(solution)/shard_map/ppermute | solution.py:809
  949.4 78.6 %collective-permute-start.77 = (f32[264,1024]{1,0:T(8,128)}, f32[264,1024]{1,0:T(8,128)}, u32[]{:S(2)}, u32[]{:S(2)}) collective-permute-start(f32[264,1024]{1,0:T(8,128)} %slice.292.refs_0_), channel_id=1, source_target_pairs={{0,2},{2,0},{1,3},{3,1},{4,6},{6,4},{5,7},{7,5},{8,10},{10,8},{9,1... | collective-permute-start | bytes 3244040 | tf_op jit(solution)/shard_map/ppermute | solution.py:809
  964.8 128.4 %collective-permute-start.78 = (f32[264,1024]{1,0:T(8,128)}, f32[264,1024]{1,0:T(8,128)}, u32[]{:S(2)}, u32[]{:S(2)}) collective-permute-start(f32[264,1024]{1,0:T(8,128)} %slice.292.refs_0_), channel_id=1, source_target_pairs={{0,1},{1,0},{2,3},{3,2},{4,5},{5,4},{6,7},{7,6},{8,9},{9,8},{10,11... | collective-permute-start | bytes 3244040 | tf_op jit(solution)/shard_map/ppermute | solution.py:809
  1028.0 83.4 %collective-permute-start.83 = (f32[528,1024]{1,0:T(8,128)}, f32[528,1024]{1,0:T(8,128)}, u32[]{:S(2)}, u32[]{:S(2)}) collective-permute-start(f32[528,1024]{1,0:T(8,128)} %reduce-scatter.5.cloned.1.call-done.refs_0_), channel_id=1, source_target_pairs={{0,1},{1,0},{2,3},{3,2},{4,5},{5,4},{6,7},{7,6},{8,9},{9,8},{10,11... | collective-permute-start | bytes 6488072 | tf_op jit(solution)/shard_map/ppermute | solution.py:809
  1028.5 82.9 %collective-permute-start.84 = (f32[528,1024]{1,0:T(8,128)}, f32[528,1024]{1,0:T(8,128)}, u32[]{:S(2)}, u32[]{:S(2)}) collective-permute-start(f32[528,1024]{1,0:T(8,128)} %collective-permute-done.82.refs_1_), channel_id=1, source_target_pairs={{0,1},{1,0},{2,3},{3,2},{4,5},{5,4},{6,7},{7,6},{8,9},{9,8},{10,11... | collective-permute-start | bytes 6488072 | tf_op jit(solution)/shard_map/ppermute | solution.py:809
  (82 other events, 3167.8 us)
Sparse Core Ops, SparseCore 0:
  9.8 44.5 all-gather.3
  56.6 173.5 all-gather.5
  560.5 102.1 reduce-scatter.2
  667.5 265.7 reduce-scatter.4
  935.4 51.7 all-gather.7

commit v7 on v6

--- a/solution.py
+++ b/solution.py
@@ -655,37 +655,40 @@
 
 def grad_kernel(has_plus, core_ref, a_ref, b_ref, *refs):
     out_ref = refs[-1]
-    n = a_ref.shape[1]
+    piece, width = out_ref.shape[2:]
+    half = a_ref.shape[1] // 2
     g = dot_tn(a_ref[...], b_ref[...])
-    out_ref[0:n, :] = g + refs[0][0:n, :] if has_plus else g
-    if out_ref.shape[0] > n:
-        out_ref[n:, :] = jnp.zeros((out_ref.shape[0] - n, out_ref.shape[1]), F32)
+    for x in range(2):
+        part = g[x * half:(x + 1) * half]
+        out_ref[x, 0, 0:half, :] = part + refs[0][x * piece:x * piece + half, :] if has_plus else part
+        if piece > half:
+            out_ref[x, 0, half:, :] = jnp.zeros((piece - half, width), F32)
 
 
 def grad_pieces(core, a, b, n_tp, piece, which, n_which, plus=None, into=None):
     n_tok, n_cols = a.shape
     width = b.shape[1]
-    bn = n_cols // (4 * n_tp)
-    out_spec = pl.BlockSpec((piece, width), lambda p, c: (n_which * p + which, 0))
-    in_specs = [pl.BlockSpec((n_tok, bn), lambda p, c: (0, 4 * (p // 2) + 2 * c[0] + p % 2)),
-                pl.BlockSpec((n_tok, width), lambda p, c: (0, 0), pipeline_mode=pl.Buffered(1))]
+    out_spec = pl.BlockSpec((2, 1, piece, width), lambda t, c: (t, which, 0, 0))
+    in_specs = [pl.BlockSpec((n_tok, n_cols // (2 * n_tp)), lambda t, c: (0, 2 * t + c[0])),
+                pl.BlockSpec((n_tok, width), lambda t, c: (0, 0), pipeline_mode=pl.Buffered(1))]
     args = [a, b]
     if plus is not None:
-        in_specs.append(pl.BlockSpec((piece, width), lambda p, c: (p, 0)))
+        in_specs.append(pl.BlockSpec((2 * piece, width), lambda t, c: (t, 0)))
         args.append(plus)
+    shape = (2 * n_tp, n_which, piece, width)
     if into is not None:
         in_specs.append(pl.BlockSpec(memory_space=pl.ANY))
-        args.append(into)
+        args.append(into.reshape(shape))
     return pl.pallas_call(
         functools.partial(grad_kernel, plus is not None),
-        grid_spec=pltpu.PrefetchScalarGridSpec(num_scalar_prefetch=1, grid=(2 * n_tp,), in_specs=in_specs, out_specs=out_spec),
-        out_shape=jax.ShapeDtypeStruct((2 * n_tp * n_which * piece, width), F32),
+        grid_spec=pltpu.PrefetchScalarGridSpec(num_scalar_prefetch=1, grid=(n_tp,), in_specs=in_specs, out_specs=out_spec),
+        out_shape=jax.ShapeDtypeStruct(shape, F32),
         input_output_aliases={} if into is None else {len(args): 0},
         name="weight_grad",
         cost_estimate=pl.CostEstimate(flops=n_tok * n_cols * width, bytes_accessed=n_tok * (n_cols + 2 * width) + 2 * n_cols * width,
                                       transcendentals=0),
         compiler_params=pltpu.CompilerParams(vmem_limit_bytes=63 * 1024 * 1024),
-    )(core, *args)
+    )(core, *args).reshape(-1, width)
 
 
 def grad_rest_kernel(spans, last, n_a2, core_ref, a1_ref, b1_ref, b2_ref, *refs):
@@ -932,7 +935,9 @@
 
         got0, place0, _ = rows_here(0, lists(0))
         code0 = (place0 // 8) * (8 * tiles) + place0 % 8
-        got0, out_grad = lax.optimization_barrier((got0, out_grad))
+        og_parts = out_grad.reshape(n_tp, n_seq, seq_local, width)
+        og_parts = [lax.dynamic_index_in_dim(og_parts, tp_index ^ k, 0, keepdims=False) for k in range(n_tp)]
+        got0, og_parts = lax.optimization_barrier((got0, og_parts))
         resid_x, hid1 = embed(code0, got0, pos_rows, gain1, bias1, n_tok)
 
         def more_rows(carry):
@@ -944,9 +949,7 @@
 
         _, resid_x, hid1 = lax.while_loop(lambda c: c[0] < rounds, more_rows, (jnp.int32(1), resid_x, hid1))
 
-        og_parts = out_grad.reshape(n_tp, n_seq, seq_local, width)
-        parts = [lax.dynamic_index_in_dim(og_parts, tp_index ^ k, 0, keepdims=False) for k in range(n_tp)]
-        parts = [swap(part, "tp", k) if k else part for k, part in enumerate(parts)]
+        parts = [swap(part, "tp", k) if k else part for k, part in enumerate(og_parts)]
         me = jnp.reshape(tp_index, (1,))
         og = assemble(me, parts, (n_seq, n_tp, seq_local, width), (n_seq, 1, seq_local, width)).reshape(n_tok, width)
 
@@ -1020,10 +1023,12 @@
         small = jnp.concatenate([small, jnp.zeros((pos_all.shape[0] - seq - n_small, width), F32)])
         pos_all = lax.dynamic_update_slice_in_dim(pos_all, small, seq, 0).reshape(n_tp * n_x, n_core, p_pos, width)
         pos_theirs = swap(lax.dynamic_index_in_dim(pos_all, 1 - c_index, 1, keepdims=False).reshape(-1, width), "cc")
-        rest = grad_rest(core, ctx, d_attn, d_qkvs, hid1, n_tp, spans, plus=rest_theirs, tail=(pos_all, pos_theirs))
+        pos_both = lax.dynamic_index_in_dim(pos_all, c_index, 1, keepdims=False).reshape(-1, width) + pos_theirs
+        pos_both = lax.psum_scatter(pos_both, ("tp", "xx"), scatter_dimension=0, tiled=True)
+        rest = grad_rest(core, ctx, d_attn, d_qkvs, hid1, n_tp, spans, plus=rest_theirs)
         rest = lax.psum_scatter(rest, ("tp", "xx"), scatter_dimension=0, tiled=True)
-        rest_w = every_piece(rest[:spans[1][1]])
-        whole = lax.all_gather(rest[spans[1][1]:], ("tp", "xx", "cc"), axis=0, tiled=True)
+        rest_w = every_piece(rest)
+        whole = lax.all_gather(pos_both, ("tp", "xx", "cc"), axis=0, tiled=True)
         d_pos = jnp.pad(whole[:seq], ((POS_OFFSET, pos_table.shape[0] - seq - POS_OFFSET), (0, 0)))
         small = whole[seq:seq + n_small].reshape(-1)
         n_b = b_qkv.size

time: 1140 us -> 1160 us (1.018)
  waiting for transfers between devices: 425 us -> 458 us
    ppermute x52, waiting for transfers between devices: 386 us -> 442 us  [swap(): return lax.ppermute(v, axis, tp_swap[k] if axis == 'tp' else pair)]
    reduce_scatter x1, waiting for transfers between devices: 38.3 us -> 0.01 us  [local_step(): lax.psum_scatter(ff_grads, ('tp', 'xx'), scatter_dimension=0, tiled=True)]
    reduce_scatter x1, waiting for transfers between devices: 0.01 us -> 15.5 us  [local_step(): rest = lax.psum_scatter(rest, ('tp', 'xx'), scatter_dimension=0, tiled=True)]
  transfers between devices with their start and end apart: 57 -> 58, of which waited for: 17 -> 19; matrix products, arithmetic and copies ran while one was open for 12% -> 11% of each run, Pallas kernels for 24% -> 25%
where the time goes in v7:
time: 1160 us; the launch traced here: 1140 us
  Pallas kernels  467 us (40%)
  waiting for transfers between devices  458 us (39%)
  local copies, waits for them, and re-layouts  93.1 us (8%)
  starting transfers between devices  36.1 us (3%)
  matrix products  33.1 us (3%)
  other arithmetic  21 us (2%)
  between operations  19 us (2%)
    ppermute x52, waiting for transfers between devices, swap(): return lax.ppermute(v, axis, tp_swap[k] if axis == 'tp' else pair)  442 us
    pallas_call x1, Pallas kernels, accum(): pl.pallas_call(functools.partial(accum_kernel, n_block, cap, sub_rows, wi...  64.5 us
    pallas_call x2, Pallas kernels, attn_bwd(): pl.pallas_call(attn_bwd_kernel, grid=(n_pair,), in_specs=[pl.BlockSpec((s...  61.4 us
    pallas_call x4, Pallas kernels, grad_pieces(): pl.pallas_call(functools.partial(grad_kernel, plus is not None), grid_spe...  58.2 us
    pallas_call x1, Pallas kernels, ffn(): pl.pallas_call(functools.partial(ffn_kernel, part), grid=(n_piece,), in_s...  56.5 us
    pallas_call x1, Pallas kernels, attn_fwd(): pl.pallas_call(attn_fwd_kernel, grid=(n_seq, n_pair), in_specs=[pl.BlockS...  41.2 us
    ppermute x52, starting transfers between devices, swap(): return lax.ppermute(v, axis, tp_swap[k] if axis == 'tp' else pair)  35.8 us
    pallas_call x2, Pallas kernels, grad_rest(): pl.pallas_call(functools.partial(grad_rest_kernel, spans, last, len(a2)),...  33.1 us
  transfers between devices with their start and end apart: 58, of which 19 were waited for; matrix products, arithmetic and copies ran while one was open for 11% of the time, Pallas kernels for 25%

profile of v7, /device:TPU:0, one launch (start us, length us, event | category | flops | bytes accessed | tf_op | source)
XLA Modules:
  0.0 1141.2 jit_solution(6875364538014211994)
XLA Ops:
  32.4 20.3 %gather_fusion.3 = bf16[1408,1024]{1,0:T(8,128)(2,1)S(1)} fusion(bf16[12568,1024]{1,0:T(8,128)(2,1)} %param.21, s32[2048]{0:T(1024)S(1)} %pad_clamp_fusion.3), kind=kCustom, calls=%fused_computation.3 | custom fusion | bytes 5772800 | tf_op jit(solution)/shard_map/jit(_take)/gather | solution.py:921
  52.7 19.4 %gather_fusion.4 = bf16[1408,1024]{1,0:T(8,128)(2,1)} fusion(bf16[12568,1024]{1,0:T(8,128)(2,1)} %param.21, s32[2048]{0:T(1024)S(1)} %pad_clamp_fusion.2), kind=kCustom, calls=%fused_computation.4 | custom fusion | bytes 5772800 | tf_op jit(solution)/shard_map/jit(_take)/gather | solution.py:923
  97.3 67.0 %collective-permute-done.37 = bf16[1792]{0:T(1024)(128)(2,1)S(1)} collective-permute-done((bf16[1792]{0:T(1024)(128)(2,1)S(1)}, bf16[1792]{0:T(1024)(128)(2,1)S(1)}, u32[]{:S(2)}, u32[]{:S(2)}) %collective-permute-start.37) | collective-permute-done | bytes 3616 | tf_op jit(solution)/shard_map/ppermute | solution.py:812
  186.2 30.2 %collective-permute-done.39.refs_1_ = bf16[2,256,1024]{2,1,0:T(8,128)(2,1)} collective-permute-done((bf16[2,256,1024]{2,1,0:T(8,128)(2,1)}, bf16[2,256,1024]{2,1,0:T(8,128)(2,1)}, u32[]{:S(2)}, u32[]{:S(2)}) %collective-permute-start.39) | collective-permute-done | bytes 1048608 | tf_op jit(solution)/shard_map/ppermute | solution.py:812
  216.4 22.7 %collective-permute-done.41.refs_3_ = bf16[2,256,1024]{2,1,0:T(8,128)(2,1)} collective-permute-done((bf16[2,256,1024]{2,1,0:T(8,128)(2,1)}, bf16[2,256,1024]{2,1,0:T(8,128)(2,1)}, u32[]{:S(2)}, u32[]{:S(2)}) %collective-permute-start.41) | collective-permute-done | bytes 1048608 | tf_op jit(solution)/shard_map/ppermute | solution.py:812
  251.0 19.4 %add_convert_fusion.1.qkv_ref = bf16[2048,3072]{1,0:T(8,128)(2,1)} fusion(bf16[2048,1024]{1,0:T(8,128)(2,1)} %get-tuple-element.1265.b2_ref, bf16[3072,1024]{1,0:T(8,128)(2,1)} %all-gather.4.cloned.1.call-done.w_ref, f32[3072]{0:T(1024)S(1)} %copy-done.29), kind=kOutput, calls=%fused_computation.280 | convolution fusion | flops 12897484800 | bytes 23080960 | tf_op jit(solution)/shard_map/dot_general | solution.py:20
  270.4 41.2 %attn_fwd.1 = (bf16[2048,1024]{1,0:T(8,128)(2,1)}, f32[2,8,2,1024]{3,2,1,0:T(2,128)}) custom-call(bf16[2048,3072]{1,0:T(8,128)(2,1)} %add_convert_fusion.1.qkv_ref), custom_call_target="tpu_custom_call" | custom-call | flops 21474836480 | bytes 16777216 | tf_op jit(solution)/shard_map/attn_fwd/pallas_call | solution.py:74
  327.3 56.5 %ffn.1 = (bf16[2048,4096]{1,0:T(8,128)(2,1)}, bf16[2048,4096]{1,0:T(8,128)(2,1)}, f32[1,4096]{1,0:T(1,128)}) custom-call(bf16[2048,1024]{1,0:T(8,128)(2,1)} %get-tuple-element.1273.h_ref.b_ref, bf16[2048,1024]{1,0:T(8,128)(2,1)} %bitcast.206, bf16[16,576,1024]{2,1,0:T(8,128)(2,1)} %bitcast.196, bf16[16,576,1024]{2,1,0:T(8,128)(2,1)} %bitcast.197, ...), custom_call_target="tpu_custom_call" | custom-call | flops 34359738368 | bytes 50331648 | tf_op jit(solution)/shard_map/ffn/pallas_call | solution.py:346
  383.8 29.6 %ffn_back.1 = (f32[2048,1024]{1,0:T(8,128)}, bf16[2048,1024]{1,0:T(8,128)(2,1)}, f32[8,1024]{1,0:T(8,128)}) custom-call(bf16[2048,4096]{1,0:T(8,128)(2,1)} %get-tuple-element.1284.dup_ref.a_ref, bf16[16,576,1024]{2,1,0:T(8,128)(2,1)} %bitcast.198, f32[2048,1024]{1,0:T(8,128)} %get-tuple-element.1279.x1_ref, bf16[2048,1024]{1,0:T(8,128)(2,1)} %bitcast.207, ...), custom_call_target="tpu_custom_call" | custom-call | flops 17179869184 | bytes 41943040 | tf_op jit(solution)/shard_map/ffn_back/pallas_call | solution.py:416
  422.8 30.9 %attn_bwd.3.dq_ref.refs_1_ = bf16[1024,3072]{1,0:T(8,128)(2,1)} custom-call(bf16[2048,3072]{1,0:T(8,128)(2,1)} %add_convert_fusion.1.qkv_ref, bf16[2048,1024]{1,0:T(8,128)(2,1)} %get-tuple-element.1268.c_ref.ctx_ref.a1_ref, bf16[2048,1024]{1,0:T(8,128)(2,1)} %convolution_convert_fusion.3.dctx_ref, f32[2,8,2,1024]{3,2,1,0:T(2,128)} %get-tuple-element.1286.lse_ref), custom_call_target="tpu_custom_call" | custom-call | flops 26843545600 | bytes 16777216 | tf_op jit(solution)/shard_map/attn_bwd/pallas_call | solution.py:140
  453.7 30.5 %attn_bwd.2.dq_ref.refs_0_ = bf16[1024,3072]{1,0:T(8,128)(2,1)} custom-call(bf16[2048,3072]{1,0:T(8,128)(2,1)} %add_convert_fusion.1.qkv_ref, bf16[2048,1024]{1,0:T(8,128)(2,1)} %get-tuple-element.1268.c_ref.ctx_ref.a1_ref, bf16[2048,1024]{1,0:T(8,128)(2,1)} %convolution_convert_fusion.3.dctx_ref, f32[2,8,2,1024]{3,2,1,0:T(2,128)} %get-tuple-element.1286.lse_ref), custom_call_target="tpu_custom_call" | custom-call | flops 26843545600 | bytes 16777216 | tf_op jit(solution)/shard_map/attn_bwd/pallas_call | solution.py:140
  617.5 17.7 %weight_grads.3 = f32[2112,1024]{1,0:T(8,128)} custom-call(s32[1]{0:T(128)} %bitcast.54.core_ref, bf16[2048,1024]{1,0:T(8,128)(2,1)} %get-tuple-element.1268.c_ref.ctx_ref.a1_ref, bf16[2048,1024]{1,0:T(8,128)(2,1)} %get-tuple-element.1285.b1_ref, bf16[2048,1024]{1,0:T(8,128)(2,1)} %get-tuple-element.1265.b2_ref, bf16[1024,3072]{1,0:T(8,128)(2,1)} %attn_bwd.2.dq_ref.refs_0_, ...), custom_call_target="tpu_custom_call" | custom-call | flops 8589934592 | bytes 25165824 | tf_op jit(solution)/shard_map/weight_grads/pallas_call | solution.py:738
  657.8 25.7 %collective-permute-done.60.refs_17_ = bf16[384,1024]{1,0:T(8,128)(2,1)} collective-permute-done((bf16[384,1024]{1,0:T(8,128)(2,1)}, bf16[384,1024]{1,0:T(8,128)(2,1)}, u32[]{:S(2)}, u32[]{:S(2)}) %collective-permute-start.60) | collective-permute-done | bytes 786464 | tf_op jit(solution)/shard_map/ppermute | solution.py:812
  684.5 22.7 %collective-permute-done.62.refs_19_ = bf16[384,1024]{1,0:T(8,128)(2,1)} collective-permute-done((bf16[384,1024]{1,0:T(8,128)(2,1)}, bf16[384,1024]{1,0:T(8,128)(2,1)}, u32[]{:S(2)}, u32[]{:S(2)}) %collective-permute-start.62) | collective-permute-done | bytes 786464 | tf_op jit(solution)/shard_map/ppermute | solution.py:812
  707.5 25.9 %down.1 = (bf16[2,256,1024]{2,1,0:T(8,128)(2,1)}, bf16[2,256,1024]{2,1,0:T(8,128)(2,1)}, bf16[2,256,1024]{2,1,0:T(8,128)(2,1)}, bf16[2,256,1024]{2,1,0:T(8,128)(2,1)}) custom-call(s32[1]{0:T(128)} %bitcast.10.me_ref, bf16[2048,4096]{1,0:T(8,128)(2,1)} %get-tuple-element.1278.act_ref.a_ref, bf16[16,576,1024]{2,1,0:T(8,128)(2,1)} %bitcast.199, ...), custom_call_target="tpu_custom_call" | custom-call | flops 17179869184 | bytes 29360128 | tf_op jit(solution)/shard_map/down/pallas_call | solution.py:373
  738.3 23.9 %collective-permute-done.47.refs_3_ = bf16[384,1024]{1,0:T(8,128)(2,1)} collective-permute-done((bf16[384,1024]{1,0:T(8,128)(2,1)}, bf16[384,1024]{1,0:T(8,128)(2,1)}, u32[]{:S(2)}, u32[]{:S(2)}) %collective-permute-start.47) | collective-permute-done | bytes 786464 | tf_op jit(solution)/shard_map/ppermute | solution.py:812
  765.6 27.9 %collective-permute-done.42.refs_1_ = bf16[2,256,1024]{2,1,0:T(8,128)(2,1)S(1)} collective-permute-done((bf16[2,256,1024]{2,1,0:T(8,128)(2,1)}, bf16[2,256,1024]{2,1,0:T(8,128)(2,1)S(1)}, u32[]{:S(2)}, u32[]{:S(2)}) %collective-permute-start.42) | collective-permute-done | bytes 1048608 | tf_op jit(solution)/shard_map/ppermute | solution.py:812
  795.0 37.0 %collective-permute-done.44.refs_3_ = bf16[2,256,1024]{2,1,0:T(8,128)(2,1)} collective-permute-done((bf16[2,256,1024]{2,1,0:T(8,128)(2,1)}, bf16[2,256,1024]{2,1,0:T(8,128)(2,1)}, u32[]{:S(2)}, u32[]{:S(2)}) %collective-permute-start.44) | collective-permute-done | bytes 1048608 | tf_op jit(solution)/shard_map/ppermute | solution.py:812
  837.7 23.7 %collective-permute-done.66.refs_23_ = bf16[384,1024]{1,0:T(8,128)(2,1)S(1)} collective-permute-done((bf16[384,1024]{1,0:T(8,128)(2,1)}, bf16[384,1024]{1,0:T(8,128)(2,1)S(1)}, u32[]{:S(2)}, u32[]{:S(2)}) %collective-permute-start.66) | collective-permute-done | bytes 786464 | tf_op jit(solution)/shard_map/ppermute | solution.py:812
  865.6 29.6 %collective-permute-done.49.refs_5_ = bf16[384,1024]{1,0:T(8,128)(2,1)} collective-permute-done((bf16[384,1024]{1,0:T(8,128)(2,1)}, bf16[384,1024]{1,0:T(8,128)(2,1)}, u32[]{:S(2)}, u32[]{:S(2)}) %collective-permute-start.49) | collective-permute-done | bytes 786464 | tf_op jit(solution)/shard_map/ppermute | solution.py:812
  900.8 20.9 %collective-permute-done.50.refs_6_ = bf16[384,1024]{1,0:T(8,128)(2,1)} collective-permute-done((bf16[384,1024]{1,0:T(8,128)(2,1)}, bf16[384,1024]{1,0:T(8,128)(2,1)}, u32[]{:S(2)}, u32[]{:S(2)}) %collective-permute-start.50) | collective-permute-done | bytes 786464 | tf_op jit(solution)/shard_map/ppermute | solution.py:812
  922.2 27.4 %collective-permute-done.51.refs_7_ = bf16[384,1024]{1,0:T(8,128)(2,1)} collective-permute-done((bf16[384,1024]{1,0:T(8,128)(2,1)}, bf16[384,1024]{1,0:T(8,128)(2,1)}, u32[]{:S(2)}, u32[]{:S(2)}) %collective-permute-start.51) | collective-permute-done | bytes 786464 | tf_op jit(solution)/shard_map/ppermute | solution.py:812
  981.5 59.6 %collective-permute-done.77.refs_1_ = f32[264,1024]{1,0:T(8,128)} collective-permute-done((f32[264,1024]{1,0:T(8,128)}, f32[264,1024]{1,0:T(8,128)}, u32[]{:S(2)}, u32[]{:S(2)}) %collective-permute-start.77) | collective-permute-done | bytes 1081376 | tf_op jit(solution)/shard_map/ppermute | solution.py:812
  1041.7 64.5 %table_accum.1 = f32[100544,128]{1,0:T(8,128)} custom-call(s32[12288]{0:T(1024)} %fusion.143.where_ref, s32[160]{0:T(256)} %min.12.first_ref, bf16[384,1024]{1,0:T(8,128)(2,1)} %get-tuple-element.1289.refs_0_, bf16[384,1024]{1,0:T(8,128)(2,1)} %collective-permute-done.45.refs_1_, bf16[384,1024]{1,0:T(8,128)(2,1)} %collective-permute-done.46.refs_2_, ...), custom_call_target="tpu_custom_call" | custom-call | flops 49999998976 | bytes 100000000 | tf_op jit(solution)/shard_map/table_accum/pallas_call | solution.py:637
  (435 shorter events, 347.7 us)
Async XLA Ops:
  7.2 243.8 %all-gather.4.cloned.1.call-start = ((), (), s32[]{:S(2)}) async-start(), calls=%async_computation.3 | async-start | bytes 7077888 | tf_op jit(solution)/shard_map/all_gather | solution.py:809
  9.4 302.2 %all-gather.6.cloned.1.call-start = ((), (), s32[]{:S(2)}) async-start(), calls=%async_computation.4 | async-start | bytes 20054016 | tf_op jit(solution)/shard_map/all_gather | solution.py:832
  26.3 736.1 %reduce-scatter.4.cloned.1.call-start = ((), (), s32[]{:S(2)}) async-start(), calls=%async_computation.5 | async-start | bytes 2654208 | tf_op jit(solution)/shard_map/reduce_scatter | solution.py:1027
  75.8 93.7 %collective-permute-start.34 = (bf16[704,1024]{1,0:T(8,128)(2,1)}, bf16[704,1024]{1,0:T(8,128)(2,1)}, u32[]{:S(2)}, u32[]{:S(2)}) collective-permute-start(bf16[704,1024]{1,0:T(8,128)(2,1)} %get-tuple-element.1586), channel_id=1, source_target_pairs={{0,8},{4,12},{8,0},{12,4},{1,9},{5,13},{9,1},{13,5},{2,10},{6,14},... | collective-permute-start | bytes 4325384 | tf_op jit(solution)/shard_map/ppermute | solution.py:812
  78.1 91.4 %collective-permute-start.35 = (bf16[704,1024]{1,0:T(8,128)(2,1)}, bf16[704,1024]{1,0:T(8,128)(2,1)}, u32[]{:S(2)}, u32[]{:S(2)}) collective-permute-start(bf16[704,1024]{1,0:T(8,128)(2,1)} %get-tuple-element.1584), channel_id=1, source_target_pairs={{0,12},{4,8},{8,4},{12,0},{1,13},{5,9},{9,5},{13,1},{2,14},{6,10},... | collective-permute-start | bytes 4325384 | tf_op jit(solution)/shard_map/ppermute | solution.py:812
  79.5 89.9 %collective-permute-start.33 = (bf16[704,1024]{1,0:T(8,128)(2,1)}, bf16[704,1024]{1,0:T(8,128)(2,1)}, u32[]{:S(2)}, u32[]{:S(2)}) collective-permute-start(bf16[704,1024]{1,0:T(8,128)(2,1)} %get-tuple-element.1585), channel_id=1, source_target_pairs={{0,4},{4,0},{8,12},{12,8},{1,5},{5,1},{9,13},{13,9},{2,6},{6,2},{1... | collective-permute-start | bytes 4325384 | tf_op jit(solution)/shard_map/ppermute | solution.py:812
  84.8 79.6 %collective-permute-start.37 = (bf16[1792]{0:T(1024)(128)(2,1)S(1)}, bf16[1792]{0:T(1024)(128)(2,1)S(1)}, u32[]{:S(2)}, u32[]{:S(2)}) collective-permute-start(bf16[1792]{0:T(1024)(128)(2,1)S(1)} %dynamic-update-slice.33), channel_id=1, source_target_pairs={{0,8},{4,12},{8,0},{12,4},{1,9},{5,13},{9,1},{13,5},{2,10},{6,14},... | collective-permute-start | bytes 10760 | tf_op jit(solution)/shard_map/ppermute | solution.py:812
  85.2 82.9 %collective-permute-start.36 = (bf16[1792]{0:T(1024)(128)(2,1)S(1)}, bf16[1792]{0:T(1024)(128)(2,1)S(1)}, u32[]{:S(2)}, u32[]{:S(2)}) collective-permute-start(bf16[1792]{0:T(1024)(128)(2,1)S(1)} %dynamic-update-slice.33), channel_id=1, source_target_pairs={{0,4},{4,0},{8,12},{12,8},{1,5},{5,1},{9,13},{13,9},{2,6},{6,2},{1... | collective-permute-start | bytes 10760 | tf_op jit(solution)/shard_map/ppermute | solution.py:812
  171.0 68.0 %collective-permute-start.41 = (bf16[2,256,1024]{2,1,0:T(8,128)(2,1)}, bf16[2,256,1024]{2,1,0:T(8,128)(2,1)}, u32[]{:S(2)}, u32[]{:S(2)}) collective-permute-start(bf16[2,256,1024]{2,1,0:T(8,128)(2,1)} %get-tuple-element.1277), channel_id=1, source_target_pairs={{0,12},{4,8},{8,4},{12,0},{1,13},{5,9},{9,5},{13,1},{2,14},{6,10},... | collective-permute-start | bytes 3145736 | tf_op jit(solution)/shard_map/ppermute | solution.py:812
  557.2 337.9 %reduce-scatter.8.cloned.1.call-start = ((), (), s32[]{:S(2)}) async-start(), calls=%async_computation.8 | async-start | bytes 19464192 | tf_op jit(solution)/shard_map/reduce_scatter | solution.py:980
  588.2 379.9 %reduce-scatter.6.cloned.1.call-start = ((), (), s32[]{:S(2)}) async-start(), calls=%async_computation.7 | async-start | bytes 9732096 | tf_op jit(solution)/shard_map/reduce_scatter | solution.py:1029
  635.2 471.1 %all-gather.8.cloned.1.call-start = ((), (), s32[]{:S(2)}) async-start(), calls=%async_computation.6 | async-start | bytes 5013504 | tf_op jit(solution)/shard_map/all_gather | solution.py:1031
  649.4 84.0 %collective-permute-start.67 = (bf16[384,1024]{1,0:T(8,128)(2,1)}, bf16[384,1024]{1,0:T(8,128)(2,1)}, u32[]{:S(2)}, u32[]{:S(2)}) collective-permute-start(bf16[384,1024]{1,0:T(8,128)(2,1)} %get-tuple-element.1297.refs_16_), channel_id=1, source_target_pairs={{0,1},{1,0},{2,3},{3,2},{4,5},{5,4},{6,7},{7,6},{8,9},{9,8},{10,11... | collective-permute-start | bytes 2359304 | tf_op jit(solution)/shard_map/ppermute | solution.py:812
  656.3 79.1 %collective-permute-start.63 = (bf16[384,1024]{1,0:T(8,128)(2,1)}, bf16[384,1024]{1,0:T(8,128)(2,1)}, u32[]{:S(2)}, u32[]{:S(2)}) collective-permute-start(bf16[384,1024]{1,0:T(8,128)(2,1)} %get-tuple-element.1297.refs_16_), channel_id=1, source_target_pairs={{0,2},{2,0},{1,3},{3,1},{4,6},{6,4},{5,7},{7,5},{8,10},{10,8},{9,1... | collective-permute-start | bytes 2359304 | tf_op jit(solution)/shard_map/ppermute | solution.py:812
  762.2 69.7 %collective-permute-start.44 = (bf16[2,256,1024]{2,1,0:T(8,128)(2,1)}, bf16[2,256,1024]{2,1,0:T(8,128)(2,1)}, u32[]{:S(2)}, u32[]{:S(2)}) collective-permute-start(bf16[2,256,1024]{2,1,0:T(8,128)(2,1)} %get-tuple-element.1283), channel_id=1, source_target_pairs={{0,12},{4,8},{8,4},{12,0},{1,13},{5,9},{9,5},{13,1},{2,14},{6,10},... | collective-permute-start | bytes 3145736 | tf_op jit(solution)/shard_map/ppermute | solution.py:812
  762.5 69.5 %collective-permute-start.68 = (bf16[384,1024]{1,0:T(8,128)(2,1)}, bf16[384,1024]{1,0:T(8,128)(2,1)}, u32[]{:S(2)}, u32[]{:S(2)}) collective-permute-start(bf16[384,1024]{1,0:T(8,128)(2,1)} %collective-permute-done.60.refs_17_), channel_id=1, source_target_pairs={{0,1},{1,0},{2,3},{3,2},{4,5},{5,4},{6,7},{7,6},{8,9},{9,8},{10,11... | collective-permute-start | bytes 2359304 | tf_op jit(solution)/shard_map/ppermute | solution.py:812
  764.1 69.3 %collective-permute-start.64 = (bf16[384,1024]{1,0:T(8,128)(2,1)}, bf16[384,1024]{1,0:T(8,128)(2,1)}, u32[]{:S(2)}, u32[]{:S(2)}) collective-permute-start(bf16[384,1024]{1,0:T(8,128)(2,1)} %collective-permute-done.60.refs_17_), channel_id=1, source_target_pairs={{0,2},{2,0},{1,3},{3,1},{4,6},{6,4},{5,7},{7,5},{8,10},{10,8},{9,1... | collective-permute-start | bytes 2359304 | tf_op jit(solution)/shard_map/ppermute | solution.py:812
  863.9 85.7 %collective-permute-start.51 = (bf16[384,1024]{1,0:T(8,128)(2,1)}, bf16[384,1024]{1,0:T(8,128)(2,1)}, u32[]{:S(2)}, u32[]{:S(2)}) collective-permute-start(bf16[384,1024]{1,0:T(8,128)(2,1)} %collective-permute-done.47.refs_3_), channel_id=1, source_target_pairs={{0,2},{2,0},{1,3},{3,1},{4,6},{6,4},{5,7},{7,5},{8,10},{10,8},{9,1... | collective-permute-start | bytes 2359304 | tf_op jit(solution)/shard_map/ppermute | solution.py:812
  895.2 146.5 %collective-permute-start.82 = (f32[528,1024]{1,0:T(8,128)}, f32[528,1024]{1,0:T(8,128)}, u32[]{:S(2)}, u32[]{:S(2)}) collective-permute-start(f32[528,1024]{1,0:T(8,128)} %reduce-scatter.8.cloned.1.call-done.refs_0_), channel_id=1, source_target_pairs={{0,2},{2,0},{1,3},{3,1},{4,6},{6,4},{5,7},{7,5},{8,10},{10,8},{9,1... | collective-permute-start | bytes 6488072 | tf_op jit(solution)/shard_map/ppermute | solution.py:812
  968.1 73.1 %collective-permute-start.77 = (f32[264,1024]{1,0:T(8,128)}, f32[264,1024]{1,0:T(8,128)}, u32[]{:S(2)}, u32[]{:S(2)}) collective-permute-start(f32[264,1024]{1,0:T(8,128)} %reduce-scatter.6.cloned.1.call-done.refs_0_), channel_id=1, source_target_pairs={{0,2},{2,0},{1,3},{3,1},{4,6},{6,4},{5,7},{7,5},{8,10},{10,8},{9,1... | collective-permute-start | bytes 3244040 | tf_op jit(solution)/shard_map/ppermute | solution.py:812
  981.1 134.1 %collective-permute-start.78 = (f32[264,1024]{1,0:T(8,128)}, f32[264,1024]{1,0:T(8,128)}, u32[]{:S(2)}, u32[]{:S(2)}) collective-permute-start(f32[264,1024]{1,0:T(8,128)} %reduce-scatter.6.cloned.1.call-done.refs_0_), channel_id=1, source_target_pairs={{0,1},{1,0},{2,3},{3,2},{4,5},{5,4},{6,7},{7,6},{8,9},{9,8},{10,11... | collective-permute-start | bytes 3244040 | tf_op jit(solution)/shard_map/ppermute | solution.py:812
  1041.1 74.0 %collective-permute-start.79 = (f32[264,1024]{1,0:T(8,128)}, f32[264,1024]{1,0:T(8,128)}, u32[]{:S(2)}, u32[]{:S(2)}) collective-permute-start(f32[264,1024]{1,0:T(8,128)} %collective-permute-done.77.refs_1_), channel_id=1, source_target_pairs={{0,1},{1,0},{2,3},{3,2},{4,5},{5,4},{6,7},{7,6},{8,9},{9,8},{10,11... | collective-permute-start | bytes 3244040 | tf_op jit(solution)/shard_map/ppermute | solution.py:812
  1041.2 83.4 %collective-permute-start.83 = (f32[528,1024]{1,0:T(8,128)}, f32[528,1024]{1,0:T(8,128)}, u32[]{:S(2)}, u32[]{:S(2)}) collective-permute-start(f32[528,1024]{1,0:T(8,128)} %reduce-scatter.8.cloned.1.call-done.refs_0_), channel_id=1, source_target_pairs={{0,1},{1,0},{2,3},{3,2},{4,5},{5,4},{6,7},{7,6},{8,9},{9,8},{10,11... | collective-permute-start | bytes 6488072 | tf_op jit(solution)/shard_map/ppermute | solution.py:812
  1041.7 82.9 %collective-permute-start.84 = (f32[528,1024]{1,0:T(8,128)}, f32[528,1024]{1,0:T(8,128)}, u32[]{:S(2)}, u32[]{:S(2)}) collective-permute-start(f32[528,1024]{1,0:T(8,128)} %collective-permute-done.82.refs_1_), channel_id=1, source_target_pairs={{0,1},{1,0},{2,3},{3,2},{4,5},{5,4},{6,7},{7,6},{8,9},{9,8},{10,11... | collective-permute-start | bytes 6488072 | tf_op jit(solution)/shard_map/ppermute | solution.py:812
  (82 other events, 3487.1 us)
Sparse Core Ops, SparseCore 0:
  9.8 44.5 all-gather.3
  56.6 159.4 all-gather.5
  557.4 40.8 reduce-scatter.3
  603.1 229.5 reduce-scatter.7
  836.8 131.1 reduce-scatter.5
  970.1 51.8 all-gather.7

commit v8 on v7

--- a/solution.py
+++ b/solution.py
@@ -385,7 +385,7 @@
     )(me, act, w, x1, b)
 
 
-def back2_kernel(dup_ref, w_ref, x1_ref, og_ref, gain_ref, dr_ref, da_ref, sums_ref):
+def back2_kernel(dup_ref, w_ref, wout_ref, x1_ref, og_ref, gain_ref, dr_ref, da_ref, dc_ref, sums_ref):
     @pl.when(pl.program_id(0) == 0)
     def _():
         sums_ref[...] = jnp.zeros(sums_ref.shape, F32)
@@ -401,29 +401,34 @@
         og = og_ref[at, :].astype(F32)
         d_resid = og + d_x
         dr_ref[at, :] = d_resid
-        da_ref[at, :] = d_resid.astype(BF16)
+        d_attn = d_resid.astype(BF16)
+        da_ref[at, :] = d_attn
+        dc_ref[at, :] = dot_nt(d_attn, wout_ref[...].reshape(-1, d_attn.shape[1])).astype(BF16)
         sums_ref[0:1, :] += col_sum(d_gain)
         sums_ref[1:2, :] += col_sum(d_y)
         sums_ref[2:3, :] += col_sum(d_resid)
         sums_ref[3:4, :] += col_sum(og)
 
 
-def back2(d_up, w, x1, og, gain):
+def back2(d_up, w, start, x1, og, gain):
     n_tok, width = x1.shape
     ff = d_up.shape[1]
     rows = 256
+    n_out = (w.shape[1] - start)
     mat = pl.BlockSpec((rows, width), lambda i: (i, 0))
     return pl.pallas_call(
         back2_kernel,
         grid=(n_tok // rows,),
         in_specs=[pl.BlockSpec((rows, ff), lambda i: (i, 0)), pl.BlockSpec((w.shape[0], ff // w.shape[0], width), lambda i: (0, 0, 0), pipeline_mode=pl.Buffered(1)),
+                  pl.BlockSpec((w.shape[0], n_out, width), lambda i: (0, start // n_out, 0), pipeline_mode=pl.Buffered(1)),
                   mat, mat, pl.BlockSpec((1, width), lambda i: (0, 0))],
-        out_specs=[mat, mat, pl.BlockSpec((8, width), lambda i: (0, 0))],
-        out_shape=[jax.ShapeDtypeStruct((n_tok, width), F32), jax.ShapeDtypeStruct((n_tok, width), BF16), jax.ShapeDtypeStruct((8, width), F32)],
+        out_specs=[mat, mat, pl.BlockSpec((rows, w.shape[0] * n_out), lambda i: (i, 0)), pl.BlockSpec((8, width), lambda i: (0, 0))],
+        out_shape=[jax.ShapeDtypeStruct((n_tok, width), F32), jax.ShapeDtypeStruct((n_tok, width), BF16),
+                   jax.ShapeDtypeStruct((n_tok, w.shape[0] * n_out), BF16), jax.ShapeDtypeStruct((8, width), F32)],
         name="ffn_back",
         cost_estimate=pl.CostEstimate(flops=2 * n_tok * ff * width, bytes_accessed=2 * n_tok * ff + n_tok * width * 12, transcendentals=0),
         compiler_params=pltpu.CompilerParams(vmem_limit_bytes=63 * 1024 * 1024),
-    )(d_up, w, x1, og, gain)
+    )(d_up, w, w, x1, og, gain)
 
 
 def back1_kernel(dq_ref, w_ref, x_ref, dr_ref, gain_ref, *refs):
@@ -831,7 +836,6 @@
         own_w = jnp.concatenate([quarter(w_up, 1).T, quarter(w_down, 0), quarter(w_out.reshape(-1, width), 0)])
         w_all = lax.all_gather(own_w, ("tp", "xx", "cc"), axis=0, tiled=True)
         w_all = w_all.reshape(n_tp * n_dp, 2 * n_ff + n_out, width)
-        wout_w = w_all[:, 2 * n_ff:].reshape(-1, width)
         n_pair = wqkv_t.shape[0] // (3 * 128)
         own_bias = jnp.concatenate([b_qkv.reshape(3, n_core, -1, b_qkv.shape[2]).transpose(1, 0, 2, 3).reshape(-1), b_up])
         biases = jnp.stack(by_owner([swap(own_bias, "tp", k) if k else own_bias for k in range(n_tp)]))
@@ -937,7 +941,6 @@
         code0 = (place0 // 8) * (8 * tiles) + place0 % 8
         og_parts = out_grad.reshape(n_tp, n_seq, seq_local, width)
         og_parts = [lax.dynamic_index_in_dim(og_parts, tp_index ^ k, 0, keepdims=False) for k in range(n_tp)]
-        got0, og_parts = lax.optimization_barrier((got0, og_parts))
         resid_x, hid1 = embed(code0, got0, pos_rows, gain1, bias1, n_tok)
 
         def more_rows(carry):
@@ -975,16 +978,16 @@
         p_ff = piece_of(n_tp * ff)
         down_theirs = swap(grad_pieces(1 - core, act, og, n_tp, p_ff, 0, 1), "cc")
         up_theirs = swap(grad_pieces(1 - core, d_up, hid2, n_tp, p_ff, 0, 1), "cc")
-        ff_grads = grad_pieces(core, act, og, n_tp, p_ff, 0, 2, plus=down_theirs)
-        ff_grads = grad_pieces(core, d_up, hid2, n_tp, p_ff, 1, 2, plus=up_theirs, into=ff_grads)
-        ff_grads = lax.psum_scatter(ff_grads, ("tp", "xx"), scatter_dimension=0, tiled=True)
-        ff_grads = every_piece(ff_grads)
-
-        d_resid1, d_attn, sums2 = back2(d_up, w_all, resid_x1, og, gain2)
-        d_ctx = dot_nt(d_attn, wout_w).astype(BF16)
+        d_down = grad_pieces(core, act, og, n_tp, p_ff, 0, 1, plus=down_theirs)
+        d_down = lax.psum_scatter(d_down, ("tp", "xx"), scatter_dimension=0, tiled=True)
+        d_upw = grad_pieces(core, d_up, hid2, n_tp, p_ff, 0, 1, plus=up_theirs)
+        d_upw = lax.psum_scatter(d_upw, ("tp", "xx"), scatter_dimension=0, tiled=True)
+        d_down, d_upw = every_piece(d_down), every_piece(d_upw)
+
+        d_resid1, d_attn, d_ctx, sums2 = back2(d_up, w_all, 2 * n_ff, resid_x1, og, gain2)
         n_small = n_tp * (b_qkv.size + ff) // width + 6
         p_pos = -(-(seq + n_small) // (24 * n_tp * n_dp)) * 24
-        p_out = piece_of(wout_w.shape[0])
+        p_out = piece_of(ctx.shape[1])
         spans = ((0, p_out), (p_out, p_out + piece_of(wqkv_t.shape[0])))
 
         def token_blocks(places, d_tok):
@@ -1004,7 +1007,8 @@
         d_qkvs = [d_qkv0, d_qkv1]
         rest_theirs = swap(grad_rest(1 - core, ctx, d_attn, d_qkvs, hid1, n_tp, spans), "cc")
 
-        d_w_down, d_w_up = pieces_out(x_and_core, ff_grads, ((0, n_ff, False), (p_ff, n_ff, True)))
+        (d_w_down,) = pieces_out(x_and_core, d_down, ((0, n_ff, False),))
+        (d_w_up,) = pieces_out(x_and_core, d_upw, ((0, n_ff, True),))
         image = accum(blocks0 + blocks1, code, block_first, sub_rows, width)
         d_emb = image.reshape(rows // 8, tiles, 8, 128).transpose(0, 2, 1, 3).reshape(rows, width)
 

time: 1160 us -> 1120 us (0.966)
  waiting for transfers between devices: 458 us -> 425 us
  Pallas kernels: 467 us -> 479 us
    ppermute x52 -> x55, waiting for transfers between devices: 442 us -> 423 us  [swap(): return lax.ppermute(v, axis, tp_swap[k] if axis == 'tp' else pair)]
    reduce_scatter x1, waiting for transfers between devices: 15.5 us -> 0.01 us  [local_step(): rest = lax.psum_scatter(rest, ('tp', 'xx'), scatter_dimension=0, tiled=True)]
    dot_general x2 -> x1, matrix products: 28.7 us -> 19.4 us  [dot_nt(): lax.dot_general(a, b, (((1,), (1,)), ((), ())), preferred_element_type=F32)]
    ppermute x52 -> x55, starting transfers between devices: 35.8 us -> 37 us  [swap(): return lax.ppermute(v, axis, tp_swap[k] if axis == 'tp' else pair)]
  transfers between devices with their start and end apart: 58 -> 62, of which waited for: 19 -> 19; matrix products, arithmetic and copies ran while one was open for 11% -> 11% of each run, Pallas kernels for 25% -> 26%
where the time goes in v8:
time: 1120 us; the launch traced here: 1110 us
  Pallas kernels  479 us (43%)
  waiting for transfers between devices  425 us (38%)
  local copies, waits for them, and re-layouts  89.1 us (8%)
  starting transfers between devices  37.3 us (3%)
  matrix products  23.8 us (2%)
  other arithmetic  20.6 us (2%)
  between operations  19 us (2%)
    ppermute x55, waiting for transfers between devices, swap(): return lax.ppermute(v, axis, tp_swap[k] if axis == 'tp' else pair)  423 us
    pallas_call x1, Pallas kernels, accum(): pl.pallas_call(functools.partial(accum_kernel, n_block, cap, sub_rows, wi...  64.5 us
    pallas_call x2, Pallas kernels, attn_bwd(): pl.pallas_call(attn_bwd_kernel, grid=(n_pair,), in_specs=[pl.BlockSpec((s...  61.6 us
    pallas_call x4, Pallas kernels, grad_pieces(): pl.pallas_call(functools.partial(grad_kernel, plus is not None), grid_spe...  58.7 us
    pallas_call x1, Pallas kernels, ffn(): pl.pallas_call(functools.partial(ffn_kernel, part), grid=(n_piece,), in_s...  56.4 us
    pallas_call x1, Pallas kernels, attn_fwd(): pl.pallas_call(attn_fwd_kernel, grid=(n_seq, n_pair), in_specs=[pl.BlockS...  41.2 us
    pallas_call x1, Pallas kernels, back2(): pl.pallas_call(back2_kernel, grid=(n_tok // rows,), in_specs=[pl.BlockSpe...  38.4 us
    ppermute x55, starting transfers between devices, swap(): return lax.ppermute(v, axis, tp_swap[k] if axis == 'tp' else pair)  37 us
  transfers between devices with their start and end apart: 62, of which 19 were waited for; matrix products, arithmetic and copies ran while one was open for 11% of the time, Pallas kernels for 26%

profile of v8, /device:TPU:0, one launch (start us, length us, event | category | flops | bytes accessed | tf_op | source)
XLA Modules:
  0.0 1108.1 jit_solution(4294556808784042321)
XLA Ops:
  41.1 18.9 %gather_fusion.3 = bf16[1408,1024]{1,0:T(8,128)(2,1)S(1)} fusion(bf16[12568,1024]{1,0:T(8,128)(2,1)} %param.21, s32[2048]{0:T(1024)S(1)} %pad_clamp_fusion.3), kind=kCustom, calls=%fused_computation.3 | custom fusion | bytes 5772800 | tf_op jit(solution)/shard_map/jit(_take)/gather | solution.py:925
  60.1 19.6 %gather_fusion.4 = bf16[1408,1024]{1,0:T(8,128)(2,1)} fusion(bf16[12568,1024]{1,0:T(8,128)(2,1)} %param.21, s32[2048]{0:T(1024)S(1)} %pad_clamp_fusion.2), kind=kCustom, calls=%fused_computation.4 | custom fusion | bytes 5772800 | tf_op jit(solution)/shard_map/jit(_take)/gather | solution.py:927
  100.3 113.6 %collective-permute-done.40.refs_2_ = bf16[2,256,1024]{2,1,0:T(8,128)(2,1)} collective-permute-done((bf16[2,256,1024]{2,1,0:T(8,128)(2,1)}, bf16[2,256,1024]{2,1,0:T(8,128)(2,1)}, u32[]{:S(2)}, u32[]{:S(2)}) %collective-permute-start.40) | collective-permute-done | bytes 1048608 | tf_op jit(solution)/shard_map/ppermute | solution.py:817
  240.5 19.4 %add_convert_fusion.1.qkv_ref = bf16[2048,3072]{1,0:T(8,128)(2,1)} fusion(bf16[2048,1024]{1,0:T(8,128)(2,1)} %get-tuple-element.1252.b2_ref, bf16[3072,1024]{1,0:T(8,128)(2,1)} %all-gather.4.cloned.1.call-done.w_ref, f32[3072]{0:T(1024)S(1)} %copy-done.28), kind=kOutput, calls=%fused_computation.280 | convolution fusion | flops 12897484800 | bytes 23080960 | tf_op jit(solution)/shard_map/dot_general | solution.py:20
  260.0 41.2 %attn_fwd.1 = (bf16[2048,1024]{1,0:T(8,128)(2,1)}, f32[2,8,2,1024]{3,2,1,0:T(2,128)}) custom-call(bf16[2048,3072]{1,0:T(8,128)(2,1)} %add_convert_fusion.1.qkv_ref), custom_call_target="tpu_custom_call" | custom-call | flops 21474836480 | bytes 16777216 | tf_op jit(solution)/shard_map/attn_fwd/pallas_call | solution.py:74
  313.7 56.4 %ffn.1 = (bf16[2048,4096]{1,0:T(8,128)(2,1)}, bf16[2048,4096]{1,0:T(8,128)(2,1)}, f32[1,4096]{1,0:T(1,128)}) custom-call(bf16[2048,1024]{1,0:T(8,128)(2,1)} %get-tuple-element.1260.h_ref.b_ref, bf16[2048,1024]{1,0:T(8,128)(2,1)} %bitcast.199, bf16[16,576,1024]{2,1,0:T(8,128)(2,1)} %bitcast.192, bf16[16,576,1024]{2,1,0:T(8,128)(2,1)} %bitcast.193, ...), custom_call_target="tpu_custom_call" | custom-call | flops 34359738368 | bytes 50331648 | tf_op jit(solution)/shard_map/ffn/pallas_call | solution.py:346
  370.1 38.4 %ffn_back.1 = (f32[2048,1024]{1,0:T(8,128)}, bf16[2048,1024]{1,0:T(8,128)(2,1)}, bf16[2048,1024]{1,0:T(8,128)(2,1)}, f32[8,1024]{1,0:T(8,128)}) custom-call(bf16[2048,4096]{1,0:T(8,128)(2,1)} %get-tuple-element.1267.dup_ref.a_ref, bf16[16,576,1024]{2,1,0:T(8,128)(2,1)} %bitcast.194, bf16[16,576,1024]{2,1,0:T(8,128)(2,1)} %bitcast.195, ...), custom_call_target="tpu_custom_call" | custom-call | flops 17179869184 | bytes 41943040 | tf_op jit(solution)/shard_map/ffn_back/pallas_call | solution.py:419
  408.5 30.6 %attn_bwd.3.dq_ref.refs_1_ = bf16[1024,3072]{1,0:T(8,128)(2,1)} custom-call(bf16[2048,3072]{1,0:T(8,128)(2,1)} %add_convert_fusion.1.qkv_ref, bf16[2048,1024]{1,0:T(8,128)(2,1)} %get-tuple-element.1255.c_ref.ctx_ref.a1_ref, bf16[2048,1024]{1,0:T(8,128)(2,1)} %get-tuple-element.1268.dctx_ref, f32[2,8,2,1024]{3,2,1,0:T(2,128)} %get-tuple-element.1269.lse_ref), custom_call_target="tpu_custom_call" | custom-call | flops 26843545600 | bytes 16777216 | tf_op jit(solution)/shard_map/attn_bwd/pallas_call | solution.py:140
  439.1 31.0 %attn_bwd.2.dq_ref.refs_0_ = bf16[1024,3072]{1,0:T(8,128)(2,1)} custom-call(bf16[2048,3072]{1,0:T(8,128)(2,1)} %add_convert_fusion.1.qkv_ref, bf16[2048,1024]{1,0:T(8,128)(2,1)} %get-tuple-element.1255.c_ref.ctx_ref.a1_ref, bf16[2048,1024]{1,0:T(8,128)(2,1)} %get-tuple-element.1268.dctx_ref, f32[2,8,2,1024]{3,2,1,0:T(2,128)} %get-tuple-element.1269.lse_ref), custom_call_target="tpu_custom_call" | custom-call | flops 26843545600 | bytes 16777216 | tf_op jit(solution)/shard_map/attn_bwd/pallas_call | solution.py:140
  483.8 16.1 %qkv_back.2 = (bf16[1024,1024]{1,0:T(8,128)(2,1)}, f32[1152,1024]{1,0:T(8,128)}, f32[8,1024]{1,0:T(8,128)}, f32[8,3072]{1,0:T(8,128)}) custom-call(bf16[1024,3072]{1,0:T(8,128)(2,1)} %attn_bwd.2.dq_ref.refs_0_, bf16[3072,1024]{1,0:T(8,128)(2,1)} %all-gather.4.cloned.1.call-done.w_ref, f32[2048,1024]{1,0:T(8,128)} %get-tuple-element.1259.x_ref, ...), custom_call_target="tpu_custom_call" | custom-call | flops 6442450944 | bytes 18874368 | tf_op jit(solution)/shard_map/qkv_back/pallas_call | solution.py:466
  500.0 16.6 %qkv_back.3 = (bf16[1024,1024]{1,0:T(8,128)(2,1)}, f32[1152,1024]{1,0:T(8,128)}, f32[8,1024]{1,0:T(8,128)}, f32[8,3072]{1,0:T(8,128)}) custom-call(bf16[1024,3072]{1,0:T(8,128)(2,1)} %attn_bwd.3.dq_ref.refs_1_, bf16[3072,1024]{1,0:T(8,128)(2,1)} %all-gather.4.cloned.1.call-done.w_ref, f32[2048,1024]{1,0:T(8,128)} %get-tuple-element.1259.x_ref, ...), custom_call_target="tpu_custom_call" | custom-call | flops 6442450944 | bytes 18874368 | tf_op jit(solution)/shard_map/qkv_back/pallas_call | solution.py:466
  574.2 16.8 %weight_grads.3 = f32[2112,1024]{1,0:T(8,128)} custom-call(s32[1]{0:T(128)} %bitcast.53.core_ref, bf16[2048,1024]{1,0:T(8,128)(2,1)} %get-tuple-element.1255.c_ref.ctx_ref.a1_ref, bf16[2048,1024]{1,0:T(8,128)(2,1)} %get-tuple-element.1290.b1_ref, bf16[2048,1024]{1,0:T(8,128)(2,1)} %get-tuple-element.1252.b2_ref, bf16[1024,3072]{1,0:T(8,128)(2,1)} %attn_bwd.2.dq_ref.refs_0_, ...), custom_call_target="tpu_custom_call" | custom-call | flops 8589934592 | bytes 25165824 | tf_op jit(solution)/shard_map/weight_grads/pallas_call | solution.py:743
  669.8 32.5 %collective-permute-done.62.refs_19_ = bf16[384,1024]{1,0:T(8,128)(2,1)} collective-permute-done((bf16[384,1024]{1,0:T(8,128)(2,1)}, bf16[384,1024]{1,0:T(8,128)(2,1)}, u32[]{:S(2)}, u32[]{:S(2)}) %collective-permute-start.62) | collective-permute-done | bytes 786464 | tf_op jit(solution)/shard_map/ppermute | solution.py:817
  705.8 26.3 %down.1 = (bf16[2,256,1024]{2,1,0:T(8,128)(2,1)}, bf16[2,256,1024]{2,1,0:T(8,128)(2,1)}, bf16[2,256,1024]{2,1,0:T(8,128)(2,1)}, bf16[2,256,1024]{2,1,0:T(8,128)(2,1)}) custom-call(s32[1]{0:T(128)} %bitcast.10.me_ref, bf16[2048,4096]{1,0:T(8,128)(2,1)} %get-tuple-element.1261.act_ref.a_ref, bf16[16,576,1024]{2,1,0:T(8,128)(2,1)} %bitcast.196, ...), custom_call_target="tpu_custom_call" | custom-call | flops 17179869184 | bytes 29360128 | tf_op jit(solution)/shard_map/down/pallas_call | solution.py:373
  734.8 28.5 %collective-permute-done.47.refs_3_ = bf16[384,1024]{1,0:T(8,128)(2,1)} collective-permute-done((bf16[384,1024]{1,0:T(8,128)(2,1)}, bf16[384,1024]{1,0:T(8,128)(2,1)}, u32[]{:S(2)}, u32[]{:S(2)}) %collective-permute-start.47) | collective-permute-done | bytes 786464 | tf_op jit(solution)/shard_map/ppermute | solution.py:817
  766.2 22.1 %collective-permute-done.42.refs_1_ = bf16[2,256,1024]{2,1,0:T(8,128)(2,1)S(1)} collective-permute-done((bf16[2,256,1024]{2,1,0:T(8,128)(2,1)}, bf16[2,256,1024]{2,1,0:T(8,128)(2,1)S(1)}, u32[]{:S(2)}, u32[]{:S(2)}) %collective-permute-start.42) | collective-permute-done | bytes 1048608 | tf_op jit(solution)/shard_map/ppermute | solution.py:817
  790.3 26.7 %collective-permute-done.44.refs_3_ = bf16[2,256,1024]{2,1,0:T(8,128)(2,1)} collective-permute-done((bf16[2,256,1024]{2,1,0:T(8,128)(2,1)}, bf16[2,256,1024]{2,1,0:T(8,128)(2,1)}, u32[]{:S(2)}, u32[]{:S(2)}) %collective-permute-start.44) | collective-permute-done | bytes 1048608 | tf_op jit(solution)/shard_map/ppermute | solution.py:817
  822.8 24.2 %collective-permute-done.66.refs_23_ = bf16[384,1024]{1,0:T(8,128)(2,1)S(1)} collective-permute-done((bf16[384,1024]{1,0:T(8,128)(2,1)}, bf16[384,1024]{1,0:T(8,128)(2,1)S(1)}, u32[]{:S(2)}, u32[]{:S(2)}) %collective-permute-start.66) | collective-permute-done | bytes 786464 | tf_op jit(solution)/shard_map/ppermute | solution.py:817
  854.0 26.8 %collective-permute-done.49.refs_5_ = bf16[384,1024]{1,0:T(8,128)(2,1)} collective-permute-done((bf16[384,1024]{1,0:T(8,128)(2,1)}, bf16[384,1024]{1,0:T(8,128)(2,1)}, u32[]{:S(2)}, u32[]{:S(2)}) %collective-permute-start.49) | collective-permute-done | bytes 786464 | tf_op jit(solution)/shard_map/ppermute | solution.py:817
  881.7 25.7 %collective-permute-done.50.refs_6_ = bf16[384,1024]{1,0:T(8,128)(2,1)} collective-permute-done((bf16[384,1024]{1,0:T(8,128)(2,1)}, bf16[384,1024]{1,0:T(8,128)(2,1)}, u32[]{:S(2)}, u32[]{:S(2)}) %collective-permute-start.50) | collective-permute-done | bytes 786464 | tf_op jit(solution)/shard_map/ppermute | solution.py:817
  910.7 23.4 %collective-permute-done.51.refs_7_ = bf16[384,1024]{1,0:T(8,128)(2,1)} collective-permute-done((bf16[384,1024]{1,0:T(8,128)(2,1)}, bf16[384,1024]{1,0:T(8,128)(2,1)}, u32[]{:S(2)}, u32[]{:S(2)}) %collective-permute-start.51) | collective-permute-done | bytes 786464 | tf_op jit(solution)/shard_map/ppermute | solution.py:817
  951.1 17.9 %collective-permute-done.81.refs_1_ = f32[264,1024]{1,0:T(8,128)} collective-permute-done((f32[264,1024]{1,0:T(8,128)}, f32[264,1024]{1,0:T(8,128)}, u32[]{:S(2)}, u32[]{:S(2)}) %collective-permute-start.81) | collective-permute-done | bytes 1081376 | tf_op jit(solution)/shard_map/ppermute | solution.py:817
  968.9 35.7 %collective-permute-done.77.refs_1_ = f32[264,1024]{1,0:T(8,128)} collective-permute-done((f32[264,1024]{1,0:T(8,128)}, f32[264,1024]{1,0:T(8,128)}, u32[]{:S(2)}, u32[]{:S(2)}) %collective-permute-start.77) | collective-permute-done | bytes 1081376 | tf_op jit(solution)/shard_map/ppermute | solution.py:817
  1004.7 64.5 %table_accum.1 = f32[100544,128]{1,0:T(8,128)} custom-call(s32[12288]{0:T(1024)} %fusion.143.where_ref, s32[160]{0:T(256)} %min.12.first_ref, bf16[384,1024]{1,0:T(8,128)(2,1)} %get-tuple-element.1272.refs_0_, bf16[384,1024]{1,0:T(8,128)(2,1)} %collective-permute-done.45.refs_1_, bf16[384,1024]{1,0:T(8,128)(2,1)} %collective-permute-done.46.refs_2_, ...), custom_call_target="tpu_custom_call" | custom-call | flops 49999998976 | bytes 100000000 | tf_op jit(solution)/shard_map/table_accum/pallas_call | solution.py:642
  (441 shorter events, 316.3 us)
Async XLA Ops:
  7.2 233.3 %all-gather.4.cloned.1.call-start = ((), (), s32[]{:S(2)}) async-start(), calls=%async_computation.4 | async-start | bytes 7077888 | tf_op jit(solution)/shard_map/all_gather | solution.py:814
  9.4 291.8 %all-gather.6.cloned.1.call-start = ((), (), s32[]{:S(2)}) async-start(), calls=%async_computation.5 | async-start | bytes 20054016 | tf_op jit(solution)/shard_map/all_gather | solution.py:837
  18.3 68.0 %collective-permute-start.38 = (bf16[1792]{0:T(1024)(128)(2,1)S(1)}, bf16[1792]{0:T(1024)(128)(2,1)S(1)}, u32[]{:S(2)}, u32[]{:S(2)}) collective-permute-start(bf16[1792]{0:T(1024)(128)(2,1)S(1)} %dynamic-update-slice.33), channel_id=1, source_target_pairs={{0,12},{4,8},{8,4},{12,0},{1,13},{5,9},{9,5},{13,1},{2,14},{6,10},... | collective-permute-start | bytes 10760 | tf_op jit(solution)/shard_map/ppermute | solution.py:817
  21.2 66.6 %collective-permute-start.37 = (bf16[1792]{0:T(1024)(128)(2,1)S(1)}, bf16[1792]{0:T(1024)(128)(2,1)S(1)}, u32[]{:S(2)}, u32[]{:S(2)}) collective-permute-start(bf16[1792]{0:T(1024)(128)(2,1)S(1)} %dynamic-update-slice.33), channel_id=1, source_target_pairs={{0,8},{4,12},{8,0},{12,4},{1,9},{5,13},{9,1},{13,5},{2,10},{6,14},... | collective-permute-start | bytes 10760 | tf_op jit(solution)/shard_map/ppermute | solution.py:817
  21.6 67.7 %collective-permute-start.36 = (bf16[1792]{0:T(1024)(128)(2,1)S(1)}, bf16[1792]{0:T(1024)(128)(2,1)S(1)}, u32[]{:S(2)}, u32[]{:S(2)}) collective-permute-start(bf16[1792]{0:T(1024)(128)(2,1)S(1)} %dynamic-update-slice.33), channel_id=1, source_target_pairs={{0,4},{4,0},{8,12},{12,8},{1,5},{5,1},{9,13},{13,9},{2,6},{6,2},{1... | collective-permute-start | bytes 10760 | tf_op jit(solution)/shard_map/ppermute | solution.py:817
  34.3 729.7 %reduce-scatter.5.cloned.1.call-start = ((), (), s32[]{:S(2)}) async-start(), calls=%async_computation.6 | async-start | bytes 2654208 | tf_op jit(solution)/shard_map/reduce_scatter | solution.py:1031
  85.8 133.9 %collective-permute-start.34 = (bf16[704,1024]{1,0:T(8,128)(2,1)}, bf16[704,1024]{1,0:T(8,128)(2,1)}, u32[]{:S(2)}, u32[]{:S(2)}) collective-permute-start(bf16[704,1024]{1,0:T(8,128)(2,1)} %get-tuple-element.1568), channel_id=1, source_target_pairs={{0,8},{4,12},{8,0},{12,4},{1,9},{5,13},{9,1},{13,5},{2,10},{6,14},... | collective-permute-start | bytes 4325384 | tf_op jit(solution)/shard_map/ppermute | solution.py:817
  86.3 133.5 %collective-permute-start.35 = (bf16[704,1024]{1,0:T(8,128)(2,1)}, bf16[704,1024]{1,0:T(8,128)(2,1)}, u32[]{:S(2)}, u32[]{:S(2)}) collective-permute-start(bf16[704,1024]{1,0:T(8,128)(2,1)} %get-tuple-element.1566), channel_id=1, source_target_pairs={{0,12},{4,8},{8,4},{12,0},{1,13},{5,9},{9,5},{13,1},{2,14},{6,10},... | collective-permute-start | bytes 4325384 | tf_op jit(solution)/shard_map/ppermute | solution.py:817
  87.7 132.0 %collective-permute-start.33 = (bf16[704,1024]{1,0:T(8,128)(2,1)}, bf16[704,1024]{1,0:T(8,128)(2,1)}, u32[]{:S(2)}, u32[]{:S(2)}) collective-permute-start(bf16[704,1024]{1,0:T(8,128)(2,1)} %get-tuple-element.1567), channel_id=1, source_target_pairs={{0,4},{4,0},{8,12},{12,8},{1,5},{5,1},{9,13},{13,9},{2,6},{6,2},{1... | collective-permute-start | bytes 4325384 | tf_op jit(solution)/shard_map/ppermute | solution.py:817
  89.4 124.5 %collective-permute-start.40 = (bf16[2,256,1024]{2,1,0:T(8,128)(2,1)}, bf16[2,256,1024]{2,1,0:T(8,128)(2,1)}, u32[]{:S(2)}, u32[]{:S(2)}) collective-permute-start(bf16[2,256,1024]{2,1,0:T(8,128)(2,1)} %get-tuple-element.1563), channel_id=1, source_target_pairs={{0,8},{4,12},{8,0},{12,4},{1,9},{5,13},{9,1},{13,5},{2,10},{6,14},... | collective-permute-start | bytes 3145736 | tf_op jit(solution)/shard_map/ppermute | solution.py:817
  89.8 125.2 %collective-permute-start.39 = (bf16[2,256,1024]{2,1,0:T(8,128)(2,1)}, bf16[2,256,1024]{2,1,0:T(8,128)(2,1)}, u32[]{:S(2)}, u32[]{:S(2)}) collective-permute-start(bf16[2,256,1024]{2,1,0:T(8,128)(2,1)} %get-tuple-element.1564), channel_id=1, source_target_pairs={{0,4},{4,0},{8,12},{12,8},{1,5},{5,1},{9,13},{13,9},{2,6},{6,2},{1... | collective-permute-start | bytes 3145736 | tf_op jit(solution)/shard_map/ppermute | solution.py:817
  528.9 405.2 %reduce-scatter.9.cloned.1.call-start = ((), (), s32[]{:S(2)}) async-start(), calls=%async_computation.9 | async-start | bytes 9732096 | tf_op jit(solution)/shard_map/reduce_scatter | solution.py:984
  544.4 391.2 %reduce-scatter.7.cloned.1.call-start = ((), (), s32[]{:S(2)}) async-start(), calls=%async_computation.8 | async-start | bytes 9732096 | tf_op jit(solution)/shard_map/reduce_scatter | solution.py:1033
  591.0 360.1 %reduce-scatter.11.cloned.1.call-start = ((), (), s32[]{:S(2)}) async-start(), calls=%async_computation.10 | async-start | bytes 9732096 | tf_op jit(solution)/shard_map/reduce_scatter | solution.py:982
  634.5 434.7 %all-gather.8.cloned.1.call-start = ((), (), s32[]{:S(2)}) async-start(), calls=%async_computation.7 | async-start | bytes 5013504 | tf_op jit(solution)/shard_map/all_gather | solution.py:1035
  669.0 95.1 %collective-permute-start.52 = (bf16[384,1024]{1,0:T(8,128)(2,1)}, bf16[384,1024]{1,0:T(8,128)(2,1)}, u32[]{:S(2)}, u32[]{:S(2)}) collective-permute-start(bf16[384,1024]{1,0:T(8,128)(2,1)} %get-tuple-element.1272.refs_0_), channel_id=1, source_target_pairs={{0,1},{1,0},{2,3},{3,2},{4,5},{5,4},{6,7},{7,6},{8,9},{9,8},{10,11... | collective-permute-start | bytes 2359304 | tf_op jit(solution)/shard_map/ppermute | solution.py:817
  669.8 94.4 %collective-permute-start.48 = (bf16[384,1024]{1,0:T(8,128)(2,1)}, bf16[384,1024]{1,0:T(8,128)(2,1)}, u32[]{:S(2)}, u32[]{:S(2)}) collective-permute-start(bf16[384,1024]{1,0:T(8,128)(2,1)} %get-tuple-element.1272.refs_0_), channel_id=1, source_target_pairs={{0,2},{2,0},{1,3},{3,1},{4,6},{6,4},{5,7},{7,5},{8,10},{10,8},{9,1... | collective-permute-start | bytes 2359304 | tf_op jit(solution)/shard_map/ppermute | solution.py:817
  853.7 80.4 %collective-permute-start.51 = (bf16[384,1024]{1,0:T(8,128)(2,1)}, bf16[384,1024]{1,0:T(8,128)(2,1)}, u32[]{:S(2)}, u32[]{:S(2)}) collective-permute-start(bf16[384,1024]{1,0:T(8,128)(2,1)} %collective-permute-done.47.refs_3_), channel_id=1, source_target_pairs={{0,2},{2,0},{1,3},{3,1},{4,6},{6,4},{5,7},{7,5},{8,10},{10,8},{9,1... | collective-permute-start | bytes 2359304 | tf_op jit(solution)/shard_map/ppermute | solution.py:817
  935.6 69.1 %collective-permute-start.77 = (f32[264,1024]{1,0:T(8,128)}, f32[264,1024]{1,0:T(8,128)}, u32[]{:S(2)}, u32[]{:S(2)}) collective-permute-start(f32[264,1024]{1,0:T(8,128)} %reduce-scatter.7.cloned.1.call-done.refs_0_), channel_id=1, source_target_pairs={{0,2},{2,0},{1,3},{3,1},{4,6},{6,4},{5,7},{7,5},{8,10},{10,8},{9,1... | collective-permute-start | bytes 3244040 | tf_op jit(solution)/shard_map/ppermute | solution.py:817
  948.9 139.1 %collective-permute-start.82 = (f32[264,1024]{1,0:T(8,128)}, f32[264,1024]{1,0:T(8,128)}, u32[]{:S(2)}, u32[]{:S(2)}) collective-permute-start(f32[264,1024]{1,0:T(8,128)} %reduce-scatter.9.cloned.1.call-done.refs_0_), channel_id=1, source_target_pairs={{0,1},{1,0},{2,3},{3,2},{4,5},{5,4},{6,7},{7,6},{8,9},{9,8},{10,11... | collective-permute-start | bytes 3244040 | tf_op jit(solution)/shard_map/ppermute | solution.py:817
  949.4 129.2 %collective-permute-start.78 = (f32[264,1024]{1,0:T(8,128)}, f32[264,1024]{1,0:T(8,128)}, u32[]{:S(2)}, u32[]{:S(2)}) collective-permute-start(f32[264,1024]{1,0:T(8,128)} %reduce-scatter.7.cloned.1.call-done.refs_0_), channel_id=1, source_target_pairs={{0,1},{1,0},{2,3},{3,2},{4,5},{5,4},{6,7},{7,6},{8,9},{9,8},{10,11... | collective-permute-start | bytes 3244040 | tf_op jit(solution)/shard_map/ppermute | solution.py:817
  951.1 127.0 %collective-permute-start.85 = (f32[264,1024]{1,0:T(8,128)}, f32[264,1024]{1,0:T(8,128)}, u32[]{:S(2)}, u32[]{:S(2)}) collective-permute-start(f32[264,1024]{1,0:T(8,128)} %reduce-scatter.11.cloned.1.call-done.refs_0_), channel_id=1, source_target_pairs={{0,2},{2,0},{1,3},{3,1},{4,6},{6,4},{5,7},{7,5},{8,10},{10,8},{9,1... | collective-permute-start | bytes 3244040 | tf_op jit(solution)/shard_map/ppermute | solution.py:817
  968.9 119.1 %collective-permute-start.83 = (f32[264,1024]{1,0:T(8,128)}, f32[264,1024]{1,0:T(8,128)}, u32[]{:S(2)}, u32[]{:S(2)}) collective-permute-start(f32[264,1024]{1,0:T(8,128)} %collective-permute-done.81.refs_1_), channel_id=1, source_target_pairs={{0,1},{1,0},{2,3},{3,2},{4,5},{5,4},{6,7},{7,6},{8,9},{9,8},{10,11... | collective-permute-start | bytes 3244040 | tf_op jit(solution)/shard_map/ppermute | solution.py:817
  1004.7 74.0 %collective-permute-start.79 = (f32[264,1024]{1,0:T(8,128)}, f32[264,1024]{1,0:T(8,128)}, u32[]{:S(2)}, u32[]{:S(2)}) collective-permute-start(f32[264,1024]{1,0:T(8,128)} %collective-permute-done.77.refs_1_), channel_id=1, source_target_pairs={{0,1},{1,0},{2,3},{3,2},{4,5},{5,4},{6,7},{7,6},{8,9},{9,8},{10,11... | collective-permute-start | bytes 3244040 | tf_op jit(solution)/shard_map/ppermute | solution.py:817
  (85 other events, 3116.2 us)
Sparse Core Ops, SparseCore 0:
  9.8 67.0 all-gather.3
  79.2 154.7 all-gather.5
  529.0 40.8 reduce-scatter.4
  574.1 78.1 reduce-scatter.8
  656.4 144.7 reduce-scatter.6
  805.3 145.6 reduce-scatter.10
  953.3 53.2 all-gather.7

commit v9 on v8

--- a/solution.py
+++ b/solution.py
@@ -11,6 +11,7 @@
 F32 = jnp.float32
 BF16 = jnp.bfloat16
 MIB = 1024 * 1024
+DEPTH = 4
 WIDEN = 32
 
 BLK = 256
@@ -553,7 +554,7 @@
     group = 8 * tiles
 
     def fetch(block, n):
-        return pltpu.make_async_copy(tok_refs[n], buf.at[block % 2], in_sem.at[block % 2])
+        return pltpu.make_async_copy(tok_refs[n], buf.at[block % DEPTH], in_sem.at[block % DEPTH])
 
     def fetch_next(block):
         for n in range(n_block):
@@ -561,7 +562,8 @@
             def _(n=n):
                 fetch(block, n).start()
 
-    fetch_next(0)
+    for n in range(min(DEPTH - 1, n_block)):
+        fetch(n, n).start()
     for s in range(n_sub):
         def clear(i, _, s=s):
             acc[s][pl.ds(pl.multiple_of(i * group, group), group), :] = jnp.zeros((group, LANES), F32)
@@ -582,11 +584,11 @@
             acc[s][pl.ds(at[j], tiles, stride=8), :] = sums[j]
 
     def add_block(block, _):
-        fetch_next(block + 1)
+        fetch_next(block + DEPTH - 1)
         fetch(block, 0).wait()
 
         def widen(g, _):
-            rows = buf[block % 2, pl.ds(pl.multiple_of(g * WIDEN, WIDEN), WIDEN), :].astype(F32)
+            rows = buf[block % DEPTH, pl.ds(pl.multiple_of(g * WIDEN, WIDEN), WIDEN), :].astype(F32)
             base = pl.multiple_of(g * (WIDEN // 8) * group, (WIDEN // 8) * group)
             for h in range(WIDEN // 8):
                 for c in range(tiles):
@@ -646,8 +648,8 @@
         out_specs=pl.BlockSpec(memory_space=pl.ANY),
         out_shape=jax.ShapeDtypeStruct((sum(sub_rows) * tiles, LANES), F32),
         scratch_shapes=[pltpu.VMEM((r * tiles, LANES), F32) for r in sub_rows]
-        + [pltpu.VMEM((2, cap, width), BF16), pltpu.VMEM((cap * tiles, LANES), F32),
-           pltpu.SemaphoreType.DMA((2,)), pltpu.SemaphoreType.DMA((n_sub,))],
+        + [pltpu.VMEM((DEPTH, cap, width), BF16), pltpu.VMEM((cap * tiles, LANES), F32),
+           pltpu.SemaphoreType.DMA((DEPTH,)), pltpu.SemaphoreType.DMA((n_sub,))],
         name="table_accum",
         cost_estimate=pl.CostEstimate(flops=50_000_000_000, bytes_accessed=100_000_000, transcendentals=0),
         compiler_params=pltpu.CompilerParams(vmem_limit_bytes=63 * 1024 * 1024),
@@ -941,6 +943,7 @@
         code0 = (place0 // 8) * (8 * tiles) + place0 % 8
         og_parts = out_grad.reshape(n_tp, n_seq, seq_local, width)
         og_parts = [lax.dynamic_index_in_dim(og_parts, tp_index ^ k, 0, keepdims=False) for k in range(n_tp)]
+        got0, og_parts = lax.optimization_barrier((got0, og_parts))
         resid_x, hid1 = embed(code0, got0, pos_rows, gain1, bias1, n_tok)
 
         def more_rows(carry):
@@ -978,11 +981,10 @@
         p_ff = piece_of(n_tp * ff)
         down_theirs = swap(grad_pieces(1 - core, act, og, n_tp, p_ff, 0, 1), "cc")
         up_theirs = swap(grad_pieces(1 - core, d_up, hid2, n_tp, p_ff, 0, 1), "cc")
-        d_down = grad_pieces(core, act, og, n_tp, p_ff, 0, 1, plus=down_theirs)
-        d_down = lax.psum_scatter(d_down, ("tp", "xx"), scatter_dimension=0, tiled=True)
-        d_upw = grad_pieces(core, d_up, hid2, n_tp, p_ff, 0, 1, plus=up_theirs)
-        d_upw = lax.psum_scatter(d_upw, ("tp", "xx"), scatter_dimension=0, tiled=True)
-        d_down, d_upw = every_piece(d_down), every_piece(d_upw)
+        ff_grads = grad_pieces(core, act, og, n_tp, p_ff, 0, 2, plus=down_theirs)
+        ff_grads = grad_pieces(core, d_up, hid2, n_tp, p_ff, 1, 2, plus=up_theirs, into=ff_grads)
+        ff_grads = lax.psum_scatter(ff_grads, ("tp", "xx"), scatter_dimension=0, tiled=True)
+        ff_grads = every_piece(ff_grads)
 
         d_resid1, d_attn, d_ctx, sums2 = back2(d_up, w_all, 2 * n_ff, resid_x1, og, gain2)
         n_small = n_tp * (b_qkv.size + ff) // width + 6
@@ -1007,8 +1009,7 @@
         d_qkvs = [d_qkv0, d_qkv1]
         rest_theirs = swap(grad_rest(1 - core, ctx, d_attn, d_qkvs, hid1, n_tp, spans), "cc")
 
-        (d_w_down,) = pieces_out(x_and_core, d_down, ((0, n_ff, False),))
-        (d_w_up,) = pieces_out(x_and_core, d_upw, ((0, n_ff, True),))
+        d_w_down, d_w_up = pieces_out(x_and_core, ff_grads, ((0, n_ff, False), (p_ff, n_ff, True)))
         image = accum(blocks0 + blocks1, code, block_first, sub_rows, width)
         d_emb = image.reshape(rows // 8, tiles, 8, 128).transpose(0, 2, 1, 3).reshape(rows, width)
 

time: 1120 us -> 1150 us (1.027)
  waiting for transfers between devices: 425 us -> 458 us
    ppermute x55 -> x52, waiting for transfers between devices: 423 us -> 443 us  [swap(): return lax.ppermute(v, axis, tp_swap[k] if axis == 'tp' else pair)]
    reduce_scatter x1, waiting for transfers between devices: 0.01 us -> 15.5 us  [local_step(): rest = lax.psum_scatter(rest, ('tp', 'xx'), scatter_dimension=0, tiled=True)]
    ppermute x55 -> x52, starting transfers between devices: 37 us -> 35.7 us  [swap(): return lax.ppermute(v, axis, tp_swap[k] if axis == 'tp' else pair)]
  transfers between devices with their start and end apart: 62 -> 58, of which waited for: 19 -> 19; matrix products, arithmetic and copies ran while one was open for 11% -> 11% of each run, Pallas kernels for 26% -> 25%
where the time goes in v9:
time: 1150 us; the launch traced here: 1140 us
  Pallas kernels  475 us (41%)
  waiting for transfers between devices  458 us (40%)
  local copies, waits for them, and re-layouts  89.9 us (8%)
  starting transfers between devices  35.9 us (3%)
  matrix products  23.8 us (2%)
  other arithmetic  21 us (2%)
  between operations  19 us (2%)
    ppermute x52, waiting for transfers between devices, swap(): return lax.ppermute(v, axis, tp_swap[k] if axis == 'tp' else pair)  443 us
    pallas_call x1, Pallas kernels, accum(): pl.pallas_call(functools.partial(accum_kernel, n_block, cap, sub_rows, wi...  64.4 us
    pallas_call x2, Pallas kernels, attn_bwd(): pl.pallas_call(attn_bwd_kernel, grid=(n_pair,), in_specs=[pl.BlockSpec((s...  61.5 us
    pallas_call x4, Pallas kernels, grad_pieces(): pl.pallas_call(functools.partial(grad_kernel, plus is not None), grid_spe...  58.2 us
    pallas_call x1, Pallas kernels, ffn(): pl.pallas_call(functools.partial(ffn_kernel, part), grid=(n_piece,), in_s...  56.5 us
    pallas_call x1, Pallas kernels, attn_fwd(): pl.pallas_call(attn_fwd_kernel, grid=(n_seq, n_pair), in_specs=[pl.BlockS...  41.2 us
    pallas_call x1, Pallas kernels, back2(): pl.pallas_call(back2_kernel, grid=(n_tok // rows,), in_specs=[pl.BlockSpe...  38.5 us
    ppermute x52, starting transfers between devices, swap(): return lax.ppermute(v, axis, tp_swap[k] if axis == 'tp' else pair)  35.7 us
  transfers between devices with their start and end apart: 58, of which 19 were waited for; matrix products, arithmetic and copies ran while one was open for 11% of the time, Pallas kernels for 25%

profile of v9, /device:TPU:0, one launch (start us, length us, event | category | flops | bytes accessed | tf_op | source)
XLA Modules:
  0.0 1137.3 jit_solution(14878055798011946873)
XLA Ops:
  32.4 20.3 %gather_fusion.3 = bf16[1408,1024]{1,0:T(8,128)(2,1)S(1)} fusion(bf16[12568,1024]{1,0:T(8,128)(2,1)} %param.21, s32[2048]{0:T(1024)S(1)} %pad_clamp_fusion.3), kind=kCustom, calls=%fused_computation.3 | custom fusion | bytes 5772800 | tf_op jit(solution)/shard_map/jit(_take)/gather | solution.py:927
  52.7 19.4 %gather_fusion.4 = bf16[1408,1024]{1,0:T(8,128)(2,1)} fusion(bf16[12568,1024]{1,0:T(8,128)(2,1)} %param.21, s32[2048]{0:T(1024)S(1)} %pad_clamp_fusion.2), kind=kCustom, calls=%fused_computation.4 | custom fusion | bytes 5772800 | tf_op jit(solution)/shard_map/jit(_take)/gather | solution.py:929
  97.2 67.2 %collective-permute-done.37 = bf16[1792]{0:T(1024)(128)(2,1)S(1)} collective-permute-done((bf16[1792]{0:T(1024)(128)(2,1)S(1)}, bf16[1792]{0:T(1024)(128)(2,1)S(1)}, u32[]{:S(2)}, u32[]{:S(2)}) %collective-permute-start.37) | collective-permute-done | bytes 3616 | tf_op jit(solution)/shard_map/ppermute | solution.py:819
  186.2 30.2 %collective-permute-done.39.refs_1_ = bf16[2,256,1024]{2,1,0:T(8,128)(2,1)} collective-permute-done((bf16[2,256,1024]{2,1,0:T(8,128)(2,1)}, bf16[2,256,1024]{2,1,0:T(8,128)(2,1)}, u32[]{:S(2)}, u32[]{:S(2)}) %collective-permute-start.39) | collective-permute-done | bytes 1048608 | tf_op jit(solution)/shard_map/ppermute | solution.py:819
  216.4 22.7 %collective-permute-done.41.refs_3_ = bf16[2,256,1024]{2,1,0:T(8,128)(2,1)} collective-permute-done((bf16[2,256,1024]{2,1,0:T(8,128)(2,1)}, bf16[2,256,1024]{2,1,0:T(8,128)(2,1)}, u32[]{:S(2)}, u32[]{:S(2)}) %collective-permute-start.41) | collective-permute-done | bytes 1048608 | tf_op jit(solution)/shard_map/ppermute | solution.py:819
  250.9 19.4 %add_convert_fusion.1.qkv_ref = bf16[2048,3072]{1,0:T(8,128)(2,1)} fusion(bf16[2048,1024]{1,0:T(8,128)(2,1)} %get-tuple-element.1266.b2_ref, bf16[3072,1024]{1,0:T(8,128)(2,1)} %all-gather.4.cloned.1.call-done.w_ref, f32[3072]{0:T(1024)S(1)} %copy-done.29), kind=kOutput, calls=%fused_computation.280 | convolution fusion | flops 12897484800 | bytes 23080960 | tf_op jit(solution)/shard_map/dot_general | solution.py:21
  270.3 41.2 %attn_fwd.1 = (bf16[2048,1024]{1,0:T(8,128)(2,1)}, f32[2,8,2,1024]{3,2,1,0:T(2,128)}) custom-call(bf16[2048,3072]{1,0:T(8,128)(2,1)} %add_convert_fusion.1.qkv_ref), custom_call_target="tpu_custom_call" | custom-call | flops 21474836480 | bytes 16777216 | tf_op jit(solution)/shard_map/attn_fwd/pallas_call | solution.py:75
  324.1 56.5 %ffn.1 = (bf16[2048,4096]{1,0:T(8,128)(2,1)}, bf16[2048,4096]{1,0:T(8,128)(2,1)}, f32[1,4096]{1,0:T(1,128)}) custom-call(bf16[2048,1024]{1,0:T(8,128)(2,1)} %get-tuple-element.1274.h_ref.b_ref, bf16[2048,1024]{1,0:T(8,128)(2,1)} %bitcast.197, bf16[16,576,1024]{2,1,0:T(8,128)(2,1)} %bitcast.191, bf16[16,576,1024]{2,1,0:T(8,128)(2,1)} %bitcast.192, ...), custom_call_target="tpu_custom_call" | custom-call | flops 34359738368 | bytes 50331648 | tf_op jit(solution)/shard_map/ffn/pallas_call | solution.py:347
  380.6 38.5 %ffn_back.1 = (f32[2048,1024]{1,0:T(8,128)}, bf16[2048,1024]{1,0:T(8,128)(2,1)}, bf16[2048,1024]{1,0:T(8,128)(2,1)}, f32[8,1024]{1,0:T(8,128)}) custom-call(bf16[2048,4096]{1,0:T(8,128)(2,1)} %get-tuple-element.1285.dup_ref.a_ref, bf16[16,576,1024]{2,1,0:T(8,128)(2,1)} %bitcast.193, bf16[16,576,1024]{2,1,0:T(8,128)(2,1)} %bitcast.194, ...), custom_call_target="tpu_custom_call" | custom-call | flops 17179869184 | bytes 41943040 | tf_op jit(solution)/shard_map/ffn_back/pallas_call | solution.py:420
  419.1 30.5 %attn_bwd.3.dq_ref.refs_1_ = bf16[1024,3072]{1,0:T(8,128)(2,1)} custom-call(bf16[2048,3072]{1,0:T(8,128)(2,1)} %add_convert_fusion.1.qkv_ref, bf16[2048,1024]{1,0:T(8,128)(2,1)} %get-tuple-element.1269.c_ref.ctx_ref.a1_ref, bf16[2048,1024]{1,0:T(8,128)(2,1)} %get-tuple-element.1286.dctx_ref, f32[2,8,2,1024]{3,2,1,0:T(2,128)} %get-tuple-element.1287.lse_ref), custom_call_target="tpu_custom_call" | custom-call | flops 26843545600 | bytes 16777216 | tf_op jit(solution)/shard_map/attn_bwd/pallas_call | solution.py:141
  449.6 30.9 %attn_bwd.2.dq_ref.refs_0_ = bf16[1024,3072]{1,0:T(8,128)(2,1)} custom-call(bf16[2048,3072]{1,0:T(8,128)(2,1)} %add_convert_fusion.1.qkv_ref, bf16[2048,1024]{1,0:T(8,128)(2,1)} %get-tuple-element.1269.c_ref.ctx_ref.a1_ref, bf16[2048,1024]{1,0:T(8,128)(2,1)} %get-tuple-element.1286.dctx_ref, f32[2,8,2,1024]{3,2,1,0:T(2,128)} %get-tuple-element.1287.lse_ref), custom_call_target="tpu_custom_call" | custom-call | flops 26843545600 | bytes 16777216 | tf_op jit(solution)/shard_map/attn_bwd/pallas_call | solution.py:141
  613.7 17.7 %weight_grads.3 = f32[2112,1024]{1,0:T(8,128)} custom-call(s32[1]{0:T(128)} %bitcast.53.core_ref, bf16[2048,1024]{1,0:T(8,128)(2,1)} %get-tuple-element.1269.c_ref.ctx_ref.a1_ref, bf16[2048,1024]{1,0:T(8,128)(2,1)} %get-tuple-element.1308.b1_ref, bf16[2048,1024]{1,0:T(8,128)(2,1)} %get-tuple-element.1266.b2_ref, bf16[1024,3072]{1,0:T(8,128)(2,1)} %attn_bwd.2.dq_ref.refs_0_, ...), custom_call_target="tpu_custom_call" | custom-call | flops 8589934592 | bytes 25165824 | tf_op jit(solution)/shard_map/weight_grads/pallas_call | solution.py:745
  654.0 25.7 %collective-permute-done.60.refs_17_ = bf16[384,1024]{1,0:T(8,128)(2,1)} collective-permute-done((bf16[384,1024]{1,0:T(8,128)(2,1)}, bf16[384,1024]{1,0:T(8,128)(2,1)}, u32[]{:S(2)}, u32[]{:S(2)}) %collective-permute-start.60) | collective-permute-done | bytes 786464 | tf_op jit(solution)/shard_map/ppermute | solution.py:819
  680.8 22.8 %collective-permute-done.62.refs_19_ = bf16[384,1024]{1,0:T(8,128)(2,1)} collective-permute-done((bf16[384,1024]{1,0:T(8,128)(2,1)}, bf16[384,1024]{1,0:T(8,128)(2,1)}, u32[]{:S(2)}, u32[]{:S(2)}) %collective-permute-start.62) | collective-permute-done | bytes 786464 | tf_op jit(solution)/shard_map/ppermute | solution.py:819
  703.8 25.9 %down.1 = (bf16[2,256,1024]{2,1,0:T(8,128)(2,1)}, bf16[2,256,1024]{2,1,0:T(8,128)(2,1)}, bf16[2,256,1024]{2,1,0:T(8,128)(2,1)}, bf16[2,256,1024]{2,1,0:T(8,128)(2,1)}) custom-call(s32[1]{0:T(128)} %bitcast.10.me_ref, bf16[2048,4096]{1,0:T(8,128)(2,1)} %get-tuple-element.1279.act_ref.a_ref, bf16[16,576,1024]{2,1,0:T(8,128)(2,1)} %bitcast.195, ...), custom_call_target="tpu_custom_call" | custom-call | flops 17179869184 | bytes 29360128 | tf_op jit(solution)/shard_map/down/pallas_call | solution.py:374
  734.5 23.9 %collective-permute-done.47.refs_3_ = bf16[384,1024]{1,0:T(8,128)(2,1)} collective-permute-done((bf16[384,1024]{1,0:T(8,128)(2,1)}, bf16[384,1024]{1,0:T(8,128)(2,1)}, u32[]{:S(2)}, u32[]{:S(2)}) %collective-permute-start.47) | collective-permute-done | bytes 786464 | tf_op jit(solution)/shard_map/ppermute | solution.py:819
  761.8 27.9 %collective-permute-done.42.refs_1_ = bf16[2,256,1024]{2,1,0:T(8,128)(2,1)S(1)} collective-permute-done((bf16[2,256,1024]{2,1,0:T(8,128)(2,1)}, bf16[2,256,1024]{2,1,0:T(8,128)(2,1)S(1)}, u32[]{:S(2)}, u32[]{:S(2)}) %collective-permute-start.42) | collective-permute-done | bytes 1048608 | tf_op jit(solution)/shard_map/ppermute | solution.py:819
  791.2 37.0 %collective-permute-done.44.refs_3_ = bf16[2,256,1024]{2,1,0:T(8,128)(2,1)} collective-permute-done((bf16[2,256,1024]{2,1,0:T(8,128)(2,1)}, bf16[2,256,1024]{2,1,0:T(8,128)(2,1)}, u32[]{:S(2)}, u32[]{:S(2)}) %collective-permute-start.44) | collective-permute-done | bytes 1048608 | tf_op jit(solution)/shard_map/ppermute | solution.py:819
  834.0 23.7 %collective-permute-done.66.refs_23_ = bf16[384,1024]{1,0:T(8,128)(2,1)S(1)} collective-permute-done((bf16[384,1024]{1,0:T(8,128)(2,1)}, bf16[384,1024]{1,0:T(8,128)(2,1)S(1)}, u32[]{:S(2)}, u32[]{:S(2)}) %collective-permute-start.66) | collective-permute-done | bytes 786464 | tf_op jit(solution)/shard_map/ppermute | solution.py:819
  861.8 29.6 %collective-permute-done.49.refs_5_ = bf16[384,1024]{1,0:T(8,128)(2,1)} collective-permute-done((bf16[384,1024]{1,0:T(8,128)(2,1)}, bf16[384,1024]{1,0:T(8,128)(2,1)}, u32[]{:S(2)}, u32[]{:S(2)}) %collective-permute-start.49) | collective-permute-done | bytes 786464 | tf_op jit(solution)/shard_map/ppermute | solution.py:819
  897.1 20.9 %collective-permute-done.50.refs_6_ = bf16[384,1024]{1,0:T(8,128)(2,1)} collective-permute-done((bf16[384,1024]{1,0:T(8,128)(2,1)}, bf16[384,1024]{1,0:T(8,128)(2,1)}, u32[]{:S(2)}, u32[]{:S(2)}) %collective-permute-start.50) | collective-permute-done | bytes 786464 | tf_op jit(solution)/shard_map/ppermute | solution.py:819
  918.5 27.4 %collective-permute-done.51.refs_7_ = bf16[384,1024]{1,0:T(8,128)(2,1)} collective-permute-done((bf16[384,1024]{1,0:T(8,128)(2,1)}, bf16[384,1024]{1,0:T(8,128)(2,1)}, u32[]{:S(2)}, u32[]{:S(2)}) %collective-permute-start.51) | collective-permute-done | bytes 786464 | tf_op jit(solution)/shard_map/ppermute | solution.py:819
  977.7 59.7 %collective-permute-done.77.refs_1_ = f32[264,1024]{1,0:T(8,128)} collective-permute-done((f32[264,1024]{1,0:T(8,128)}, f32[264,1024]{1,0:T(8,128)}, u32[]{:S(2)}, u32[]{:S(2)}) %collective-permute-start.77) | collective-permute-done | bytes 1081376 | tf_op jit(solution)/shard_map/ppermute | solution.py:819
  1037.9 64.4 %table_accum.1 = f32[100544,128]{1,0:T(8,128)} custom-call(s32[12288]{0:T(1024)} %fusion.143.where_ref, s32[160]{0:T(256)} %min.12.first_ref, bf16[384,1024]{1,0:T(8,128)(2,1)} %get-tuple-element.1290.refs_0_, bf16[384,1024]{1,0:T(8,128)(2,1)} %collective-permute-done.45.refs_1_, bf16[384,1024]{1,0:T(8,128)(2,1)} %collective-permute-done.46.refs_2_, ...), custom_call_target="tpu_custom_call" | custom-call | flops 49999998976 | bytes 100000000 | tf_op jit(solution)/shard_map/table_accum/pallas_call | solution.py:644
  (433 shorter events, 334.8 us)
Async XLA Ops:
  7.2 243.7 %all-gather.4.cloned.1.call-start = ((), (), s32[]{:S(2)}) async-start(), calls=%async_computation.3 | async-start | bytes 7077888 | tf_op jit(solution)/shard_map/all_gather | solution.py:816
  9.4 302.1 %all-gather.6.cloned.1.call-start = ((), (), s32[]{:S(2)}) async-start(), calls=%async_computation.4 | async-start | bytes 20054016 | tf_op jit(solution)/shard_map/all_gather | solution.py:839
  26.3 732.4 %reduce-scatter.4.cloned.1.call-start = ((), (), s32[]{:S(2)}) async-start(), calls=%async_computation.5 | async-start | bytes 2654208 | tf_op jit(solution)/shard_map/reduce_scatter | solution.py:1032
  75.8 93.7 %collective-permute-start.34 = (bf16[704,1024]{1,0:T(8,128)(2,1)}, bf16[704,1024]{1,0:T(8,128)(2,1)}, u32[]{:S(2)}, u32[]{:S(2)}) collective-permute-start(bf16[704,1024]{1,0:T(8,128)(2,1)} %get-tuple-element.1588), channel_id=1, source_target_pairs={{0,8},{4,12},{8,0},{12,4},{1,9},{5,13},{9,1},{13,5},{2,10},{6,14},... | collective-permute-start | bytes 4325384 | tf_op jit(solution)/shard_map/ppermute | solution.py:819
  78.1 91.4 %collective-permute-start.35 = (bf16[704,1024]{1,0:T(8,128)(2,1)}, bf16[704,1024]{1,0:T(8,128)(2,1)}, u32[]{:S(2)}, u32[]{:S(2)}) collective-permute-start(bf16[704,1024]{1,0:T(8,128)(2,1)} %get-tuple-element.1586), channel_id=1, source_target_pairs={{0,12},{4,8},{8,4},{12,0},{1,13},{5,9},{9,5},{13,1},{2,14},{6,10},... | collective-permute-start | bytes 4325384 | tf_op jit(solution)/shard_map/ppermute | solution.py:819
  79.5 89.9 %collective-permute-start.33 = (bf16[704,1024]{1,0:T(8,128)(2,1)}, bf16[704,1024]{1,0:T(8,128)(2,1)}, u32[]{:S(2)}, u32[]{:S(2)}) collective-permute-start(bf16[704,1024]{1,0:T(8,128)(2,1)} %get-tuple-element.1587), channel_id=1, source_target_pairs={{0,4},{4,0},{8,12},{12,8},{1,5},{5,1},{9,13},{13,9},{2,6},{6,2},{1... | collective-permute-start | bytes 4325384 | tf_op jit(solution)/shard_map/ppermute | solution.py:819
  84.8 79.7 %collective-permute-start.37 = (bf16[1792]{0:T(1024)(128)(2,1)S(1)}, bf16[1792]{0:T(1024)(128)(2,1)S(1)}, u32[]{:S(2)}, u32[]{:S(2)}) collective-permute-start(bf16[1792]{0:T(1024)(128)(2,1)S(1)} %dynamic-update-slice.33), channel_id=1, source_target_pairs={{0,8},{4,12},{8,0},{12,4},{1,9},{5,13},{9,1},{13,5},{2,10},{6,14},... | collective-permute-start | bytes 10760 | tf_op jit(solution)/shard_map/ppermute | solution.py:819
  85.2 82.9 %collective-permute-start.36 = (bf16[1792]{0:T(1024)(128)(2,1)S(1)}, bf16[1792]{0:T(1024)(128)(2,1)S(1)}, u32[]{:S(2)}, u32[]{:S(2)}) collective-permute-start(bf16[1792]{0:T(1024)(128)(2,1)S(1)} %dynamic-update-slice.33), channel_id=1, source_target_pairs={{0,4},{4,0},{8,12},{12,8},{1,5},{5,1},{9,13},{13,9},{2,6},{6,2},{1... | collective-permute-start | bytes 10760 | tf_op jit(solution)/shard_map/ppermute | solution.py:819
  171.0 68.1 %collective-permute-start.41 = (bf16[2,256,1024]{2,1,0:T(8,128)(2,1)}, bf16[2,256,1024]{2,1,0:T(8,128)(2,1)}, u32[]{:S(2)}, u32[]{:S(2)}) collective-permute-start(bf16[2,256,1024]{2,1,0:T(8,128)(2,1)} %get-tuple-element.1278), channel_id=1, source_target_pairs={{0,12},{4,8},{8,4},{12,0},{1,13},{5,9},{9,5},{13,1},{2,14},{6,10},... | collective-permute-start | bytes 3145736 | tf_op jit(solution)/shard_map/ppermute | solution.py:819
  553.5 337.9 %reduce-scatter.8.cloned.1.call-start = ((), (), s32[]{:S(2)}) async-start(), calls=%async_computation.8 | async-start | bytes 19464192 | tf_op jit(solution)/shard_map/reduce_scatter | solution.py:986
  584.4 379.9 %reduce-scatter.6.cloned.1.call-start = ((), (), s32[]{:S(2)}) async-start(), calls=%async_computation.7 | async-start | bytes 9732096 | tf_op jit(solution)/shard_map/reduce_scatter | solution.py:1034
  631.5 470.9 %all-gather.8.cloned.1.call-start = ((), (), s32[]{:S(2)}) async-start(), calls=%async_computation.6 | async-start | bytes 5013504 | tf_op jit(solution)/shard_map/all_gather | solution.py:1036
  645.7 84.0 %collective-permute-start.67 = (bf16[384,1024]{1,0:T(8,128)(2,1)}, bf16[384,1024]{1,0:T(8,128)(2,1)}, u32[]{:S(2)}, u32[]{:S(2)}) collective-permute-start(bf16[384,1024]{1,0:T(8,128)(2,1)} %get-tuple-element.1298.refs_16_), channel_id=1, source_target_pairs={{0,1},{1,0},{2,3},{3,2},{4,5},{5,4},{6,7},{7,6},{8,9},{9,8},{10,11... | collective-permute-start | bytes 2359304 | tf_op jit(solution)/shard_map/ppermute | solution.py:819
  652.6 79.1 %collective-permute-start.63 = (bf16[384,1024]{1,0:T(8,128)(2,1)}, bf16[384,1024]{1,0:T(8,128)(2,1)}, u32[]{:S(2)}, u32[]{:S(2)}) collective-permute-start(bf16[384,1024]{1,0:T(8,128)(2,1)} %get-tuple-element.1298.refs_16_), channel_id=1, source_target_pairs={{0,2},{2,0},{1,3},{3,1},{4,6},{6,4},{5,7},{7,5},{8,10},{10,8},{9,1... | collective-permute-start | bytes 2359304 | tf_op jit(solution)/shard_map/ppermute | solution.py:819
  758.5 69.7 %collective-permute-start.44 = (bf16[2,256,1024]{2,1,0:T(8,128)(2,1)}, bf16[2,256,1024]{2,1,0:T(8,128)(2,1)}, u32[]{:S(2)}, u32[]{:S(2)}) collective-permute-start(bf16[2,256,1024]{2,1,0:T(8,128)(2,1)} %get-tuple-element.1284), channel_id=1, source_target_pairs={{0,12},{4,8},{8,4},{12,0},{1,13},{5,9},{9,5},{13,1},{2,14},{6,10},... | collective-permute-start | bytes 3145736 | tf_op jit(solution)/shard_map/ppermute | solution.py:819
  758.7 69.5 %collective-permute-start.68 = (bf16[384,1024]{1,0:T(8,128)(2,1)}, bf16[384,1024]{1,0:T(8,128)(2,1)}, u32[]{:S(2)}, u32[]{:S(2)}) collective-permute-start(bf16[384,1024]{1,0:T(8,128)(2,1)} %collective-permute-done.60.refs_17_), channel_id=1, source_target_pairs={{0,1},{1,0},{2,3},{3,2},{4,5},{5,4},{6,7},{7,6},{8,9},{9,8},{10,11... | collective-permute-start | bytes 2359304 | tf_op jit(solution)/shard_map/ppermute | solution.py:819
  760.4 69.3 %collective-permute-start.64 = (bf16[384,1024]{1,0:T(8,128)(2,1)}, bf16[384,1024]{1,0:T(8,128)(2,1)}, u32[]{:S(2)}, u32[]{:S(2)}) collective-permute-start(bf16[384,1024]{1,0:T(8,128)(2,1)} %collective-permute-done.60.refs_17_), channel_id=1, source_target_pairs={{0,2},{2,0},{1,3},{3,1},{4,6},{6,4},{5,7},{7,5},{8,10},{10,8},{9,1... | collective-permute-start | bytes 2359304 | tf_op jit(solution)/shard_map/ppermute | solution.py:819
  860.1 85.7 %collective-permute-start.51 = (bf16[384,1024]{1,0:T(8,128)(2,1)}, bf16[384,1024]{1,0:T(8,128)(2,1)}, u32[]{:S(2)}, u32[]{:S(2)}) collective-permute-start(bf16[384,1024]{1,0:T(8,128)(2,1)} %collective-permute-done.47.refs_3_), channel_id=1, source_target_pairs={{0,2},{2,0},{1,3},{3,1},{4,6},{6,4},{5,7},{7,5},{8,10},{10,8},{9,1... | collective-permute-start | bytes 2359304 | tf_op jit(solution)/shard_map/ppermute | solution.py:819
  891.4 146.5 %collective-permute-start.82 = (f32[528,1024]{1,0:T(8,128)}, f32[528,1024]{1,0:T(8,128)}, u32[]{:S(2)}, u32[]{:S(2)}) collective-permute-start(f32[528,1024]{1,0:T(8,128)} %reduce-scatter.8.cloned.1.call-done.refs_0_), channel_id=1, source_target_pairs={{0,2},{2,0},{1,3},{3,1},{4,6},{6,4},{5,7},{7,5},{8,10},{10,8},{9,1... | collective-permute-start | bytes 6488072 | tf_op jit(solution)/shard_map/ppermute | solution.py:819
  964.3 73.1 %collective-permute-start.77 = (f32[264,1024]{1,0:T(8,128)}, f32[264,1024]{1,0:T(8,128)}, u32[]{:S(2)}, u32[]{:S(2)}) collective-permute-start(f32[264,1024]{1,0:T(8,128)} %reduce-scatter.6.cloned.1.call-done.refs_0_), channel_id=1, source_target_pairs={{0,2},{2,0},{1,3},{3,1},{4,6},{6,4},{5,7},{7,5},{8,10},{10,8},{9,1... | collective-permute-start | bytes 3244040 | tf_op jit(solution)/shard_map/ppermute | solution.py:819
  977.2 134.0 %collective-permute-start.78 = (f32[264,1024]{1,0:T(8,128)}, f32[264,1024]{1,0:T(8,128)}, u32[]{:S(2)}, u32[]{:S(2)}) collective-permute-start(f32[264,1024]{1,0:T(8,128)} %reduce-scatter.6.cloned.1.call-done.refs_0_), channel_id=1, source_target_pairs={{0,1},{1,0},{2,3},{3,2},{4,5},{5,4},{6,7},{7,6},{8,9},{9,8},{10,11... | collective-permute-start | bytes 3244040 | tf_op jit(solution)/shard_map/ppermute | solution.py:819
  1037.4 73.9 %collective-permute-start.79 = (f32[264,1024]{1,0:T(8,128)}, f32[264,1024]{1,0:T(8,128)}, u32[]{:S(2)}, u32[]{:S(2)}) collective-permute-start(f32[264,1024]{1,0:T(8,128)} %collective-permute-done.77.refs_1_), channel_id=1, source_target_pairs={{0,1},{1,0},{2,3},{3,2},{4,5},{5,4},{6,7},{7,6},{8,9},{9,8},{10,11... | collective-permute-start | bytes 3244040 | tf_op jit(solution)/shard_map/ppermute | solution.py:819
  1037.4 83.2 %collective-permute-start.83 = (f32[528,1024]{1,0:T(8,128)}, f32[528,1024]{1,0:T(8,128)}, u32[]{:S(2)}, u32[]{:S(2)}) collective-permute-start(f32[528,1024]{1,0:T(8,128)} %reduce-scatter.8.cloned.1.call-done.refs_0_), channel_id=1, source_target_pairs={{0,1},{1,0},{2,3},{3,2},{4,5},{5,4},{6,7},{7,6},{8,9},{9,8},{10,11... | collective-permute-start | bytes 6488072 | tf_op jit(solution)/shard_map/ppermute | solution.py:819
  1037.9 82.7 %collective-permute-start.84 = (f32[528,1024]{1,0:T(8,128)}, f32[528,1024]{1,0:T(8,128)}, u32[]{:S(2)}, u32[]{:S(2)}) collective-permute-start(f32[528,1024]{1,0:T(8,128)} %collective-permute-done.82.refs_1_), channel_id=1, source_target_pairs={{0,1},{1,0},{2,3},{3,2},{4,5},{5,4},{6,7},{7,6},{8,9},{9,8},{10,11... | collective-permute-start | bytes 6488072 | tf_op jit(solution)/shard_map/ppermute | solution.py:819
  (82 other events, 3510.7 us)
Sparse Core Ops, SparseCore 0:
  9.8 44.5 all-gather.3
  56.6 159.4 all-gather.5
  553.6 40.8 reduce-scatter.3
  599.4 229.4 reduce-scatter.7
  833.0 131.1 reduce-scatter.5
  966.3 51.7 all-gather.7
